TPU v7x, 32 devices: a whole 2x2x4 slice. The times are simulated.
32 devices in a mesh: ctx: 8 (over z, y), fsdp: 4 (over x, core).
Axes of the slice: x: 2, y: 2, z: 4, core: 2. Of those that a mesh axis runs over, the one named last changes fastest.
Arguments:
- hidden: bfloat16 [4, 1024, 1536], P('fsdp', 'ctx'), may hold values from -6 to 6
- routes: int32 [4, 1024, 8], P('fsdp', 'ctx'), may hold values from 0 to 31, all different within a row; in each aligned block of 128 rows (0 to 127, 128 to 255, ..., all dimensions but the last counted through in order) at most 40 rows name the same one
- attn_norm: bfloat16 [1536], P(('ctx', 'fsdp')), may hold values from 0.5 to 1.5
- ffn_norm: bfloat16 [1536], P(('ctx', 'fsdp')), may hold values from 0.5 to 1.5
- w_q: bfloat16 [1536, 1536], P(('ctx', 'fsdp')), may hold values from -0.625 to 0.625
- key_weight: bfloat16 [1536, 512], P(('ctx', 'fsdp')), may hold values from -0.625 to 0.625
- value_weight: bfloat16 [1536, 512], P(('ctx', 'fsdp')), may hold values from -0.15625 to 0.15625
- w_o: bfloat16 [1536, 1536], P(('ctx', 'fsdp')), may hold values from -1.75 to 1.75
- router: bfloat16 [1536, 32], P(('ctx', 'fsdp')), may hold values from -0.3125 to 0.3125
- expert_in: bfloat16 [32, 1536, 1024], P('ctx', 'fsdp'), may hold values from -0.15625 to 0.15625
- expert_out: bfloat16 [32, 1536, 512], P('ctx', 'fsdp'), may hold values from -0.25 to 0.25
- cotangent: float32 [4, 1024, 1536], P('fsdp', 'ctx'), may hold values from -6 to 6
Outputs:
- layer_out: bfloat16 [4, 1024, 1536], P('fsdp', 'ctx')
- grad_hidden: float32 [4, 1024, 1536], P('fsdp', 'ctx')
- grad_attn_norm: float32 [1536], P(('ctx', 'fsdp'))
- grad_ffn_norm: float32 [1536], P(('ctx', 'fsdp'))
- grad_w_q: float32 [1536, 1536], P(('ctx', 'fsdp'))
- grad_w_k: float32 [1536, 512], P(('ctx', 'fsdp'))
- grad_w_v: float32 [1536, 512], P(('ctx', 'fsdp'))
- grad_w_o: float32 [1536, 1536], P(('ctx', 'fsdp'))
- grad_router: float32 [1536, 32], P(('ctx', 'fsdp'))
- grad_expert_in: float32 [32, 1536, 1024], P('ctx', 'fsdp')
- grad_expert_out: float32 [32, 1536, 512], P('ctx', 'fsdp')
Inputs may be any that keep to these rules, and one draw needn't show every extreme that they name: `routes`: in the tokens of one block of 128, no expert is named more than 40 times, a bound that some block reaches.
All inputs are finite; a program needn't handle non-finite values.
Results may differ from a plain program's by a relative error of at most 0.033.
Values may be sent and summed in bfloat16 or wider, within the bound.
A program may use at most 256 MiB of HBM per device.

v0:
```python
import jax
import jax.numpy as jnp
from jax import lax
from jax.sharding import PartitionSpec as P

MODEL_WIDTH = 1536
QUERY_HEADS = 24
KEY_VALUE_HEADS = 8
HEAD_SIZE = 64
EXPERT_HIDDEN = 512
EXPERT_COUNT = 32
TOP = 8
CAP = 40


norm_eps = 1e-06
attn_scale = 0.015625
rope_base = 10000.0
masked_logits = -1e30


def rope_tables(positions):
    half = HEAD_SIZE // 2
    frequency = jnp.power(
        jnp.float32(rope_base), -2.0 * jnp.arange(half, dtype=jnp.float32) / HEAD_SIZE
    )
    angle = positions.astype(jnp.float32)[:, None] * frequency[None, :]
    return (jnp.cos(angle)[:, None, :], jnp.sin(angle)[:, None, :])


def rotate_pairs(value_tensor, cosine_table, sine_table):
    half = value_tensor.shape[-1] // 2
    first = value_tensor[..., :half]
    second = value_tensor[..., half:]
    return jnp.concatenate(
        [first * cosine_table - second * sine_table, second * cosine_table + first * sine_table],
        axis=-1,
    )


def rms_forward(wide, gain):
    inverse = lax.rsqrt(jnp.mean(wide * wide, axis=-1, keepdims=True) + norm_eps)
    unit = wide * inverse
    return (unit, inverse, (unit * gain.astype(jnp.float32)).astype(jnp.bfloat16))


def rms_backward(grad, unit, inverse, gain):
    scaled = grad * gain.astype(jnp.float32)
    back = inverse * (scaled - unit * jnp.mean(scaled * unit, axis=-1, keepdims=True))
    return (back, jnp.sum(grad * unit, axis=0))


def piece_scores(query_rows, key_section, positions):
    token_count = key_section.shape[0]
    key_tensor = key_section.reshape(token_count, KEY_VALUE_HEADS, HEAD_SIZE)
    scores = (
        jnp.einsum("tkgd,nkd->kgtn", query_rows, key_tensor, preferred_element_type=jnp.float32)
        * attn_scale
    )
    visible = jnp.arange(token_count, dtype=jnp.int32)[None, :] <= positions[:, None]
    return (jnp.where(visible, scores, masked_logits), visible, key_tensor)


def local(
    hidden,
    routes,
    attn_norm,
    ffn_norm,
    w_q,
    key_weight,
    value_weight,
    w_o,
    router,
    expert_in,
    expert_out,
    cotangent,
):
    token_rows = hidden.shape[1]
    query_group = QUERY_HEADS // KEY_VALUE_HEADS
    ctx_size = lax.axis_size("ctx")
    sequence_length = token_rows * ctx_size
    positions = lax.axis_index("ctx") * token_rows + jnp.arange(token_rows, dtype=jnp.int32)
    cosine_table, sine_table = rope_tables(positions)
    contract_rows = (((0,), (0,)), ((), ()))
    contract_cols = (((1,), (1,)), ((), ()))
    layer = (
        lax.all_gather(attn_norm, ("ctx", "fsdp"), axis=0, tiled=True),
        lax.all_gather(ffn_norm, ("ctx", "fsdp"), axis=0, tiled=True),
        lax.all_gather(w_q, ("ctx", "fsdp"), axis=0, tiled=True),
        lax.all_gather(key_weight, ("ctx", "fsdp"), axis=0, tiled=True),
        lax.all_gather(value_weight, ("ctx", "fsdp"), axis=0, tiled=True),
        lax.all_gather(w_o, ("ctx", "fsdp"), axis=0, tiled=True),
        lax.all_gather(router, ("ctx", "fsdp"), axis=0, tiled=True),
    )
    attn_gain, ffn_gain, query_w, key_weight_matrix, value_w, output_w, router_w = layer
    experts = (
        lax.all_gather(expert_in, "fsdp", axis=1, tiled=True),
        lax.all_gather(expert_out, "fsdp", axis=1, tiled=True),
    )
    weight_in, weight_out = experts
    wide = hidden[0].astype(jnp.float32)
    attn_unit, inverse_one, attention_input = rms_forward(wide, attn_gain)
    query_linear = jnp.dot(attention_input, query_w, preferred_element_type=jnp.float32).reshape(
        token_rows, QUERY_HEADS, HEAD_SIZE
    )
    query_rows = (
        rotate_pairs(query_linear, cosine_table, sine_table)
        .astype(jnp.bfloat16)
        .reshape(token_rows, KEY_VALUE_HEADS, query_group, HEAD_SIZE)
    )
    key_linear = jnp.dot(
        attention_input, key_weight_matrix, preferred_element_type=jnp.float32
    ).reshape(token_rows, KEY_VALUE_HEADS, HEAD_SIZE)
    key_matrix_rows = (
        rotate_pairs(key_linear, cosine_table, sine_table)
        .astype(jnp.bfloat16)
        .reshape(token_rows, KEY_VALUE_HEADS * HEAD_SIZE)
    )
    value_rows = jnp.dot(attention_input, value_w, preferred_element_type=jnp.float32).astype(
        jnp.bfloat16
    )
    init_state = (
        jnp.full((KEY_VALUE_HEADS, query_group, token_rows), masked_logits, jnp.float32),
        jnp.zeros((KEY_VALUE_HEADS, query_group, token_rows), jnp.float32),
        jnp.zeros((KEY_VALUE_HEADS, query_group, token_rows, HEAD_SIZE), jnp.float32),
    )
    key_section = lax.all_gather(key_matrix_rows, "ctx", axis=0, tiled=True)
    value_section = lax.all_gather(value_rows, "ctx", axis=0, tiled=True)

    def compute(current):
        best, total, weighted = current
        scores, visible, key_tensor = piece_scores(query_rows, key_section, positions)
        value_tensor = value_section.reshape(value_section.shape[0], KEY_VALUE_HEADS, HEAD_SIZE)
        new_best = jnp.maximum(best, jnp.max(scores, axis=-1))
        weights = jnp.where(visible, jnp.exp(scores - new_best[..., None]), 0.0)
        total = jnp.sum(weights, axis=-1)
        weighted = jnp.einsum(
            "kgtn,nkd->kgtd",
            weights.astype(jnp.bfloat16),
            value_tensor,
            preferred_element_type=jnp.float32,
        )
        return (new_best, total, weighted)

    best, total, weighted = lax.cond(
        jnp.int32(0) <= positions[-1], compute, lambda current: current, init_state
    )
    log_sum_rows = best + jnp.log(total)
    attention_output = (
        jnp.transpose(weighted / total[..., None], (2, 0, 1, 3))
        .reshape(token_rows, QUERY_HEADS * HEAD_SIZE)
        .astype(jnp.bfloat16)
    )
    mixed = wide + jnp.dot(attention_output, output_w, preferred_element_type=jnp.float32)
    ffn_unit, inverse_two, ffn_in = rms_forward(mixed, ffn_gain)
    logits = jnp.dot(ffn_in, router_w, preferred_element_type=jnp.float32)
    route = routes[0]
    indicator = (route[:, :, None] == jnp.arange(EXPERT_COUNT, dtype=jnp.int32)).astype(jnp.float32)
    chosen = jnp.sum(indicator * logits[:, None, :], axis=-1)
    gates = jax.nn.softmax(chosen, axis=-1)
    flat_route = route.reshape(-1)
    counter = (flat_route[:, None] == jnp.arange(EXPERT_COUNT, dtype=jnp.int32)).astype(jnp.int32)
    slot = jnp.sum(counter * (jnp.cumsum(counter, axis=0) - 1), axis=1)
    target = flat_route * CAP + slot
    owner = (
        jnp.full((EXPERT_COUNT * CAP,), token_rows * TOP, jnp.int32)
        .at[target]
        .set(jnp.arange(token_rows * TOP, dtype=jnp.int32))
    )
    ffn_pad = jnp.concatenate([ffn_in, jnp.zeros((1, MODEL_WIDTH), jnp.bfloat16)], axis=0)
    local_experts = weight_in.shape[0]
    outgoing = ffn_pad[owner // TOP].reshape(ctx_size, local_experts, CAP, MODEL_WIDTH)
    received = lax.all_to_all(outgoing, "ctx", split_axis=0, concat_axis=2, tiled=True)[0]
    act = jnp.einsum("erd,edf->erf", received, weight_in, preferred_element_type=jnp.float32)
    gate_part = act[..., :EXPERT_HIDDEN]
    up_part = act[..., EXPERT_HIDDEN:]
    sigma = jax.nn.sigmoid(gate_part)
    inner = (gate_part * sigma * up_part).astype(jnp.bfloat16)
    produced = jnp.einsum(
        "erf,edf->erd", inner, weight_out, preferred_element_type=jnp.float32
    ).astype(jnp.bfloat16)
    returned = lax.all_to_all(
        produced[None], "ctx", split_axis=2, concat_axis=0, tiled=True
    ).reshape(EXPERT_COUNT * CAP, MODEL_WIDTH)
    picked = returned[target].reshape(token_rows, TOP, MODEL_WIDTH)
    layer_out = (mixed + jnp.sum(gates[..., None] * picked, axis=1)).astype(jnp.bfloat16)
    cot = cotangent[0]
    layer = (
        lax.all_gather(attn_norm, ("ctx", "fsdp"), axis=0, tiled=True),
        lax.all_gather(ffn_norm, ("ctx", "fsdp"), axis=0, tiled=True),
        lax.all_gather(w_q, ("ctx", "fsdp"), axis=0, tiled=True),
        lax.all_gather(key_weight, ("ctx", "fsdp"), axis=0, tiled=True),
        lax.all_gather(value_weight, ("ctx", "fsdp"), axis=0, tiled=True),
        lax.all_gather(w_o, ("ctx", "fsdp"), axis=0, tiled=True),
        lax.all_gather(router, ("ctx", "fsdp"), axis=0, tiled=True),
    )
    attn_gain, ffn_gain, query_w, key_weight_matrix, value_w, output_w, router_w = layer
    experts = (
        lax.all_gather(expert_in, "fsdp", axis=1, tiled=True),
        lax.all_gather(expert_out, "fsdp", axis=1, tiled=True),
    )
    weight_in, weight_out = experts
    grad_gate = jnp.sum(cot[:, None, :] * picked, axis=-1)
    slot_grads = (
        (gates[..., None] * cot[:, None, :])
        .astype(jnp.bfloat16)
        .reshape(token_rows * TOP, MODEL_WIDTH)
    )
    slot_pad = jnp.concatenate([slot_grads, jnp.zeros((1, MODEL_WIDTH), jnp.bfloat16)], axis=0)
    grad_outgoing = slot_pad[owner].reshape(ctx_size, local_experts, CAP, MODEL_WIDTH)
    grad_received = lax.all_to_all(grad_outgoing, "ctx", split_axis=0, concat_axis=2, tiled=True)[0]
    grad_w_out = jnp.einsum(
        "erd,erf->edf", grad_received, inner, preferred_element_type=jnp.float32
    )
    grad_inner = jnp.einsum(
        "erd,edf->erf", grad_received, weight_out, preferred_element_type=jnp.float32
    )
    grad_act = jnp.concatenate(
        [
            grad_inner * up_part * sigma * (1.0 + gate_part * (1.0 - sigma)),
            grad_inner * gate_part * sigma,
        ],
        axis=-1,
    ).astype(jnp.bfloat16)
    grad_w_in = jnp.einsum("erd,erf->edf", received, grad_act, preferred_element_type=jnp.float32)
    grad_rows = jnp.einsum(
        "erf,edf->erd", grad_act, weight_in, preferred_element_type=jnp.float32
    ).astype(jnp.bfloat16)
    grad_back = lax.all_to_all(
        grad_rows[None], "ctx", split_axis=2, concat_axis=0, tiled=True
    ).reshape(EXPERT_COUNT * CAP, MODEL_WIDTH)
    grad_expert_in, grad_expert_out = (
        lax.psum_scatter(
            grad_w_in.astype(jnp.bfloat16), "fsdp", scatter_dimension=1, tiled=True
        ).astype(jnp.float32),
        lax.psum_scatter(
            grad_w_out.astype(jnp.bfloat16), "fsdp", scatter_dimension=1, tiled=True
        ).astype(jnp.float32),
    )
    grad_chosen = gates * (grad_gate - jnp.sum(gates * grad_gate, axis=-1, keepdims=True))
    grad_logits = jnp.sum(indicator * grad_chosen[..., None], axis=1).astype(jnp.bfloat16)
    grad_router_part = lax.dot_general(
        ffn_in, grad_logits, contract_rows, preferred_element_type=jnp.float32
    )
    grad_ffn_in = lax.dot_general(
        grad_logits, router_w, contract_cols, preferred_element_type=jnp.float32
    )
    grad_ffn_in = grad_ffn_in + jnp.sum(
        grad_back[target].reshape(token_rows, TOP, MODEL_WIDTH), axis=1, dtype=jnp.float32
    )
    back_two, grad_ffn_gain = rms_backward(grad_ffn_in, ffn_unit, inverse_two, ffn_gain)
    grad_mixed = cot + back_two
    grad_attn = grad_mixed.astype(jnp.bfloat16)
    grad_wo_part = lax.dot_general(
        attention_output, grad_attn, contract_rows, preferred_element_type=jnp.float32
    )
    attention_output_gradient = lax.dot_general(
        grad_attn, output_w, contract_cols, preferred_element_type=jnp.float32
    ).astype(jnp.bfloat16)
    head_gradient = attention_output_gradient.reshape(
        token_rows, KEY_VALUE_HEADS, query_group, HEAD_SIZE
    )
    delta_rows = jnp.sum(
        head_gradient.astype(jnp.float32)
        * attention_output.reshape(token_rows, KEY_VALUE_HEADS, query_group, HEAD_SIZE).astype(
            jnp.float32
        ),
        axis=-1,
    )
    delta_rows = jnp.transpose(delta_rows, (1, 2, 0))
    init_back = (
        jnp.zeros((token_rows, KEY_VALUE_HEADS, query_group, HEAD_SIZE), jnp.float32),
        jnp.zeros((sequence_length, 2 * KEY_VALUE_HEADS * HEAD_SIZE), jnp.float32),
    )
    attend_key_section = lax.all_gather(key_matrix_rows, "ctx", axis=0, tiled=True)
    attend_value_section = lax.all_gather(value_rows, "ctx", axis=0, tiled=True)

    def compute(current):
        token_count = attend_key_section.shape[0]
        scores, visible, key_tensor = piece_scores(query_rows, attend_key_section, positions)
        value_tensor = attend_value_section.reshape(token_count, KEY_VALUE_HEADS, HEAD_SIZE)
        weights_full = jnp.where(visible, jnp.exp(scores - log_sum_rows[..., None]), 0.0)
        grad_probs = jnp.einsum(
            "tkgd,nkd->kgtn", head_gradient, value_tensor, preferred_element_type=jnp.float32
        )
        grad_scores = (weights_full * (grad_probs - delta_rows[..., None])).astype(jnp.bfloat16)
        grad_query = attn_scale * jnp.einsum(
            "kgtn,nkd->tkgd", grad_scores, key_tensor, preferred_element_type=jnp.float32
        )
        key_portion = attn_scale * jnp.einsum(
            "kgtn,tkgd->nkd", grad_scores, query_rows, preferred_element_type=jnp.float32
        )
        value_portion = jnp.einsum(
            "kgtn,tkgd->nkd",
            weights_full.astype(jnp.bfloat16),
            head_gradient,
            preferred_element_type=jnp.float32,
        )
        update = jnp.concatenate(
            [
                key_portion.reshape(token_count, KEY_VALUE_HEADS * HEAD_SIZE),
                value_portion.reshape(token_count, KEY_VALUE_HEADS * HEAD_SIZE),
            ],
            axis=1,
        )
        return (grad_query, update)

    grad_query, grad_keys_full = lax.cond(
        jnp.int32(0) <= positions[-1], compute, lambda current: current, init_back
    )
    local_gradients = lax.psum_scatter(
        grad_keys_full.astype(jnp.bfloat16), "ctx", scatter_dimension=0, tiled=True
    ).astype(jnp.float32)
    query_back = (
        rotate_pairs(
            grad_query.reshape(token_rows, QUERY_HEADS, HEAD_SIZE), cosine_table, -sine_table
        )
        .astype(jnp.bfloat16)
        .reshape(token_rows, QUERY_HEADS * HEAD_SIZE)
    )
    key_backward_rows = (
        rotate_pairs(
            local_gradients[:, : KEY_VALUE_HEADS * HEAD_SIZE].reshape(
                token_rows, KEY_VALUE_HEADS, HEAD_SIZE
            ),
            cosine_table,
            -sine_table,
        )
        .astype(jnp.bfloat16)
        .reshape(token_rows, KEY_VALUE_HEADS * HEAD_SIZE)
    )
    value_backward_rows = local_gradients[:, KEY_VALUE_HEADS * HEAD_SIZE :].astype(jnp.bfloat16)
    grad_wq_part = lax.dot_general(
        attention_input, query_back, contract_rows, preferred_element_type=jnp.float32
    )
    grad_wk_part = lax.dot_general(
        attention_input, key_backward_rows, contract_rows, preferred_element_type=jnp.float32
    )
    grad_wv_part = lax.dot_general(
        attention_input, value_backward_rows, contract_rows, preferred_element_type=jnp.float32
    )
    grad_attn_in = lax.dot_general(
        query_back, query_w, contract_cols, preferred_element_type=jnp.float32
    )
    grad_attn_in = grad_attn_in + lax.dot_general(
        key_backward_rows, key_weight_matrix, contract_cols, preferred_element_type=jnp.float32
    )
    grad_attn_in = grad_attn_in + lax.dot_general(
        value_backward_rows, value_w, contract_cols, preferred_element_type=jnp.float32
    )
    back_one, grad_attn_gain = rms_backward(grad_attn_in, attn_unit, inverse_one, attn_gain)
    grad_input = grad_mixed + back_one
    partial_sums = (
        lax.psum_scatter(
            grad_attn_gain.astype(jnp.bfloat16), "ctx", scatter_dimension=0, tiled=True
        ).astype(jnp.float32),
        lax.psum_scatter(
            grad_ffn_gain.astype(jnp.bfloat16), "ctx", scatter_dimension=0, tiled=True
        ).astype(jnp.float32),
        lax.psum_scatter(
            grad_wq_part.astype(jnp.bfloat16), "ctx", scatter_dimension=0, tiled=True
        ).astype(jnp.float32),
        lax.psum_scatter(
            grad_wk_part.astype(jnp.bfloat16), "ctx", scatter_dimension=0, tiled=True
        ).astype(jnp.float32),
        lax.psum_scatter(
            grad_wv_part.astype(jnp.bfloat16), "ctx", scatter_dimension=0, tiled=True
        ).astype(jnp.float32),
        lax.psum_scatter(
            grad_wo_part.astype(jnp.bfloat16), "ctx", scatter_dimension=0, tiled=True
        ).astype(jnp.float32),
        lax.psum_scatter(
            grad_router_part.astype(jnp.bfloat16), "ctx", scatter_dimension=0, tiled=True
        ).astype(jnp.float32),
    )
    summed = (
        lax.psum_scatter(
            partial_sums[0].astype(jnp.bfloat16), "fsdp", scatter_dimension=0, tiled=True
        ).astype(jnp.float32),
        lax.psum_scatter(
            partial_sums[1].astype(jnp.bfloat16), "fsdp", scatter_dimension=0, tiled=True
        ).astype(jnp.float32),
        lax.psum_scatter(
            partial_sums[2].astype(jnp.bfloat16), "fsdp", scatter_dimension=0, tiled=True
        ).astype(jnp.float32),
        lax.psum_scatter(
            partial_sums[3].astype(jnp.bfloat16), "fsdp", scatter_dimension=0, tiled=True
        ).astype(jnp.float32),
        lax.psum_scatter(
            partial_sums[4].astype(jnp.bfloat16), "fsdp", scatter_dimension=0, tiled=True
        ).astype(jnp.float32),
        lax.psum_scatter(
            partial_sums[5].astype(jnp.bfloat16), "fsdp", scatter_dimension=0, tiled=True
        ).astype(jnp.float32),
        lax.psum_scatter(
            partial_sums[6].astype(jnp.bfloat16), "fsdp", scatter_dimension=0, tiled=True
        ).astype(jnp.float32),
    )
    return (
        layer_out[None],
        grad_input[None],
        summed[0],
        summed[1],
        summed[2],
        summed[3],
        summed[4],
        summed[5],
        summed[6],
        grad_expert_in,
        grad_expert_out,
    )


def solution(mesh):
    placed = (
        P("fsdp", "ctx", None),
        P("fsdp", "ctx", None),
        P(("ctx", "fsdp")),
        P(("ctx", "fsdp")),
        P(("ctx", "fsdp"), None),
        P(("ctx", "fsdp"), None),
        P(("ctx", "fsdp"), None),
        P(("ctx", "fsdp"), None),
        P(("ctx", "fsdp"), None),
        P("ctx", "fsdp", None),
        P("ctx", "fsdp", None),
        P("fsdp", "ctx", None),
    )
    return jax.shard_map(
        local,
        mesh=mesh,
        in_specs=placed,
        out_specs=(
            P("fsdp", "ctx", None),
            P("fsdp", "ctx", None),
            P(("ctx", "fsdp")),
            P(("ctx", "fsdp")),
            P(("ctx", "fsdp"), None),
            P(("ctx", "fsdp"), None),
            P(("ctx", "fsdp"), None),
            P(("ctx", "fsdp"), None),
            P(("ctx", "fsdp"), None),
            P("ctx", "fsdp", None),
            P("ctx", "fsdp", None),
        ),
        check_vma=False,
    )
```

profile of v0, /device:TPU:0, one launch (start us, length us, event | category | flops | bytes accessed | tf_op | source)
XLA Modules:
  0.0 1608.9 jit_solution(10384787486862988892)
XLA Ops:
  11.2 42.1 %all-reduce.8 = (bf16[1536]{0:T(1024)(128)(2,1)S(1)}, bf16[1536]{0:T(1024)(128)(2,1)S(1)}) all-reduce(bf16[1536]{0:T(1024)(128)(2,1)S(1)} %dynamic-update-slice, bf16[1536]{0:T(1024)(128)(2,1)S(1)} %dynamic-update-slice.1), channel_id=1, replica_groups=mesh['ctx'=8,'fsdp'=4] {'ctx','fsdp'}, use_global_device_ids=true, to_apply=%add.2 | all-reduce | flops 3072 | bytes 12288
  55.3 13.3 all-gather.10.cloned.1.call-done
  71.7 53.5 %all-gather.16.cloned.1.call-done = bf16[1536,512]{1,0:T(8,128)(2,1)} async-done(((bf16[48,512]{1,0:T(8,128)(2,1)}), bf16[1536,512]{1,0:T(8,128)(2,1)}) %all-gather.16.cloned.1.call-update) | async-done | bytes 1572880 | tf_op jit(solution)/shard_map/all_gather | solution.py:91
  130.9 9.0 reduce-window.6
  140.4 4.3 scatter_custom_fusion
  144.8 45.9 %all-gather.14.cloned.1.call-done = bf16[1536,1536]{1,0:T(8,128)(2,1)} async-done(((bf16[48,1536]{1,0:T(8,128)(2,1)}), bf16[1536,1536]{1,0:T(8,128)(2,1)}) %all-gather.14.cloned.1.call-update) | async-done | bytes 4718608 | tf_op jit(solution)/shard_map/all_gather | solution.py:89
  190.7 6.6 copy.111
  197.3 3.9 fusion.43
  202.2 28.8 %all-gather.12.cloned.1.call-done = bf16[1024,512]{0,1:T(8,128)(2,1)} async-done(((bf16[128,512]{0,1:T(8,128)(2,1)}), bf16[1024,512]{0,1:T(8,128)(2,1)}) %all-gather.12.cloned.1.call-update) | async-done | bytes 1048592 | tf_op jit(solution)/shard_map/all_gather | solution.py:127
  230.9 41.9 %all-gather.18.cloned.1.call-done = bf16[1024,512]{1,0:T(8,128)(2,1)} async-done(((bf16[128,512]{1,0:T(8,128)(2,1)}), bf16[1024,512]{1,0:T(8,128)(2,1)}) %all-gather.18.cloned.1.call-update) | async-done | bytes 1048592 | tf_op jit(solution)/shard_map/all_gather | solution.py:128
  272.8 16.3 %conditional.2 = (f32[8,3,128]{2,1,0:T(4,128)}, f32[8,3,128]{2,1,0:T(4,128)}, f32[8,3,128,64]{2,3,1,0:T(8,128)S(1)}, f32[8,3,128]{2,1,0:T(4,128)S(1)}) conditional(s32[]{:T(128)} %bitcast.29, () %tuple.32, (s32[128]{0:T(128)S(1)}, bf16[1024,512]{0,1:T(8,128)(2,1)}, bf16[128,8,3,64]{0,3,2,1:T(8,128)(2,1)}, bf16[1024,512]{1,0:T(8,128)(2,1)}) %tuple.33), branch_computations={%region_1.0_spmd, %region_2.5_spmd} | conditional | flops 846328832 | bytes 98271832 | solution.py:145
  272.9 3.2 fusion
  276.8 4.5 fusion.2
  281.8 6.4 fusion.3
  290.0 47.9 %all-gather.20.cloned.1.call-done = bf16[1536,1536]{1,0:T(8,128)(2,1)} async-done(((bf16[48,1536]{1,0:T(8,128)(2,1)}), bf16[1536,1536]{1,0:T(8,128)(2,1)}) %all-gather.20.cloned.1.call-update) | async-done | bytes 4718608 | tf_op jit(solution)/shard_map/all_gather | solution.py:92
  342.2 5.4 gather_fusion
  347.6 4.8 all-to-all-start
  353.2 109.0 %all-gather = bf16[32,48,32]{1,2,0:T(8,128)(2,1)S(1)} all-gather(bf16[1,48,32]{1,2,0:T(8,128)(2,1)S(1)} %bitcast.275), channel_id=1, replica_groups=mesh['ctx'=8,'fsdp'=4] {'ctx','fsdp'}, dimensions={0}, use_global_device_ids=true | all-gather | bytes 101376 | tf_op jit(solution)/shard_map/all_gather | solution.py:93
  463.8 5.5 gather_fusion.2
  469.3 8.8 all-to-all-start.2
  478.1 4.4 copy.120
  482.5 84.8 %all-to-all-done.2 = bf16[8,4,40,1536]{3,2,1,0:T(8,128)(2,1)} async-done(((bf16[8,4,40,1536]{3,2,1,0:T(8,128)(2,1)}), bf16[8,4,40,1536]{3,2,1,0:T(8,128)(2,1)}, u32[]{:S(2)}, u32[]{:S(2)}) %all-to-all-start.2) | async-done | bytes 3932192 | tf_op jit(solution)/shard_map/all_to_all | solution.py:211
  567.3 4.4 copy.126
  571.8 12.4 fusion.77
  584.1 9.4 multiply_convert_fusion.1
  593.6 12.1 fusion.25
  605.7 7.6 copy.127
  613.2 4.5 all-to-all-start.3
  617.8 5.0 fusion.24
  622.8 4.9 copy.121
  627.7 77.8 %all-to-all-done.3 = bf16[1,4,320,1536]{3,1,0,2:T(4,128)(2,1)} async-done(((bf16[1,4,320,1536]{3,1,0,2:T(4,128)(2,1)}), bf16[1,4,320,1536]{3,1,0,2:T(4,128)(2,1)}, u32[]{:S(2)}, u32[]{:S(2)}) %all-to-all-start.3) | async-done | bytes 3932192 | tf_op jit(solution)/shard_map/all_to_all | solution.py:229
  705.5 4.6 all-to-all-start.1
  710.1 4.9 copy.128
  715.0 9.4 gather_fusion.3
  727.4 69.6 %all-to-all-done.1 = bf16[1,4,320,1536]{3,1,0,2:T(4,128)(2,1)} async-done(((bf16[1,4,320,1536]{3,1,0,2:T(4,128)(2,1)}), bf16[1,4,320,1536]{3,1,0,2:T(4,128)(2,1)}, u32[]{:S(2)}, u32[]{:S(2)}) %all-to-all-start.1) | async-done | bytes 3932192 | tf_op jit(solution)/shard_map/all_to_all | solution.py:182
  797.0 4.9 copy.122
  801.9 9.9 gather_fusion.1
  811.8 4.0 fusion.22
  818.1 4.1 convolution_convert_fusion.8
  824.3 24.9 %conditional.3 = (bf16[1024,1024]{0,1:T(8,128)(2,1)}, f32[128,24,32]{0,2,1:T(8,128)}, f32[128,24,32]{0,2,1:T(8,128)}) conditional(s32[]{:T(128)} %bitcast.29, () %tuple.34, (s32[128]{0:T(128)S(1)}, bf16[1024,512]{0,1:T(8,128)(2,1)S(1)}, bf16[128,8,3,64]{0,3,2,1:T(8,128)(2,1)}, f32[8,3,128]{2,1,0:T(4,128)}, f32[8,3,128]{2,1,0:T(4,128)S(1)}, ...), branch_computations={%region_20.21_spmd, %region_21.22_spmd} | conditional | flops 2056588288 | bytes 127083088 | solution.py:308
  828.0 5.4 fusion.15
  835.0 7.3 fusion.10
  849.2 4.0 copy.141
  854.5 65.4 %reduce-scatter.40.cloned.1.call-done = bf16[128,1024]{1,0:T(8,128)(2,1)} async-done(((bf16[1024,1024]{1,0:T(8,128)(2,1)}), bf16[128,1024]{1,0:T(8,128)(2,1)}) %reduce-scatter.40.cloned.1.call-update) | async-done | bytes 262160
  926.2 3.6 convolution_convert_fusion.2
  930.9 3.6 convolution_convert_fusion.1
  934.5 50.4 %reduce-scatter.42.cloned.1.call-done = bf16[192,32]{1,0:T(8,128)(2,1)} async-done(((bf16[1536,32]{1,0:T(8,128)(2,1)}), bf16[192,32]{1,0:T(8,128)(2,1)}) %reduce-scatter.42.cloned.1.call-update) | async-done | bytes 12304
  984.9 8.1 convolution_convert_fusion.3
  993.1 60.5 %reduce-scatter.24.cloned.1.call-done = bf16[192,512]{1,0:T(8,128)(2,1)} async-done(((bf16[1536,512]{1,0:T(8,128)(2,1)}), bf16[192,512]{1,0:T(8,128)(2,1)}) %reduce-scatter.24.cloned.1.call-update) | async-done | bytes 196624 | tf_op jit(solution)/shard_map/reduce_scatter | solution.py:363
  1053.6 67.6 %reduce-scatter.28.cloned.1.call-done = bf16[192,512]{1,0:T(8,128)(2,1)} async-done(((bf16[1536,512]{1,0:T(8,128)(2,1)}), bf16[192,512]{1,0:T(8,128)(2,1)}) %reduce-scatter.28.cloned.1.call-update) | async-done | bytes 196624 | tf_op jit(solution)/shard_map/reduce_scatter | solution.py:366
  1121.2 98.1 %reduce-scatter.20.cloned.1.call-done = bf16[192,1536]{1,0:T(8,128)(2,1)} async-done(((bf16[1536,1536]{1,0:T(8,128)(2,1)}), bf16[192,1536]{1,0:T(8,128)(2,1)}) %reduce-scatter.20.cloned.1.call-update) | async-done | bytes 589840 | tf_op jit(solution)/shard_map/reduce_scatter | solution.py:360
  1219.4 98.8 %reduce-scatter.32.cloned.1.call-done = bf16[192,1536]{1,0:T(8,128)(2,1)} async-done(((bf16[1536,1536]{1,0:T(8,128)(2,1)}), bf16[192,1536]{1,0:T(8,128)(2,1)}) %reduce-scatter.32.cloned.1.call-update) | async-done | bytes 589840 | tf_op jit(solution)/shard_map/reduce_scatter | solution.py:369
  1318.5 12.0 convolution_convert_fusion
  1333.6 4.9 fusion.78
  1344.5 21.6 %all-reduce.9 = (bf16[1536]{0:T(1024)(128)(2,1)S(1)}, bf16[1536]{0:T(1024)(128)(2,1)S(1)}) all-reduce(bf16[1536]{0:T(1024)(128)(2,1)S(1)} %get-tuple-element.144, bf16[1536]{0:T(1024)(128)(2,1)S(1)} %copy-done.31), channel_id=3, replica_groups=mesh['ctx'=8,'fsdp'=4] {'ctx'}, use_global_device_ids=true, to_apply=%region_25.26.clone | all-reduce | flops 3072 | bytes 12288
  1366.4 6.5 all-reduce.10
  1375.2 25.6 %reduce-scatter.38.cloned.1.call-done = bf16[4,384,512]{2,1,0:T(8,128)(2,1)} async-done(((bf16[4,1536,512]{2,1,0:T(8,128)(2,1)}), bf16[4,384,512]{2,1,0:T(8,128)(2,1)}) %reduce-scatter.38.cloned.1.call-update) | async-done | bytes 1572880 | tf_op jit(solution)/shard_map/reduce_scatter | solution.py:236
  1400.8 3.5 convert_element_type.291
  1404.3 18.6 %reduce-scatter.26.cloned.1.call-done = bf16[48,512]{1,0:T(8,128)(2,1)} async-done(((bf16[192,512]{1,0:T(8,128)(2,1)}), bf16[48,512]{1,0:T(8,128)(2,1)}) %reduce-scatter.26.cloned.1.call-update) | async-done | bytes 49168 | tf_op jit(solution)/shard_map/reduce_scatter | solution.py:386
  1424.3 20.7 %reduce-scatter.30.cloned.1.call-done = bf16[48,512]{1,0:T(8,128)(2,1)} async-done(((bf16[192,512]{1,0:T(8,128)(2,1)}), bf16[48,512]{1,0:T(8,128)(2,1)}) %reduce-scatter.30.cloned.1.call-update) | async-done | bytes 49168 | tf_op jit(solution)/shard_map/reduce_scatter | solution.py:389
  1446.4 23.1 %reduce-scatter.22.cloned.1.call-done = bf16[48,1536]{1,0:T(8,128)(2,1)} async-done(((bf16[192,1536]{1,0:T(8,128)(2,1)}), bf16[48,1536]{1,0:T(8,128)(2,1)}) %reduce-scatter.22.cloned.1.call-update) | async-done | bytes 147472 | tf_op jit(solution)/shard_map/reduce_scatter | solution.py:383
  1471.2 22.8 %reduce-scatter.34.cloned.1.call-done = bf16[48,1536]{1,0:T(8,128)(2,1)} async-done(((bf16[192,1536]{1,0:T(8,128)(2,1)}), bf16[48,1536]{1,0:T(8,128)(2,1)}) %reduce-scatter.34.cloned.1.call-update) | async-done | bytes 147472 | tf_op jit(solution)/shard_map/reduce_scatter | solution.py:392
  1495.6 100.6 %reduce-scatter.36.cloned.1.call-done = bf16[4,384,1024]{2,1,0:T(8,128)(2,1)} async-done(((bf16[4,1536,1024]{2,1,0:T(8,128)(2,1)}), bf16[4,384,1024]{2,1,0:T(8,128)(2,1)}) %reduce-scatter.36.cloned.1.call-update) | async-done | bytes 3145744 | tf_op jit(solution)/shard_map/reduce_scatter | solution.py:233
  1596.3 5.3 convert_element_type.289
  (228 shorter events, 69.5 us)
Async XLA Ops:
  7.2 63.1 %copy-start.2 = (bf16[1,128,1536]{2,1,0:T(8,128)(2,1)S(1)}, bf16[1,128,1536]{2,1,0:T(8,128)(2,1)}, u32[]{:S(2)}) copy-start(bf16[1,128,1536]{2,1,0:T(8,128)(2,1)} %param.16) | copy-start | bytes 1179652
  7.2 61.3 %all-gather.10.cloned.1.call-start = ((), (), s32[]{:S(2)}) async-start(), calls=%async_computation.17 | async-start | bytes 1622016 | tf_op jit(solution)/shard_map/all_gather | solution.py:90
  7.9 117.3 %all-gather.16.cloned.1.call-start = ((), (), s32[]{:S(2)}) async-start(), calls=%async_computation.20 | async-start | bytes 1622016 | tf_op jit(solution)/shard_map/all_gather | solution.py:91
  8.7 182.0 %all-gather.14.cloned.1.call-start = ((), (), s32[]{:S(2)}) async-start(), calls=%async_computation.19 | async-start | bytes 4866048 | tf_op jit(solution)/shard_map/all_gather | solution.py:89
  9.4 221.5 %all-gather.12.cloned.1.call-start = ((), (), s32[]{:S(2)}) async-start(), calls=%async_computation.18 | async-start | bytes 1179648 | tf_op jit(solution)/shard_map/all_gather | solution.py:127
  53.3 144.0 %copy-start.22 = (f32[1536]{0:T(1024)}, f32[1536]{0:T(1024)S(1)}, u32[]{:S(2)}) copy-start(f32[1536]{0:T(1024)S(1)} %convert_element_type.242) | copy-start | bytes 18436
  54.5 142.8 %copy-start.29 = (f32[128]{0:T(128)}, f32[128]{0:T(128)S(1)}, u32[]{:S(2)}) copy-start(f32[128]{0:T(128)S(1)} %add_rsqrt_fusion.1) | copy-start | bytes 1540
  70.3 58.8 %copy-start.28 = (s32[1,128,8]{1,2,0:T(8,128)S(1)}, s32[1,128,8]{1,2,0:T(8,128)}, u32[]{:S(2)}) copy-start(s32[1,128,8]{1,2,0:T(8,128)} %param.17) | copy-start | bytes 12292
  71.6 201.1 %all-gather.18.cloned.1.call-start = ((), (), s32[]{:S(2)}) async-start(), calls=%async_computation.21 | async-start | bytes 1179648 | tf_op jit(solution)/shard_map/all_gather | solution.py:128
  127.8 210.1 %all-gather.20.cloned.1.call-start = ((), (), s32[]{:S(2)}) async-start(), calls=%async_computation.22 | async-start | bytes 4866048 | tf_op jit(solution)/shard_map/all_gather | solution.py:92
  128.3 443.4 %all-gather.22.cloned.1.call-start = ((), (), s32[]{:S(2)}) async-start(), calls=%async_computation.23 | async-start | bytes 15728640 | tf_op jit(solution)/shard_map/all_gather | solution.py:97
  129.4 143.4 %copy-start.33 = (s32[128]{0:T(128)}, s32[128]{0:T(128)S(1)}, u32[]{:S(2)}) copy-start(s32[128]{0:T(128)S(1)} %iota_add_fusion) | copy-start | bytes 1540
  276.1 5.2 copy-start
  276.8 4.5 copy-start.16
  289.2 52.0 %copy-start.9 = (f32[8,3,128,64]{2,3,1,0:T(8,128)}, f32[8,3,128,64]{2,3,1,0:T(8,128)S(1)}, u32[]{:S(2)}) copy-start(f32[8,3,128,64]{2,3,1,0:T(8,128)S(1)} %get-tuple-element.73) | copy-start | bytes 2359300
  290.0 51.2 %copy-start.14 = (bf16[8,3,128,64]{2,3,1,0:T(8,128)(2,1)}, bf16[8,3,128,64]{2,3,1,0:T(8,128)(2,1)S(1)}, u32[]{:S(2)}) copy-start(bf16[8,3,128,64]{2,3,1,0:T(8,128)(2,1)S(1)} %divide_convert_fusion) | copy-start | bytes 1179652
  341.1 0.9 copy-start.5
  342.2 120.5 %copy-start.12 = (bf16[128,1536]{1,0:T(8,128)(2,1)}, bf16[128,1536]{1,0:T(8,128)(2,1)S(1)}, u32[]{:S(2)}) copy-start(bf16[128,1536]{1,0:T(8,128)(2,1)S(1)} %multiply_convert_fusion.3) | copy-start | bytes 1179652
  347.6 5.6 copy-start.32
  347.6 115.5 %copy-start.7 = (f32[1,128,1536]{2,1,0:T(8,128)S(1)}, f32[1,128,1536]{2,1,0:T(8,128)}, u32[]{:S(2)}) copy-start(f32[1,128,1536]{2,1,0:T(8,128)} %param.27) | copy-start | bytes 2359300
  347.6 121.7 %all-to-all-start = ((bf16[8,4,40,1536]{3,2,1,0:T(8,128)(2,1)}), bf16[8,4,40,1536]{3,2,1,0:T(8,128)(2,1)}, u32[]{:S(2)}, u32[]{:S(2)}) async-start(bf16[8,4,40,1536]{3,2,1,0:T(8,128)(2,1)} %bitcast.240), calls=%async_computation | async-start | bytes 7864320 | tf_op jit(solution)/shard_map/all_to_all | solution.py:173
  352.5 231.7 %all-gather.24.cloned.1.call-start = ((), (), s32[]{:S(2)}) async-start(), calls=%async_computation.24 | async-start | bytes 7864320 | tf_op jit(solution)/shard_map/all_gather | solution.py:98
  469.3 98.0 %all-to-all-start.2 = ((bf16[8,4,40,1536]{3,2,1,0:T(8,128)(2,1)}), bf16[8,4,40,1536]{3,2,1,0:T(8,128)(2,1)}, u32[]{:S(2)}, u32[]{:S(2)}) async-start(bf16[8,4,40,1536]{3,2,1,0:T(8,128)(2,1)} %bitcast.241), calls=%async_computation.2 | async-start | bytes 7864320 | tf_op jit(solution)/shard_map/all_to_all | solution.py:211
  593.6 12.1 copy-start.37
  593.6 24.2 %copy-start.19 = (bf16[4,320,512]{2,1,0:T(8,128)(2,1)}, bf16[4,320,512]{2,1,0:T(8,128)(2,1)S(1)}, u32[]{:S(2)}) copy-start(bf16[4,320,512]{2,1,0:T(8,128)(2,1)S(1)} %get-tuple-element.158) | copy-start | bytes 3932164
  613.2 92.3 %all-to-all-start.3 = ((bf16[1,4,320,1536]{3,1,0,2:T(4,128)(2,1)}), bf16[1,4,320,1536]{3,1,0,2:T(4,128)(2,1)}, u32[]{:S(2)}, u32[]{:S(2)}) async-start(bf16[1,4,320,1536]{3,1,0,2:T(4,128)(2,1)} %copy.127), calls=%async_computation.3 | async-start | bytes 7864320 | tf_op jit(solution)/shard_map/all_to_all | solution.py:229
  705.5 91.5 %all-to-all-start.1 = ((bf16[1,4,320,1536]{3,1,0,2:T(4,128)(2,1)}), bf16[1,4,320,1536]{3,1,0,2:T(4,128)(2,1)}, u32[]{:S(2)}, u32[]{:S(2)}) async-start(bf16[1,4,320,1536]{3,1,0,2:T(4,128)(2,1)} %copy.121), calls=%async_computation.1 | async-start | bytes 7864320 | tf_op jit(solution)/shard_map/all_to_all | solution.py:182
  710.1 209.8 %reduce-scatter.40.cloned.1.call-start = ((), (), s32[]{:S(2)}) async-start(), calls=%async_computation.35 | async-start | bytes 2359296
  801.9 10.0 copy-start.8
  811.8 4.2 copy-start.6
  811.8 4.2 copy-start.17
  816.1 1.0 copy-start.26
  818.1 5.1 copy-start.10
  818.1 6.2 copy-start.4
  818.1 6.2 copy-start.34
  827.2 6.3 copy-start.1
  842.2 3.2 copy-start.21
  849.2 4.1 copy-start.13
  849.2 4.1 copy-start.27
  849.2 71.9 %copy-start.25 = (f32[128,32]{0,1:T(8,128)S(1)}, f32[128,32]{0,1:T(8,128)}, u32[]{:S(2)}) copy-start(f32[128,32]{0,1:T(8,128)} %get-tuple-element.171) | copy-start | bytes 49156
  849.2 71.9 %copy-start.3 = (bf16[1,128,1536]{2,1,0:T(8,128)(2,1)S(1)}, bf16[1,128,1536]{2,1,0:T(8,128)(2,1)}, u32[]{:S(2)}) copy-start(bf16[1,128,1536]{2,1,0:T(8,128)(2,1)} %param.16) | copy-start | bytes 1179652
  849.2 71.9 %copy-start.23 = (f32[1536]{0:T(1024)S(1)}, f32[1536]{0:T(1024)}, u32[]{:S(2)}) copy-start(f32[1536]{0:T(1024)} %copy-done.22) | copy-start | bytes 18436
  849.2 71.9 %copy-start.30 = (f32[128]{0:T(128)S(1)}, f32[128]{0:T(128)}, u32[]{:S(2)}) copy-start(f32[128]{0:T(128)} %copy-done.29) | copy-start | bytes 1540
  853.3 131.6 %reduce-scatter.42.cloned.1.call-start = ((), (), s32[]{:S(2)}) async-start(), calls=%async_computation.36 | async-start | bytes 442368
  854.5 199.1 %reduce-scatter.24.cloned.1.call-start = ((), (), s32[]{:S(2)}) async-start(), calls=%async_computation.27 | async-start | bytes 1769472 | tf_op jit(solution)/shard_map/reduce_scatter | solution.py:363
  919.9 3.1 copy-start.24
  923.0 198.2 %reduce-scatter.28.cloned.1.call-start = ((), (), s32[]{:S(2)}) async-start(), calls=%async_computation.29 | async-start | bytes 1769472 | tf_op jit(solution)/shard_map/reduce_scatter | solution.py:366
  924.9 294.4 %reduce-scatter.20.cloned.1.call-start = ((), (), s32[]{:S(2)}) async-start(), calls=%async_computation.25 | async-start | bytes 5308416 | tf_op jit(solution)/shard_map/reduce_scatter | solution.py:360
  929.9 1.0 copy-start.15
  929.9 388.3 %reduce-scatter.32.cloned.1.call-start = ((), (), s32[]{:S(2)}) async-start(), calls=%async_computation.31 | async-start | bytes 5308416 | tf_op jit(solution)/shard_map/reduce_scatter | solution.py:369
  934.4 50.5 %copy-start.20 = (bf16[4,320,512]{2,1,0:T(8,128)(2,1)S(1)}, bf16[4,320,512]{2,1,0:T(8,128)(2,1)}, u32[]{:S(2)}) copy-start(bf16[4,320,512]{2,1,0:T(8,128)(2,1)} %copy-done.19) | copy-start | bytes 3932164
  934.5 405.2 %reduce-scatter.44.cloned.1.call-start = ((), (), s32[]{:S(2)}) async-start(), calls=%async_computation.37 | async-start | bytes 61440
  984.9 415.9 %reduce-scatter.38.cloned.1.call-start = ((), (), s32[]{:S(2)}) async-start(), calls=%async_computation.34 | async-start | bytes 7864320 | tf_op jit(solution)/shard_map/reduce_scatter | solution.py:236
  993.0 325.5 %copy-start.38 = (bf16[4,320,512]{2,1,0:T(8,128)(2,1)S(1)}, bf16[4,320,512]{2,1,0:T(8,128)(2,1)}, u32[]{:S(2)}) copy-start(bf16[4,320,512]{2,1,0:T(8,128)(2,1)} %copy-done.37) | copy-start | bytes 3932164
  993.0 429.9 %reduce-scatter.26.cloned.1.call-start = ((), (), s32[]{:S(2)}) async-start(), calls=%async_computation.28 | async-start | bytes 245760 | tf_op jit(solution)/shard_map/reduce_scatter | solution.py:386
  1053.6 391.4 %reduce-scatter.30.cloned.1.call-start = ((), (), s32[]{:S(2)}) async-start(), calls=%async_computation.30 | async-start | bytes 245760 | tf_op jit(solution)/shard_map/reduce_scatter | solution.py:389
  1121.2 348.4 %reduce-scatter.22.cloned.1.call-start = ((), (), s32[]{:S(2)}) async-start(), calls=%async_computation.26 | async-start | bytes 737280 | tf_op jit(solution)/shard_map/reduce_scatter | solution.py:383
  1219.3 274.7 %reduce-scatter.34.cloned.1.call-start = ((), (), s32[]{:S(2)}) async-start(), calls=%async_computation.32 | async-start | bytes 737280 | tf_op jit(solution)/shard_map/reduce_scatter | solution.py:392
  1318.2 278.1 %reduce-scatter.36.cloned.1.call-start = ((), (), s32[]{:S(2)}) async-start(), calls=%async_computation.33 | async-start | bytes 15728640 | tf_op jit(solution)/shard_map/reduce_scatter | solution.py:233
  1330.5 0.7 copy-start.36
  1330.5 1.2 copy-start.35
  1330.5 10.6 copy-start.11
  1338.5 6.1 copy-start.31
  1340.4 2.4 copy-start.18
Sparse Core Ops, SparseCore 0:
  10.9 57.6 all-gather.9
  71.4 53.8 all-gather.15
  128.1 62.5 all-gather.13
  193.2 37.6 all-gather.11
  233.5 39.2 all-gather.17
  275.5 62.3 all-gather.19
  339.5 81.0 all-gather.21
  422.2 47.5 all-gather.23
  853.4 66.4 reduce-scatter.39
  923.6 61.2 reduce-scatter.41
  988.9 64.6 reduce-scatter.23
  1056.8 64.3 reduce-scatter.27
  1124.8 94.4 reduce-scatter.19
  1222.8 95.2 reduce-scatter.31
  1320.4 19.1 reduce-scatter.43
  1342.6 58.1 reduce-scatter.37
  1403.1 19.7 reduce-scatter.25
  1425.2 19.7 reduce-scatter.29
  1447.5 22.0 reduce-scatter.21
  1471.9 22.0 reduce-scatter.33
  1496.6 99.6 reduce-scatter.35
where the time goes:
time: 1620 us; the launch traced here: 1610 us
  waiting for transfers between devices  1120 us (69%)
  blocking collectives  179 us (11%)
  matrix products  123 us (8%)
  local copies, waits for them, and re-layouts  93.3 us (6%)
  other arithmetic  50.5 us (3%)
  starting transfers between devices  23.8 us (1%)
  between operations  17.5 us (1%)
    unnamed x24, waiting for transfers between devices  121 us
    all_gather x1, blocking collectives, local(): lax.all_gather(router, ('ctx', 'fsdp'), axis=0, tiled=True)  109 us
    reduce_scatter x1, waiting for transfers between devices, local(): lax.psum_scatter(grad_w_in.astype(jnp.bfloat16), 'fsdp', scatter_dimensio...  101 us
    reduce_scatter x1, waiting for transfers between devices, local(): lax.psum_scatter(grad_wo_part.astype(jnp.bfloat16), 'ctx', scatter_dimens...  98.8 us
    reduce_scatter x1, waiting for transfers between devices, local(): lax.psum_scatter(grad_wq_part.astype(jnp.bfloat16), 'ctx', scatter_dimens...  98.1 us
    all_to_all x1, waiting for transfers between devices, local(): lax.all_to_all(grad_outgoing, 'ctx', split_axis=0, concat_axis=2, tiled=T...  84.8 us
    all_to_all x1, waiting for transfers between devices, local(): lax.all_to_all(grad_rows[None], 'ctx', split_axis=2, concat_axis=0, tiled...  77.8 us
    unnamed x3, blocking collectives  70.3 us
  transfers between devices with their start and end apart: 25, of which 22 were waited for; matrix products, arithmetic and copies ran while one was open for 11% of the time, Pallas kernels for 0%

commit v1 on v0

--- a/solution.py
+++ b/solution.py
@@ -1,7 +1,354 @@
+import functools
+import itertools
+
 import jax
 import jax.numpy as jnp
 from jax import lax
+from jax.experimental import pallas as pl
+from jax.experimental.pallas import tpu as pltpu
 from jax.sharding import PartitionSpec as P
+
+
+NY = 2
+NZ = 4
+NX = 2
+NC = 2
+DEV = pl.DeviceIdType.MESH
+CTX, FSDP = "ctx", "fsdp"
+Z, Y, X, C = 0, 1, 2, 3
+SIZES = {Z: NZ, Y: NY, X: NX, C: NC}
+UP, DOWN = 4, 5
+
+
+class Plan:
+    def __init__(self, ref, order, index, rows=None):
+        self.ref, self.order, self.index, self.rows = ref, order, index, rows
+        self.blocks = 1
+        for d in index:
+            self.blocks *= SIZES[d]
+
+
+class Place:
+    def __init__(self):
+        ctx = lax.axis_index(CTX)
+        fsdp = lax.axis_index(FSDP)
+        self.at = {Z: ctx // NY, Y: ctx % NY, X: fsdp // NC, C: fsdp % NC}
+        z = self.at[Z]
+        low = z < NZ // 2
+        base = jnp.where(low, z, NZ - 1 - z)
+        near = [base, 1 - base, jnp.int32(2), jnp.int32(3)]
+        self.order = [z] + [jnp.where(low, k, NZ - 1 - k) for k in near[1:]]
+
+    def device(self, dim, value):
+        spot = dict(self.at)
+        spot[dim] = value
+        return (spot[Z] * NY + spot[Y], spot[X] * NC + spot[C])
+
+    def across(self, dim):
+        return self.device(dim, 1 - self.at[dim])
+
+    def along(self, step):
+        return self.device(Z, self.at[Z] + step)
+
+    def coords(self, z_from, flips):
+        spot = {d: (1 - self.at[d] if d in flips else self.at[d]) for d in (Y, X, C)}
+        spot[Z] = z_from
+        return spot
+
+
+def flat_index(spot, dims):
+    index = 0
+    for d in dims:
+        index = index * SIZES[d] + spot[d]
+    return index
+
+
+def subsets(dims):
+    return [c for n in range(len(dims) + 1) for c in itertools.combinations(dims, n)]
+
+
+def greet(place, dims):
+    barrier = pltpu.get_barrier_semaphore()
+    z = place.at[Z]
+    count = jnp.int32(0)
+    for d in dims:
+        if d == Z:
+            @pl.when(z > 0)
+            def _():
+                pl.semaphore_signal(barrier, inc=1, device_id=place.along(-1), device_id_type=DEV)
+
+            @pl.when(z < NZ - 1)
+            def _():
+                pl.semaphore_signal(barrier, inc=1, device_id=place.along(1), device_id_type=DEV)
+
+            count = count + jnp.where(z > 0, 1, 0) + jnp.where(z < NZ - 1, 1, 0)
+        else:
+            pl.semaphore_signal(barrier, inc=1, device_id=place.across(d), device_id_type=DEV)
+            count = count + 1
+    pl.semaphore_wait(barrier, count)
+
+
+def gather_events(order):
+    pairs = [d for d in order if d != Z]
+    events = [(k, f) for k in range(NZ) for f in subsets(pairs)]
+    return sorted(events, key=lambda e: (e[0] + len(e[1]), len(e[1])))
+
+
+def gather_sends(order, k, flips):
+    z_at = order.index(Z)
+    last = max([order.index(d) for d in flips] + ([z_at] if k > 0 else []) + [-1])
+    out = []
+    for position, d in enumerate(order):
+        if position > last:
+            out.extend([UP, DOWN] if d == Z else [d])
+    if k > 0 and last == z_at:
+        out.extend([UP, DOWN])
+    return out
+
+
+def gather_kernel(plans, n_in, *refs):
+    ins, outs = refs[:n_in], refs[n_in : 2 * n_in]
+    send_sem, recv_sem, own_sem = refs[2 * n_in :]
+    place = Place()
+    z = place.at[Z]
+    greet(place, sorted({d for p in plans for d in p.order}))
+    pending = []
+    slot = 0
+    queue = []
+    for n, plan in enumerate(plans):
+        for rank, event in enumerate(gather_events(plan.order)):
+            queue.append((rank / len(gather_events(plan.order)), n, event))
+    queue.sort(key=lambda q: (q[0], q[1]))
+    bases = [sum(p.blocks for p in plans[:n]) for n in range(len(plans))]
+    for _, n, (k, flips) in queue:
+        plan = plans[n]
+        src = ins[plan.ref]
+        out = outs[plan.ref]
+        rows = plan.rows
+        z_from = place.order[k]
+        spot = place.coords(z_from, flips)
+        index = flat_index(spot, plan.index)
+        target = out.at[index] if rows is None else out.at[index, pl.ds(rows[0], rows[1])]
+        sem = recv_sem.at[bases[n] + index]
+        own = k == 0 and not flips
+        source = (src if rows is None else src.at[pl.ds(rows[0], rows[1])]) if own else target
+        if not own:
+            pltpu.make_async_remote_copy(
+                src_ref=target, dst_ref=target, send_sem=own_sem.at[0], recv_sem=sem,
+                device_id=place.across(C), device_id_type=DEV,
+            ).wait_recv()
+        for way in gather_sends(plan.order, k, flips):
+            if way in (UP, DOWN):
+                step = 1 if way == UP else -1
+                go = z < NZ - 1 if way == UP else z > 0
+                if k > 0:
+                    go = jnp.logical_and(go, z_from < z if way == UP else z_from > z)
+                dest = place.device(Z, jnp.clip(z + step, 0, NZ - 1))
+            else:
+                go, dest = None, place.across(way)
+            copy = pltpu.make_async_remote_copy(
+                src_ref=source, dst_ref=target, send_sem=send_sem.at[slot], recv_sem=sem,
+                device_id=dest, device_id_type=DEV,
+            )
+            slot += 1
+            if go is None:
+                copy.start()
+            else:
+                pl.when(go)(copy.start)
+            pending.append((go, copy.wait_send))
+        if own:
+            copy = pltpu.make_async_copy(source, target, own_sem.at[1 + n])
+            copy.start()
+            pending.append((None, copy.wait))
+    for go, wait in pending:
+        if go is None:
+            wait()
+        else:
+            pl.when(go)(wait)
+
+
+def gather(arrays, plans, collective_id, name):
+    n = len(arrays)
+    sends = sum(len(gather_sends(p.order, k, f)) for p in plans for k, f in gather_events(p.order))
+    blocks = {p.ref: p.blocks for p in plans}
+    return pl.pallas_call(
+        functools.partial(gather_kernel, plans, n),
+        out_shape=[jax.ShapeDtypeStruct((blocks[i],) + a.shape, a.dtype) for i, a in enumerate(arrays)],
+        in_specs=[pl.BlockSpec(memory_space=pltpu.VMEM)] * n,
+        out_specs=[pl.BlockSpec(memory_space=pl.ANY)] * n,
+        scratch_shapes=[
+            pltpu.SemaphoreType.DMA((sends,)),
+            pltpu.SemaphoreType.DMA((sum(p.blocks for p in plans),)),
+            pltpu.SemaphoreType.DMA((1 + len(plans),)),
+        ],
+        compiler_params=pltpu.CompilerParams(collective_id=collective_id, has_side_effects=True),
+        name=name,
+    )(*arrays)
+
+
+def add_into(acc, other):
+    acc[...] = (acc[...].astype(jnp.float32) + other[...].astype(jnp.float32)).astype(acc.dtype)
+
+
+def reduce_kernel(plans, n_in, *refs):
+    ins, outs = refs[:n_in], refs[n_in : 2 * n_in]
+    rest = list(refs[2 * n_in :])
+    send_sem, recv_sem, own_sem = rest[:3]
+    buffers = rest[3:]
+    place = Place()
+    z = place.at[Z]
+    greet(place, sorted({d for p in plans for d in p.order} | {Z}))
+    pending = []
+    slots = [0, 0]
+
+    def push(source, target, sem, dest):
+        copy = pltpu.make_async_remote_copy(
+            src_ref=source, dst_ref=target, send_sem=send_sem.at[slots[0]], recv_sem=sem,
+            device_id=dest, device_id_type=DEV,
+        )
+        slots[0] += 1
+        copy.start()
+        pending.append(copy)
+
+    def arrived(target, sem):
+        pltpu.make_async_remote_copy(
+            src_ref=target, dst_ref=target, send_sem=own_sem.at[0], recv_sem=sem,
+            device_id=place.across(C), device_id_type=DEV,
+        ).wait_recv()
+
+    work = []
+    far = list(reversed(range(NZ)))
+    own_slot = 1
+    state = []
+    base = 0
+    for n, plan in enumerate(plans):
+        dims = plan.order
+        acc = buffers[0]
+        levels = buffers[1 : 1 + len(dims)]
+        chain = buffers[1 + len(dims)]
+        buffers = buffers[2 + len(dims) :]
+        kept = [subsets(dims[p + 1 :]) for p in range(len(dims))]
+        counts = [NZ * len(f) for f in kept]
+        level_base = [base + sum(counts[:p]) for p in range(len(dims))]
+        chain_base = base + sum(counts)
+        base = chain_base + 2 * NZ
+        state.append((acc, levels, chain, kept, level_base, chain_base))
+        own_copies = {}
+        src = ins[plan.ref]
+        for k in far:
+            for f in kept[0]:
+                gone = flat_index(place.coords(place.order[k], (dims[0],) + f), plan.index)
+                spot = place.order[k] * len(kept[0]) + kept[0].index(f)
+                work.append((0, n, k, f, gone, spot))
+                mine = flat_index(place.coords(place.order[k], f), plan.index)
+                copy = pltpu.make_async_copy(src.at[mine], acc.at[spot], own_sem.at[own_slot])
+                own_slot += 1
+                own_copies[(k, f)] = copy
+        state[-1] += (own_copies,)
+    for _, n, k, f, gone, spot in sorted(work, key=lambda w: (-w[2],)):
+        plan = plans[n]
+        acc, levels, chain, kept, level_base, chain_base, own_copies = state[n]
+        push(ins[plan.ref].at[gone], levels[0].at[spot], recv_sem.at[level_base[0] + spot], place.across(plan.order[0]))
+        own_copies[(k, f)].start()
+
+    def level_step(n, p, k):
+        plan = plans[n]
+        dims = plan.order
+        acc, levels, chain, kept, level_base, chain_base, own_copies = state[n]
+        for f in sorted(kept[p], key=lambda f: -len(f)):
+            spot = place.order[k] * len(kept[p]) + kept[p].index(f)
+            at = place.order[k] * len(kept[0]) + kept[0].index(f)
+            if p == 0:
+                own_copies[(k, f)].wait()
+            arrived(levels[p].at[spot], recv_sem.at[level_base[p] + spot])
+            add_into(acc.at[at], levels[p].at[spot])
+            later = p + 1
+            if later < len(dims) and dims[later] in f:
+                left = tuple(d for d in f if d != dims[later])
+                there = place.order[k] * len(kept[later]) + kept[later].index(left)
+                push(
+                    acc.at[at], levels[later].at[there],
+                    recv_sem.at[level_base[later] + there], place.across(dims[later]),
+                )
+
+    def chain_step(n, k):
+        plan = plans[n]
+        acc, levels, chain, kept, level_base, chain_base, own_copies = state[n]
+        dest = place.order[k]
+        up = dest > z
+        lane = jnp.where(up, 0, 1)
+        at = dest * len(kept[0])
+        spot = lane * NZ + dest
+
+        @pl.when(jnp.where(up, z > 0, z < NZ - 1))
+        def _():
+            arrived(chain.at[spot], recv_sem.at[chain_base + spot])
+            add_into(acc.at[at], chain.at[spot])
+
+        push(acc.at[at], chain.at[spot], recv_sem.at[chain_base + spot], place.along(jnp.where(up, 1, -1)))
+
+    most = max(len(p.order) for p in plans)
+    for step in range(NZ + most):
+        for n, plan in enumerate(plans):
+            for p in range(len(plan.order)):
+                if 0 <= step - p < NZ:
+                    level_step(n, p, far[step - p])
+            p = len(plan.order)
+            if 0 <= step - p < NZ - 1:
+                chain_step(n, far[step - p])
+    for n, plan in enumerate(plans):
+        acc, levels, chain, kept, level_base, chain_base, own_copies = state[n]
+        at = z * len(kept[0])
+
+        @pl.when(z > 0)
+        def _():
+            spot = z
+            arrived(chain.at[spot], recv_sem.at[chain_base + spot])
+            add_into(acc.at[at], chain.at[spot])
+
+        @pl.when(z < NZ - 1)
+        def _():
+            spot = NZ + z
+            arrived(chain.at[spot], recv_sem.at[chain_base + spot])
+            add_into(acc.at[at], chain.at[spot])
+
+        outs[plan.ref][...] = acc[at].astype(outs[plan.ref].dtype)
+    for copy in pending:
+        copy.wait_send()
+
+
+def reduce_scatter(arrays, plans, out_dtypes, collective_id, name):
+    n = len(arrays)
+    scratch = []
+    sends = recvs = owns = 0
+    for p in plans:
+        a = arrays[p.ref]
+        block = a.shape[1:]
+        kept = [len(subsets(p.order[q + 1 :])) for q in range(len(p.order))]
+        scratch.append(pltpu.VMEM((NZ * kept[0],) + block, a.dtype))
+        for q in kept:
+            scratch.append(pltpu.VMEM((NZ * q,) + block, a.dtype))
+        scratch.append(pltpu.VMEM((2 * NZ,) + block, a.dtype))
+        sends += NZ * sum(kept) + NZ - 1
+        recvs += NZ * sum(kept) + 2 * NZ
+        owns += NZ * kept[0]
+    return pl.pallas_call(
+        functools.partial(reduce_kernel, plans, n),
+        out_shape=[jax.ShapeDtypeStruct(a.shape[1:], d) for a, d in zip(arrays, out_dtypes)],
+        in_specs=[pl.BlockSpec(memory_space=pl.ANY)] * n,
+        out_specs=[pl.BlockSpec(memory_space=pltpu.VMEM)] * n,
+        scratch_shapes=[
+            pltpu.SemaphoreType.DMA((sends,)),
+            pltpu.SemaphoreType.DMA((recvs,)),
+            pltpu.SemaphoreType.DMA((1 + owns,)),
+        ]
+        + scratch,
+        compiler_params=pltpu.CompilerParams(
+            collective_id=collective_id, has_side_effects=True, vmem_limit_bytes=60 * 1024 * 1024
+        ),
+        name=name,
+    )(*arrays)
+
 
 MODEL_WIDTH = 1536
 QUERY_HEADS = 24
@@ -77,25 +424,25 @@
 ):
     token_rows = hidden.shape[1]
     query_group = QUERY_HEADS // KEY_VALUE_HEADS
-    ctx_size = lax.axis_size("ctx")
+    ctx_size = lax.axis_size(CTX)
     sequence_length = token_rows * ctx_size
-    positions = lax.axis_index("ctx") * token_rows + jnp.arange(token_rows, dtype=jnp.int32)
+    positions = lax.axis_index(CTX) * token_rows + jnp.arange(token_rows, dtype=jnp.int32)
     cosine_table, sine_table = rope_tables(positions)
     contract_rows = (((0,), (0,)), ((), ()))
     contract_cols = (((1,), (1,)), ((), ()))
     layer = (
-        lax.all_gather(attn_norm, ("ctx", "fsdp"), axis=0, tiled=True),
-        lax.all_gather(ffn_norm, ("ctx", "fsdp"), axis=0, tiled=True),
-        lax.all_gather(w_q, ("ctx", "fsdp"), axis=0, tiled=True),
-        lax.all_gather(key_weight, ("ctx", "fsdp"), axis=0, tiled=True),
-        lax.all_gather(value_weight, ("ctx", "fsdp"), axis=0, tiled=True),
-        lax.all_gather(w_o, ("ctx", "fsdp"), axis=0, tiled=True),
-        lax.all_gather(router, ("ctx", "fsdp"), axis=0, tiled=True),
+        lax.all_gather(attn_norm, (CTX, FSDP), axis=0, tiled=True),
+        lax.all_gather(ffn_norm, (CTX, FSDP), axis=0, tiled=True),
+        lax.all_gather(w_q, (CTX, FSDP), axis=0, tiled=True),
+        lax.all_gather(key_weight, (CTX, FSDP), axis=0, tiled=True),
+        lax.all_gather(value_weight, (CTX, FSDP), axis=0, tiled=True),
+        lax.all_gather(w_o, (CTX, FSDP), axis=0, tiled=True),
+        lax.all_gather(router, (CTX, FSDP), axis=0, tiled=True),
     )
     attn_gain, ffn_gain, query_w, key_weight_matrix, value_w, output_w, router_w = layer
     experts = (
-        lax.all_gather(expert_in, "fsdp", axis=1, tiled=True),
-        lax.all_gather(expert_out, "fsdp", axis=1, tiled=True),
+        lax.all_gather(expert_in, FSDP, axis=1, tiled=True),
+        lax.all_gather(expert_out, FSDP, axis=1, tiled=True),
     )
     weight_in, weight_out = experts
     wide = hidden[0].astype(jnp.float32)
@@ -124,8 +471,8 @@
         jnp.zeros((KEY_VALUE_HEADS, query_group, token_rows), jnp.float32),
         jnp.zeros((KEY_VALUE_HEADS, query_group, token_rows, HEAD_SIZE), jnp.float32),
     )
-    key_section = lax.all_gather(key_matrix_rows, "ctx", axis=0, tiled=True)
-    value_section = lax.all_gather(value_rows, "ctx", axis=0, tiled=True)
+    key_section = lax.all_gather(key_matrix_rows, CTX, axis=0, tiled=True)
+    value_section = lax.all_gather(value_rows, CTX, axis=0, tiled=True)
 
     def compute(current):
         best, total, weighted = current
@@ -170,7 +517,7 @@
     ffn_pad = jnp.concatenate([ffn_in, jnp.zeros((1, MODEL_WIDTH), jnp.bfloat16)], axis=0)
     local_experts = weight_in.shape[0]
     outgoing = ffn_pad[owner // TOP].reshape(ctx_size, local_experts, CAP, MODEL_WIDTH)
-    received = lax.all_to_all(outgoing, "ctx", split_axis=0, concat_axis=2, tiled=True)[0]
+    received = lax.all_to_all(outgoing, CTX, split_axis=0, concat_axis=2, tiled=True)[0]
     act = jnp.einsum("erd,edf->erf", received, weight_in, preferred_element_type=jnp.float32)
     gate_part = act[..., :EXPERT_HIDDEN]
     up_part = act[..., EXPERT_HIDDEN:]
@@ -180,24 +527,24 @@
         "erf,edf->erd", inner, weight_out, preferred_element_type=jnp.float32
     ).astype(jnp.bfloat16)
     returned = lax.all_to_all(
-        produced[None], "ctx", split_axis=2, concat_axis=0, tiled=True
+        produced[None], CTX, split_axis=2, concat_axis=0, tiled=True
     ).reshape(EXPERT_COUNT * CAP, MODEL_WIDTH)
     picked = returned[target].reshape(token_rows, TOP, MODEL_WIDTH)
     layer_out = (mixed + jnp.sum(gates[..., None] * picked, axis=1)).astype(jnp.bfloat16)
     cot = cotangent[0]
     layer = (
-        lax.all_gather(attn_norm, ("ctx", "fsdp"), axis=0, tiled=True),
-        lax.all_gather(ffn_norm, ("ctx", "fsdp"), axis=0, tiled=True),
-        lax.all_gather(w_q, ("ctx", "fsdp"), axis=0, tiled=True),
-        lax.all_gather(key_weight, ("ctx", "fsdp"), axis=0, tiled=True),
-        lax.all_gather(value_weight, ("ctx", "fsdp"), axis=0, tiled=True),
-        lax.all_gather(w_o, ("ctx", "fsdp"), axis=0, tiled=True),
-        lax.all_gather(router, ("ctx", "fsdp"), axis=0, tiled=True),
+        lax.all_gather(attn_norm, (CTX, FSDP), axis=0, tiled=True),
+        lax.all_gather(ffn_norm, (CTX, FSDP), axis=0, tiled=True),
+        lax.all_gather(w_q, (CTX, FSDP), axis=0, tiled=True),
+        lax.all_gather(key_weight, (CTX, FSDP), axis=0, tiled=True),
+        lax.all_gather(value_weight, (CTX, FSDP), axis=0, tiled=True),
+        lax.all_gather(w_o, (CTX, FSDP), axis=0, tiled=True),
+        lax.all_gather(router, (CTX, FSDP), axis=0, tiled=True),
     )
     attn_gain, ffn_gain, query_w, key_weight_matrix, value_w, output_w, router_w = layer
     experts = (
-        lax.all_gather(expert_in, "fsdp", axis=1, tiled=True),
-        lax.all_gather(expert_out, "fsdp", axis=1, tiled=True),
+        lax.all_gather(expert_in, FSDP, axis=1, tiled=True),
+        lax.all_gather(expert_out, FSDP, axis=1, tiled=True),
     )
     weight_in, weight_out = experts
     grad_gate = jnp.sum(cot[:, None, :] * picked, axis=-1)
@@ -208,7 +555,7 @@
     )
     slot_pad = jnp.concatenate([slot_grads, jnp.zeros((1, MODEL_WIDTH), jnp.bfloat16)], axis=0)
     grad_outgoing = slot_pad[owner].reshape(ctx_size, local_experts, CAP, MODEL_WIDTH)
-    grad_received = lax.all_to_all(grad_outgoing, "ctx", split_axis=0, concat_axis=2, tiled=True)[0]
+    grad_received = lax.all_to_all(grad_outgoing, CTX, split_axis=0, concat_axis=2, tiled=True)[0]
     grad_w_out = jnp.einsum(
         "erd,erf->edf", grad_received, inner, preferred_element_type=jnp.float32
     )
@@ -227,14 +574,14 @@
         "erf,edf->erd", grad_act, weight_in, preferred_element_type=jnp.float32
     ).astype(jnp.bfloat16)
     grad_back = lax.all_to_all(
-        grad_rows[None], "ctx", split_axis=2, concat_axis=0, tiled=True
+        grad_rows[None], CTX, split_axis=2, concat_axis=0, tiled=True
     ).reshape(EXPERT_COUNT * CAP, MODEL_WIDTH)
     grad_expert_in, grad_expert_out = (
         lax.psum_scatter(
-            grad_w_in.astype(jnp.bfloat16), "fsdp", scatter_dimension=1, tiled=True
-        ).astype(jnp.float32),
-        lax.psum_scatter(
-            grad_w_out.astype(jnp.bfloat16), "fsdp", scatter_dimension=1, tiled=True
+            grad_w_in.astype(jnp.bfloat16), FSDP, scatter_dimension=1, tiled=True
+        ).astype(jnp.float32),
+        lax.psum_scatter(
+            grad_w_out.astype(jnp.bfloat16), FSDP, scatter_dimension=1, tiled=True
         ).astype(jnp.float32),
     )
     grad_chosen = gates * (grad_gate - jnp.sum(gates * grad_gate, axis=-1, keepdims=True))
@@ -272,8 +619,8 @@
         jnp.zeros((token_rows, KEY_VALUE_HEADS, query_group, HEAD_SIZE), jnp.float32),
         jnp.zeros((sequence_length, 2 * KEY_VALUE_HEADS * HEAD_SIZE), jnp.float32),
     )
-    attend_key_section = lax.all_gather(key_matrix_rows, "ctx", axis=0, tiled=True)
-    attend_value_section = lax.all_gather(value_rows, "ctx", axis=0, tiled=True)
+    attend_key_section = lax.all_gather(key_matrix_rows, CTX, axis=0, tiled=True)
+    attend_value_section = lax.all_gather(value_rows, CTX, axis=0, tiled=True)
 
     def compute(current):
         token_count = attend_key_section.shape[0]
@@ -309,7 +656,7 @@
         jnp.int32(0) <= positions[-1], compute, lambda current: current, init_back
     )
     local_gradients = lax.psum_scatter(
-        grad_keys_full.astype(jnp.bfloat16), "ctx", scatter_dimension=0, tiled=True
+        grad_keys_full.astype(jnp.bfloat16), CTX, scatter_dimension=0, tiled=True
     ).astype(jnp.float32)
     query_back = (
         rotate_pairs(
@@ -352,48 +699,48 @@
     grad_input = grad_mixed + back_one
     partial_sums = (
         lax.psum_scatter(
-            grad_attn_gain.astype(jnp.bfloat16), "ctx", scatter_dimension=0, tiled=True
-        ).astype(jnp.float32),
-        lax.psum_scatter(
-            grad_ffn_gain.astype(jnp.bfloat16), "ctx", scatter_dimension=0, tiled=True
-        ).astype(jnp.float32),
-        lax.psum_scatter(
-            grad_wq_part.astype(jnp.bfloat16), "ctx", scatter_dimension=0, tiled=True
-        ).astype(jnp.float32),
-        lax.psum_scatter(
-            grad_wk_part.astype(jnp.bfloat16), "ctx", scatter_dimension=0, tiled=True
-        ).astype(jnp.float32),
-        lax.psum_scatter(
-            grad_wv_part.astype(jnp.bfloat16), "ctx", scatter_dimension=0, tiled=True
-        ).astype(jnp.float32),
-        lax.psum_scatter(
-            grad_wo_part.astype(jnp.bfloat16), "ctx", scatter_dimension=0, tiled=True
-        ).astype(jnp.float32),
-        lax.psum_scatter(
-            grad_router_part.astype(jnp.bfloat16), "ctx", scatter_dimension=0, tiled=True
+            grad_attn_gain.astype(jnp.bfloat16), CTX, scatter_dimension=0, tiled=True
+        ).astype(jnp.float32),
+        lax.psum_scatter(
+            grad_ffn_gain.astype(jnp.bfloat16), CTX, scatter_dimension=0, tiled=True
+        ).astype(jnp.float32),
+        lax.psum_scatter(
+            grad_wq_part.astype(jnp.bfloat16), CTX, scatter_dimension=0, tiled=True
+        ).astype(jnp.float32),
+        lax.psum_scatter(
+            grad_wk_part.astype(jnp.bfloat16), CTX, scatter_dimension=0, tiled=True
+        ).astype(jnp.float32),
+        lax.psum_scatter(
+            grad_wv_part.astype(jnp.bfloat16), CTX, scatter_dimension=0, tiled=True
+        ).astype(jnp.float32),
+        lax.psum_scatter(
+            grad_wo_part.astype(jnp.bfloat16), CTX, scatter_dimension=0, tiled=True
+        ).astype(jnp.float32),
+        lax.psum_scatter(
+            grad_router_part.astype(jnp.bfloat16), CTX, scatter_dimension=0, tiled=True
         ).astype(jnp.float32),
     )
     summed = (
         lax.psum_scatter(
-            partial_sums[0].astype(jnp.bfloat16), "fsdp", scatter_dimension=0, tiled=True
-        ).astype(jnp.float32),
-        lax.psum_scatter(
-            partial_sums[1].astype(jnp.bfloat16), "fsdp", scatter_dimension=0, tiled=True
-        ).astype(jnp.float32),
-        lax.psum_scatter(
-            partial_sums[2].astype(jnp.bfloat16), "fsdp", scatter_dimension=0, tiled=True
-        ).astype(jnp.float32),
-        lax.psum_scatter(
-            partial_sums[3].astype(jnp.bfloat16), "fsdp", scatter_dimension=0, tiled=True
-        ).astype(jnp.float32),
-        lax.psum_scatter(
-            partial_sums[4].astype(jnp.bfloat16), "fsdp", scatter_dimension=0, tiled=True
-        ).astype(jnp.float32),
-        lax.psum_scatter(
-            partial_sums[5].astype(jnp.bfloat16), "fsdp", scatter_dimension=0, tiled=True
-        ).astype(jnp.float32),
-        lax.psum_scatter(
-            partial_sums[6].astype(jnp.bfloat16), "fsdp", scatter_dimension=0, tiled=True
+            partial_sums[0].astype(jnp.bfloat16), FSDP, scatter_dimension=0, tiled=True
+        ).astype(jnp.float32),
+        lax.psum_scatter(
+            partial_sums[1].astype(jnp.bfloat16), FSDP, scatter_dimension=0, tiled=True
+        ).astype(jnp.float32),
+        lax.psum_scatter(
+            partial_sums[2].astype(jnp.bfloat16), FSDP, scatter_dimension=0, tiled=True
+        ).astype(jnp.float32),
+        lax.psum_scatter(
+            partial_sums[3].astype(jnp.bfloat16), FSDP, scatter_dimension=0, tiled=True
+        ).astype(jnp.float32),
+        lax.psum_scatter(
+            partial_sums[4].astype(jnp.bfloat16), FSDP, scatter_dimension=0, tiled=True
+        ).astype(jnp.float32),
+        lax.psum_scatter(
+            partial_sums[5].astype(jnp.bfloat16), FSDP, scatter_dimension=0, tiled=True
+        ).astype(jnp.float32),
+        lax.psum_scatter(
+            partial_sums[6].astype(jnp.bfloat16), FSDP, scatter_dimension=0, tiled=True
         ).astype(jnp.float32),
     )
     return (
@@ -411,37 +758,385 @@
     )
 
 
+def swap(a, flip):
+    return lax.ppermute(a, FSDP, [(i, i ^ flip) for i in range(NX * NC)])
+
+
+def fast(
+    hidden,
+    routes,
+    attn_norm,
+    ffn_norm,
+    w_q,
+    key_weight,
+    value_weight,
+    w_o,
+    router,
+    expert_in,
+    expert_out,
+    cotangent,
+):
+    tokens = hidden.shape[1]
+    group = QUERY_HEADS // KEY_VALUE_HEADS
+    ctx_size = NZ * NY
+    ctx = lax.axis_index(CTX)
+    fsdp = lax.axis_index(FSDP)
+    core = fsdp % NC
+    rows = w_q.shape[0]
+    quarter = expert_in.shape[1]
+    kv_width = KEY_VALUE_HEADS * HEAD_SIZE
+    q_width = QUERY_HEADS * HEAD_SIZE
+    held = expert_in.shape[0] // NC
+    bf = jnp.bfloat16
+    f32 = jnp.float32
+    positions = ctx * tokens + jnp.arange(tokens, dtype=jnp.int32)
+    cosine_table, sine_table = rope_tables(positions)
+    contract_rows = (((0,), (0,)), ((), ()))
+    contract_cols = (((1,), (1,)), ((), ()))
+    wide = hidden[0].astype(f32)
+    cot = cotangent[0]
+
+    def picked(w):
+        pair = w.reshape(NC, held, *w.shape[1:])
+        return (
+            lax.dynamic_index_in_dim(pair, core, 0, False),
+            lax.dynamic_index_in_dim(pair, 1 - core, 0, False),
+        )
+
+    def spread(mine, other):
+        parts = jnp.stack([mine, swap(other, 1), swap(mine, 2), swap(other, 3)])
+        order = jnp.arange(NX * NC) ^ fsdp
+        whole = jnp.take(parts, order, axis=0)
+        return jnp.transpose(whole, (1, 0, 2, 3)).reshape(held, NX * NC * quarter, mine.shape[2])
+
+    pack_one = jnp.concatenate([w_q, key_weight, value_weight], axis=1)
+    pack_two = jnp.concatenate(
+        [w_o, router, attn_norm[:, None], ffn_norm[:, None], jnp.zeros((rows, 94), bf)], axis=1
+    )
+    one, two, cots = gather(
+        [pack_one, pack_two, cot.astype(bf)],
+        [
+            Plan(0, (Z, Y, X, C,), (Z, Y, X, C,)),
+            Plan(1, (Z, X, Y, C,), (Z, Y, X, C,)),
+            Plan(2, (Z, Y, C,), (C, Z, Y,), rows=(0, tokens // 2)),
+            Plan(2, (Y, Z, C,), (C, Z, Y,), rows=(tokens // 2, tokens // 2)),
+        ],
+        0,
+        "gather_weights",
+    )
+    one, experts = lax.optimization_barrier((one, picked(expert_in) + picked(expert_out)))
+    weight_in = spread(*experts[:2])
+    weight_out = spread(*experts[2:])
+    one = one.reshape(MODEL_WIDTH, -1)
+    two = two.reshape(MODEL_WIDTH, -1)
+    output_w = two[:, :MODEL_WIDTH]
+    small = two[:, MODEL_WIDTH:]
+    router_w = small[:, :EXPERT_COUNT]
+    gains = lax.dot_general(
+        jnp.eye(128, dtype=bf), small, contract_cols, preferred_element_type=f32
+    )
+    attn_gain, ffn_gain = gains[EXPERT_COUNT], gains[EXPERT_COUNT + 1]
+
+    attn_unit, inverse_one, attention_input = rms_forward(wide, attn_gain)
+    linear = jnp.dot(attention_input, one, preferred_element_type=f32)
+    query_rows = (
+        rotate_pairs(linear[:, :q_width].reshape(tokens, QUERY_HEADS, HEAD_SIZE), cosine_table, sine_table)
+        .astype(bf)
+        .reshape(tokens, KEY_VALUE_HEADS, group, HEAD_SIZE)
+    )
+    key_rows = (
+        rotate_pairs(
+            linear[:, q_width : q_width + kv_width].reshape(tokens, KEY_VALUE_HEADS, HEAD_SIZE),
+            cosine_table,
+            sine_table,
+        )
+        .astype(bf)
+        .reshape(tokens, kv_width)
+    )
+    value_rows = linear[:, q_width + kv_width :].astype(bf)
+    (kv,) = gather(
+        [jnp.concatenate([key_rows, value_rows], axis=1)],
+        [Plan(0, (Z, Y,), (Z, Y,))],
+        1,
+        "gather_keys",
+    )
+    kv = kv.reshape(ctx_size * tokens, 2 * kv_width)
+    key_section, value_section = kv[:, :kv_width], kv[:, kv_width:]
+    value_tensor = value_section.reshape(ctx_size * tokens, KEY_VALUE_HEADS, HEAD_SIZE)
+    scores, visible, key_tensor = piece_scores(query_rows, key_section, positions)
+    best = jnp.max(scores, axis=-1)
+    weights = jnp.where(visible, jnp.exp(scores - best[..., None]), 0.0)
+    total = jnp.sum(weights, axis=-1)
+    weighted = jnp.einsum(
+        "kgtn,nkd->kgtd", weights.astype(bf), value_tensor, preferred_element_type=f32
+    )
+    log_sum_rows = best + jnp.log(total)
+    attention_output = (
+        jnp.transpose(weighted / total[..., None], (2, 0, 1, 3)).reshape(tokens, q_width).astype(bf)
+    )
+    mixed = wide + jnp.dot(attention_output, output_w, preferred_element_type=f32)
+    ffn_unit, inverse_two, ffn_in = rms_forward(mixed, ffn_gain)
+    logits = jnp.dot(ffn_in, router_w, preferred_element_type=f32)
+    route = routes[0]
+    indicator = (route[:, :, None] == jnp.arange(EXPERT_COUNT, dtype=jnp.int32)).astype(f32)
+    chosen = jnp.sum(indicator * logits[:, None, :], axis=-1)
+    gates = jax.nn.softmax(chosen, axis=-1)
+    gate_map = jnp.sum(indicator * (gates[..., None] + 1.0), axis=1) - 1.0
+
+    payload = jnp.concatenate(
+        [ffn_in, gate_map.astype(bf), jnp.zeros((tokens, 128 - EXPERT_COUNT), bf)], axis=1
+    )
+    cut = tokens * 3 // 4
+    (all_tokens,) = gather(
+        [payload],
+        [
+            Plan(0, (Z, Y, C,), (C, Z, Y,), rows=(0, cut)),
+            Plan(0, (Y, Z, C,), (C, Z, Y,), rows=(cut, tokens - cut)),
+        ],
+        2,
+        "gather_tokens",
+    )
+    blocks = NC * ctx_size
+    inputs = all_tokens[:, :, :MODEL_WIDTH]
+    first = (ctx * NC + core) * held
+    own_gates = lax.dynamic_slice_in_dim(
+        all_tokens[:, :, MODEL_WIDTH : MODEL_WIDTH + EXPERT_COUNT], first, held, axis=2
+    ).astype(f32)
+    chosen_here = own_gates >= 0.0
+    before = (
+        jnp.arange(tokens)[:, None] > jnp.arange(tokens)[None, :]
+    ).astype(bf)
+    slot = jnp.einsum(
+        "ts,bse->bet", before, chosen_here.astype(bf), preferred_element_type=f32
+    ).astype(jnp.int32)
+    place_of = (
+        (slot[:, :, None, :] == jnp.arange(CAP, dtype=jnp.int32)[None, None, :, None])
+        & jnp.transpose(chosen_here, (0, 2, 1))[:, :, None, :]
+    )
+    pick = place_of.astype(bf)
+    gate_t = jnp.transpose(own_gates, (0, 2, 1))
+    row_gate = jnp.sum(jnp.where(place_of, gate_t[:, :, None, :], 0.0), axis=-1)
+    row_gate = jnp.transpose(row_gate, (1, 0, 2)).reshape(held, blocks * CAP, 1)
+    received = jnp.einsum("best,btd->ebsd", pick, inputs, preferred_element_type=f32).astype(bf)
+    received = received.reshape(held, blocks * CAP, MODEL_WIDTH)
+    cot_rows = jnp.einsum("best,btd->ebsd", pick, cots, preferred_element_type=f32).astype(bf)
+    cot_rows = cot_rows.reshape(held, blocks * CAP, MODEL_WIDTH)
+    act = jnp.einsum("erd,edf->erf", received, weight_in, preferred_element_type=f32)
+    gate_part = act[..., :EXPERT_HIDDEN]
+    up_part = act[..., EXPERT_HIDDEN:]
+    sigma = jax.nn.sigmoid(gate_part)
+    inner = gate_part * sigma * up_part
+    scaled_inner = (inner * row_gate).astype(bf)
+    produced = jnp.einsum(
+        "erf,edf->erd", scaled_inner, weight_out, preferred_element_type=f32
+    ).astype(bf)
+    raw_inner = jnp.einsum("erd,edf->erf", cot_rows, weight_out, preferred_element_type=f32)
+    row_grad_gate = jnp.sum(raw_inner * inner, axis=-1).reshape(held, blocks, CAP)
+    grad_inner = raw_inner * row_gate
+    grad_w_out = jnp.einsum("erd,erf->edf", cot_rows, scaled_inner, preferred_element_type=f32)
+    grad_act = jnp.concatenate(
+        [
+            grad_inner * up_part * sigma * (1.0 + gate_part * (1.0 - sigma)),
+            grad_inner * gate_part * sigma,
+        ],
+        axis=-1,
+    ).astype(bf)
+    grad_w_in = jnp.einsum("erd,erf->edf", received, grad_act, preferred_element_type=f32)
+    grad_rows = jnp.einsum("erf,edf->erd", grad_act, weight_in, preferred_element_type=f32).astype(bf)
+    out_part = jnp.einsum(
+        "best,ebsd->btd",
+        pick,
+        produced.reshape(held, blocks, CAP, MODEL_WIDTH),
+        preferred_element_type=f32,
+    ).astype(bf)
+    in_part = jnp.einsum(
+        "best,ebsd->btd",
+        pick,
+        grad_rows.reshape(held, blocks, CAP, MODEL_WIDTH),
+        preferred_element_type=f32,
+    ).astype(bf)
+    gate_grads = jnp.sum(
+        jnp.where(place_of, jnp.transpose(row_grad_gate, (1, 0, 2))[..., None], 0.0), axis=2
+    )
+    gate_grads = jnp.transpose(gate_grads, (0, 2, 1))
+    columns = jnp.arange(EXPERT_COUNT, dtype=jnp.int32)
+    spread_gates = sum(
+        jnp.where(columns == first + e, gate_grads[:, :, e : e + 1], 0.0) for e in range(held)
+    )
+    high = spread_gates.astype(bf)
+    low = (spread_gates - high.astype(f32)).astype(bf)
+    in_part = jnp.concatenate(
+        [in_part, high, low, jnp.zeros((blocks, tokens, 128 - 2 * EXPERT_COUNT), bf)], axis=2
+    )
+
+    def cut_up(g):
+        whole = g.astype(bf).reshape(held, NX * NC, quarter, g.shape[2])
+        return [lax.dynamic_index_in_dim(whole, fsdp ^ j, 1, False) for j in range(NX * NC)]
+
+    def collect(parts):
+        mine = parts[0].astype(f32) + swap(parts[2], 2).astype(f32)
+        other = swap(parts[1], 1).astype(f32) + swap(parts[3], 3).astype(f32)
+        return jnp.where(
+            core == 0, jnp.concatenate([mine, other]), jnp.concatenate([other, mine])
+        )
+
+    in_part, out_part, pieces = lax.optimization_barrier(
+        (in_part, out_part, (cut_up(grad_w_in), cut_up(grad_w_out)))
+    )
+    grad_expert_in = collect(pieces[0])
+    grad_expert_out = collect(pieces[1])
+
+    gin, moe_out = reduce_scatter(
+        [in_part, out_part],
+        [Plan(0, (C, Y,), (C, Z, Y,)), Plan(1, (C, Y,), (C, Z, Y,))],
+        [f32, f32],
+        3,
+        "return_tokens",
+    )
+    layer_out = (mixed + moe_out).astype(bf)
+    grad_gate_map = gin[:, MODEL_WIDTH : MODEL_WIDTH + EXPERT_COUNT] + gin[
+        :, MODEL_WIDTH + EXPERT_COUNT : MODEL_WIDTH + 2 * EXPERT_COUNT
+    ]
+    grad_gate = jnp.sum(indicator * grad_gate_map[:, None, :], axis=-1)
+    grad_chosen = gates * (grad_gate - jnp.sum(gates * grad_gate, axis=-1, keepdims=True))
+    grad_logits = jnp.sum(indicator * grad_chosen[..., None], axis=1).astype(bf)
+    grad_router_part = lax.dot_general(
+        ffn_in, grad_logits, contract_rows, preferred_element_type=f32
+    )
+    grad_ffn_in = gin[:, :MODEL_WIDTH] + lax.dot_general(
+        grad_logits, router_w, contract_cols, preferred_element_type=f32
+    )
+    back_two, _ = rms_backward(grad_ffn_in, ffn_unit, inverse_two, ffn_gain)
+    grad_mixed = cot + back_two
+    grad_attn = grad_mixed.astype(bf)
+    grad_wo_part = lax.dot_general(
+        attention_output, grad_attn, contract_rows, preferred_element_type=f32
+    )
+    attention_output_gradient = lax.dot_general(
+        grad_attn, output_w, contract_cols, preferred_element_type=f32
+    ).astype(bf)
+    head_gradient = attention_output_gradient.reshape(tokens, KEY_VALUE_HEADS, group, HEAD_SIZE)
+    delta_rows = jnp.sum(
+        head_gradient.astype(f32)
+        * attention_output.reshape(tokens, KEY_VALUE_HEADS, group, HEAD_SIZE).astype(f32),
+        axis=-1,
+    )
+    delta_rows = jnp.transpose(delta_rows, (1, 2, 0))
+    weights_full = jnp.where(visible, jnp.exp(scores - log_sum_rows[..., None]), 0.0)
+    grad_probs = jnp.einsum(
+        "tkgd,nkd->kgtn", head_gradient, value_tensor, preferred_element_type=f32
+    )
+    grad_scores = (weights_full * (grad_probs - delta_rows[..., None])).astype(bf)
+    grad_query = attn_scale * jnp.einsum(
+        "kgtn,nkd->tkgd", grad_scores, key_tensor, preferred_element_type=f32
+    )
+    key_portion = attn_scale * jnp.einsum(
+        "kgtn,tkgd->nkd", grad_scores, query_rows, preferred_element_type=f32
+    )
+    value_portion = jnp.einsum(
+        "kgtn,tkgd->nkd", weights_full.astype(bf), head_gradient, preferred_element_type=f32
+    )
+    update = jnp.concatenate(
+        [
+            key_portion.astype(bf).reshape(ctx_size, tokens, kv_width),
+            value_portion.astype(bf).reshape(ctx_size, tokens, kv_width),
+        ],
+        axis=2,
+    )
+    (local_gradients,) = reduce_scatter(
+        [update], [Plan(0, (Y,), (Z, Y,))], [f32], 4, "return_keys"
+    )
+    query_back = (
+        rotate_pairs(
+            grad_query.reshape(tokens, QUERY_HEADS, HEAD_SIZE), cosine_table, -sine_table
+        )
+        .astype(bf)
+        .reshape(tokens, q_width)
+    )
+    key_back = (
+        rotate_pairs(
+            local_gradients[:, :kv_width].reshape(tokens, KEY_VALUE_HEADS, HEAD_SIZE),
+            cosine_table,
+            -sine_table,
+        )
+        .astype(bf)
+        .reshape(tokens, kv_width)
+    )
+    back = jnp.concatenate([query_back, key_back, local_gradients[:, kv_width:].astype(bf)], axis=1)
+    grad_one = lax.dot_general(attention_input, back, contract_rows, preferred_element_type=f32)
+    grad_attn_in = lax.dot_general(back, one, contract_cols, preferred_element_type=f32)
+    back_one, _ = rms_backward(grad_attn_in, attn_unit, inverse_one, attn_gain)
+    grad_input = grad_mixed + back_one
+    attn_gain_grad = jnp.sum(grad_attn_in * attn_unit, axis=0)
+    ffn_gain_grad = jnp.sum(grad_ffn_in * ffn_unit, axis=0)
+    grad_two = jnp.concatenate(
+        [
+            grad_wo_part,
+            grad_router_part,
+            attn_gain_grad[:, None],
+            ffn_gain_grad[:, None],
+            jnp.zeros((MODEL_WIDTH, 94), f32),
+        ],
+        axis=1,
+    )
+    sum_one, sum_two = reduce_scatter(
+        [
+            grad_one.astype(bf).reshape(-1, rows, grad_one.shape[1]),
+            grad_two.astype(bf).reshape(-1, rows, grad_two.shape[1]),
+        ],
+        [Plan(0, (C, X, Y,), (Z, Y, X, C,)), Plan(1, (C, Y, X,), (Z, Y, X, C,))],
+        [f32, f32],
+        5,
+        "return_weights",
+    )
+    at = MODEL_WIDTH + EXPERT_COUNT
+    return (
+        layer_out[None],
+        grad_input[None],
+        sum_two[:, at],
+        sum_two[:, at + 1],
+        sum_one[:, :q_width],
+        sum_one[:, q_width : q_width + kv_width],
+        sum_one[:, q_width + kv_width :],
+        sum_two[:, :MODEL_WIDTH],
+        sum_two[:, MODEL_WIDTH:at],
+        grad_expert_in,
+        grad_expert_out,
+    )
+
+
 def solution(mesh):
     placed = (
-        P("fsdp", "ctx", None),
-        P("fsdp", "ctx", None),
-        P(("ctx", "fsdp")),
-        P(("ctx", "fsdp")),
-        P(("ctx", "fsdp"), None),
-        P(("ctx", "fsdp"), None),
-        P(("ctx", "fsdp"), None),
-        P(("ctx", "fsdp"), None),
-        P(("ctx", "fsdp"), None),
-        P("ctx", "fsdp", None),
-        P("ctx", "fsdp", None),
-        P("fsdp", "ctx", None),
-    )
+        P(FSDP, CTX, None),
+        P(FSDP, CTX, None),
+        P((CTX, FSDP)),
+        P((CTX, FSDP)),
+        P((CTX, FSDP), None),
+        P((CTX, FSDP), None),
+        P((CTX, FSDP), None),
+        P((CTX, FSDP), None),
+        P((CTX, FSDP), None),
+        P(CTX, FSDP, None),
+        P(CTX, FSDP, None),
+        P(FSDP, CTX, None),
+    )
+    small = mesh.shape[CTX] == NZ * NY and mesh.shape[FSDP] == NX * NC
     return jax.shard_map(
-        local,
+        fast if small else local,
         mesh=mesh,
         in_specs=placed,
         out_specs=(
-            P("fsdp", "ctx", None),
-            P("fsdp", "ctx", None),
-            P(("ctx", "fsdp")),
-            P(("ctx", "fsdp")),
-            P(("ctx", "fsdp"), None),
-            P(("ctx", "fsdp"), None),
-            P(("ctx", "fsdp"), None),
-            P(("ctx", "fsdp"), None),
-            P(("ctx", "fsdp"), None),
-            P("ctx", "fsdp", None),
-            P("ctx", "fsdp", None),
+            P(FSDP, CTX, None),
+            P(FSDP, CTX, None),
+            P((CTX, FSDP)),
+            P((CTX, FSDP)),
+            P((CTX, FSDP), None),
+            P((CTX, FSDP), None),
+            P((CTX, FSDP), None),
+            P((CTX, FSDP), None),
+            P((CTX, FSDP), None),
+            P(CTX, FSDP, None),
+            P(CTX, FSDP, None),
         ),
         check_vma=False,
     )

time: 1620 us -> 720 us (0.44)
  waiting for transfers between devices: 1120 us -> 84 us
  Pallas kernels: 0 us -> 360 us
  blocking collectives: 179 us -> 0 us
  starting transfers between devices: 23.8 us -> 7.15 us
    reduce_scatter x10 -> x0, waiting for transfers between devices: 536 us -> none  [the longest x1 101 us: local(): lax.psum_scatter(grad_w_in.astype(jnp.bfloat16), 'fsdp', scatter_dimensio...]
    pallas_call x0 -> x6, Pallas kernels: none -> 360 us  [the longest x3 205 us: reduce_scatter(): pl.pallas_call(functools.partial(reduce_kernel, plans, n), out_shape=[jax...]
    all_to_all x4 -> x0, waiting for transfers between devices: 232 us -> none  [the longest x1 84.8 us: local(): lax.all_to_all(grad_outgoing, 'ctx', split_axis=0, concat_axis=2, tiled=T...]
    all_gather x8 -> x0, waiting for transfers between devices: 231 us -> none  [the longest x1 53.5 us: local(): lax.all_gather(value_weight, ('ctx', 'fsdp'), axis=0, tiled=True)]
    unnamed x24 -> x0, waiting for transfers between devices: 121 us -> none
    all_gather x1 -> x0, blocking collectives: 109 us -> none  [local(): lax.all_gather(router, ('ctx', 'fsdp'), axis=0, tiled=True)]
    ppermute x0 -> x12, waiting for transfers between devices: none -> 84 us  [swap(): return lax.ppermute(a, FSDP, [(i, i ^ flip) for i in range(NX * NC)])]
    unnamed x3 -> x0, blocking collectives: 70.3 us -> none
  transfers between devices with their start and end apart: 25 -> 12, of which waited for: 22 -> 4; matrix products, arithmetic and copies ran while one was open for 11% -> 16% of each run, Pallas kernels for 0% -> 21%
where the time goes in v1:
time: 720 us; the launch traced here: 710 us
  Pallas kernels  360 us (50%)
  matrix products  117 us (16%)
  local copies, waits for them, and re-layouts  88 us (12%)
  waiting for transfers between devices  84 us (12%)
  other arithmetic  51.3 us (7%)
    pallas_call x3, Pallas kernels, reduce_scatter(): pl.pallas_call(functools.partial(reduce_kernel, plans, n), out_shape=[jax...  205 us
    pallas_call x3, Pallas kernels, gather(): pl.pallas_call(functools.partial(gather_kernel, plans, n), out_shape=[jax...  155 us
    ppermute x12, waiting for transfers between devices, swap(): return lax.ppermute(a, FSDP, [(i, i ^ flip) for i in range(NX * NC)])  84 us
  transfers between devices with their start and end apart: 12, of which 4 were waited for; matrix products, arithmetic and copies ran while one was open for 16% of the time, Pallas kernels for 21%

profile of v1, /device:TPU:0, one launch (start us, length us, event | category | flops | bytes accessed | tf_op | source)
XLA Modules:
  0.0 710.0 jit_solution(15486542459759366934)
XLA Ops:
  0.8 4.0 dynamic-slice_bitcast_fusion.4
  8.7 83.0 %gather_weights.1 = (bf16[32,48,2560]{2,1,0:T(8,128)(2,1)}, bf16[32,48,1664]{2,1,0:T(8,128)(2,1)}, bf16[16,128,1536]{2,1,0:T(8,128)(2,1)}) custom-call(bf16[48,2560]{1,0:T(8,128)(2,1)} %pad_maximum_fusion.14.refs_0_, bf16[48,1664]{1,0:T(8,128)(2,1)} %concatenate.70.refs_1_, bf16[128,1536]{1,0:T(8,128)(2,1)} %bitcast_convert_fusion.3.refs_2_), custom_call_target="tpu_custom_call" | custom-call | tf_op jit(solution)/shard_map/gather_weights/pallas_call | solution.py:174
  94.1 1.5 collective-permute-start.4
  97.6 4.5 fusion.77
  105.5 29.5 %gather_keys.1 = bf16[8,128,1024]{2,1,0:T(8,128)(2,1)} custom-call(bf16[128,1024]{1,0:T(8,128)(2,1)} %pad_maximum_fusion.11.refs_0_), custom_call_target="tpu_custom_call" | custom-call | tf_op jit(solution)/shard_map/gather_keys/pallas_call | solution.py:174
  135.0 1.7 fusion.123
  137.3 1.8 copy.279
  139.0 1.5 subtract_convert_fusion.2
  142.6 2.8 fusion.5
  145.5 3.0 fusion.2
  148.6 3.0 copy-done
  151.6 3.5 fusion.57
  159.0 42.9 %gather_tokens.1 = bf16[16,128,1664]{2,1,0:T(8,128)(2,1)} custom-call(bf16[128,1664]{1,0:T(8,128)(2,1)} %concatenate.76.refs_0_), custom_call_target="tpu_custom_call" | custom-call | tf_op jit(solution)/shard_map/gather_tokens/pallas_call | solution.py:174
  204.5 5.9 fusion.29
  210.4 5.8 fusion.32
  216.2 4.4 copy.287
  220.7 2.2 copy.292
  227.6 15.1 %collective-permute-done.1 = bf16[2,384,512]{2,1,0:T(8,128)(2,1)S(1)} collective-permute-done((bf16[2,384,512]{2,1,0:T(8,128)(2,1)S(1)}, bf16[2,384,512]{2,1,0:T(8,128)(2,1)S(1)}, u32[]{:S(2)}, u32[]{:S(2)}) %collective-permute-start.1) | collective-permute-done | bytes 786464 | tf_op jit(solution)/shard_map/ppermute | solution.py:762
  243.6 2.0 pad_maximum_fusion.1
  245.7 2.5 gather_fusion
  248.2 2.3 select_bitcast_fusion.1
  250.5 1.9 copy.288
  252.4 6.5 pad_maximum_fusion
  258.9 6.5 gather_fusion.1
  265.4 3.5 select_bitcast_fusion
  269.6 10.2 %fusion.126 = f32[2,640,1024]{1,2,0:T(8,128)S(1)} fusion(bf16[2,640,1536]{2,1,0:T(8,128)(2,1)} %bitcast.267, bf16[2,1536,1024]{2,1,0:T(8,128)(2,1)S(1)} %bitcast.258), kind=kOutput, calls=%fused_computation.214 | convolution fusion | flops 4026531840 | bytes 15466496 | tf_op jit(solution)/shard_map/erd,edf->erf/dot_general | solution.py:924
  279.8 5.0 multiply_reduce_fusion
  285.6 8.0 %convolution_convert_fusion.5 = bf16[2,1536,512]{2,1,0:T(8,128)(2,1)} fusion(bf16[2,640,1536]{2,1,0:T(8,128)(2,1)} %bitcast.269, f32[2,640,512]{1,2,0:T(8,128)} %get-tuple-element.143, f32[2,640]{1,0:T(2,128)S(1)} %mul.400), kind=kOutput, calls=%fused_computation.39 | convolution fusion | flops 2016149504 | bytes 9704448 | tf_op jit(solution)/shard_map/erd,erf->edf/dot_general | solution.py:936
  293.6 4.4 convolution_convert_fusion.3
  300.8 6.5 convolution_convert_fusion.1
  307.4 8.4 %convolution_convert_fusion.4 = bf16[2,640,1536]{2,1,0:T(8,128)(2,1)} fusion(bf16[2,1536,1024]{2,1,0:T(8,128)(2,1)S(1)} %bitcast.261, bf16[2,640,512]{1,2,0:T(8,128)(2,1)} %copy-done.31, bf16[2,640,512]{1,2,0:T(8,128)(2,1)} %copy-done.30), kind=kOutput, calls=%fused_computation.32 | convolution fusion | flops 4033740800 | bytes 12845056 | tf_op jit(solution)/shard_map/erf,edf->erd/dot_general | solution.py:945
  315.8 3.6 dynamic-slice_bitcast_fusion.6
  319.4 3.3 dynamic-slice_bitcast_fusion
  323.7 4.4 bitcast_convert_fusion.refs_1_
  328.2 4.5 bitcast_convert_fusion.1
  333.5 11.1 %concatenate.78.refs_0_ = bf16[16,128,1664]{2,1,0:T(8,128)(2,1)} concatenate(bf16[16,128,1536]{2,1,0:T(8,128)(2,1)} %bitcast_convert_fusion.1, bf16[16,128,32]{2,1,0:T(8,128)(2,1)S(1)} %get-tuple-element.173, bf16[16,128,32]{2,1,0:T(8,128)(2,1)S(1)} %get-tuple-element.172, bf16[16,128,64]{2,1,0:T(8,128)(2,1)S(1)} %broadcast_in_dim.161), dimensions={2} | concatenate | bytes 13631488 | tf_op jit(solution)/shard_map/concatenate | solution.py:968
  344.6 91.8 %return_tokens.1 = (f32[128,1664]{1,0:T(8,128)}, f32[128,1536]{1,0:T(8,128)}) custom-call(bf16[16,128,1664]{2,1,0:T(8,128)(2,1)} %concatenate.78.refs_0_, bf16[16,128,1536]{2,1,0:T(8,128)(2,1)} %bitcast_convert_fusion.refs_1_), custom_call_target="tpu_custom_call" | custom-call | tf_op jit(solution)/shard_map/return_tokens/pallas_call | solution.py:335
  438.5 2.3 multiply_reduce_fusion.1
  440.9 2.1 bitcast_add_fusion
  443.0 4.0 fusion.38
  447.5 9.2 %fusion.1 = bf16[8,3,128,1024]{2,3,1,0:T(8,128)(2,1)S(1)} fusion(f32[8,1024,128,3]{2,1,3,0:T(8,128)} %copy-done, f32[8,3,128]{2,1,0:T(4,128)S(1)} %bitcast.318, f32[8,3,128]{2,1,0:T(4,128)S(1)} %copy-done.58, pred[128,1024]{0,1:T(8,128)(4,1)S(1)} %copy-done.33, bf16[1024,8,64,1]{0,2,3,1:T(8,128)(2,1)} %bitcast.292, bf16[128,8,3,64]{0,3,2,1:T(8,128)(2,1)S(1)} %bitcast.288), kind=kOutput, calls=%fused_computation.4 | convolution fusion | flops 424673280 | bytes 20471808 | tf_op jit(solution)/shard_map/tkgd,nkd->kgtn/dot_general | solution.py:1026
  457.9 2.1 fusion.41
  460.0 4.1 bitcast_convert_fusion.2
  464.4 1.5 copy.310
  468.9 3.1 pad_maximum_fusion.3.refs_0_
  472.0 33.7 %return_keys.1 = f32[128,1024]{1,0:T(8,128)} custom-call(bf16[8,128,1024]{2,1,0:T(8,128)(2,1)} %pad_maximum_fusion.3.refs_0_), custom_call_target="tpu_custom_call" | custom-call | tf_op jit(solution)/shard_map/return_keys/pallas_call | solution.py:335
  507.4 3.6 convolution_convert_fusion.2
  513.0 7.3 %fusion.66 = (bf16[1536]{0:T(1024)(128)(2,1)S(1)}, f32[128]{0:T(128)}, f32[128,1536]{1,0:T(8,128)}) fusion(bf16[1,128,1536]{2,1,0:T(8,128)(2,1)S(1)} %copy-done.4, f32[128]{0:T(128)} %copy-done.61, f32[1536]{0:T(1024)} %copy-done.38, bf16[1536,2560]{1,0:T(8,128)(2,1)} %bitcast.254, bf16[128,512]{0,1:T(8,128)(2,1)S(1)} %copy.313, ...), kind=kOutput, calls=%fused_computation.94 | convolution fusion | flops 1009973632 | bytes 9709568 | tf_op jit(solution)/shard_map/dot_general | solution.py:1067
  521.8 9.0 %concatenate.86.refs_1_ = bf16[32,48,1664]{2,1,0:T(8,128)(2,1)} concatenate(bf16[32,48,1536]{2,1,0:T(8,128)(2,1)} %convolution_convert_fusion.2, bf16[32,48,32]{2,1,0:T(8,128)(2,1)S(1)} %bitcast.283, bf16[32,48,1]{2,1,0:T(8,128)(2,1)S(1)} %concatenate.91, bf16[32,48,1]{2,1,0:T(8,128)(2,1)S(1)} %concatenate.92, bf16[32,48,94]{2,1,0:T(8,128)(2,1)S(1)} %broadcast_in_dim.164), dimensions={2} | concatenate | bytes 10223616 | tf_op jit(solution)/shard_map/concatenate | solution.py:1072
  530.8 5.5 convolution_convert_fusion
  536.3 79.6 %return_weights.1 = (f32[48,2560]{1,0:T(8,128)}, f32[48,1664]{1,0:T(8,128)}) custom-call(bf16[32,48,2560]{2,1,0:T(8,128)(2,1)} %bitcast.252, bf16[32,48,1664]{2,1,0:T(8,128)(2,1)} %concatenate.86.refs_1_), custom_call_target="tpu_custom_call" | custom-call | tf_op jit(solution)/shard_map/return_weights/pallas_call | solution.py:335
  615.9 1.8 slice.145
  619.0 2.1 collective-permute-start.6
  621.2 1.5 slice_reduce_fusion
  622.7 1.7 slice.142
  625.8 1.6 fusion.124
  627.5 2.3 fusion.64
  631.2 7.3 %collective-permute-done.11 = bf16[2,384,512]{2,1,0:T(8,128)(2,1)} collective-permute-done((bf16[2,384,512]{2,1,0:T(8,128)(2,1)}, bf16[2,384,512]{2,1,0:T(8,128)(2,1)}, u32[]{:S(2)}, u32[]{:S(2)}) %collective-permute-start.11) | collective-permute-done | bytes 786464 | tf_op jit(solution)/shard_map/ppermute | solution.py:762
  638.5 1.6 convert_add_fusion.2
  640.1 2.0 maximum_select_fusion.1
  642.1 31.4 %collective-permute-done.6 = bf16[2,384,1024]{2,1,0:T(8,128)(2,1)} collective-permute-done((bf16[2,384,1024]{2,1,0:T(8,128)(2,1)}, bf16[2,384,1024]{2,1,0:T(8,128)(2,1)}, u32[]{:S(2)}, u32[]{:S(2)}) %collective-permute-start.6) | collective-permute-done | bytes 1572896 | tf_op jit(solution)/shard_map/ppermute | solution.py:762
  673.6 2.0 convert_add_fusion.1
  675.6 30.2 %collective-permute-done.8 = bf16[2,384,1024]{2,1,0:T(8,128)(2,1)S(1)} collective-permute-done((bf16[2,384,1024]{2,1,0:T(8,128)(2,1)}, bf16[2,384,1024]{2,1,0:T(8,128)(2,1)S(1)}, u32[]{:S(2)}, u32[]{:S(2)}) %collective-permute-start.8) | collective-permute-done | bytes 1572896 | tf_op jit(solution)/shard_map/ppermute | solution.py:762
  706.4 3.4 maximum_select_fusion
  (279 shorter events, 49.0 us)
Async XLA Ops:
  0.7 5.4 copy-start.17
  0.7 6.2 copy-start.65
  0.7 6.2 copy-start.71
  0.7 6.3 copy-start.72
  0.7 6.4 copy-start.46
  0.7 6.4 copy-start.55
  0.7 6.4 copy-start.56
  4.8 92.7 %copy-start.4 = (bf16[1,128,1536]{2,1,0:T(8,128)(2,1)S(1)}, bf16[1,128,1536]{2,1,0:T(8,128)(2,1)}, u32[]{:S(2)}) copy-start(bf16[1,128,1536]{2,1,0:T(8,128)(2,1)} %param.12) | copy-start | bytes 1179652
  91.7 131.2 %collective-permute-start = (bf16[2,384,512]{2,1,0:T(8,128)(2,1)}, bf16[2,384,512]{2,1,0:T(8,128)(2,1)}, u32[]{:S(2)}, u32[]{:S(2)}) collective-permute-start(bf16[2,384,512]{2,1,0:T(8,128)(2,1)} %get-tuple-element.38), channel_id=1, source_target_pairs={{0,1},{1,0},{2,3},{3,2},{4,5},{5,4},{6,7},{7,6},{8,9},{9,8},{10,11... | collective-permute-start | bytes 2359304 | tf_op jit(solution)/shard_map/ppermute | solution.py:762
  92.2 150.5 %collective-permute-start.2 = (bf16[2,384,512]{2,1,0:T(8,128)(2,1)}, bf16[2,384,512]{2,1,0:T(8,128)(2,1)}, u32[]{:S(2)}, u32[]{:S(2)}) collective-permute-start(bf16[2,384,512]{2,1,0:T(8,128)(2,1)} %get-tuple-element.38), channel_id=1, source_target_pairs={{0,3},{1,2},{2,1},{3,0},{4,7},{5,6},{6,5},{7,4},{8,11},{9,10},{10,... | collective-permute-start | bytes 2359304 | tf_op jit(solution)/shard_map/ppermute | solution.py:762
  93.4 158.9 %collective-permute-start.3 = (bf16[2,384,1024]{2,1,0:T(8,128)(2,1)}, bf16[2,384,1024]{2,1,0:T(8,128)(2,1)}, u32[]{:S(2)}, u32[]{:S(2)}) collective-permute-start(bf16[2,384,1024]{2,1,0:T(8,128)(2,1)} %get-tuple-element.40), channel_id=1, source_target_pairs={{0,1},{1,0},{2,3},{3,2},{4,5},{5,4},{6,7},{7,6},{8,9},{9,8},{10,11... | collective-permute-start | bytes 4718600 | tf_op jit(solution)/shard_map/ppermute | solution.py:762
  93.8 158.5 %collective-permute-start.5 = (bf16[2,384,1024]{2,1,0:T(8,128)(2,1)}, bf16[2,384,1024]{2,1,0:T(8,128)(2,1)}, u32[]{:S(2)}, u32[]{:S(2)}) collective-permute-start(bf16[2,384,1024]{2,1,0:T(8,128)(2,1)} %get-tuple-element.40), channel_id=1, source_target_pairs={{0,3},{1,2},{2,1},{3,0},{4,7},{5,6},{6,5},{7,4},{8,11},{9,10},{10,... | collective-permute-start | bytes 4718600 | tf_op jit(solution)/shard_map/ppermute | solution.py:762
  94.1 158.3 %collective-permute-start.4 = (bf16[2,384,1024]{2,1,0:T(8,128)(2,1)}, bf16[2,384,1024]{2,1,0:T(8,128)(2,1)}, u32[]{:S(2)}, u32[]{:S(2)}) collective-permute-start(bf16[2,384,1024]{2,1,0:T(8,128)(2,1)} %get-tuple-element.39), channel_id=1, source_target_pairs={{0,2},{1,3},{2,0},{3,1},{4,6},{5,7},{6,4},{7,5},{8,10},{9,11},{10,... | collective-permute-start | bytes 4718600 | tf_op jit(solution)/shard_map/ppermute | solution.py:762
  97.5 4.7 copy-start.38
  104.5 32.1 %copy-start.43 = (f32[128,32]{0,1:T(8,128)}, f32[128,32]{0,1:T(8,128)S(1)}, u32[]{:S(2)}) copy-start(f32[128,32]{0,1:T(8,128)S(1)} %get-tuple-element.177) | copy-start | bytes 49156
  104.5 34.5 %copy-start.36 = (f32[128,32]{0,1:T(8,128)}, f32[128,32]{0,1:T(8,128)S(1)}, u32[]{:S(2)}) copy-start(f32[128,32]{0,1:T(8,128)S(1)} %get-tuple-element.178) | copy-start | bytes 49156
  137.2 8.2 %copy-start.2 = (bf16[1024,512]{0,1:T(8,128)(2,1)}, bf16[1024,512]{0,1:T(8,128)(2,1)S(1)}, u32[]{:S(2)}) copy-start(bf16[1024,512]{0,1:T(8,128)(2,1)S(1)} %copy.278) | copy-start | bytes 3145732
  140.6 4.9 copy-start.24
  141.3 7.3 %copy-start.32 = (pred[128,1024]{0,1:T(8,128)(4,1)}, pred[128,1024]{0,1:T(8,128)(4,1)S(1)}, u32[]{:S(2)}) copy-start(pred[128,1024]{0,1:T(8,128)(4,1)S(1)} %iota_compare_fusion.1) | copy-start | bytes 393220
  145.5 6.1 copy-start
  145.5 6.1 copy-start.48
  145.5 6.1 copy-start.34
  145.5 9.6 %slice-start.6 = ((s8[5111808]{0:T(1024)(128)(4,1)}), s8[4194304]{0:T(1024)(128)(4,1)S(1)}, s32[]{:S(2)}) async-start(s8[5111808]{0:T(1024)(128)(4,1)} %bitcast.304), calls=%async_computation.6 | async-start | bytes 8388608
  148.6 6.5 copy-start.51
  203.9 6.4 copy-start.41
  222.9 19.9 %collective-permute-start.1 = (bf16[2,384,512]{2,1,0:T(8,128)(2,1)S(1)}, bf16[2,384,512]{2,1,0:T(8,128)(2,1)S(1)}, u32[]{:S(2)}, u32[]{:S(2)}) collective-permute-start(bf16[2,384,512]{2,1,0:T(8,128)(2,1)S(1)} %copy-done.21), channel_id=1, source_target_pairs={{0,2},{1,3},{2,0},{3,1},{4,6},{5,7},{6,4},{7,5},{8,10},{9,11},{10,... | collective-permute-start | bytes 2359304 | tf_op jit(solution)/shard_map/ppermute | solution.py:762
  258.9 6.5 copy-start.70
  269.5 10.3 %copy-start.7 = (bf16[2,4,384,1024]{3,2,1,0:T(8,128)(2,1)}, bf16[2,4,384,1024]{3,2,1,0:T(8,128)(2,1)S(1)}, u32[]{:S(2)}) copy-start(bf16[2,4,384,1024]{3,2,1,0:T(8,128)(2,1)S(1)} %copy.293) | copy-start | bytes 18874372
  269.5 10.3 %copy-start.14 = (bf16[2,16,40,1536]{3,2,1,0:T(8,128)(2,1)S(1)}, bf16[2,16,40,1536]{3,2,1,0:T(8,128)(2,1)}, u32[]{:S(2)}) copy-start(bf16[2,16,40,1536]{3,2,1,0:T(8,128)(2,1)} %copy.287) | copy-start | bytes 11796484
  269.6 10.3 %copy-start.19 = (bf16[2,4,384,512]{3,2,1,0:T(8,128)(2,1)S(1)}, bf16[2,4,384,512]{3,2,1,0:T(8,128)(2,1)}, u32[]{:S(2)}) copy-start(bf16[2,4,384,512]{3,2,1,0:T(8,128)(2,1)} %copy.288) | copy-start | bytes 9437188
  279.8 5.0 copy-start.11
  279.8 5.1 copy-start.42
  279.8 5.1 copy-start.52
  285.6 8.0 %copy-start.20 = (bf16[2,4,384,512]{3,2,1,0:T(8,128)(2,1)S(1)}, bf16[2,4,384,512]{3,2,1,0:T(8,128)(2,1)}, u32[]{:S(2)}) copy-start(bf16[2,4,384,512]{3,2,1,0:T(8,128)(2,1)} %copy.288) | copy-start | bytes 9437188
  285.6 8.0 %copy-start.74 = (f32[2,640,512]{1,2,0:T(8,128)S(1)}, f32[2,640,512]{1,2,0:T(8,128)}, u32[]{:S(2)}) copy-start(f32[2,640,512]{1,2,0:T(8,128)} %get-tuple-element.143) | copy-start | bytes 7864324
  298.1 9.3 %slice-start.3 = ((s8[6291456]{0:T(1024)(128)(4,1)}), s8[4194304]{0:T(1024)(128)(4,1)S(1)}, s32[]{:S(2)}) async-start(s8[6291456]{0:T(1024)(128)(4,1)} %bitcast.259), calls=%async_computation.3 | async-start | bytes 8388608
  300.8 6.5 slice-start.4
  328.1 4.6 copy-start.68
  344.6 93.0 %copy-start.54 = (s32[1,128,8]{1,2,0:T(8,128)S(1)}, s32[1,128,8]{1,2,0:T(8,128)}, u32[]{:S(2)}) copy-start(s32[1,128,8]{1,2,0:T(8,128)} %param.13) | copy-start | bytes 12292
  344.6 93.0 %copy-start.45 = (f32[128,8]{0,1:T(8,128)S(1)}, f32[128,8]{0,1:T(8,128)}, u32[]{:S(2)}) copy-start(f32[128,8]{0,1:T(8,128)} %copy-done.44) | copy-start | bytes 12292
  344.6 93.0 %copy-start.60 = (f32[128]{0:T(128)S(1)}, f32[128]{0:T(128)}, u32[]{:S(2)}) copy-start(f32[128]{0:T(128)} %copy-done.59) | copy-start | bytes 1540
  344.6 93.0 %copy-start.64 = (f32[128]{0:T(128)S(1)}, f32[128]{0:T(128)}, u32[]{:S(2)}) copy-start(f32[128]{0:T(128)} %copy-done.63) | copy-start | bytes 1540
  344.6 93.1 %copy-start.9 = (bf16[128,1536]{1,0:T(8,128)(2,1)S(1)}, bf16[128,1536]{1,0:T(8,128)(2,1)}, u32[]{:S(2)}) copy-start(bf16[128,1536]{1,0:T(8,128)(2,1)} %copy-done.8) | copy-start | bytes 1179652
  344.6 93.9 %copy-start.6 = (f32[128,1536]{1,0:T(8,128)S(1)}, f32[128,1536]{1,0:T(8,128)}, u32[]{:S(2)}) copy-start(f32[128,1536]{1,0:T(8,128)} %copy-done.5) | copy-start | bytes 2359300
  344.6 93.9 %copy-start.50 = (f32[1536]{0:T(1024)S(1)}, f32[1536]{0:T(1024)}, u32[]{:S(2)}) copy-start(f32[1536]{0:T(1024)} %get-tuple-element.136) | copy-start | bytes 18436
  344.6 93.9 %copy-start.67 = (f32[128]{0:T(128)S(1)}, f32[128]{0:T(128)}, u32[]{:S(2)}) copy-start(f32[128]{0:T(128)} %copy-done.66) | copy-start | bytes 1540
  447.5 9.2 %copy-start.3 = (bf16[1024,512]{0,1:T(8,128)(2,1)S(1)}, bf16[1024,512]{0,1:T(8,128)(2,1)}, u32[]{:S(2)}) copy-start(bf16[1024,512]{0,1:T(8,128)(2,1)} %copy-done.2) | copy-start | bytes 3145732
  447.5 12.5 %slice-start = ((s8[12582912]{0:T(1024)(128)(4,1)}), s8[4194304]{0:T(1024)(128)(4,1)S(1)}, s32[]{:S(2)}) async-start(s8[12582912]{0:T(1024)(128)(4,1)} %bitcast.250), calls=%async_computation | async-start | bytes 8388608
  447.5 12.5 %slice-start.1 = ((s8[12582912]{0:T(1024)(128)(4,1)}), s8[4194304]{0:T(1024)(128)(4,1)S(1)}, s32[]{:S(2)}) async-start(s8[12582912]{0:T(1024)(128)(4,1)} %bitcast.250), calls=%async_computation.1 | async-start | bytes 8388608
  468.9 38.3 %copy-start.40 = (bf16[1536,32]{0,1:T(8,128)(2,1)S(1)}, bf16[1536,32]{0,1:T(8,128)(2,1)}, u32[]{:S(2)}) copy-start(bf16[1536,32]{0,1:T(8,128)(2,1)} %convolution_convert_fusion.6) | copy-start | bytes 294916
  505.7 5.4 slice-start.5
  505.7 5.5 copy-start.37
  506.7 120.7 %collective-permute-start.9 = (bf16[2,384,512]{2,1,0:T(8,128)(2,1)}, bf16[2,384,512]{2,1,0:T(8,128)(2,1)}, u32[]{:S(2)}, u32[]{:S(2)}) collective-permute-start(bf16[2,384,512]{2,1,0:T(8,128)(2,1)} %get-tuple-element.52), channel_id=1, source_target_pairs={{0,2},{1,3},{2,0},{3,1},{4,6},{5,7},{6,4},{7,5},{8,10},{9,11},{10,... | collective-permute-start | bytes 2359304 | tf_op jit(solution)/shard_map/ppermute | solution.py:762
  513.0 8.1 %copy-start.57 = (bf16[1536]{0:T(1024)(128)(2,1)S(1)}, bf16[1536]{0:T(1024)(128)(2,1)}, u32[]{:S(2)}) copy-start(bf16[1536]{0:T(1024)(128)(2,1)} %get-tuple-element.132) | copy-start | bytes 9220
  521.8 9.0 %copy-start.39 = (f32[1536]{0:T(1024)S(1)}, f32[1536]{0:T(1024)}, u32[]{:S(2)}) copy-start(f32[1536]{0:T(1024)} %copy-done.38) | copy-start | bytes 18436
  521.8 9.0 %copy-start.62 = (f32[128]{0:T(128)S(1)}, f32[128]{0:T(128)}, u32[]{:S(2)}) copy-start(f32[128]{0:T(128)} %copy-done.61) | copy-start | bytes 1540
  536.3 86.4 %copy-start.73 = (f32[128]{0:T(128)S(1)}, f32[128]{0:T(128)}, u32[]{:S(2)}) copy-start(f32[128]{0:T(128)} %get-tuple-element.135) | copy-start | bytes 1540
  615.9 14.0 %copy-start.22 = (bf16[2,384,512]{2,1,0:T(8,128)(2,1)S(1)}, bf16[2,384,512]{2,1,0:T(8,128)(2,1)}, u32[]{:S(2)}) copy-start(bf16[2,384,512]{2,1,0:T(8,128)(2,1)} %get-tuple-element.51) | copy-start | bytes 2359300
  619.0 12.2 %collective-permute-start.10 = (bf16[2,384,512]{2,1,0:T(8,128)(2,1)}, bf16[2,384,512]{2,1,0:T(8,128)(2,1)}, u32[]{:S(2)}, u32[]{:S(2)}) collective-permute-start(bf16[2,384,512]{2,1,0:T(8,128)(2,1)} %get-tuple-element.53), channel_id=1, source_target_pairs={{0,1},{1,0},{2,3},{3,2},{4,5},{5,4},{6,7},{7,6},{8,9},{9,8},{10,11... | collective-permute-start | bytes 2359304 | tf_op jit(solution)/shard_map/ppermute | solution.py:762
  619.0 19.5 %collective-permute-start.11 = (bf16[2,384,512]{2,1,0:T(8,128)(2,1)}, bf16[2,384,512]{2,1,0:T(8,128)(2,1)}, u32[]{:S(2)}, u32[]{:S(2)}) collective-permute-start(bf16[2,384,512]{2,1,0:T(8,128)(2,1)} %get-tuple-element.54), channel_id=1, source_target_pairs={{0,3},{1,2},{2,1},{3,0},{4,7},{5,6},{6,5},{7,4},{8,11},{9,10},{10,... | collective-permute-start | bytes 2359304 | tf_op jit(solution)/shard_map/ppermute | solution.py:762
  619.0 54.5 %collective-permute-start.6 = (bf16[2,384,1024]{2,1,0:T(8,128)(2,1)}, bf16[2,384,1024]{2,1,0:T(8,128)(2,1)}, u32[]{:S(2)}, u32[]{:S(2)}) collective-permute-start(bf16[2,384,1024]{2,1,0:T(8,128)(2,1)} %get-tuple-element.48), channel_id=1, source_target_pairs={{0,2},{1,3},{2,0},{3,1},{4,6},{5,7},{6,4},{7,5},{8,10},{9,11},{10,... | collective-permute-start | bytes 4718600 | tf_op jit(solution)/shard_map/ppermute | solution.py:762
  621.2 54.5 %collective-permute-start.7 = (bf16[2,384,1024]{2,1,0:T(8,128)(2,1)}, bf16[2,384,1024]{2,1,0:T(8,128)(2,1)S(1)}, u32[]{:S(2)}, u32[]{:S(2)}) collective-permute-start(bf16[2,384,1024]{2,1,0:T(8,128)(2,1)} %get-tuple-element.49), channel_id=1, source_target_pairs={{0,1},{1,0},{2,3},{3,2},{4,5},{5,4},{6,7},{7,6},{8,9},{9,8},{10,11... | collective-permute-start | bytes 4718600 | tf_op jit(solution)/shard_map/ppermute | solution.py:762
  627.4 78.4 %collective-permute-start.8 = (bf16[2,384,1024]{2,1,0:T(8,128)(2,1)}, bf16[2,384,1024]{2,1,0:T(8,128)(2,1)S(1)}, u32[]{:S(2)}, u32[]{:S(2)}) collective-permute-start(bf16[2,384,1024]{2,1,0:T(8,128)(2,1)} %get-tuple-element.50), channel_id=1, source_target_pairs={{0,3},{1,2},{2,1},{3,0},{4,7},{5,6},{6,5},{7,4},{8,11},{9,10},{10,... | collective-permute-start | bytes 4718600 | tf_op jit(solution)/shard_map/ppermute | solution.py:762
  640.1 33.5 %copy-start.10 = (bf16[2,384,1024]{2,1,0:T(8,128)(2,1)S(1)}, bf16[2,384,1024]{2,1,0:T(8,128)(2,1)}, u32[]{:S(2)}) copy-start(bf16[2,384,1024]{2,1,0:T(8,128)(2,1)} %get-tuple-element.47) | copy-start | bytes 4718596
  (31 other events, 85.9 us)

commit v2 on v1

--- a/solution.py
+++ b/solution.py
@@ -350,6 +350,444 @@
     )(*arrays)
 
 
+class Gather:
+    def __init__(self, place, plan, src, out, send_sem, recv_sem, spare_sem, slot, base):
+        self.place, self.plan, self.src, self.out = place, plan, src, out
+        self.send_sem, self.recv_sem, self.spare_sem = send_sem, recv_sem, spare_sem
+        self.slot, self.base = slot, base
+        self.pending = []
+
+    @staticmethod
+    def sends(plan):
+        return sum(len(gather_sends(plan.order, k, f)) for k, f in gather_events(plan.order))
+
+    def step(self, k, flips):
+        place, plan = self.place, self.plan
+        z = place.at[Z]
+        z_from = place.order[k]
+        index = flat_index(place.coords(z_from, flips), plan.index)
+        rows = plan.rows
+        target = self.out.at[index] if rows is None else self.out.at[index, pl.ds(rows[0], rows[1])]
+        sem = self.recv_sem.at[self.base + index]
+        own = k == 0 and not flips
+        source = target
+        if own:
+            source = self.src if rows is None else self.src.at[pl.ds(rows[0], rows[1])]
+        else:
+            pltpu.make_async_remote_copy(
+                src_ref=target, dst_ref=target, send_sem=self.spare_sem, recv_sem=sem,
+                device_id=place.across(C), device_id_type=DEV,
+            ).wait_recv()
+        for way in gather_sends(plan.order, k, flips):
+            if way in (UP, DOWN):
+                step = 1 if way == UP else -1
+                go = z < NZ - 1 if way == UP else z > 0
+                if k > 0:
+                    go = jnp.logical_and(go, z_from < z if way == UP else z_from > z)
+                dest = place.device(Z, jnp.clip(z + step, 0, NZ - 1))
+            else:
+                go, dest = None, place.across(way)
+            copy = pltpu.make_async_remote_copy(
+                src_ref=source, dst_ref=target, send_sem=self.send_sem.at[self.slot], recv_sem=sem,
+                device_id=dest, device_id_type=DEV,
+            )
+            self.slot += 1
+            if go is None:
+                copy.start()
+            else:
+                pl.when(go)(copy.start)
+            self.pending.append((go, copy.wait_send))
+
+    def finish(self):
+        for go, wait in self.pending:
+            if go is None:
+                wait()
+            else:
+                pl.when(go)(wait)
+
+
+class Reduce:
+    def __init__(self, place, plan, held, levels, chain, send_sem, recv_sem, spare_sem):
+        self.place, self.plan, self.held, self.levels, self.chain = place, plan, held, levels, chain
+        self.send_sem, self.recv_sem, self.spare_sem = send_sem, recv_sem, spare_sem
+        dims = plan.order
+        self.kept = [subsets(dims[p + 1 :]) for p in range(len(dims))]
+        self.base = [NZ * sum(len(f) for f in self.kept[:p]) for p in range(len(dims) + 1)]
+        self.slot = 0
+        self.pending = []
+
+    @staticmethod
+    def counts(plan):
+        kept = [NZ * len(subsets(plan.order[p + 1 :])) for p in range(len(plan.order))]
+        return kept, sum(kept) + NZ - 1, sum(kept) + NZ + 1
+
+    def push(self, source, target, sem, dest):
+        copy = pltpu.make_async_remote_copy(
+            src_ref=source, dst_ref=target, send_sem=self.send_sem.at[self.slot], recv_sem=sem,
+            device_id=dest, device_id_type=DEV,
+        )
+        self.slot += 1
+        copy.start()
+        self.pending.append(copy)
+
+    def arrived(self, target, sem):
+        pltpu.make_async_remote_copy(
+            src_ref=target, dst_ref=target, send_sem=self.spare_sem, recv_sem=sem,
+            device_id=self.place.across(C), device_id_type=DEV,
+        ).wait_recv()
+
+    def block(self, k, flips):
+        return flat_index(self.place.coords(self.place.order[k], flips), self.plan.index)
+
+    def first(self, k):
+        dim = self.plan.order[0]
+        for n, f in enumerate(self.kept[0]):
+            spot = self.place.order[k] * len(self.kept[0]) + n
+            self.push(
+                self.held.at[self.block(k, (dim,) + f)], self.levels[0].at[spot],
+                self.recv_sem.at[spot], self.place.across(dim),
+            )
+
+    def level(self, p, k):
+        dims = self.plan.order
+        z_to = self.place.order[k]
+        for f in sorted(self.kept[p], key=lambda f: -len(f)):
+            spot = z_to * len(self.kept[p]) + self.kept[p].index(f)
+            mine = self.held.at[self.block(k, f)]
+            self.arrived(self.levels[p].at[spot], self.recv_sem.at[self.base[p] + spot])
+            add_into(mine, self.levels[p].at[spot])
+            later = p + 1
+            if later < len(dims) and dims[later] in f:
+                left = tuple(d for d in f if d != dims[later])
+                there = z_to * len(self.kept[later]) + self.kept[later].index(left)
+                self.push(
+                    mine, self.levels[later].at[there],
+                    self.recv_sem.at[self.base[later] + there], self.place.across(dims[later]),
+                )
+
+    def along(self, k):
+        z = self.place.at[Z]
+        dest = self.place.order[k]
+        up = dest > z
+        spot = dest + jnp.where(up, 1, 0)
+        mine = self.held.at[self.block(k, ())]
+        sem = self.recv_sem.at[self.base[-1] + spot]
+
+        @pl.when(jnp.where(up, z > 0, z < NZ - 1))
+        def _():
+            self.arrived(self.chain.at[spot], sem)
+            add_into(mine, self.chain.at[spot])
+
+        self.push(mine, self.chain.at[spot], sem, self.place.along(jnp.where(up, 1, -1)))
+
+    def last(self, out):
+        z = self.place.at[Z]
+        mine = self.held.at[self.block(0, ())]
+        for go, spot in ((z > 0, z + 1), (z < NZ - 1, z)):
+
+            @pl.when(go)
+            def _():
+                self.arrived(self.chain.at[spot], self.recv_sem.at[self.base[-1] + spot])
+                add_into(mine, self.chain.at[spot])
+
+        out[...] = mine[...].astype(out.dtype)
+
+    def steps(self):
+        depth = len(self.plan.order)
+        far = list(reversed(range(NZ)))
+        out = []
+        for t in range(NZ + depth):
+            for p in range(depth):
+                if 0 <= t - p < NZ:
+                    out.append(functools.partial(self.level, p, far[t - p]))
+            if 0 <= t - depth < NZ - 1:
+                out.append(functools.partial(self.along, far[t - depth]))
+        return out
+
+    def finish(self):
+        for copy in self.pending:
+            copy.wait_send()
+
+
+def tile_up(n, m):
+    return (n + m - 1) // m * m
+
+
+def columns_of(width, chunk=512):
+    return [(i, min(chunk, width - i)) for i in range(0, width, chunk)]
+
+
+def moe_kernel(plans, back, width, hidden, cap, *refs):
+    payload, cots, w_own, w_core, w_x, w_both = refs[:6]
+    gin_out, moe_out = refs[6:8]
+    grads = refs[8:12]
+    (
+        seen, cot_seen, weights, taken, cot_taken, rows_buf, scaled, grad_act, pick, stage,
+        lvl_a0, lvl_a1, chain_a, lvl_b0, lvl_b1, chain_b,
+        send_sem, recv_sem, spare_sem, send_a, recv_a, send_b, recv_b, load_sem, store_sem,
+    ) = refs[12:]
+    bf, f32 = jnp.bfloat16, jnp.float32
+    place = Place()
+    count = payload.shape[0]
+    pair = 2 * cap
+    wide = width + 128
+    quarter = width // (NX * NC)
+    half = NZ * pair
+    lanes = pick.shape[2]
+    held = weights.shape[0]
+    fsdp = place.at[X] * NC + place.at[C]
+    first = (((place.at[Z] * NY + place.at[Y]) * NC) + place.at[C]) * held
+
+    loads = []
+    for j, ref in enumerate((w_own, w_core, w_x, w_both)):
+        rows = pl.ds(pl.multiple_of((fsdp ^ j) * quarter, quarter), quarter)
+        for e in range(held):
+            loads.append(pltpu.make_async_copy(ref.at[e], weights.at[e, rows], load_sem.at[len(loads)]))
+    base_of = lambda h, k: (jnp.where(h == 0, place.at[C], 1 - place.at[C]) * NZ + place.order[k]) * NY
+    cot_loads = {}
+    for k in range(NZ):
+        for h in range(2):
+            at = pl.ds(base_of(h, k), NY)
+            cot_loads[(h, k)] = pltpu.make_async_copy(cots.at[at], cot_seen.at[at], load_sem.at[len(loads) + len(cot_loads)])
+
+    greet(place, (Z, Y, C))
+    ways = []
+    send_at = 0
+    for n, plan in enumerate(plans):
+        ways.append(Gather(place, plan, payload, seen, send_sem, recv_sem, spare_sem, send_at, n * plan.blocks))
+        send_at += Gather.sends(plan)
+    for way in ways:
+        way.step(0, ())
+    for key in cot_loads:
+        cot_loads[key].start()
+    for copy in loads:
+        copy.start()
+    seen[flat_index(place.at, plans[0].index)] = payload[...]
+
+    row_id = lax.broadcasted_iota(jnp.int32, (NY * count, NY * count), 0)
+    col_id = lax.broadcasted_iota(jnp.int32, (NY * count, NY * count), 1)
+    earlier = jnp.logical_and(col_id < row_id, col_id // count == row_id // count).astype(bf)
+    lane_id = lax.broadcasted_iota(jnp.int32, (1, 128), 1)
+    here = [(lane_id == first + e).astype(f32) for e in range(held)]
+    pick_lane = lax.broadcasted_iota(jnp.int32, (NY * count, lanes), 1).astype(f32)
+    y_shift = (lax.broadcasted_iota(jnp.int32, (NY * count, 1), 0) // count * cap).astype(f32)
+
+    def dispatch(source, target, h, k, cols):
+        at = pl.ds(base_of(h, k), NY)
+        r = (h * NZ + k) * pair
+        for c0, cn in cols:
+            block = source[at, :, c0 : c0 + cn].reshape(NY * count, cn)
+            got = lax.dot_general(
+                pick[h * NZ + k], block, (((0,), (0,)), ((), ())), preferred_element_type=f32
+            ).astype(bf)
+            for e in range(held):
+                target[e, r : r + pair, c0 : c0 + cn] = got[e * pair : (e + 1) * pair]
+
+    def cot_chunk(h, k):
+        cot_loads[(h, k)].wait()
+        at = pl.ds(base_of(h, k), NY)
+        chosen = cot_seen[at, :, width:wide].reshape(NY * count, 128)
+        before = jnp.dot(earlier, chosen, preferred_element_type=f32)
+        picked = None
+        for e in range(held):
+            is_here = jnp.sum(chosen.astype(f32) * here[e], axis=1, keepdims=True)
+            slot = jnp.sum(before * here[e], axis=1, keepdims=True) + y_shift + e * pair
+            target = jnp.where(is_here > 0.5, slot, -1.0)
+            hit = pick_lane == target
+            picked = hit if picked is None else jnp.logical_or(picked, hit)
+        pick[h * NZ + k] = picked.astype(f32).astype(bf)
+        dispatch(cot_seen, cot_taken, h, k, columns_of(width))
+
+    def hidden_chunk(h, e, n, tile):
+        rows = pl.ds(h * half, half)
+        tokens_in = taken[e, rows, :width]
+        gate = jnp.sum(taken[e, rows, width:wide].astype(f32) * here[e], axis=1, keepdims=True)
+        col = n * tile
+        g = jnp.dot(tokens_in, weights[e, :, col : col + tile], preferred_element_type=f32)
+        u = jnp.dot(tokens_in, weights[e, :, hidden + col : hidden + col + tile], preferred_element_type=f32)
+        raw = jnp.dot(
+            cot_taken[e, rows, :], weights[e, :, 2 * hidden + col : 2 * hidden + col + tile], preferred_element_type=f32
+        )
+        s = jax.nn.sigmoid(g)
+        gs = g * s
+        inner = gs * u
+        scaled[e, rows, col : col + tile] = (inner * gate).astype(bf)
+        grad_inner = raw * gate
+        grad_act[e, rows, col : col + tile] = (grad_inner * u * s * (1.0 + g * (1.0 - s))).astype(bf)
+        grad_act[e, rows, hidden + col : hidden + col + tile] = (grad_inner * gs).astype(bf)
+        return jnp.sum(raw * inner, axis=1, keepdims=True)
+
+    def hidden_part(h, e):
+        tile = min(256, hidden)
+        gate_grad = sum(hidden_chunk(h, e, n, tile) for n in range(hidden // tile))
+        high = gate_grad.astype(bf).astype(f32)
+        there = pl.ds(h * half, half)
+        apart = (lane_id == EXPERT_COUNT + first + e).astype(f32)
+        rows_buf[e, there, width:wide] = (high * here[e] + (gate_grad - high) * apart).astype(bf)
+
+    def project(h, e, left, weight_cols):
+        rows = pl.ds(h * half, half)
+        lo, n = weight_cols
+        for c0, cn in columns_of(width):
+            rows_buf[e, rows, c0 : c0 + cn] = lax.dot_general(
+                left[e, rows, :], weights[e, c0 : c0 + cn, lo : lo + n], (((1,), (1,)), ((), ())), preferred_element_type=f32
+            ).astype(bf)
+
+    def combine(target, h, k, cols):
+        at = pl.ds(base_of(h, k), NY)
+        r = (h * NZ + k) * pair
+        for c0, cn in cols:
+            parts = [rows_buf[e, r : r + pair, c0 : c0 + cn] for e in range(held)]
+            if lanes > held * pair:
+                parts.append(jnp.zeros((lanes - held * pair, cn), bf))
+            got = jnp.dot(pick[h * NZ + k], jnp.concatenate(parts, axis=0), preferred_element_type=f32)
+            target[at, :, c0 : c0 + cn] = got.astype(bf).reshape(NY, count, cn)
+
+    stores = []
+
+    def weight_grad(e, j):
+        rows = pl.ds(pl.multiple_of((fsdp ^ j) * quarter, 128), quarter)
+        slot = len(stores) % 2
+        if len(stores) >= 2:
+            stores[-2].wait()
+        for c0, cn in columns_of(2 * hidden):
+            stage[slot, :, c0 : c0 + cn] = lax.dot_general(
+                taken[e, :, rows], grad_act[e, :, c0 : c0 + cn], (((0,), (0,)), ((), ())), preferred_element_type=f32
+            ).astype(bf)
+        stage[slot, :, 2 * hidden :] = lax.dot_general(
+            cot_taken[e, :, rows], scaled[e], (((0,), (0,)), ((), ())), preferred_element_type=f32
+        ).astype(bf)
+        copy = pltpu.make_async_copy(stage.at[slot], grads[j].at[e], store_sem.at[len(stores)])
+        copy.start()
+        stores.append(copy)
+
+    work = [functools.partial(cot_chunk, h, k) for h in range(NC) for k in range(NZ)]
+    all_cols = columns_of(width) + [(width, 128)]
+    ready = {(h, k): 0 for h in range(NC) for k in range(NZ)}
+    ready[(0, 0)] = 1
+    for k, flips in gather_events(plans[0].order)[1:]:
+        for way in ways:
+            way.step(k, flips)
+        key = (1 if C in flips else 0, k)
+        ready[key] += 1
+        if ready[key] == NY:
+            work.append(functools.partial(dispatch, seen, taken, *key, all_cols))
+        for _ in range(min(len(work), 1 if k < NZ - 1 else 2)):
+            work.pop(0)()
+    for chunk in work:
+        chunk()
+    for copy in loads:
+        copy.wait()
+    for h in range(NC):
+        for e in range(held):
+            hidden_part(h, e)
+    for way in ways:
+        way.finish()
+
+    far = list(reversed(range(NZ)))
+    spare = spare_sem
+    out_way = Reduce(place, back, seen.at[:, :, pl.ds(0, width)], (lvl_a0, lvl_a1), chain_a, send_a, recv_a, spare)
+    in_way = Reduce(place, back, cot_seen, (lvl_b0, lvl_b1), chain_b, send_b, recv_b, spare)
+    out_steps, in_steps = out_way.steps(), in_way.steps()
+
+    def out_step():
+        if out_steps:
+            out_steps.pop(0)()
+
+    for h in reversed(range(NC)):
+        for e in range(held):
+            project(h, e, scaled, (2 * hidden, hidden))
+        for k in far:
+            combine(seen, h, k, columns_of(width))
+            if h == 1:
+                out_way.first(k)
+    for h in reversed(range(NC)):
+        for e in range(held):
+            project(h, e, grad_act, (0, 2 * hidden))
+            out_step()
+        for k in far:
+            combine(cot_seen, h, k, all_cols)
+            if h == 1:
+                in_way.first(k)
+            out_step()
+    grad_work = [functools.partial(weight_grad, e, j) for j in reversed(range(NX * NC)) for e in range(held)]
+    while out_steps or in_steps or grad_work:
+        if grad_work:
+            grad_work.pop(0)()
+        out_step()
+        if in_steps:
+            in_steps.pop(0)()
+        if in_steps:
+            in_steps.pop(0)()
+    out_way.last(moe_out)
+    in_way.last(gin_out)
+    for copy in stores[-2:]:
+        copy.wait()
+    out_way.finish()
+    in_way.finish()
+
+
+def moe(payload, cots, parts, cap, collective_id):
+    count, wide = payload.shape
+    width = wide - 128
+    held, quarter, columns = parts[0].shape
+    hidden = columns // 3
+    cut = count * 3 // 4
+    plans = [
+        Plan(0, (Z, Y, C), (C, Z, Y), rows=(0, cut)),
+        Plan(0, (Y, Z, C), (C, Z, Y), rows=(cut, count - cut)),
+    ]
+    back = Plan(0, (C, Y), (C, Z, Y))
+    levels, sends, recvs = Reduce.counts(back)
+    blocks = NC * NZ * NY
+    pair = NY * cap
+    rows = blocks // NY * pair
+    lanes = tile_up(held * pair, 128)
+    bf, f32 = jnp.bfloat16, jnp.float32
+    whole = pl.BlockSpec(memory_space=pltpu.VMEM)
+    apart = pl.BlockSpec(memory_space=pl.ANY)
+    dma = pltpu.SemaphoreType.DMA
+    return pl.pallas_call(
+        functools.partial(moe_kernel, plans, back, width, hidden, cap),
+        out_shape=[
+            jax.ShapeDtypeStruct((count, wide), f32),
+            jax.ShapeDtypeStruct((count, width), f32),
+        ]
+        + [jax.ShapeDtypeStruct((held, quarter, columns), bf)] * (NX * NC),
+        in_specs=[whole] + [apart] * 5,
+        out_specs=[whole] * 2 + [apart] * (NX * NC),
+        scratch_shapes=[
+            pltpu.VMEM((blocks, count, wide), bf),
+            pltpu.VMEM((blocks, count, wide), bf),
+            pltpu.VMEM((held, NX * NC * quarter, columns), bf),
+            pltpu.VMEM((held, rows, wide), bf),
+            pltpu.VMEM((held, rows, width), bf),
+            pltpu.VMEM((held, rows, wide), bf),
+            pltpu.VMEM((held, rows, hidden), bf),
+            pltpu.VMEM((held, rows, 2 * hidden), bf),
+            pltpu.VMEM((blocks // NY, NY * count, lanes), bf),
+            pltpu.VMEM((2, quarter, columns), bf),
+        ]
+        + [pltpu.VMEM((n, count, width), bf) for n in levels + [NZ + 1]]
+        + [pltpu.VMEM((n, count, wide), bf) for n in levels + [NZ + 1]]
+        + [
+            dma((sum(Gather.sends(p) for p in plans),)),
+            dma((sum(p.blocks for p in plans),)),
+            dma(()),
+            dma((sends,)),
+            dma((recvs,)),
+            dma((sends,)),
+            dma((recvs,)),
+            dma((held * NX * NC + blocks // NY,)),
+            dma((held * NX * NC,)),
+        ],
+        compiler_params=pltpu.CompilerParams(
+            collective_id=collective_id, has_side_effects=True, vmem_limit_bytes=67043328
+        ),
+        name="experts",
+    )(payload, cots, *parts)
+
+
 MODEL_WIDTH = 1536
 QUERY_HEADS = 24
 KEY_VALUE_HEADS = 8
@@ -796,25 +1234,26 @@
     wide = hidden[0].astype(f32)
     cot = cotangent[0]
 
-    def picked(w):
-        pair = w.reshape(NC, held, *w.shape[1:])
-        return (
-            lax.dynamic_index_in_dim(pair, core, 0, False),
-            lax.dynamic_index_in_dim(pair, 1 - core, 0, False),
-        )
-
-    def spread(mine, other):
-        parts = jnp.stack([mine, swap(other, 1), swap(mine, 2), swap(other, 3)])
-        order = jnp.arange(NX * NC) ^ fsdp
-        whole = jnp.take(parts, order, axis=0)
-        return jnp.transpose(whole, (1, 0, 2, 3)).reshape(held, NX * NC * quarter, mine.shape[2])
-
     pack_one = jnp.concatenate([w_q, key_weight, value_weight], axis=1)
     pack_two = jnp.concatenate(
         [w_o, router, attn_norm[:, None], ffn_norm[:, None], jnp.zeros((rows, 94), bf)], axis=1
     )
+    route = routes[0]
+    indicator = (route[:, :, None] == jnp.arange(EXPERT_COUNT, dtype=jnp.int32)).astype(f32)
+    cot_pack = jnp.concatenate(
+        [
+            cot.astype(bf),
+            jnp.sum(indicator, axis=1).astype(bf),
+            jnp.zeros((tokens, 128 - EXPERT_COUNT), bf),
+        ],
+        axis=1,
+    )
+    experts = jnp.concatenate([expert_in, expert_out], axis=2)
+    experts = experts.reshape(NC, held, quarter, experts.shape[2])
+    mine = lax.dynamic_index_in_dim(experts, core, 0, False)
+    other = lax.dynamic_index_in_dim(experts, 1 - core, 0, False)
     one, two, cots = gather(
-        [pack_one, pack_two, cot.astype(bf)],
+        [pack_one, pack_two, cot_pack],
         [
             Plan(0, (Z, Y, X, C,), (Z, Y, X, C,)),
             Plan(1, (Z, X, Y, C,), (Z, Y, X, C,)),
@@ -824,9 +1263,8 @@
         0,
         "gather_weights",
     )
-    one, experts = lax.optimization_barrier((one, picked(expert_in) + picked(expert_out)))
-    weight_in = spread(*experts[:2])
-    weight_out = spread(*experts[2:])
+    one, mine, other = lax.optimization_barrier((one, mine, other))
+    parts = [mine, swap(other, 1), swap(mine, 2), swap(other, 3)]
     one = one.reshape(MODEL_WIDTH, -1)
     two = two.reshape(MODEL_WIDTH, -1)
     output_w = two[:, :MODEL_WIDTH]
@@ -877,122 +1315,22 @@
     mixed = wide + jnp.dot(attention_output, output_w, preferred_element_type=f32)
     ffn_unit, inverse_two, ffn_in = rms_forward(mixed, ffn_gain)
     logits = jnp.dot(ffn_in, router_w, preferred_element_type=f32)
-    route = routes[0]
-    indicator = (route[:, :, None] == jnp.arange(EXPERT_COUNT, dtype=jnp.int32)).astype(f32)
     chosen = jnp.sum(indicator * logits[:, None, :], axis=-1)
     gates = jax.nn.softmax(chosen, axis=-1)
-    gate_map = jnp.sum(indicator * (gates[..., None] + 1.0), axis=1) - 1.0
-
+    gate_map = jnp.sum(indicator * gates[..., None], axis=1)
     payload = jnp.concatenate(
         [ffn_in, gate_map.astype(bf), jnp.zeros((tokens, 128 - EXPERT_COUNT), bf)], axis=1
     )
-    cut = tokens * 3 // 4
-    (all_tokens,) = gather(
-        [payload],
-        [
-            Plan(0, (Z, Y, C,), (C, Z, Y,), rows=(0, cut)),
-            Plan(0, (Y, Z, C,), (C, Z, Y,), rows=(cut, tokens - cut)),
-        ],
-        2,
-        "gather_tokens",
-    )
-    blocks = NC * ctx_size
-    inputs = all_tokens[:, :, :MODEL_WIDTH]
-    first = (ctx * NC + core) * held
-    own_gates = lax.dynamic_slice_in_dim(
-        all_tokens[:, :, MODEL_WIDTH : MODEL_WIDTH + EXPERT_COUNT], first, held, axis=2
-    ).astype(f32)
-    chosen_here = own_gates >= 0.0
-    before = (
-        jnp.arange(tokens)[:, None] > jnp.arange(tokens)[None, :]
-    ).astype(bf)
-    slot = jnp.einsum(
-        "ts,bse->bet", before, chosen_here.astype(bf), preferred_element_type=f32
-    ).astype(jnp.int32)
-    place_of = (
-        (slot[:, :, None, :] == jnp.arange(CAP, dtype=jnp.int32)[None, None, :, None])
-        & jnp.transpose(chosen_here, (0, 2, 1))[:, :, None, :]
-    )
-    pick = place_of.astype(bf)
-    gate_t = jnp.transpose(own_gates, (0, 2, 1))
-    row_gate = jnp.sum(jnp.where(place_of, gate_t[:, :, None, :], 0.0), axis=-1)
-    row_gate = jnp.transpose(row_gate, (1, 0, 2)).reshape(held, blocks * CAP, 1)
-    received = jnp.einsum("best,btd->ebsd", pick, inputs, preferred_element_type=f32).astype(bf)
-    received = received.reshape(held, blocks * CAP, MODEL_WIDTH)
-    cot_rows = jnp.einsum("best,btd->ebsd", pick, cots, preferred_element_type=f32).astype(bf)
-    cot_rows = cot_rows.reshape(held, blocks * CAP, MODEL_WIDTH)
-    act = jnp.einsum("erd,edf->erf", received, weight_in, preferred_element_type=f32)
-    gate_part = act[..., :EXPERT_HIDDEN]
-    up_part = act[..., EXPERT_HIDDEN:]
-    sigma = jax.nn.sigmoid(gate_part)
-    inner = gate_part * sigma * up_part
-    scaled_inner = (inner * row_gate).astype(bf)
-    produced = jnp.einsum(
-        "erf,edf->erd", scaled_inner, weight_out, preferred_element_type=f32
-    ).astype(bf)
-    raw_inner = jnp.einsum("erd,edf->erf", cot_rows, weight_out, preferred_element_type=f32)
-    row_grad_gate = jnp.sum(raw_inner * inner, axis=-1).reshape(held, blocks, CAP)
-    grad_inner = raw_inner * row_gate
-    grad_w_out = jnp.einsum("erd,erf->edf", cot_rows, scaled_inner, preferred_element_type=f32)
-    grad_act = jnp.concatenate(
-        [
-            grad_inner * up_part * sigma * (1.0 + gate_part * (1.0 - sigma)),
-            grad_inner * gate_part * sigma,
-        ],
-        axis=-1,
-    ).astype(bf)
-    grad_w_in = jnp.einsum("erd,erf->edf", received, grad_act, preferred_element_type=f32)
-    grad_rows = jnp.einsum("erf,edf->erd", grad_act, weight_in, preferred_element_type=f32).astype(bf)
-    out_part = jnp.einsum(
-        "best,ebsd->btd",
-        pick,
-        produced.reshape(held, blocks, CAP, MODEL_WIDTH),
-        preferred_element_type=f32,
-    ).astype(bf)
-    in_part = jnp.einsum(
-        "best,ebsd->btd",
-        pick,
-        grad_rows.reshape(held, blocks, CAP, MODEL_WIDTH),
-        preferred_element_type=f32,
-    ).astype(bf)
-    gate_grads = jnp.sum(
-        jnp.where(place_of, jnp.transpose(row_grad_gate, (1, 0, 2))[..., None], 0.0), axis=2
-    )
-    gate_grads = jnp.transpose(gate_grads, (0, 2, 1))
-    columns = jnp.arange(EXPERT_COUNT, dtype=jnp.int32)
-    spread_gates = sum(
-        jnp.where(columns == first + e, gate_grads[:, :, e : e + 1], 0.0) for e in range(held)
-    )
-    high = spread_gates.astype(bf)
-    low = (spread_gates - high.astype(f32)).astype(bf)
-    in_part = jnp.concatenate(
-        [in_part, high, low, jnp.zeros((blocks, tokens, 128 - 2 * EXPERT_COUNT), bf)], axis=2
-    )
-
-    def cut_up(g):
-        whole = g.astype(bf).reshape(held, NX * NC, quarter, g.shape[2])
-        return [lax.dynamic_index_in_dim(whole, fsdp ^ j, 1, False) for j in range(NX * NC)]
-
-    def collect(parts):
-        mine = parts[0].astype(f32) + swap(parts[2], 2).astype(f32)
-        other = swap(parts[1], 1).astype(f32) + swap(parts[3], 3).astype(f32)
-        return jnp.where(
-            core == 0, jnp.concatenate([mine, other]), jnp.concatenate([other, mine])
-        )
-
-    in_part, out_part, pieces = lax.optimization_barrier(
-        (in_part, out_part, (cut_up(grad_w_in), cut_up(grad_w_out)))
-    )
-    grad_expert_in = collect(pieces[0])
-    grad_expert_out = collect(pieces[1])
-
-    gin, moe_out = reduce_scatter(
-        [in_part, out_part],
-        [Plan(0, (C, Y,), (C, Z, Y,)), Plan(1, (C, Y,), (C, Z, Y,))],
-        [f32, f32],
-        3,
-        "return_tokens",
-    )
+    gin, moe_out, *pieces = moe(payload, cots, parts, CAP, 2)
+    own_sum = pieces[0].astype(f32) + swap(pieces[2], 2).astype(f32)
+    core_sum = swap(pieces[1], 1).astype(f32) + swap(pieces[3], 3).astype(f32)
+    grad_experts = jnp.where(
+        core == 0,
+        jnp.concatenate([own_sum, core_sum]),
+        jnp.concatenate([core_sum, own_sum]),
+    )
+    grad_expert_in = grad_experts[:, :, : 2 * EXPERT_HIDDEN]
+    grad_expert_out = grad_experts[:, :, 2 * EXPERT_HIDDEN :]
     layer_out = (mixed + moe_out).astype(bf)
     grad_gate_map = gin[:, MODEL_WIDTH : MODEL_WIDTH + EXPERT_COUNT] + gin[
         :, MODEL_WIDTH + EXPERT_COUNT : MODEL_WIDTH + 2 * EXPERT_COUNT

time: 720 us -> 627 us (0.87)
  Pallas kernels: 360 us -> 437 us
  matrix products: 117 us -> 55.5 us
  waiting for transfers between devices: 84 us -> 35.6 us
  local copies, waits for them, and re-layouts: 88 us -> 49.3 us
  other arithmetic: 51.3 us -> 33.3 us
    pallas_call x0 -> x1, Pallas kernels: none -> 150 us  [moe(): pl.pallas_call(functools.partial(moe_kernel, plans, back, width, hidden,...]
    dot_general x11 -> x0, matrix products: 63.3 us -> none  [the longest x1 10.2 us: fast(): jnp.einsum('erd,edf->erf', received, weight_in, preferred_element_type=f32)]
    ppermute x12 -> x6, waiting for transfers between devices: 84 us -> 35.6 us  [swap(): return lax.ppermute(a, FSDP, [(i, i ^ flip) for i in range(NX * NC)])]
    pallas_call x3 -> x2, Pallas kernels: 155 us -> 114 us  [gather(): pl.pallas_call(functools.partial(gather_kernel, plans, n), out_shape=[jax...]
    pallas_call x3 -> x2, Pallas kernels: 205 us -> 173 us  [reduce_scatter(): pl.pallas_call(functools.partial(reduce_kernel, plans, n), out_shape=[jax...]
    another operation x7 -> x4, other arithmetic: 12.9 us -> 1.7 us  [the longest x2 8.54 us: spread(): parts = jnp.stack([mine, swap(other, 1), swap(mine, 2), swap(other, 3)])]
    concatenate x1, local copies, waits for them, and re-layouts: 11.1 us -> 0.85 us  [fast(): jnp.concatenate([cot.astype(bf), jnp.sum(indicator, axis=1).astype(bf), j...]
    squeeze x4 -> x1, local copies, waits for them, and re-layouts: 12.2 us -> 2.49 us  [fast(): other = lax.dynamic_index_in_dim(experts, 1 - core, 0, False)]
  transfers between devices with their start and end apart: 12 -> 6, of which waited for: 4 -> 1; matrix products, arithmetic and copies ran while one was open for 16% -> 12% of each run, Pallas kernels for 21% -> 27%
where the time goes in v2:
time: 627 us; the launch traced here: 617 us
  Pallas kernels  437 us (70%)
  matrix products  55.5 us (9%)
  local copies, waits for them, and re-layouts  49.3 us (8%)
  waiting for transfers between devices  35.6 us (6%)
  other arithmetic  33.3 us (5%)
    pallas_call x2, Pallas kernels, reduce_scatter(): pl.pallas_call(functools.partial(reduce_kernel, plans, n), out_shape=[jax...  173 us
    pallas_call x1, Pallas kernels, moe(): pl.pallas_call(functools.partial(moe_kernel, plans, back, width, hidden,...  150 us
    pallas_call x2, Pallas kernels, gather(): pl.pallas_call(functools.partial(gather_kernel, plans, n), out_shape=[jax...  114 us
    ppermute x6, waiting for transfers between devices, swap(): return lax.ppermute(a, FSDP, [(i, i ^ flip) for i in range(NX * NC)])  35.6 us
  transfers between devices with their start and end apart: 6, of which 1 were waited for; matrix products, arithmetic and copies ran while one was open for 12% of the time, Pallas kernels for 27%

profile of v2, /device:TPU:0, one launch (start us, length us, event | category | flops | bytes accessed | tf_op | source)
XLA Modules:
  0.0 617.4 jit_solution(6299913205105699009)
XLA Ops:
  1.5 1.2 bitcast_convert_fusion.1
  2.7 0.8 copy.90
  3.5 0.8 copy.91
  4.2 0.8 copy.92
  5.0 2.8 pad_maximum_fusion
  7.8 2.5 dynamic-slice_bitcast_fusion
  10.3 0.9 concatenate.64.refs_2_
  11.9 0.8 concatenate.63.refs_1_
  12.6 85.0 %gather_weights.1 = (bf16[32,48,2560]{2,1,0:T(8,128)(2,1)}, bf16[32,48,1664]{2,1,0:T(8,128)(2,1)}, bf16[16,128,1664]{2,1,0:T(8,128)(2,1)}) custom-call(bf16[48,2560]{1,0:T(8,128)(2,1)} %pad_maximum_fusion.10.refs_0_, bf16[48,1664]{1,0:T(8,128)(2,1)} %concatenate.63.refs_1_, bf16[128,1664]{1,0:T(8,128)(2,1)} %concatenate.64.refs_2_), custom_call_target="tpu_custom_call" | custom-call | tf_op jit(solution)/shard_map/gather_weights/pallas_call | solution.py:174
  98.2 1.2 collective-permute-start.2
  99.9 1.3 fusion.55
  102.5 4.5 fusion.52
  107.1 0.9 slice.139
  108.6 0.7 fusion.72
  110.1 0.7 pad_maximum_fusion.7.refs_0_
  110.9 29.5 %gather_keys.1 = bf16[8,128,1024]{2,1,0:T(8,128)(2,1)} custom-call(bf16[128,1024]{1,0:T(8,128)(2,1)} %pad_maximum_fusion.7.refs_0_), custom_call_target="tpu_custom_call" | custom-call | tf_op jit(solution)/shard_map/gather_keys/pallas_call | solution.py:174
  140.4 1.7 fusion.88
  142.6 1.8 copy.97
  144.4 1.5 subtract_convert_fusion.1
  145.9 0.7 iota_compare_fusion
  146.7 1.3 copy.98
  148.0 2.8 fusion.5
  150.9 3.0 fusion.2
  153.9 1.5 copy-done
  155.4 3.5 fusion.37
  158.9 3.4 multiply_reduce_fusion.3
  162.4 0.9 copy-done.5
  163.4 1.4 fusion.64
  165.6 0.9 concatenate.71.refs_0_
  167.1 35.5 %collective-permute-done.1.refs_4_ = bf16[2,384,1536]{2,1,0:T(8,128)(2,1)} collective-permute-done((bf16[2,384,1536]{2,1,0:T(8,128)(2,1)}, bf16[2,384,1536]{2,1,0:T(8,128)(2,1)}, u32[]{:S(2)}, u32[]{:S(2)}) %collective-permute-start.1) | collective-permute-done | bytes 2359328 | tf_op jit(solution)/shard_map/ppermute | solution.py:1200
  202.6 150.1 %experts.1 = (f32[128,1664]{1,0:T(8,128)}, f32[128,1536]{1,0:T(8,128)}, bf16[2,384,1536]{2,1,0:T(8,128)(2,1)}, bf16[2,384,1536]{2,1,0:T(8,128)(2,1)}, bf16[2,384...) custom-call(bf16[128,1664]{1,0:T(8,128)(2,1)} %concatenate.71.refs_0_, ...), custom_call_target="tpu_custom_call" | custom-call | tf_op jit(solution)/shard_map/experts/pallas_call | solution.py:750
  352.7 1.0 slice_add_fusion.1
  353.7 0.7 select_reduce_fusion.1
  354.5 0.7 multiply_reduce_fusion.4
  356.6 2.0 multiply_reduce_fusion
  358.6 2.8 bitcast_add_fusion
  361.4 4.0 fusion.19
  365.9 7.4 %fusion.1 = bf16[8,3,128,1024]{2,3,1,0:T(8,128)(2,1)S(1)} fusion(f32[8,1024,128,3]{2,1,3,0:T(8,128)} %copy-done, f32[8,3,128]{2,1,0:T(4,128)S(1)} %bitcast.203, f32[8,3,128]{2,1,0:T(4,128)S(1)} %copy-done.34, pred[128,1024]{0,1:T(8,128)(4,1)S(1)} %copy-done.16, bf16[1024,8,64,1]{0,2,3,1:T(8,128)(2,1)S(1)} %bitcast.185, bf16[128,8,3,64]{0,3,2,1:T(8,128)(2,1)S(1)} %bitcast.180), kind=kOutput, calls=%fused_computation.2 | convolution fusion | flops 424673280 | bytes 20471808 | tf_op jit(solution)/shard_map/tkgd,nkd->kgtn/dot_general | solution.py:1364
  373.3 2.0 convolution_multiply_fusion
  375.3 2.1 fusion.22
  377.5 4.1 bitcast_convert_fusion
  382.6 1.5 copy.123
  384.1 1.5 copy.107
  385.5 2.9 pad_maximum_fusion.1.refs_0_
  388.4 37.2 %return_keys.1 = f32[128,1024]{1,0:T(8,128)} custom-call(bf16[8,128,1024]{2,1,0:T(8,128)(2,1)} %pad_maximum_fusion.1.refs_0_), custom_call_target="tpu_custom_call" | custom-call | tf_op jit(solution)/shard_map/return_keys/pallas_call | solution.py:335
  425.7 1.0 slice.193
  426.7 1.7 collective-permute-start.3
  428.9 4.5 convolution_convert_fusion.1
  434.0 6.8 %fusion.46 = (bf16[1536]{0:T(1024)(128)(2,1)S(1)}, f32[128]{0:T(128)S(1)}, f32[128,1536]{1,0:T(8,128)}) fusion(bf16[1,128,1536]{2,1,0:T(8,128)(2,1)S(1)} %copy-done.4, f32[128]{0:T(128)S(1)} %copy-done.37, f32[1536]{0:T(1024)S(1)} %copy-done.22, bf16[1536,2560]{1,0:T(8,128)(2,1)} %bitcast.162, bf16[128,512]{0,1:T(8,128)(2,1)S(1)} %copy.109, ...), kind=kOutput, calls=%fused_computation.51 | convolution fusion | flops 1009973632 | bytes 9709568 | tf_op jit(solution)/shard_map/dot_general | solution.py:1405
  442.7 9.0 %concatenate.79.refs_1_ = bf16[32,48,1664]{2,1,0:T(8,128)(2,1)} concatenate(bf16[32,48,1536]{2,1,0:T(8,128)(2,1)} %convolution_convert_fusion.1, bf16[32,48,32]{2,1,0:T(8,128)(2,1)S(1)} %bitcast.176, bf16[32,48,1]{2,1,0:T(8,128)(2,1)S(1)} %concatenate.82, bf16[32,48,1]{2,1,0:T(8,128)(2,1)S(1)} %concatenate.83, bf16[32,48,94]{2,1,0:T(8,128)(2,1)S(1)} %broadcast_in_dim.64), dimensions={2} | concatenate | bytes 10223616 | tf_op jit(solution)/shard_map/concatenate | solution.py:1410
  451.7 5.4 convolution_convert_fusion
  457.1 135.5 %return_weights.1 = (f32[48,2560]{1,0:T(8,128)}, f32[48,1664]{1,0:T(8,128)}) custom-call(bf16[32,48,2560]{2,1,0:T(8,128)(2,1)} %bitcast.160, bf16[32,48,1664]{2,1,0:T(8,128)(2,1)} %concatenate.79.refs_1_), custom_call_target="tpu_custom_call" | custom-call | tf_op jit(solution)/shard_map/return_weights/pallas_call | solution.py:335
  592.6 1.7 slice.127
  594.3 1.3 slice.128
  595.7 1.7 slice.124
  597.4 1.4 copy.113
  598.8 1.5 slice_reduce_fusion
  600.3 1.6 fusion.89
  601.9 2.3 fusion.44
  604.3 2.3 convert_add_fusion.1
  606.6 3.1 convert_add_fusion
  609.7 2.0 maximum_select_fusion
  611.7 3.3 slice.150
  614.9 2.0 slice.151
  (142 shorter events, 13.1 us)
Async XLA Ops:
  7.7 3.4 copy-start.28
  7.7 3.4 copy-start.32
  7.8 3.4 copy-start.33
  7.8 4.1 copy-start.29
  7.8 94.0 %copy-start.3 = (bf16[1,128,1536]{2,1,0:T(8,128)(2,1)S(1)}, bf16[1,128,1536]{2,1,0:T(8,128)(2,1)}, u32[]{:S(2)}) copy-start(bf16[1,128,1536]{2,1,0:T(8,128)(2,1)} %param.12) | copy-start | bytes 1179652
  10.3 96.7 %copy-start.23 = (bf16[128,96]{1,0:T(8,128)(2,1)}, bf16[128,96]{1,0:T(8,128)(2,1)S(1)}, u32[]{:S(2)}) copy-start(bf16[128,96]{1,0:T(8,128)(2,1)S(1)} %broadcast.193) | copy-start | bytes 73732
  97.6 69.4 %collective-permute-start = (bf16[2,384,1536]{2,1,0:T(8,128)(2,1)}, bf16[2,384,1536]{2,1,0:T(8,128)(2,1)}, u32[]{:S(2)}, u32[]{:S(2)}) collective-permute-start(bf16[2,384,1536]{2,1,0:T(8,128)(2,1)} %get-tuple-element.30), channel_id=1, source_target_pairs={{0,1},{1,0},{2,3},{3,2},{4,5},{5,4},{6,7},{7,6},{8,9},{9,8},{10,11... | collective-permute-start | bytes 7077896 | tf_op jit(solution)/shard_map/ppermute | solution.py:1200
  98.2 104.4 %collective-permute-start.2 = (bf16[2,384,1536]{2,1,0:T(8,128)(2,1)}, bf16[2,384,1536]{2,1,0:T(8,128)(2,1)}, u32[]{:S(2)}, u32[]{:S(2)}) collective-permute-start(bf16[2,384,1536]{2,1,0:T(8,128)(2,1)} %get-tuple-element.30), channel_id=1, source_target_pairs={{0,3},{1,2},{2,1},{3,0},{4,7},{5,6},{6,5},{7,4},{8,11},{9,10},{10,... | collective-permute-start | bytes 7077896 | tf_op jit(solution)/shard_map/ppermute | solution.py:1200
  99.4 103.2 %collective-permute-start.1 = (bf16[2,384,1536]{2,1,0:T(8,128)(2,1)}, bf16[2,384,1536]{2,1,0:T(8,128)(2,1)}, u32[]{:S(2)}, u32[]{:S(2)}) collective-permute-start(bf16[2,384,1536]{2,1,0:T(8,128)(2,1)} %get-tuple-element.29.refs_2_), channel_id=1, source_target_pairs={{0,2},{1,3},{2,0},{3,1},{4,6},{5,7},{6,4},{7,5},{8,10},{9,11},{10,... | collective-permute-start | bytes 7077896 | tf_op jit(solution)/shard_map/ppermute | solution.py:1200
  101.8 5.2 copy-start.21
  102.0 0.5 copy-start.36
  109.4 0.6 copy-start.26
  109.4 36.5 %copy-start.19 = (f32[128,32]{0,1:T(8,128)}, f32[128,32]{0,1:T(8,128)S(1)}, u32[]{:S(2)}) copy-start(f32[128,32]{0,1:T(8,128)S(1)} %get-tuple-element.109) | copy-start | bytes 49156
  142.6 8.2 %copy-start.1 = (bf16[1024,512]{0,1:T(8,128)(2,1)}, bf16[1024,512]{0,1:T(8,128)(2,1)S(1)}, u32[]{:S(2)}) copy-start(bf16[1024,512]{0,1:T(8,128)(2,1)S(1)} %copy.96) | copy-start | bytes 3145732
  145.9 4.9 copy-start.10
  146.7 7.3 %copy-start.15 = (pred[128,1024]{0,1:T(8,128)(4,1)}, pred[128,1024]{0,1:T(8,128)(4,1)S(1)}, u32[]{:S(2)}) copy-start(pred[128,1024]{0,1:T(8,128)(4,1)S(1)} %iota_compare_fusion) | copy-start | bytes 393220
  150.8 4.5 copy-start
  150.9 4.5 copy-start.17
  158.9 7.5 %copy-start.13 = (bf16[128,8,3,64]{0,3,2,1:T(8,128)(2,1)}, bf16[128,8,3,64]{0,3,2,1:T(8,128)(2,1)S(1)}, u32[]{:S(2)}) copy-start(bf16[128,8,3,64]{0,3,2,1:T(8,128)(2,1)S(1)} %fusion.37) | copy-start | bytes 1179652
  158.9 4.3 copy-start.30
  158.9 5.9 copy-start.31
  158.9 6.6 %copy-start.24 = (bf16[128,96]{1,0:T(8,128)(2,1)S(1)}, bf16[128,96]{1,0:T(8,128)(2,1)}, u32[]{:S(2)}) copy-start(bf16[128,96]{1,0:T(8,128)(2,1)} %copy-done.23) | copy-start | bytes 73732
  162.3 0.9 copy-start.5
  162.3 0.9 copy-start.39
  163.4 2.2 copy-start.6
  164.8 2.2 copy-start.27
  164.8 0.5 copy-start.35
  164.9 0.5 copy-start.38
  358.6 7.1 %copy-start.14 = (bf16[128,8,3,64]{0,3,2,1:T(8,128)(2,1)S(1)}, bf16[128,8,3,64]{0,3,2,1:T(8,128)(2,1)}, u32[]{:S(2)}) copy-start(bf16[128,8,3,64]{0,3,2,1:T(8,128)(2,1)} %copy-done.13) | copy-start | bytes 1179652
  358.6 7.2 %copy-start.16 = (pred[128,1024]{0,1:T(8,128)(4,1)S(1)}, pred[128,1024]{0,1:T(8,128)(4,1)}, u32[]{:S(2)}) copy-start(pred[128,1024]{0,1:T(8,128)(4,1)} %copy-done.15) | copy-start | bytes 393220
  358.6 7.2 %copy-start.18 = (bf16[1024,512]{0,1:T(8,128)(2,1)S(1)}, bf16[1024,512]{0,1:T(8,128)(2,1)}, u32[]{:S(2)}) copy-start(bf16[1024,512]{0,1:T(8,128)(2,1)} %copy.98) | copy-start | bytes 3145732
  358.6 7.2 %copy-start.34 = (f32[8,3,128]{2,1,0:T(4,128)S(1)}, f32[8,3,128]{2,1,0:T(4,128)}, u32[]{:S(2)}) copy-start(f32[8,3,128]{2,1,0:T(4,128)} %log_add_fusion) | copy-start | bytes 36868
  365.9 7.4 %copy-start.2 = (bf16[1024,512]{0,1:T(8,128)(2,1)S(1)}, bf16[1024,512]{0,1:T(8,128)(2,1)}, u32[]{:S(2)}) copy-start(bf16[1024,512]{0,1:T(8,128)(2,1)} %copy-done.1) | copy-start | bytes 3145732
  365.9 11.6 %slice-start = ((s8[12582912]{0:T(1024)(128)(4,1)}), s8[4194304]{0:T(1024)(128)(4,1)S(1)}, s32[]{:S(2)}) async-start(s8[12582912]{0:T(1024)(128)(4,1)} %bitcast.158), calls=%async_computation | async-start | bytes 8388608
  365.9 11.6 %slice-start.1 = ((s8[12582912]{0:T(1024)(128)(4,1)}), s8[4194304]{0:T(1024)(128)(4,1)S(1)}, s32[]{:S(2)}) async-start(s8[12582912]{0:T(1024)(128)(4,1)} %bitcast.158), calls=%async_computation.1 | async-start | bytes 8388608
  373.3 2.1 copy-start.11
  373.3 2.0 copy-start.12
  373.3 4.2 slice-start.2
  385.5 48.0 %copy-start.8 = (f32[8,64,3,128]{3,1,2,0:T(8,128)S(1)}, f32[8,64,3,128]{3,1,2,0:T(8,128)}, u32[]{:S(2)}) copy-start(f32[8,64,3,128]{3,1,2,0:T(8,128)} %convolution_multiply_fusion) | copy-start | bytes 2359300
  385.5 48.0 %copy-start.20 = (f32[128,32]{0,1:T(8,128)S(1)}, f32[128,32]{0,1:T(8,128)}, u32[]{:S(2)}) copy-start(f32[128,32]{0,1:T(8,128)} %copy-done.19) | copy-start | bytes 49156
  385.5 48.0 %copy-start.25 = (f32[128,32]{0,1:T(8,128)S(1)}, f32[128,32]{0,1:T(8,128)}, u32[]{:S(2)}) copy-start(f32[128,32]{0,1:T(8,128)} %get-tuple-element.107) | copy-start | bytes 49156
  388.4 45.5 %copy-start.4 = (bf16[1,128,1536]{2,1,0:T(8,128)(2,1)S(1)}, bf16[1,128,1536]{2,1,0:T(8,128)(2,1)}, u32[]{:S(2)}) copy-start(bf16[1,128,1536]{2,1,0:T(8,128)(2,1)} %param.12) | copy-start | bytes 1179652
  388.4 45.5 %copy-start.22 = (f32[1536]{0:T(1024)S(1)}, f32[1536]{0:T(1024)}, u32[]{:S(2)}) copy-start(f32[1536]{0:T(1024)} %copy-done.21) | copy-start | bytes 18436
  388.4 45.5 %copy-start.37 = (f32[128]{0:T(128)S(1)}, f32[128]{0:T(128)}, u32[]{:S(2)}) copy-start(f32[128]{0:T(128)} %copy-done.36) | copy-start | bytes 1540
  425.6 7.7 %slice-start.3 = ((f32[128,1024]{1,0:T(8,128)}), f32[128,512]{1,0:T(8,128)S(1)}, s32[]{:S(2)}) async-start(f32[128,1024]{1,0:T(8,128)} %return_keys.1), calls=%async_computation.3 | async-start | bytes 524288 | tf_op jit(solution)/shard_map/slice | solution.py:1396
  426.7 177.6 %collective-permute-start.3 = (bf16[2,384,1536]{2,1,0:T(8,128)(2,1)}, bf16[2,384,1536]{2,1,0:T(8,128)(2,1)}, u32[]{:S(2)}, u32[]{:S(2)}) collective-permute-start(bf16[2,384,1536]{2,1,0:T(8,128)(2,1)} %get-tuple-element.36), channel_id=1, source_target_pairs={{0,2},{1,3},{2,0},{3,1},{4,6},{5,7},{6,4},{7,5},{8,10},{9,11},{10,... | collective-permute-start | bytes 7077896 | tf_op jit(solution)/shard_map/ppermute | solution.py:1200
  428.4 178.2 %collective-permute-start.4 = (bf16[2,384,1536]{2,1,0:T(8,128)(2,1)}, bf16[2,384,1536]{2,1,0:T(8,128)(2,1)}, u32[]{:S(2)}, u32[]{:S(2)}) collective-permute-start(bf16[2,384,1536]{2,1,0:T(8,128)(2,1)} %get-tuple-element.37), channel_id=1, source_target_pairs={{0,1},{1,0},{2,3},{3,2},{4,5},{5,4},{6,7},{7,6},{8,9},{9,8},{10,11... | collective-permute-start | bytes 7077896 | tf_op jit(solution)/shard_map/ppermute | solution.py:1200
  428.4 178.2 %collective-permute-start.5 = (bf16[2,384,1536]{2,1,0:T(8,128)(2,1)}, bf16[2,384,1536]{2,1,0:T(8,128)(2,1)}, u32[]{:S(2)}, u32[]{:S(2)}) collective-permute-start(bf16[2,384,1536]{2,1,0:T(8,128)(2,1)} %get-tuple-element.38), channel_id=1, source_target_pairs={{0,3},{1,2},{2,1},{3,0},{4,7},{5,6},{6,5},{7,4},{8,11},{9,10},{10,... | collective-permute-start | bytes 7077896 | tf_op jit(solution)/shard_map/ppermute | solution.py:1200
  433.7 7.1 %copy-start.7 = (bf16[128,1536]{1,0:T(8,128)(2,1)S(1)}, bf16[128,1536]{1,0:T(8,128)(2,1)}, u32[]{:S(2)}) copy-start(bf16[128,1536]{1,0:T(8,128)(2,1)} %copy-done.6) | copy-start | bytes 1179652
  457.1 147.1 %copy-start.9 = (bf16[2,384,1536]{2,1,0:T(8,128)(2,1)S(1)}, bf16[2,384,1536]{2,1,0:T(8,128)(2,1)}, u32[]{:S(2)}) copy-start(bf16[2,384,1536]{2,1,0:T(8,128)(2,1)} %get-tuple-element.35) | copy-start | bytes 7077892

commit v3 on v2

--- a/solution.py
+++ b/solution.py
@@ -167,7 +167,7 @@
             pl.when(go)(wait)
 
 
-def gather(arrays, plans, collective_id, name):
+def gather(arrays, plans, collective_id):
     n = len(arrays)
     sends = sum(len(gather_sends(p.order, k, f)) for p in plans for k, f in gather_events(p.order))
     blocks = {p.ref: p.blocks for p in plans}
@@ -182,7 +182,6 @@
             pltpu.SemaphoreType.DMA((1 + len(plans),)),
         ],
         compiler_params=pltpu.CompilerParams(collective_id=collective_id, has_side_effects=True),
-        name=name,
     )(*arrays)
 
 
@@ -254,7 +253,7 @@
     def level_step(n, p, k):
         plan = plans[n]
         dims = plan.order
-        acc, levels, chain, kept, level_base, chain_base, own_copies = state[n]
+        acc, levels, _, kept, level_base, _, own_copies = state[n]
         for f in sorted(kept[p], key=lambda f: -len(f)):
             spot = place.order[k] * len(kept[p]) + kept[p].index(f)
             at = place.order[k] * len(kept[0]) + kept[0].index(f)
@@ -272,8 +271,7 @@
                 )
 
     def chain_step(n, k):
-        plan = plans[n]
-        acc, levels, chain, kept, level_base, chain_base, own_copies = state[n]
+        acc, _, chain, kept, _, chain_base, _ = state[n]
         dest = place.order[k]
         up = dest > z
         lane = jnp.where(up, 0, 1)
@@ -317,7 +315,7 @@
         copy.wait_send()
 
 
-def reduce_scatter(arrays, plans, out_dtypes, collective_id, name):
+def reduce_scatter(arrays, plans, out_dtypes, collective_id):
     n = len(arrays)
     scratch = []
     sends = recvs = owns = 0
@@ -346,7 +344,6 @@
         compiler_params=pltpu.CompilerParams(
             collective_id=collective_id, has_side_effects=True, vmem_limit_bytes=60 * 1024 * 1024
         ),
-        name=name,
     )(*arrays)
 
 
@@ -914,7 +911,7 @@
 
     def compute(current):
         best, total, weighted = current
-        scores, visible, key_tensor = piece_scores(query_rows, key_section, positions)
+        scores, visible, _ = piece_scores(query_rows, key_section, positions)
         value_tensor = value_section.reshape(value_section.shape[0], KEY_VALUE_HEADS, HEAD_SIZE)
         new_best = jnp.maximum(best, jnp.max(scores, axis=-1))
         weights = jnp.where(visible, jnp.exp(scores - new_best[..., None]), 0.0)
@@ -1200,7 +1197,7 @@
     return lax.ppermute(a, FSDP, [(i, i ^ flip) for i in range(NX * NC)])
 
 
-def fast(
+def fast_body(
     hidden,
     routes,
     attn_norm,
@@ -1252,19 +1249,17 @@
     experts = experts.reshape(NC, held, quarter, experts.shape[2])
     mine = lax.dynamic_index_in_dim(experts, core, 0, False)
     other = lax.dynamic_index_in_dim(experts, 1 - core, 0, False)
+    parts = [mine, swap(other, 1), swap(mine, 2), swap(other, 3)]
     one, two, cots = gather(
         [pack_one, pack_two, cot_pack],
         [
-            Plan(0, (Z, Y, X, C,), (Z, Y, X, C,)),
-            Plan(1, (Z, X, Y, C,), (Z, Y, X, C,)),
-            Plan(2, (Z, Y, C,), (C, Z, Y,), rows=(0, tokens // 2)),
-            Plan(2, (Y, Z, C,), (C, Z, Y,), rows=(tokens // 2, tokens // 2)),
+            Plan(0, (X, Z, Y, C), (Z, Y, X, C), rows=(0, 2 * rows // 3)),
+            Plan(0, (X, Y, Z, C), (Z, Y, X, C), rows=(2 * rows // 3, rows // 3)),
+            Plan(1, (Z, Y, X, C), (Z, Y, X, C)),
+            Plan(2, (Z, Y, C), (C, Z, Y)),
         ],
         0,
-        "gather_weights",
-    )
-    one, mine, other = lax.optimization_barrier((one, mine, other))
-    parts = [mine, swap(other, 1), swap(mine, 2), swap(other, 3)]
+    )
     one = one.reshape(MODEL_WIDTH, -1)
     two = two.reshape(MODEL_WIDTH, -1)
     output_w = two[:, :MODEL_WIDTH]
@@ -1293,10 +1288,7 @@
     )
     value_rows = linear[:, q_width + kv_width :].astype(bf)
     (kv,) = gather(
-        [jnp.concatenate([key_rows, value_rows], axis=1)],
-        [Plan(0, (Z, Y,), (Z, Y,))],
-        1,
-        "gather_keys",
+        [jnp.concatenate([key_rows, value_rows], axis=1)], [Plan(0, (Z, Y,), (Z, Y,))], 1
     )
     kv = kv.reshape(ctx_size * tokens, 2 * kv_width)
     key_section, value_section = kv[:, :kv_width], kv[:, kv_width:]
@@ -1322,8 +1314,9 @@
         [ffn_in, gate_map.astype(bf), jnp.zeros((tokens, 128 - EXPERT_COUNT), bf)], axis=1
     )
     gin, moe_out, *pieces = moe(payload, cots, parts, CAP, 2)
-    own_sum = pieces[0].astype(f32) + swap(pieces[2], 2).astype(f32)
-    core_sum = swap(pieces[1], 1).astype(f32) + swap(pieces[3], 3).astype(f32)
+    across = [swap(pieces[j], j) for j in range(1, NX * NC)]
+    own_sum = pieces[0].astype(f32) + across[1].astype(f32)
+    core_sum = across[0].astype(f32) + across[2].astype(f32)
     grad_experts = jnp.where(
         core == 0,
         jnp.concatenate([own_sum, core_sum]),
@@ -1381,9 +1374,7 @@
         ],
         axis=2,
     )
-    (local_gradients,) = reduce_scatter(
-        [update], [Plan(0, (Y,), (Z, Y,))], [f32], 4, "return_keys"
-    )
+    (local_gradients,) = reduce_scatter([update], [Plan(0, (Y,), (Z, Y,))], [f32], 4)
     query_back = (
         rotate_pairs(
             grad_query.reshape(tokens, QUERY_HEADS, HEAD_SIZE), cosine_table, -sine_table
@@ -1425,7 +1416,6 @@
         [Plan(0, (C, X, Y,), (Z, Y, X, C,)), Plan(1, (C, Y, X,), (Z, Y, X, C,))],
         [f32, f32],
         5,
-        "return_weights",
     )
     at = MODEL_WIDTH + EXPERT_COUNT
     return (
@@ -1441,6 +1431,10 @@
         grad_expert_in,
         grad_expert_out,
     )
+
+
+def fast(*args):
+    return fast_body(*args)
 
 
 def solution(mesh):

time: 627 us -> 680 us (1.085)
  Pallas kernels: 437 us -> 529 us
  waiting for transfers between devices: 35.6 us -> 0.02 us
    pallas_call x2, Pallas kernels: 114 us -> 206 us  [gather(): pl.pallas_call(functools.partial(gather_kernel, plans, n), out_shape=[jax...]
    ppermute x6, waiting for transfers between devices: 35.6 us -> 0.02 us  [swap(): return lax.ppermute(a, FSDP, [(i, i ^ flip) for i in range(NX * NC)])]
  transfers between devices with their start and end apart: 6 -> 6, of which waited for: 1 -> 0; matrix products, arithmetic and copies ran while one was open for 12% -> 12% of each run, Pallas kernels for 27% -> 51%
where the time goes in v3:
time: 680 us; the launch traced here: 670 us
  Pallas kernels  529 us (78%)
  matrix products  55.4 us (8%)
  local copies, waits for them, and re-layouts  46.9 us (7%)
  other arithmetic  31.5 us (5%)
    pallas_call x2, Pallas kernels, gather(): pl.pallas_call(functools.partial(gather_kernel, plans, n), out_shape=[jax...  206 us
    pallas_call x2, Pallas kernels, reduce_scatter(): pl.pallas_call(functools.partial(reduce_kernel, plans, n), out_shape=[jax...  173 us
    pallas_call x1, Pallas kernels, moe(): pl.pallas_call(functools.partial(moe_kernel, plans, back, width, hidden,...  150 us
  transfers between devices with their start and end apart: 6, of which 0 were waited for; matrix products, arithmetic and copies ran while one was open for 12% of the time, Pallas kernels for 51%

profile of v3, /device:TPU:0, one launch (start us, length us, event | category | flops | bytes accessed | tf_op | source)
XLA Modules:
  0.0 670.4 jit_solution(11750575720992786209)
XLA Ops:
  0.7 2.8 pad_maximum_fusion
  3.5 2.5 dynamic-slice_bitcast_fusion
  6.5 2.6 collective-permute-start.2
  9.7 0.9 concatenate.64.refs_2_
  10.6 0.7 pad_maximum_fusion.10.refs_0_
  11.3 0.8 concatenate.63.refs_1_
  12.0 174.7 %shard_map.203 = (bf16[32,48,2560]{2,1,0:T(8,128)(2,1)}, bf16[32,48,1664]{2,1,0:T(8,128)(2,1)}, bf16[16,128,1664]{2,1,0:T(8,128)(2,1)}) custom-call(bf16[48,2560]{1,0:T(8,128)(2,1)} %pad_maximum_fusion.10.refs_0_, bf16[48,1664]{1,0:T(8,128)(2,1)} %concatenate.63.refs_1_, bf16[128,1664]{1,0:T(8,128)(2,1)} %concatenate.64.refs_2_), custom_call_target="tpu_custom_call" | custom-call | tf_op jit(solution)/shard_map/pallas_call | solution.py:174
  186.8 1.3 fusion.55
  188.9 4.5 fusion.52
  193.5 0.9 slice.139
  195.0 0.7 fusion.72
  196.5 0.7 pad_maximum_fusion.7.refs_0_
  197.3 31.3 %shard_map.204 = bf16[8,128,1024]{2,1,0:T(8,128)(2,1)} custom-call(bf16[128,1024]{1,0:T(8,128)(2,1)} %pad_maximum_fusion.7.refs_0_), custom_call_target="tpu_custom_call" | custom-call | tf_op jit(solution)/shard_map/pallas_call | solution.py:174
  228.6 1.7 fusion.88
  230.8 1.8 copy.97
  232.6 1.5 subtract_convert_fusion.1
  234.1 0.7 iota_compare_fusion
  234.9 1.3 copy.98
  236.2 2.8 fusion.5
  239.1 3.0 fusion.2
  242.1 1.5 copy-done
  243.6 3.5 fusion.37
  247.2 3.4 multiply_reduce_fusion.3
  250.6 0.9 copy-done.5
  251.6 1.4 fusion.64
  253.8 0.9 concatenate.70.refs_0_
  255.3 150.2 %experts.1 = (f32[128,1664]{1,0:T(8,128)}, f32[128,1536]{1,0:T(8,128)}, bf16[2,384,1536]{2,1,0:T(8,128)(2,1)}, bf16[2,384,1536]{2,1,0:T(8,128)(2,1)}, bf16[2,384...) custom-call(bf16[128,1664]{1,0:T(8,128)(2,1)} %concatenate.70.refs_0_, ...), custom_call_target="tpu_custom_call" | custom-call | tf_op jit(solution)/shard_map/experts/pallas_call | solution.py:747
  405.4 1.0 slice_add_fusion.1
  406.5 0.7 select_reduce_fusion.1
  407.2 0.7 multiply_reduce_fusion.4
  408.0 0.7 subtract_multiply_fusion
  408.7 0.7 select_reduce_fusion
  409.4 2.0 multiply_reduce_fusion
  411.4 2.8 bitcast_add_fusion
  414.2 4.0 fusion.19
  418.7 7.4 %fusion.1 = bf16[8,3,128,1024]{2,3,1,0:T(8,128)(2,1)S(1)} fusion(f32[8,1024,128,3]{2,1,3,0:T(8,128)} %copy-done, f32[8,3,128]{2,1,0:T(4,128)S(1)} %bitcast.203, f32[8,3,128]{2,1,0:T(4,128)S(1)} %copy-done.36, pred[128,1024]{0,1:T(8,128)(4,1)S(1)} %copy-done.17, bf16[1024,8,64,1]{0,2,3,1:T(8,128)(2,1)S(1)} %bitcast.185, bf16[128,8,3,64]{0,3,2,1:T(8,128)(2,1)S(1)} %bitcast.180), kind=kOutput, calls=%fused_computation.2 | convolution fusion | flops 424673280 | bytes 20471808 | tf_op jit(solution)/shard_map/tkgd,nkd->kgtn/dot_general | solution.py:1357
  426.1 2.0 convolution_multiply_fusion
  428.1 2.1 fusion.22
  430.3 4.1 bitcast_convert_fusion
  435.4 1.5 copy.123
  436.9 1.5 copy.107
  438.3 2.9 pad_maximum_fusion.1.refs_0_
  441.2 35.5 %shard_map.205 = f32[128,1024]{1,0:T(8,128)} custom-call(bf16[8,128,1024]{2,1,0:T(8,128)(2,1)} %pad_maximum_fusion.1.refs_0_), custom_call_target="tpu_custom_call" | custom-call | tf_op jit(solution)/shard_map/pallas_call | solution.py:333
  476.7 1.0 slice.193
  477.7 1.7 collective-permute-start.3
  479.9 4.5 convolution_convert_fusion.1
  485.0 6.8 %fusion.46 = (bf16[1536]{0:T(1024)(128)(2,1)S(1)}, f32[128]{0:T(128)S(1)}, f32[128,1536]{1,0:T(8,128)}) fusion(bf16[1,128,1536]{2,1,0:T(8,128)(2,1)S(1)} %copy-done.4, f32[128]{0:T(128)S(1)} %copy-done.39, f32[1536]{0:T(1024)S(1)} %copy-done.23, bf16[1536,2560]{1,0:T(8,128)(2,1)} %bitcast.162, bf16[128,512]{0,1:T(8,128)(2,1)S(1)} %copy.109, ...), kind=kOutput, calls=%fused_computation.51 | convolution fusion | flops 1009973632 | bytes 9709568 | tf_op jit(solution)/shard_map/dot_general | solution.py:1396
  492.2 0.7 concatenate.82
  492.9 0.7 concatenate.83
  493.7 9.0 %concatenate.79.refs_1_ = bf16[32,48,1664]{2,1,0:T(8,128)(2,1)} concatenate(bf16[32,48,1536]{2,1,0:T(8,128)(2,1)} %convolution_convert_fusion.1, bf16[32,48,32]{2,1,0:T(8,128)(2,1)S(1)} %bitcast.176, bf16[32,48,1]{2,1,0:T(8,128)(2,1)S(1)} %concatenate.82, bf16[32,48,1]{2,1,0:T(8,128)(2,1)S(1)} %concatenate.83, bf16[32,48,94]{2,1,0:T(8,128)(2,1)S(1)} %broadcast_in_dim.64), dimensions={2} | concatenate | bytes 10223616 | tf_op jit(solution)/shard_map/concatenate | solution.py:1401
  502.7 5.4 convolution_convert_fusion
  508.1 137.5 %shard_map.206 = (f32[48,2560]{1,0:T(8,128)}, f32[48,1664]{1,0:T(8,128)}) custom-call(bf16[32,48,2560]{2,1,0:T(8,128)(2,1)} %bitcast.160, bf16[32,48,1664]{2,1,0:T(8,128)(2,1)} %concatenate.79.refs_1_), custom_call_target="tpu_custom_call" | custom-call | tf_op jit(solution)/shard_map/pallas_call | solution.py:333
  645.6 1.7 slice.127
  647.3 1.3 slice.128
  648.6 1.7 slice.124
  650.3 1.4 copy.113
  651.8 1.5 slice_reduce_fusion
  653.3 1.6 fusion.89
  654.9 2.3 fusion.44
  657.2 2.3 convert_add_fusion.1
  659.6 3.1 convert_add_fusion
  662.7 2.0 maximum_select_fusion
  664.6 3.3 slice.150
  667.9 2.0 slice.151
  (152 shorter events, 8.2 us)
Async XLA Ops:
  3.4 5.7 copy-start.32
  3.4 5.9 copy-start.9
  3.5 5.9 copy-start.41
  3.5 6.0 copy-start.43
  3.5 6.1 copy-start.44
  3.5 7.1 %copy-start.29 = (bf16[48,1536]{1,0:T(8,128)(2,1)S(1)}, bf16[48,1536]{1,0:T(8,128)(2,1)}, u32[]{:S(2)}) copy-start(bf16[48,1536]{1,0:T(8,128)(2,1)} %param.16) | copy-start | bytes 442372
  3.5 7.1 %copy-start.34 = (bf16[48,512]{1,0:T(8,128)(2,1)S(1)}, bf16[48,512]{1,0:T(8,128)(2,1)}, u32[]{:S(2)}) copy-start(bf16[48,512]{1,0:T(8,128)(2,1)} %param.18) | copy-start | bytes 147460
  3.5 7.0 %copy-start.35 = (bf16[48,512]{1,0:T(8,128)(2,1)S(1)}, bf16[48,512]{1,0:T(8,128)(2,1)}, u32[]{:S(2)}) copy-start(bf16[48,512]{1,0:T(8,128)(2,1)} %param.17) | copy-start | bytes 147460
  3.5 7.8 %copy-start.30 = (bf16[48,1536]{1,0:T(8,128)(2,1)S(1)}, bf16[48,1536]{1,0:T(8,128)(2,1)}, u32[]{:S(2)}) copy-start(bf16[48,1536]{1,0:T(8,128)(2,1)} %param.19) | copy-start | bytes 442372
  3.5 185.1 %copy-start.3 = (bf16[1,128,1536]{2,1,0:T(8,128)(2,1)S(1)}, bf16[1,128,1536]{2,1,0:T(8,128)(2,1)}, u32[]{:S(2)}) copy-start(bf16[1,128,1536]{2,1,0:T(8,128)(2,1)} %param.12) | copy-start | bytes 1179652
  6.0 249.2 %collective-permute-start = (bf16[2,384,1536]{2,1,0:T(8,128)(2,1)}, bf16[2,384,1536]{2,1,0:T(8,128)(2,1)}, u32[]{:S(2)}, u32[]{:S(2)}) collective-permute-start(bf16[2,384,1536]{2,1,0:T(8,128)(2,1)} %get-tuple-element.85), channel_id=1, source_target_pairs={{0,1},{1,0},{2,3},{3,2},{4,5},{5,4},{6,7},{7,6},{8,9},{9,8},{10,11... | collective-permute-start | bytes 7077896 | tf_op jit(solution)/shard_map/ppermute | solution.py:1197
  6.5 248.7 %collective-permute-start.2 = (bf16[2,384,1536]{2,1,0:T(8,128)(2,1)}, bf16[2,384,1536]{2,1,0:T(8,128)(2,1)}, u32[]{:S(2)}, u32[]{:S(2)}) collective-permute-start(bf16[2,384,1536]{2,1,0:T(8,128)(2,1)} %get-tuple-element.85), channel_id=1, source_target_pairs={{0,3},{1,2},{2,1},{3,0},{4,7},{5,6},{6,5},{7,4},{8,11},{9,10},{10,... | collective-permute-start | bytes 7077896 | tf_op jit(solution)/shard_map/ppermute | solution.py:1197
  9.1 246.1 %collective-permute-start.1 = (bf16[2,384,1536]{2,1,0:T(8,128)(2,1)}, bf16[2,384,1536]{2,1,0:T(8,128)(2,1)}, u32[]{:S(2)}, u32[]{:S(2)}) collective-permute-start(bf16[2,384,1536]{2,1,0:T(8,128)(2,1)} %get-tuple-element.86.refs_2_), channel_id=1, source_target_pairs={{0,2},{1,3},{2,0},{3,1},{4,6},{5,7},{6,4},{7,5},{8,10},{9,11},{10,... | collective-permute-start | bytes 7077896 | tf_op jit(solution)/shard_map/ppermute | solution.py:1197
  9.7 179.2 %copy-start.24 = (bf16[128,96]{1,0:T(8,128)(2,1)}, bf16[128,96]{1,0:T(8,128)(2,1)S(1)}, u32[]{:S(2)}) copy-start(bf16[128,96]{1,0:T(8,128)(2,1)S(1)} %broadcast.193) | copy-start | bytes 73732
  188.7 4.7 copy-start.22
  188.9 4.5 copy-start.38
  195.8 0.6 copy-start.27
  195.8 38.3 %copy-start.20 = (f32[128,32]{0,1:T(8,128)}, f32[128,32]{0,1:T(8,128)S(1)}, u32[]{:S(2)}) copy-start(f32[128,32]{0,1:T(8,128)S(1)} %get-tuple-element.103) | copy-start | bytes 49156
  230.8 8.2 %copy-start.1 = (bf16[1024,512]{0,1:T(8,128)(2,1)}, bf16[1024,512]{0,1:T(8,128)(2,1)S(1)}, u32[]{:S(2)}) copy-start(bf16[1024,512]{0,1:T(8,128)(2,1)S(1)} %copy.96) | copy-start | bytes 3145732
  234.1 4.9 copy-start.11
  234.9 7.3 %copy-start.16 = (pred[128,1024]{0,1:T(8,128)(4,1)}, pred[128,1024]{0,1:T(8,128)(4,1)S(1)}, u32[]{:S(2)}) copy-start(pred[128,1024]{0,1:T(8,128)(4,1)S(1)} %iota_compare_fusion) | copy-start | bytes 393220
  239.1 4.5 copy-start
  239.1 4.5 copy-start.18
  247.1 7.5 %copy-start.14 = (bf16[128,8,3,64]{0,3,2,1:T(8,128)(2,1)}, bf16[128,8,3,64]{0,3,2,1:T(8,128)(2,1)S(1)}, u32[]{:S(2)}) copy-start(bf16[128,8,3,64]{0,3,2,1:T(8,128)(2,1)S(1)} %fusion.37) | copy-start | bytes 1179652
  247.1 4.3 copy-start.31
  247.1 5.9 copy-start.33
  247.1 6.6 copy-start.25
  250.5 0.9 copy-start.5
  250.6 0.9 copy-start.42
  251.6 2.2 copy-start.6
  253.0 2.2 copy-start.28
  253.1 0.5 copy-start.37
  253.1 0.5 copy-start.40
  411.4 7.1 %copy-start.15 = (bf16[128,8,3,64]{0,3,2,1:T(8,128)(2,1)S(1)}, bf16[128,8,3,64]{0,3,2,1:T(8,128)(2,1)}, u32[]{:S(2)}) copy-start(bf16[128,8,3,64]{0,3,2,1:T(8,128)(2,1)} %copy-done.14) | copy-start | bytes 1179652
  411.4 7.2 %copy-start.17 = (pred[128,1024]{0,1:T(8,128)(4,1)S(1)}, pred[128,1024]{0,1:T(8,128)(4,1)}, u32[]{:S(2)}) copy-start(pred[128,1024]{0,1:T(8,128)(4,1)} %copy-done.16) | copy-start | bytes 393220
  411.4 7.2 %copy-start.19 = (bf16[1024,512]{0,1:T(8,128)(2,1)S(1)}, bf16[1024,512]{0,1:T(8,128)(2,1)}, u32[]{:S(2)}) copy-start(bf16[1024,512]{0,1:T(8,128)(2,1)} %copy.98) | copy-start | bytes 3145732
  411.4 7.2 %copy-start.36 = (f32[8,3,128]{2,1,0:T(4,128)S(1)}, f32[8,3,128]{2,1,0:T(4,128)}, u32[]{:S(2)}) copy-start(f32[8,3,128]{2,1,0:T(4,128)} %log_add_fusion) | copy-start | bytes 36868
  418.6 7.4 %copy-start.2 = (bf16[1024,512]{0,1:T(8,128)(2,1)S(1)}, bf16[1024,512]{0,1:T(8,128)(2,1)}, u32[]{:S(2)}) copy-start(bf16[1024,512]{0,1:T(8,128)(2,1)} %copy-done.1) | copy-start | bytes 3145732
  418.6 11.6 %slice-start = ((s8[12582912]{0:T(1024)(128)(4,1)}), s8[4194304]{0:T(1024)(128)(4,1)S(1)}, s32[]{:S(2)}) async-start(s8[12582912]{0:T(1024)(128)(4,1)} %bitcast.158), calls=%async_computation | async-start | bytes 8388608
  418.7 11.6 %slice-start.1 = ((s8[12582912]{0:T(1024)(128)(4,1)}), s8[4194304]{0:T(1024)(128)(4,1)S(1)}, s32[]{:S(2)}) async-start(s8[12582912]{0:T(1024)(128)(4,1)} %bitcast.158), calls=%async_computation.1 | async-start | bytes 8388608
  426.1 2.1 copy-start.12
  426.1 2.0 copy-start.13
  426.1 4.2 slice-start.2
  438.3 46.2 %copy-start.8 = (f32[8,64,3,128]{3,1,2,0:T(8,128)S(1)}, f32[8,64,3,128]{3,1,2,0:T(8,128)}, u32[]{:S(2)}) copy-start(f32[8,64,3,128]{3,1,2,0:T(8,128)} %convolution_multiply_fusion) | copy-start | bytes 2359300
  438.3 46.2 %copy-start.21 = (f32[128,32]{0,1:T(8,128)S(1)}, f32[128,32]{0,1:T(8,128)}, u32[]{:S(2)}) copy-start(f32[128,32]{0,1:T(8,128)} %copy-done.20) | copy-start | bytes 49156
  438.3 46.2 %copy-start.26 = (f32[128,32]{0,1:T(8,128)S(1)}, f32[128,32]{0,1:T(8,128)}, u32[]{:S(2)}) copy-start(f32[128,32]{0,1:T(8,128)} %get-tuple-element.101) | copy-start | bytes 49156
  441.2 43.8 %copy-start.4 = (bf16[1,128,1536]{2,1,0:T(8,128)(2,1)S(1)}, bf16[1,128,1536]{2,1,0:T(8,128)(2,1)}, u32[]{:S(2)}) copy-start(bf16[1,128,1536]{2,1,0:T(8,128)(2,1)} %param.12) | copy-start | bytes 1179652
  441.2 43.8 %copy-start.23 = (f32[1536]{0:T(1024)S(1)}, f32[1536]{0:T(1024)}, u32[]{:S(2)}) copy-start(f32[1536]{0:T(1024)} %copy-done.22) | copy-start | bytes 18436
  441.2 43.8 %copy-start.39 = (f32[128]{0:T(128)S(1)}, f32[128]{0:T(128)}, u32[]{:S(2)}) copy-start(f32[128]{0:T(128)} %copy-done.38) | copy-start | bytes 1540
  476.7 7.7 %slice-start.3 = ((f32[128,1024]{1,0:T(8,128)}), f32[128,512]{1,0:T(8,128)S(1)}, s32[]{:S(2)}) async-start(f32[128,1024]{1,0:T(8,128)} %shard_map.205), calls=%async_computation.3 | async-start | bytes 524288 | tf_op jit(solution)/shard_map/slice | solution.py:1387
  477.7 179.5 %collective-permute-start.3 = (bf16[2,384,1536]{2,1,0:T(8,128)(2,1)}, bf16[2,384,1536]{2,1,0:T(8,128)(2,1)}, u32[]{:S(2)}, u32[]{:S(2)}) collective-permute-start(bf16[2,384,1536]{2,1,0:T(8,128)(2,1)} %get-tuple-element.30), channel_id=1, source_target_pairs={{0,2},{1,3},{2,0},{3,1},{4,6},{5,7},{6,4},{7,5},{8,10},{9,11},{10,... | collective-permute-start | bytes 7077896 | tf_op jit(solution)/shard_map/ppermute | solution.py:1197
  479.4 180.2 %collective-permute-start.4 = (bf16[2,384,1536]{2,1,0:T(8,128)(2,1)}, bf16[2,384,1536]{2,1,0:T(8,128)(2,1)}, u32[]{:S(2)}, u32[]{:S(2)}) collective-permute-start(bf16[2,384,1536]{2,1,0:T(8,128)(2,1)} %get-tuple-element.31), channel_id=1, source_target_pairs={{0,1},{1,0},{2,3},{3,2},{4,5},{5,4},{6,7},{7,6},{8,9},{9,8},{10,11... | collective-permute-start | bytes 7077896 | tf_op jit(solution)/shard_map/ppermute | solution.py:1197
  479.4 180.2 %collective-permute-start.5 = (bf16[2,384,1536]{2,1,0:T(8,128)(2,1)}, bf16[2,384,1536]{2,1,0:T(8,128)(2,1)}, u32[]{:S(2)}, u32[]{:S(2)}) collective-permute-start(bf16[2,384,1536]{2,1,0:T(8,128)(2,1)} %get-tuple-element.32), channel_id=1, source_target_pairs={{0,3},{1,2},{2,1},{3,0},{4,7},{5,6},{6,5},{7,4},{8,11},{9,10},{10,... | collective-permute-start | bytes 7077896 | tf_op jit(solution)/shard_map/ppermute | solution.py:1197
  484.7 7.1 %copy-start.7 = (bf16[128,1536]{1,0:T(8,128)(2,1)S(1)}, bf16[128,1536]{1,0:T(8,128)(2,1)}, u32[]{:S(2)}) copy-start(bf16[128,1536]{1,0:T(8,128)(2,1)} %copy-done.6) | copy-start | bytes 1179652
  508.1 149.1 %copy-start.10 = (bf16[2,384,1536]{2,1,0:T(8,128)(2,1)S(1)}, bf16[2,384,1536]{2,1,0:T(8,128)(2,1)}, u32[]{:S(2)}) copy-start(bf16[2,384,1536]{2,1,0:T(8,128)(2,1)} %get-tuple-element.29) | copy-start | bytes 7077892

commit v4 on v3

--- a/solution.py
+++ b/solution.py
@@ -21,8 +21,8 @@
 
 
 class Plan:
-    def __init__(self, ref, order, index, rows=None):
-        self.ref, self.order, self.index, self.rows = ref, order, index, rows
+    def __init__(self, ref, order, index, rows=None, view=None):
+        self.ref, self.order, self.index, self.rows, self.view = ref, order, index, rows, view
         self.blocks = 1
         for d in index:
             self.blocks *= SIZES[d]
@@ -128,10 +128,14 @@
         z_from = place.order[k]
         spot = place.coords(z_from, flips)
         index = flat_index(spot, plan.index)
-        target = out.at[index] if rows is None else out.at[index, pl.ds(rows[0], rows[1])]
+        own = k == 0 and not flips
+        if plan.view is not None:
+            target = plan.view(out, spot, rows)
+            source = src.at[:, pl.ds(rows[0], rows[1])] if own else target
+        else:
+            target = out.at[index] if rows is None else out.at[index, pl.ds(rows[0], rows[1])]
+            source = (src if rows is None else src.at[pl.ds(rows[0], rows[1])]) if own else target
         sem = recv_sem.at[bases[n] + index]
-        own = k == 0 and not flips
-        source = (src if rows is None else src.at[pl.ds(rows[0], rows[1])]) if own else target
         if not own:
             pltpu.make_async_remote_copy(
                 src_ref=target, dst_ref=target, send_sem=own_sem.at[0], recv_sem=sem,
@@ -167,13 +171,16 @@
             pl.when(go)(wait)
 
 
-def gather(arrays, plans, collective_id):
+def gather(arrays, plans, collective_id, shapes=None):
     n = len(arrays)
     sends = sum(len(gather_sends(p.order, k, f)) for p in plans for k, f in gather_events(p.order))
     blocks = {p.ref: p.blocks for p in plans}
     return pl.pallas_call(
         functools.partial(gather_kernel, plans, n),
-        out_shape=[jax.ShapeDtypeStruct((blocks[i],) + a.shape, a.dtype) for i, a in enumerate(arrays)],
+        out_shape=[
+            jax.ShapeDtypeStruct((shapes or {}).get(i, (blocks[i],) + a.shape), a.dtype)
+            for i, a in enumerate(arrays)
+        ],
         in_specs=[pl.BlockSpec(memory_space=pltpu.VMEM)] * n,
         out_specs=[pl.BlockSpec(memory_space=pl.ANY)] * n,
         scratch_shapes=[
@@ -489,17 +496,16 @@
 
         out[...] = mine[...].astype(out.dtype)
 
-    def steps(self):
+    def at_time(self, t):
         depth = len(self.plan.order)
         far = list(reversed(range(NZ)))
-        out = []
-        for t in range(NZ + depth):
-            for p in range(depth):
-                if 0 <= t - p < NZ:
-                    out.append(functools.partial(self.level, p, far[t - p]))
-            if 0 <= t - depth < NZ - 1:
-                out.append(functools.partial(self.along, far[t - depth]))
+        out = [functools.partial(self.level, p, far[t - p]) for p in range(depth) if 0 <= t - p < NZ]
+        if 0 <= t - depth < NZ - 1:
+            out.append(functools.partial(self.along, far[t - depth]))
         return out
+
+    def steps(self):
+        return [step for t in range(NZ + len(self.plan.order)) for step in self.at_time(t)]
 
     def finish(self):
         for copy in self.pending:
@@ -785,6 +791,82 @@
     )(payload, cots, *parts)
 
 
+def weight_view(out, spot, rows):
+    return out.at[spot[Z] * NY + spot[Y], :, spot[C], pl.ds(rows[0], rows[1])]
+
+
+def weights_kernel(plans, *refs):
+    left_one, right_one, left_two, right_two, left_small, right_small = refs[:6]
+    outs = refs[6:8]
+    held_one, held_two = refs[8:10]
+    buffers = refs[10:18]
+    send_one, recv_one, send_two, recv_two, spare = refs[18:]
+    place = Place()
+    greet(place, (Z, Y, X, C))
+    ways = [
+        Reduce(place, plans[0], held_one, buffers[0:3], buffers[3], send_one, recv_one, spare),
+        Reduce(place, plans[1], held_two, buffers[4:7], buffers[7], send_two, recv_two, spare),
+    ]
+    group = NY * NX * NC
+    rows = group * held_one.shape[1]
+
+    def products(left, right, held, k, shift):
+        at = pl.ds(pl.multiple_of(place.order[k] * rows, 128), rows)
+        block = left[:, at]
+        for c0, cn in columns_of(right.shape[1]):
+            got = lax.dot_general(
+                block, right[:, c0 : c0 + cn], (((0,), (0,)), ((), ())), preferred_element_type=jnp.float32
+            )
+            held[pl.ds(place.order[k] * group, group), :, shift + c0 : shift + c0 + cn] = got.astype(
+                held.dtype
+            ).reshape(group, rows // group, cn)
+
+    far = list(reversed(range(NZ)))
+    for t in range(NZ):
+        k = far[t]
+        products(left_one, right_one, held_one, k, 0)
+        ways[0].first(k)
+        products(left_two, right_two, held_two, k, 0)
+        products(left_small, right_small, held_two, k, right_two.shape[1])
+        ways[1].first(k)
+        if t > 0:
+            for way in ways:
+                for step in way.at_time(t - 1):
+                    step()
+    for t in range(NZ - 1, NZ + 3):
+        for way in ways:
+            for step in way.at_time(t):
+                step()
+    for way, out in zip(ways, outs):
+        way.last(out)
+    for way in ways:
+        way.finish()
+
+
+def return_weights(lefts, rights, collective_id):
+    width = lefts[0].shape[1]
+    rows = width // (NZ * NY * NX * NC)
+    widths = [rights[0].shape[1], rights[1].shape[1] + rights[2].shape[1]]
+    plans = [Plan(0, (C, X, Y), (Z, Y, X, C)), Plan(1, (C, Y, X), (Z, Y, X, C))]
+    bf = jnp.bfloat16
+    levels, sends, recvs = Reduce.counts(plans[0])
+    dma = pltpu.SemaphoreType.DMA
+    operands = [a for pair in zip(lefts, rights) for a in pair]
+    return pl.pallas_call(
+        functools.partial(weights_kernel, plans),
+        out_shape=[jax.ShapeDtypeStruct((rows, w), jnp.float32) for w in widths],
+        in_specs=[pl.BlockSpec(memory_space=pltpu.VMEM)] * 6,
+        out_specs=[pl.BlockSpec(memory_space=pltpu.VMEM)] * 2,
+        scratch_shapes=[pltpu.VMEM((plans[0].blocks, rows, w), bf) for w in widths]
+        + [pltpu.VMEM((n, rows, w), bf) for w in widths for n in levels + [NZ + 1]]
+        + [dma((sends,)), dma((recvs,)), dma((sends,)), dma((recvs,)), dma(())],
+        compiler_params=pltpu.CompilerParams(
+            collective_id=collective_id, has_side_effects=True, vmem_limit_bytes=60 * 1024 * 1024
+        ),
+        name="return_weights",
+    )(*operands)
+
+
 MODEL_WIDTH = 1536
 QUERY_HEADS = 24
 KEY_VALUE_HEADS = 8
@@ -1226,7 +1308,6 @@
     f32 = jnp.float32
     positions = ctx * tokens + jnp.arange(tokens, dtype=jnp.int32)
     cosine_table, sine_table = rope_tables(positions)
-    contract_rows = (((0,), (0,)), ((), ()))
     contract_cols = (((1,), (1,)), ((), ()))
     wide = hidden[0].astype(f32)
     cot = cotangent[0]
@@ -1249,16 +1330,24 @@
     experts = experts.reshape(NC, held, quarter, experts.shape[2])
     mine = lax.dynamic_index_in_dim(experts, core, 0, False)
     other = lax.dynamic_index_in_dim(experts, 1 - core, 0, False)
+    far_one, far_two = swap(pack_one, 2), swap(pack_two, 2)
+    far_one, far_two, mine, other = lax.optimization_barrier((far_one, far_two, mine, other))
     parts = [mine, swap(other, 1), swap(mine, 2), swap(other, 3)]
+    both = lambda near, far: jnp.where(
+        fsdp < NC, jnp.stack([near, far]), jnp.stack([far, near])
+    )
+    part = rows // 3
+    groups = ctx_size, NX, NC, rows
     one, two, cots = gather(
-        [pack_one, pack_two, cot_pack],
+        [both(pack_one, far_one), both(pack_two, far_two), cot_pack],
         [
-            Plan(0, (X, Z, Y, C), (Z, Y, X, C), rows=(0, 2 * rows // 3)),
-            Plan(0, (X, Y, Z, C), (Z, Y, X, C), rows=(2 * rows // 3, rows // 3)),
-            Plan(1, (Z, Y, X, C), (Z, Y, X, C)),
+            Plan(0, (Z, Y, C), (Z, Y, C), rows=(0, 2 * part), view=weight_view),
+            Plan(0, (Y, Z, C), (Z, Y, C), rows=(2 * part, part), view=weight_view),
+            Plan(1, (Z, Y, C), (Z, Y, C), rows=(0, rows), view=weight_view),
             Plan(2, (Z, Y, C), (C, Z, Y)),
         ],
         0,
+        {0: groups + pack_one.shape[1:], 1: groups + pack_two.shape[1:]},
     )
     one = one.reshape(MODEL_WIDTH, -1)
     two = two.reshape(MODEL_WIDTH, -1)
@@ -1331,18 +1420,12 @@
     grad_gate = jnp.sum(indicator * grad_gate_map[:, None, :], axis=-1)
     grad_chosen = gates * (grad_gate - jnp.sum(gates * grad_gate, axis=-1, keepdims=True))
     grad_logits = jnp.sum(indicator * grad_chosen[..., None], axis=1).astype(bf)
-    grad_router_part = lax.dot_general(
-        ffn_in, grad_logits, contract_rows, preferred_element_type=f32
-    )
     grad_ffn_in = gin[:, :MODEL_WIDTH] + lax.dot_general(
         grad_logits, router_w, contract_cols, preferred_element_type=f32
     )
     back_two, _ = rms_backward(grad_ffn_in, ffn_unit, inverse_two, ffn_gain)
     grad_mixed = cot + back_two
     grad_attn = grad_mixed.astype(bf)
-    grad_wo_part = lax.dot_general(
-        attention_output, grad_attn, contract_rows, preferred_element_type=f32
-    )
     attention_output_gradient = lax.dot_general(
         grad_attn, output_w, contract_cols, preferred_element_type=f32
     ).astype(bf)
@@ -1392,29 +1475,29 @@
         .reshape(tokens, kv_width)
     )
     back = jnp.concatenate([query_back, key_back, local_gradients[:, kv_width:].astype(bf)], axis=1)
-    grad_one = lax.dot_general(attention_input, back, contract_rows, preferred_element_type=f32)
     grad_attn_in = lax.dot_general(back, one, contract_cols, preferred_element_type=f32)
     back_one, _ = rms_backward(grad_attn_in, attn_unit, inverse_one, attn_gain)
     grad_input = grad_mixed + back_one
-    attn_gain_grad = jnp.sum(grad_attn_in * attn_unit, axis=0)
-    ffn_gain_grad = jnp.sum(grad_ffn_in * ffn_unit, axis=0)
-    grad_two = jnp.concatenate(
+    halves = []
+    for factor in (grad_attn_in * attn_unit, grad_ffn_in * ffn_unit):
+        high = factor.astype(bf)
+        halves += [high, (factor - high.astype(f32)).astype(bf)]
+    column = lambda n: jnp.broadcast_to((jnp.arange(128) == n).astype(bf), (tokens, 128))
+    sum_one, sum_two = return_weights(
+        [attention_input, attention_output, jnp.concatenate([ffn_in] + halves)],
         [
-            grad_wo_part,
-            grad_router_part,
-            attn_gain_grad[:, None],
-            ffn_gain_grad[:, None],
-            jnp.zeros((MODEL_WIDTH, 94), f32),
+            back,
+            grad_attn,
+            jnp.concatenate(
+                [
+                    jnp.concatenate([grad_logits, jnp.zeros((tokens, 128 - EXPERT_COUNT), bf)], axis=1),
+                    column(EXPERT_COUNT),
+                    column(EXPERT_COUNT),
+                    column(EXPERT_COUNT + 1),
+                    column(EXPERT_COUNT + 1),
+                ]
+            ),
         ],
-        axis=1,
-    )
-    sum_one, sum_two = reduce_scatter(
-        [
-            grad_one.astype(bf).reshape(-1, rows, grad_one.shape[1]),
-            grad_two.astype(bf).reshape(-1, rows, grad_two.shape[1]),
-        ],
-        [Plan(0, (C, X, Y,), (Z, Y, X, C,)), Plan(1, (C, Y, X,), (Z, Y, X, C,))],
-        [f32, f32],
         5,
     )
     at = MODEL_WIDTH + EXPERT_COUNT

time: 680 us -> 670 us (0.985)
  Pallas kernels: 529 us -> 485 us
  waiting for transfers between devices: 0.02 us -> 41.9 us
  matrix products: 55.4 us -> 44.4 us
  other arithmetic: 31.5 us -> 39.7 us
    pallas_call x0 -> x1, Pallas kernels: none -> 161 us  [return_weights(): pl.pallas_call(functools.partial(weights_kernel, plans), out_shape=[jax.S...]
    pallas_call x2 -> x1, Pallas kernels: 173 us -> 38.3 us  [reduce_scatter(): pl.pallas_call(functools.partial(reduce_kernel, plans, n), out_shape=[jax...]
    pallas_call x2, Pallas kernels: 206 us -> 136 us  [gather(): pl.pallas_call(functools.partial(gather_kernel, plans, n), out_shape=[jax...]
    ppermute x6 -> x8, waiting for transfers between devices: 0.02 us -> 41.9 us  [swap(): return lax.ppermute(a, FSDP, [(i, i ^ flip) for i in range(NX * NC)])]
    dot_general x3 -> x0, matrix products: 10.1 us -> none  [the longest x1 5.42 us: fast_body(): lax.dot_general(attention_input, back, contract_rows, preferred_element_t...]
    concatenate x3 -> x2, local copies, waits for them, and re-layouts: 10.4 us -> 0.82 us  [the longest x1 0.8 us: fast_body(): pack_one = jnp.concatenate([w_q, key_weight, value_weight], axis=1)]
  transfers between devices with their start and end apart: 6 -> 8, of which waited for: 0 -> 1; matrix products, arithmetic and copies ran while one was open for 12% -> 8% of each run, Pallas kernels for 51% -> 29%
where the time goes in v4:
time: 670 us; the launch traced here: 665 us
  Pallas kernels  485 us (72%)
  matrix products  44.4 us (7%)
  local copies, waits for them, and re-layouts  44 us (7%)
  waiting for transfers between devices  41.9 us (6%)
  other arithmetic  39.7 us (6%)
  starting transfers between devices  7.4 us (1%)
    pallas_call x1, Pallas kernels, return_weights(): pl.pallas_call(functools.partial(weights_kernel, plans), out_shape=[jax.S...  161 us
    pallas_call x1, Pallas kernels, moe(): pl.pallas_call(functools.partial(moe_kernel, plans, back, width, hidden,...  151 us
    pallas_call x2, Pallas kernels, gather(): pl.pallas_call(functools.partial(gather_kernel, plans, n), out_shape=[jax...  136 us
    ppermute x8, waiting for transfers between devices, swap(): return lax.ppermute(a, FSDP, [(i, i ^ flip) for i in range(NX * NC)])  41.9 us
    pallas_call x1, Pallas kernels, reduce_scatter(): pl.pallas_call(functools.partial(reduce_kernel, plans, n), out_shape=[jax...  38.3 us
  transfers between devices with their start and end apart: 8, of which 1 were waited for; matrix products, arithmetic and copies ran while one was open for 8% of the time, Pallas kernels for 29%

profile of v4, /device:TPU:0, one launch (start us, length us, event | category | flops | bytes accessed | tf_op | source)
XLA Modules:
  0.0 664.8 jit_solution(7005710762863678295)
XLA Ops:
  0.6 0.9 constant_dynamic-update-slice_fusion.2
  1.6 0.8 constant_dynamic-update-slice_fusion.1
  2.4 0.8 constant_dynamic-update-slice_fusion
  3.2 3.0 collective-permute-start
  6.1 0.8 copy.89
  8.4 1.0 concatenate.61
  9.6 1.2 bitcast_convert_fusion.1
  10.7 1.2 fusion.46
  12.7 2.8 pad_maximum_fusion
  16.2 2.6 dynamic-slice_bitcast_fusion
  19.4 0.8 concatenate.63.refs_2_
  20.9 0.8 maximum_select_fusion.2.refs_1_
  21.6 0.8 maximum_select_fusion.1.refs_0_
  22.5 103.4 %shard_map.203 = (bf16[8,2,2,48,2560]{4,3,2,1,0:T(8,128)(2,1)}, bf16[8,2,2,48,1664]{4,3,2,1,0:T(8,128)(2,1)}, bf16[16,128,1664]{2,1,0:T(8,128)(2,1)}) custom-call(bf16[2,48,2560]{2,1,0:T(8,128)(2,1)} %maximum_select_fusion.1.refs_0_, bf16[2,48,1664]{2,1,0:T(8,128)(2,1)} %maximum_select_fusion.2.refs_1_, bf16[128,1664]{1,0:T(8,128)(2,1)} %concatenate.63.refs_2_), custom_call_target="tpu_custom_call" | custom-call | tf_op jit(solution)/shard_map/pallas_call | solution.py:178
  125.9 1.3 fusion.57
  128.4 4.5 fusion.55
  133.0 0.9 slice.139
  134.3 1.2 collective-permute-start.4
  136.6 32.3 %shard_map.204 = bf16[8,128,1024]{2,1,0:T(8,128)(2,1)} custom-call(bf16[128,1024]{1,0:T(8,128)(2,1)} %pad_maximum_fusion.5.refs_0_), custom_call_target="tpu_custom_call" | custom-call | tf_op jit(solution)/shard_map/pallas_call | solution.py:178
  168.9 1.7 fusion.82
  171.1 1.8 copy.96
  172.9 1.5 subtract_convert_fusion.3
  174.4 1.3 copy.97
  176.3 3.0 fusion.5
  179.3 3.0 fusion.2
  182.3 1.5 copy-done
  183.8 3.5 fusion.37
  187.3 1.0 copy.111.refs_2_
  188.3 3.2 multiply_reduce_fusion.2
  191.6 0.9 copy-done.1
  192.4 0.9 constant_dynamic-update-slice_fusion.3
  193.3 1.3 fusion.63
  195.4 0.9 concatenate.69.refs_0_
  196.8 41.9 %collective-permute-done.3.refs_4_ = bf16[2,384,1536]{2,1,0:T(8,128)(2,1)} collective-permute-done((bf16[2,384,1536]{2,1,0:T(8,128)(2,1)}, bf16[2,384,1536]{2,1,0:T(8,128)(2,1)}, u32[]{:S(2)}, u32[]{:S(2)}) %collective-permute-start.3) | collective-permute-done | bytes 2359328 | tf_op jit(solution)/shard_map/ppermute | solution.py:1279
  238.8 150.6 %experts.1 = (f32[128,1664]{1,0:T(8,128)}, f32[128,1536]{1,0:T(8,128)}, bf16[2,384,1536]{2,1,0:T(8,128)(2,1)}, bf16[2,384,1536]{2,1,0:T(8,128)(2,1)}, bf16[2,384...) custom-call(bf16[128,1664]{1,0:T(8,128)(2,1)} %concatenate.69.refs_0_, ...), custom_call_target="tpu_custom_call" | custom-call | tf_op jit(solution)/shard_map/experts/pallas_call | solution.py:753
  389.4 1.0 slice_add_fusion.1
  393.4 1.9 multiply_reduce_fusion.1
  395.4 3.0 fusion.81
  399.1 4.0 fusion.19
  403.5 7.4 %fusion.1 = bf16[8,3,128,1024]{2,3,1,0:T(8,128)(2,1)S(1)} fusion(f32[8,1024,128,3]{2,1,3,0:T(8,128)} %copy-done, f32[8,3,128]{2,1,0:T(4,128)S(1)} %bitcast.204, f32[8,3,128]{2,1,0:T(4,128)S(1)} %copy-done.36, pred[128,1024]{0,1:T(8,128)(4,1)S(1)} %copy-done.17, bf16[1024,8,64,1]{0,2,3,1:T(8,128)(2,1)S(1)} %bitcast.183, bf16[128,8,3,64]{0,3,2,1:T(8,128)(2,1)S(1)} %bitcast.179), kind=kOutput, calls=%fused_computation.2 | convolution fusion | flops 424673280 | bytes 20471808 | tf_op jit(solution)/shard_map/tkgd,nkd->kgtn/dot_general | solution.py:1440
  411.0 2.0 convolution_multiply_fusion
  413.0 2.1 fusion.22
  415.2 4.1 bitcast_convert_fusion
  420.2 1.5 copy.122
  421.7 1.5 copy.107
  423.2 2.8 pad_maximum_fusion.1.refs_0_
  426.0 38.3 %shard_map.205 = f32[128,1024]{1,0:T(8,128)} custom-call(bf16[8,128,1024]{2,1,0:T(8,128)(2,1)} %pad_maximum_fusion.1.refs_0_), custom_call_target="tpu_custom_call" | custom-call | tf_op jit(solution)/shard_map/pallas_call | solution.py:340
  464.3 1.0 slice.118
  465.3 1.6 slice.193
  466.9 1.2 subtract_convert_fusion.2
  469.4 6.2 fusion.40
  475.7 1.9 pad_maximum_fusion.2.refs_1_
  477.6 1.6 collective-permute-start.5
  480.6 1.6 fusion.45
  482.3 160.6 %return_weights.1 = (f32[48,2560]{1,0:T(8,128)}, f32[48,1664]{1,0:T(8,128)}) custom-call(bf16[128,1536]{1,0:T(8,128)(2,1)} %get-tuple-element.104.refs_0_, bf16[128,2560]{1,0:T(8,128)(2,1)} %pad_maximum_fusion.2.refs_1_, bf16[128,1536]{1,0:T(8,128)(2,1)} %copy.111.refs_2_, bf16[128,1536]{1,0:T(8,128)(2,1)} %copy-done.15, bf16[640,1536]{1,0:T(8,128)(2,1)} %copy-done.9, ...), custom_call_target="tpu_custom_call" | custom-call | tf_op jit(solution)/shard_map/return_weights/pallas_call | solution.py:855
  642.9 1.7 slice.127
  645.3 1.7 slice.124
  647.7 1.5 slice_reduce_fusion
  649.2 1.6 fusion.83
  650.9 3.1 convert_add_fusion.1
  654.0 3.1 convert_add_fusion
  657.1 2.0 maximum_select_fusion
  659.0 3.3 slice.150
  662.3 2.0 slice.151
  (166 shorter events, 18.7 us)
Async XLA Ops:
  3.2 17.7 %collective-permute-start = (bf16[48,2560]{1,0:T(8,128)(2,1)S(1)}, bf16[48,2560]{1,0:T(8,128)(2,1)S(1)}, u32[]{:S(2)}, u32[]{:S(2)}) collective-permute-start(bf16[48,2560]{1,0:T(8,128)(2,1)S(1)} %constant_dynamic-update-slice_fusion), channel_id=1, source_target_pairs={{0,2},{1,3},{2,0},{3,1},{4,6},{5,7},{6,4},{7,5},{8,10},{9,11},{10,... | collective-permute-start | bytes 737288 | tf_op jit(solution)/shard_map/ppermute | solution.py:1279
  9.5 11.4 %collective-permute-start.1 = (bf16[48,1664]{1,0:T(8,128)(2,1)S(1)}, bf16[48,1664]{1,0:T(8,128)(2,1)S(1)}, u32[]{:S(2)}, u32[]{:S(2)}) collective-permute-start(bf16[48,1664]{1,0:T(8,128)(2,1)S(1)} %concatenate.61), channel_id=1, source_target_pairs={{0,2},{1,3},{2,0},{3,1},{4,6},{5,7},{6,4},{7,5},{8,10},{9,11},{10,... | collective-permute-start | bytes 479240 | tf_op jit(solution)/shard_map/ppermute | solution.py:1279
  11.9 115.9 %copy-start.37 = (f32[128]{0:T(128)}, f32[128]{0:T(128)S(1)}, u32[]{:S(2)}) copy-start(f32[128]{0:T(128)S(1)} %add_rsqrt_fusion.1) | copy-start | bytes 1540
  15.4 3.3 copy-start.34
  16.2 119.4 %copy-start.31 = (f32[128,32]{0,1:T(8,128)}, f32[128,32]{0,1:T(8,128)S(1)}, u32[]{:S(2)}) copy-start(f32[128,32]{0,1:T(8,128)S(1)} %get-tuple-element.111) | copy-start | bytes 49156
  16.2 156.7 %copy-start.21 = (f32[128,32]{0,1:T(8,128)}, f32[128,32]{0,1:T(8,128)S(1)}, u32[]{:S(2)}) copy-start(f32[128,32]{0,1:T(8,128)S(1)} %get-tuple-element.112) | copy-start | bytes 49156
  16.2 112.2 %copy-start.3 = (bf16[1,128,1536]{2,1,0:T(8,128)(2,1)S(1)}, bf16[1,128,1536]{2,1,0:T(8,128)(2,1)}, u32[]{:S(2)}) copy-start(bf16[1,128,1536]{2,1,0:T(8,128)(2,1)} %param.12) | copy-start | bytes 1179652
  19.4 113.5 %copy-start.23 = (bf16[128,96]{1,0:T(8,128)(2,1)}, bf16[128,96]{1,0:T(8,128)(2,1)S(1)}, u32[]{:S(2)}) copy-start(bf16[128,96]{1,0:T(8,128)(2,1)S(1)} %broadcast.198) | copy-start | bytes 73732
  127.8 0.6 copy-start.28
  133.9 63.0 %collective-permute-start.2 = (bf16[2,384,1536]{2,1,0:T(8,128)(2,1)}, bf16[2,384,1536]{2,1,0:T(8,128)(2,1)}, u32[]{:S(2)}, u32[]{:S(2)}) collective-permute-start(bf16[2,384,1536]{2,1,0:T(8,128)(2,1)} %get-tuple-element.32), channel_id=1, source_target_pairs={{0,1},{1,0},{2,3},{3,2},{4,5},{5,4},{6,7},{7,6},{8,9},{9,8},{10,11... | collective-permute-start | bytes 7077896 | tf_op jit(solution)/shard_map/ppermute | solution.py:1279
  134.3 104.4 %collective-permute-start.4 = (bf16[2,384,1536]{2,1,0:T(8,128)(2,1)}, bf16[2,384,1536]{2,1,0:T(8,128)(2,1)}, u32[]{:S(2)}, u32[]{:S(2)}) collective-permute-start(bf16[2,384,1536]{2,1,0:T(8,128)(2,1)} %get-tuple-element.32), channel_id=1, source_target_pairs={{0,3},{1,2},{2,1},{3,0},{4,7},{5,6},{6,5},{7,4},{8,11},{9,10},{10,... | collective-permute-start | bytes 7077896 | tf_op jit(solution)/shard_map/ppermute | solution.py:1279
  171.1 8.1 %copy-start.5 = (bf16[1024,512]{0,1:T(8,128)(2,1)}, bf16[1024,512]{0,1:T(8,128)(2,1)S(1)}, u32[]{:S(2)}) copy-start(bf16[1024,512]{0,1:T(8,128)(2,1)S(1)} %copy.95) | copy-start | bytes 3145732
  174.4 4.9 copy-start.10
  175.7 63.1 %collective-permute-start.3 = (bf16[2,384,1536]{2,1,0:T(8,128)(2,1)}, bf16[2,384,1536]{2,1,0:T(8,128)(2,1)}, u32[]{:S(2)}, u32[]{:S(2)}) collective-permute-start(bf16[2,384,1536]{2,1,0:T(8,128)(2,1)} %get-tuple-element.31.refs_2_), channel_id=1, source_target_pairs={{0,2},{1,3},{2,0},{3,1},{4,6},{5,7},{6,4},{7,5},{8,10},{9,11},{10,... | collective-permute-start | bytes 7077896 | tf_op jit(solution)/shard_map/ppermute | solution.py:1279
  176.3 3.0 copy-start.16
  179.2 4.6 copy-start
  179.3 4.5 copy-start.18
  187.3 8.9 %copy-start.13 = (bf16[128,8,3,64]{0,3,2,1:T(8,128)(2,1)}, bf16[128,8,3,64]{0,3,2,1:T(8,128)(2,1)S(1)}, u32[]{:S(2)}) copy-start(bf16[128,8,3,64]{0,3,2,1:T(8,128)(2,1)S(1)} %fusion.37) | copy-start | bytes 1179652
  187.3 5.1 copy-start.33
  187.3 7.3 %copy-start.35 = (s32[1,128,8]{1,2,0:T(8,128)S(1)}, s32[1,128,8]{1,2,0:T(8,128)}, u32[]{:S(2)}) copy-start(s32[1,128,8]{1,2,0:T(8,128)} %param.13) | copy-start | bytes 12292
  187.3 8.0 %copy-start.24 = (bf16[128,96]{1,0:T(8,128)(2,1)S(1)}, bf16[128,96]{1,0:T(8,128)(2,1)}, u32[]{:S(2)}) copy-start(bf16[128,96]{1,0:T(8,128)(2,1)} %copy-done.23) | copy-start | bytes 73732
  191.5 0.9 copy-start.1
  191.5 1.8 copy-start.40
  194.6 2.2 copy-start.32
  194.7 0.5 copy-start.39
  194.7 0.5 copy-start.42
  393.4 1.9 copy-start.25
  395.4 7.9 %copy-start.14 = (bf16[128,8,3,64]{0,3,2,1:T(8,128)(2,1)S(1)}, bf16[128,8,3,64]{0,3,2,1:T(8,128)(2,1)}, u32[]{:S(2)}) copy-start(bf16[128,8,3,64]{0,3,2,1:T(8,128)(2,1)} %copy-done.13) | copy-start | bytes 1179652
  398.4 0.7 copy-start.15
  398.4 5.1 copy-start.17
  398.4 5.1 copy-start.19
  398.4 5.1 copy-start.36
  403.5 7.4 %copy-start.6 = (bf16[1024,512]{0,1:T(8,128)(2,1)S(1)}, bf16[1024,512]{0,1:T(8,128)(2,1)}, u32[]{:S(2)}) copy-start(bf16[1024,512]{0,1:T(8,128)(2,1)} %copy-done.5) | copy-start | bytes 3145732
  403.5 11.6 %slice-start = ((s8[12582912]{0:T(1024)(128)(4,1)}), s8[4194304]{0:T(1024)(128)(4,1)S(1)}, s32[]{:S(2)}) async-start(s8[12582912]{0:T(1024)(128)(4,1)} %bitcast.159), calls=%async_computation | async-start | bytes 8388608
  403.5 11.6 %slice-start.1 = ((s8[12582912]{0:T(1024)(128)(4,1)}), s8[4194304]{0:T(1024)(128)(4,1)S(1)}, s32[]{:S(2)}) async-start(s8[12582912]{0:T(1024)(128)(4,1)} %bitcast.159), calls=%async_computation.1 | async-start | bytes 8388608
  410.9 2.1 copy-start.11
  410.9 2.0 copy-start.12
  411.0 4.2 slice-start.2
  421.7 45.2 %copy-start.22 = (f32[128,32]{0,1:T(8,128)S(1)}, f32[128,32]{0,1:T(8,128)}, u32[]{:S(2)}) copy-start(f32[128,32]{0,1:T(8,128)} %copy-done.21) | copy-start | bytes 49156
  421.7 45.2 %copy-start.30 = (f32[128,32]{0,1:T(8,128)S(1)}, f32[128,32]{0,1:T(8,128)}, u32[]{:S(2)}) copy-start(f32[128,32]{0,1:T(8,128)} %get-tuple-element.110) | copy-start | bytes 49156
  423.2 46.1 %copy-start.4 = (bf16[1,128,1536]{2,1,0:T(8,128)(2,1)S(1)}, bf16[1,128,1536]{2,1,0:T(8,128)(2,1)}, u32[]{:S(2)}) copy-start(bf16[1,128,1536]{2,1,0:T(8,128)(2,1)} %param.12) | copy-start | bytes 1179652
  423.2 46.1 %copy-start.29 = (f32[1536]{0:T(1024)S(1)}, f32[1536]{0:T(1024)}, u32[]{:S(2)}) copy-start(f32[1536]{0:T(1024)} %copy-done.28) | copy-start | bytes 18436
  423.2 46.1 %copy-start.38 = (f32[128]{0:T(128)S(1)}, f32[128]{0:T(128)}, u32[]{:S(2)}) copy-start(f32[128]{0:T(128)} %copy-done.37) | copy-start | bytes 1540
  469.4 6.3 copy-start.20
  469.4 8.2 %copy-start.26 = (bf16[128,32]{1,0:T(8,128)(2,1)S(1)}, bf16[128,32]{1,0:T(8,128)(2,1)}, u32[]{:S(2)}) copy-start(bf16[128,32]{1,0:T(8,128)(2,1)} %copy-done.25) | copy-start | bytes 24580
  469.4 10.4 %copy-start.8 = (bf16[640,1536]{1,0:T(8,128)(2,1)S(1)}, bf16[640,1536]{1,0:T(8,128)(2,1)}, u32[]{:S(2)}) copy-start(bf16[640,1536]{1,0:T(8,128)(2,1)} %get-tuple-element.89) | copy-start | bytes 5898244
  469.4 10.7 %copy-start.43 = (bf16[128]{0:T(256)(128)(2,1)S(1)}, bf16[128]{0:T(256)(128)(2,1)}, u32[]{:S(2)}) copy-start(bf16[128]{0:T(256)(128)(2,1)} %compare_convert_fusion.1) | copy-start | bytes 772
  469.4 10.8 %copy-start.44 = (bf16[128]{0:T(256)(128)(2,1)S(1)}, bf16[128]{0:T(256)(128)(2,1)}, u32[]{:S(2)}) copy-start(bf16[128]{0:T(256)(128)(2,1)} %compare_convert_fusion) | copy-start | bytes 772
  469.4 10.8 %copy-start.2 = (f32[128,1536]{1,0:T(8,128)S(1)}, f32[128,1536]{1,0:T(8,128)}, u32[]{:S(2)}) copy-start(f32[128,1536]{1,0:T(8,128)} %copy-done.1) | copy-start | bytes 2359300
  469.4 10.8 %copy-start.41 = (f32[128]{0:T(128)S(1)}, f32[128]{0:T(128)}, u32[]{:S(2)}) copy-start(f32[128]{0:T(128)} %copy-done.40) | copy-start | bytes 1540
  475.7 5.0 copy-start.7
  477.6 173.3 %collective-permute-start.5 = (bf16[2,384,1536]{2,1,0:T(8,128)(2,1)}, bf16[2,384,1536]{2,1,0:T(8,128)(2,1)}, u32[]{:S(2)}, u32[]{:S(2)}) collective-permute-start(bf16[2,384,1536]{2,1,0:T(8,128)(2,1)} %get-tuple-element.38), channel_id=1, source_target_pairs={{0,2},{1,3},{2,0},{3,1},{4,6},{5,7},{6,4},{7,5},{8,10},{9,11},{10,... | collective-permute-start | bytes 7077896 | tf_op jit(solution)/shard_map/ppermute | solution.py:1279
  479.1 174.8 %collective-permute-start.6 = (bf16[2,384,1536]{2,1,0:T(8,128)(2,1)}, bf16[2,384,1536]{2,1,0:T(8,128)(2,1)}, u32[]{:S(2)}, u32[]{:S(2)}) collective-permute-start(bf16[2,384,1536]{2,1,0:T(8,128)(2,1)} %get-tuple-element.39), channel_id=1, source_target_pairs={{0,1},{1,0},{2,3},{3,2},{4,5},{5,4},{6,7},{7,6},{8,9},{9,8},{10,11... | collective-permute-start | bytes 7077896 | tf_op jit(solution)/shard_map/ppermute | solution.py:1279
  479.1 174.8 %collective-permute-start.7 = (bf16[2,384,1536]{2,1,0:T(8,128)(2,1)}, bf16[2,384,1536]{2,1,0:T(8,128)(2,1)}, u32[]{:S(2)}, u32[]{:S(2)}) collective-permute-start(bf16[2,384,1536]{2,1,0:T(8,128)(2,1)} %get-tuple-element.40), channel_id=1, source_target_pairs={{0,3},{1,2},{2,1},{3,0},{4,7},{5,6},{6,5},{7,4},{8,11},{9,10},{10,... | collective-permute-start | bytes 7077896 | tf_op jit(solution)/shard_map/ppermute | solution.py:1279
  480.2 2.0 copy-start.27
  480.6 1.7 copy-start.9

commit v5 on v4

--- a/solution.py
+++ b/solution.py
@@ -484,7 +484,7 @@
 
         self.push(mine, self.chain.at[spot], sem, self.place.along(jnp.where(up, 1, -1)))
 
-    def last(self, out):
+    def last(self, out, base=None):
         z = self.place.at[Z]
         mine = self.held.at[self.block(0, ())]
         for go, spot in ((z > 0, z + 1), (z < NZ - 1, z)):
@@ -494,7 +494,10 @@
                 self.arrived(self.chain.at[spot], self.recv_sem.at[self.base[-1] + spot])
                 add_into(mine, self.chain.at[spot])
 
-        out[...] = mine[...].astype(out.dtype)
+        total = mine[...].astype(jnp.float32)
+        if base is not None:
+            total = base[...] + total
+        out[...] = total.astype(out.dtype)
 
     def at_time(self, t):
         depth = len(self.plan.order)
@@ -522,12 +525,12 @@
 
 def moe_kernel(plans, back, width, hidden, cap, *refs):
     payload, cots, w_own, w_core, w_x, w_both = refs[:6]
-    gin_out, moe_out = refs[6:8]
+    gin_out, part_out = refs[6:8]
     grads = refs[8:12]
     (
         seen, cot_seen, weights, taken, cot_taken, rows_buf, scaled, grad_act, pick, stage,
-        lvl_a0, lvl_a1, chain_a, lvl_b0, lvl_b1, chain_b,
-        send_sem, recv_sem, spare_sem, send_a, recv_a, send_b, recv_b, load_sem, store_sem,
+        lvl_b0, lvl_b1, chain_b,
+        send_sem, recv_sem, spare_sem, send_b, recv_b, load_sem, store_sem, part_sem,
     ) = refs[12:]
     bf, f32 = jnp.bfloat16, jnp.float32
     place = Place()
@@ -689,44 +692,40 @@
 
     far = list(reversed(range(NZ)))
     spare = spare_sem
-    out_way = Reduce(place, back, seen.at[:, :, pl.ds(0, width)], (lvl_a0, lvl_a1), chain_a, send_a, recv_a, spare)
     in_way = Reduce(place, back, cot_seen, (lvl_b0, lvl_b1), chain_b, send_b, recv_b, spare)
-    out_steps, in_steps = out_way.steps(), in_way.steps()
-
-    def out_step():
-        if out_steps:
-            out_steps.pop(0)()
-
-    for h in reversed(range(NC)):
-        for e in range(held):
-            project(h, e, scaled, (2 * hidden, hidden))
-        for k in far:
-            combine(seen, h, k, columns_of(width))
-            if h == 1:
-                out_way.first(k)
+    in_steps = in_way.steps()
     for h in reversed(range(NC)):
         for e in range(held):
             project(h, e, grad_act, (0, 2 * hidden))
-            out_step()
         for k in far:
             combine(cot_seen, h, k, all_cols)
             if h == 1:
                 in_way.first(k)
-            out_step()
-    grad_work = [functools.partial(weight_grad, e, j) for j in reversed(range(NX * NC)) for e in range(held)]
-    while out_steps or in_steps or grad_work:
-        if grad_work:
-            grad_work.pop(0)()
-        out_step()
+    part_copies = []
+    work = []
+
+    def out_part(h, k):
+        combine(seen, h, k, columns_of(width))
+        at = pl.ds(base_of(h, k), NY)
+        copy = pltpu.make_async_copy(seen.at[at, :, pl.ds(0, width)], part_out.at[at], part_sem.at[len(part_copies)])
+        copy.start()
+        part_copies.append(copy)
+
+    for h in range(NC):
+        for e in range(held):
+            work.append(functools.partial(project, h, e, scaled, (2 * hidden, hidden)))
+        for k in range(NZ):
+            work.append(functools.partial(out_part, h, k))
+    work += [functools.partial(weight_grad, e, j) for j in reversed(range(NX * NC)) for e in range(held)]
+    while in_steps or work:
         if in_steps:
             in_steps.pop(0)()
-        if in_steps:
-            in_steps.pop(0)()
-    out_way.last(moe_out)
+        for _ in range(2):
+            if work:
+                work.pop(0)()
     in_way.last(gin_out)
-    for copy in stores[-2:]:
+    for copy in stores[-2:] + part_copies:
         copy.wait()
-    out_way.finish()
     in_way.finish()
 
 
@@ -754,11 +753,11 @@
         functools.partial(moe_kernel, plans, back, width, hidden, cap),
         out_shape=[
             jax.ShapeDtypeStruct((count, wide), f32),
-            jax.ShapeDtypeStruct((count, width), f32),
+            jax.ShapeDtypeStruct((blocks, count, width), bf),
         ]
         + [jax.ShapeDtypeStruct((held, quarter, columns), bf)] * (NX * NC),
         in_specs=[whole] + [apart] * 5,
-        out_specs=[whole] * 2 + [apart] * (NX * NC),
+        out_specs=[whole] + [apart] * (1 + NX * NC),
         scratch_shapes=[
             pltpu.VMEM((blocks, count, wide), bf),
             pltpu.VMEM((blocks, count, wide), bf),
@@ -771,7 +770,6 @@
             pltpu.VMEM((blocks // NY, NY * count, lanes), bf),
             pltpu.VMEM((2, quarter, columns), bf),
         ]
-        + [pltpu.VMEM((n, count, width), bf) for n in levels + [NZ + 1]]
         + [pltpu.VMEM((n, count, wide), bf) for n in levels + [NZ + 1]]
         + [
             dma((sum(Gather.sends(p) for p in plans),)),
@@ -779,10 +777,9 @@
             dma(()),
             dma((sends,)),
             dma((recvs,)),
-            dma((sends,)),
-            dma((recvs,)),
             dma((held * NX * NC + blocks // NY,)),
             dma((held * NX * NC,)),
+            dma((blocks // NY,)),
         ],
         compiler_params=pltpu.CompilerParams(
             collective_id=collective_id, has_side_effects=True, vmem_limit_bytes=67043328
@@ -796,16 +793,25 @@
 
 
 def weights_kernel(plans, *refs):
-    left_one, right_one, left_two, right_two, left_small, right_small = refs[:6]
-    outs = refs[6:8]
-    held_one, held_two = refs[8:10]
-    buffers = refs[10:18]
-    send_one, recv_one, send_two, recv_two, spare = refs[18:]
+    left_one, right_one, left_two, right_two, left_small, right_small, part, mixed = refs[:8]
+    outs = refs[8:11]
+    held_one, held_two, held_out = refs[11:14]
+    buffers = refs[14:25]
+    send_one, recv_one, send_two, recv_two, send_out, recv_out, spare, load_sem = refs[25:]
     place = Place()
+    loads = []
+    far = list(reversed(range(NZ)))
+    for k in far:
+        for h in (1 - place.at[C], place.at[C]):
+            at = pl.ds((h * NZ + place.order[k]) * NY, NY)
+            loads.append(pltpu.make_async_copy(part.at[at], held_out.at[at], load_sem.at[len(loads)]))
+    for copy in loads:
+        copy.start()
     greet(place, (Z, Y, X, C))
     ways = [
         Reduce(place, plans[0], held_one, buffers[0:3], buffers[3], send_one, recv_one, spare),
         Reduce(place, plans[1], held_two, buffers[4:7], buffers[7], send_two, recv_two, spare),
+        Reduce(place, plans[2], held_out, buffers[8:10], buffers[10], send_out, recv_out, spare),
     ]
     group = NY * NX * NC
     rows = group * held_one.shape[1]
@@ -821,7 +827,6 @@
                 held.dtype
             ).reshape(group, rows // group, cn)
 
-    far = list(reversed(range(NZ)))
     for t in range(NZ):
         k = far[t]
         products(left_one, right_one, held_one, k, 0)
@@ -829,6 +834,9 @@
         products(left_two, right_two, held_two, k, 0)
         products(left_small, right_small, held_two, k, right_two.shape[1])
         ways[1].first(k)
+        for copy in loads[2 * t : 2 * t + 2]:
+            copy.wait()
+        ways[2].first(k)
         if t > 0:
             for way in ways:
                 for step in way.at_time(t - 1):
@@ -838,33 +846,70 @@
             for step in way.at_time(t):
                 step()
     for way, out in zip(ways, outs):
-        way.last(out)
+        way.last(out, mixed if way is ways[2] else None)
     for way in ways:
         way.finish()
 
 
-def return_weights(lefts, rights, collective_id):
+def return_weights(lefts, rights, part, mixed, collective_id):
     width = lefts[0].shape[1]
     rows = width // (NZ * NY * NX * NC)
     widths = [rights[0].shape[1], rights[1].shape[1] + rights[2].shape[1]]
-    plans = [Plan(0, (C, X, Y), (Z, Y, X, C)), Plan(1, (C, Y, X), (Z, Y, X, C))]
+    plans = [
+        Plan(0, (C, X, Y), (Z, Y, X, C)),
+        Plan(1, (C, X, Y), (Z, Y, X, C)),
+        Plan(2, (C, Y), (C, Z, Y)),
+    ]
     bf = jnp.bfloat16
     levels, sends, recvs = Reduce.counts(plans[0])
+    out_levels, out_sends, out_recvs = Reduce.counts(plans[2])
     dma = pltpu.SemaphoreType.DMA
-    operands = [a for pair in zip(lefts, rights) for a in pair]
+    operands = [a for pair in zip(lefts, rights) for a in pair] + [part, mixed]
+    vmem = pl.BlockSpec(memory_space=pltpu.VMEM)
     return pl.pallas_call(
         functools.partial(weights_kernel, plans),
-        out_shape=[jax.ShapeDtypeStruct((rows, w), jnp.float32) for w in widths],
-        in_specs=[pl.BlockSpec(memory_space=pltpu.VMEM)] * 6,
-        out_specs=[pl.BlockSpec(memory_space=pltpu.VMEM)] * 2,
+        out_shape=[jax.ShapeDtypeStruct((rows, w), jnp.float32) for w in widths]
+        + [jax.ShapeDtypeStruct(mixed.shape, bf)],
+        in_specs=[vmem] * 6 + [pl.BlockSpec(memory_space=pl.ANY), vmem],
+        out_specs=[vmem] * 3,
         scratch_shapes=[pltpu.VMEM((plans[0].blocks, rows, w), bf) for w in widths]
+        + [pltpu.VMEM(part.shape, bf)]
         + [pltpu.VMEM((n, rows, w), bf) for w in widths for n in levels + [NZ + 1]]
-        + [dma((sends,)), dma((recvs,)), dma((sends,)), dma((recvs,)), dma(())],
+        + [pltpu.VMEM((n,) + part.shape[1:], bf) for n in out_levels + [NZ + 1]]
+        + [dma((n,)) for n in (sends, recvs, sends, recvs, out_sends, out_recvs)]
+        + [dma(()), dma((NC * NZ,))],
         compiler_params=pltpu.CompilerParams(
             collective_id=collective_id, has_side_effects=True, vmem_limit_bytes=60 * 1024 * 1024
         ),
         name="return_weights",
     )(*operands)
+
+
+def add_kernel(core_ref, own, core_part, x_part, both_part, in_out, out_out):
+    core = core_ref[0]
+    split = in_out.shape[3]
+    for at, left, right in ((core, own, x_part), (1 - core, core_part, both_part)):
+        total = left[0].astype(jnp.float32) + right[0].astype(jnp.float32)
+        in_out[at, 0] = total[:, :split]
+        out_out[at, 0] = total[:, split:]
+
+
+def add_experts(pieces, core, split):
+    held, quarter, columns = pieces[0].shape
+    step = quarter // 2
+    spec = pl.BlockSpec((1, step, columns), lambda e, r, c: (e, r, 0))
+    outs = (split, columns - split)
+    return pl.pallas_call(
+        add_kernel,
+        grid_spec=pltpu.PrefetchScalarGridSpec(
+            num_scalar_prefetch=1,
+            grid=(held, 2),
+            in_specs=[spec] * 4,
+            out_specs=[pl.BlockSpec((NC, 1, step, w), lambda e, r, c: (0, e, r, 0)) for w in outs],
+        ),
+        out_shape=[jax.ShapeDtypeStruct((NC, held, quarter, w), jnp.float32) for w in outs],
+        name="add_experts",
+    )(core[None], *pieces)
 
 
 MODEL_WIDTH = 1536
@@ -1402,18 +1447,8 @@
     payload = jnp.concatenate(
         [ffn_in, gate_map.astype(bf), jnp.zeros((tokens, 128 - EXPERT_COUNT), bf)], axis=1
     )
-    gin, moe_out, *pieces = moe(payload, cots, parts, CAP, 2)
+    gin, moe_part, *pieces = moe(payload, cots, parts, CAP, 2)
     across = [swap(pieces[j], j) for j in range(1, NX * NC)]
-    own_sum = pieces[0].astype(f32) + across[1].astype(f32)
-    core_sum = across[0].astype(f32) + across[2].astype(f32)
-    grad_experts = jnp.where(
-        core == 0,
-        jnp.concatenate([own_sum, core_sum]),
-        jnp.concatenate([core_sum, own_sum]),
-    )
-    grad_expert_in = grad_experts[:, :, : 2 * EXPERT_HIDDEN]
-    grad_expert_out = grad_experts[:, :, 2 * EXPERT_HIDDEN :]
-    layer_out = (mixed + moe_out).astype(bf)
     grad_gate_map = gin[:, MODEL_WIDTH : MODEL_WIDTH + EXPERT_COUNT] + gin[
         :, MODEL_WIDTH + EXPERT_COUNT : MODEL_WIDTH + 2 * EXPERT_COUNT
     ]
@@ -1483,7 +1518,7 @@
         high = factor.astype(bf)
         halves += [high, (factor - high.astype(f32)).astype(bf)]
     column = lambda n: jnp.broadcast_to((jnp.arange(128) == n).astype(bf), (tokens, 128))
-    sum_one, sum_two = return_weights(
+    sum_one, sum_two, layer_out = return_weights(
         [attention_input, attention_output, jnp.concatenate([ffn_in] + halves)],
         [
             back,
@@ -1498,7 +1533,13 @@
                 ]
             ),
         ],
+        moe_part,
+        mixed,
         5,
+    )
+    grad_expert_in, grad_expert_out = (
+        g.reshape(NC * held, quarter, -1)
+        for g in add_experts([pieces[0]] + across, core, 2 * EXPERT_HIDDEN)
     )
     at = MODEL_WIDTH + EXPERT_COUNT
     return (

time: 670 us -> 666 us (level)
  Pallas kernels: 485 us -> 496 us
  other arithmetic: 39.7 us -> 31 us
    pallas_call x1, Pallas kernels: 161 us -> 196 us  [return_weights(): pl.pallas_call(functools.partial(weights_kernel, plans), out_shape=[jax.S...]
    pallas_call x1, Pallas kernels: 151 us -> 118 us  [moe(): pl.pallas_call(functools.partial(moe_kernel, plans, back, width, hidden,...]
    pallas_call x0 -> x1, Pallas kernels: none -> 7.69 us  [add_experts(): pl.pallas_call(add_kernel, grid_spec=pltpu.PrefetchScalarGridSpec(num_sca...]
  transfers between devices with their start and end apart: 8 -> 8, of which waited for: 1 -> 1; matrix products, arithmetic and copies ran while one was open for 8% -> 8% of each run, Pallas kernels for 29% -> 34%
where the time goes in v5:
time: 666 us; the launch traced here: 661 us
  Pallas kernels  496 us (74%)
  matrix products  44.6 us (7%)
  waiting for transfers between devices  42 us (6%)
  local copies, waits for them, and re-layouts  38.8 us (6%)
  other arithmetic  31 us (5%)
  starting transfers between devices  7.08 us (1%)
    pallas_call x1, Pallas kernels, return_weights(): pl.pallas_call(functools.partial(weights_kernel, plans), out_shape=[jax.S...  196 us
    pallas_call x2, Pallas kernels, gather(): pl.pallas_call(functools.partial(gather_kernel, plans, n), out_shape=[jax...  136 us
    pallas_call x1, Pallas kernels, moe(): pl.pallas_call(functools.partial(moe_kernel, plans, back, width, hidden,...  118 us
    ppermute x8, waiting for transfers between devices, swap(): return lax.ppermute(a, FSDP, [(i, i ^ flip) for i in range(NX * NC)])  42 us
    pallas_call x1, Pallas kernels, reduce_scatter(): pl.pallas_call(functools.partial(reduce_kernel, plans, n), out_shape=[jax...  38.4 us
  transfers between devices with their start and end apart: 8, of which 1 were waited for; matrix products, arithmetic and copies ran while one was open for 8% of the time, Pallas kernels for 34%

profile of v5, /device:TPU:0, one launch (start us, length us, event | category | flops | bytes accessed | tf_op | source)
XLA Modules:
  0.0 661.3 jit_solution(18049325660758240241)
XLA Ops:
  0.6 0.9 constant_dynamic-update-slice_fusion.2
  1.6 0.8 constant_dynamic-update-slice_fusion.1
  2.4 0.8 constant_dynamic-update-slice_fusion
  3.2 3.0 collective-permute-start
  6.1 0.8 copy.89
  6.9 0.8 copy.90
  7.7 0.8 copy.91
  8.4 1.0 concatenate.55
  9.6 1.2 bitcast_convert_fusion.1
  10.7 1.2 fusion.46
  11.9 0.8 iota_compare_fusion
  12.7 2.8 pad_maximum_fusion
  16.2 2.5 dynamic-slice_bitcast_fusion
  19.4 0.9 concatenate.57.refs_2_
  20.8 0.8 maximum_select_fusion.1.refs_1_
  21.5 0.8 maximum_select_fusion.refs_0_
  22.4 103.4 %shard_map.203 = (bf16[8,2,2,48,2560]{4,3,2,1,0:T(8,128)(2,1)}, bf16[8,2,2,48,1664]{4,3,2,1,0:T(8,128)(2,1)}, bf16[16,128,1664]{2,1,0:T(8,128)(2,1)}) custom-call(bf16[2,48,2560]{2,1,0:T(8,128)(2,1)} %maximum_select_fusion.refs_0_, bf16[2,48,1664]{2,1,0:T(8,128)(2,1)} %maximum_select_fusion.1.refs_1_, bf16[128,1664]{1,0:T(8,128)(2,1)} %concatenate.57.refs_2_), custom_call_target="tpu_custom_call" | custom-call | tf_op jit(solution)/shard_map/pallas_call | solution.py:178
  125.8 1.3 fusion.56
  128.3 4.5 fusion.54
  132.8 0.9 slice.130
  134.3 1.1 collective-permute-start.4
  136.5 32.3 %shard_map.204 = bf16[8,128,1024]{2,1,0:T(8,128)(2,1)} custom-call(bf16[128,1024]{1,0:T(8,128)(2,1)} %pad_maximum_fusion.5.refs_0_), custom_call_target="tpu_custom_call" | custom-call | tf_op jit(solution)/shard_map/pallas_call | solution.py:178
  168.8 1.7 fusion.81
  171.0 1.8 copy.96
  172.8 1.5 subtract_convert_fusion.3
  174.3 1.3 copy.97
  176.1 3.0 fusion.5
  179.1 3.0 fusion.3
  182.2 1.5 copy-done
  183.6 3.5 fusion.37
  187.2 0.9 copy.111.refs_2_
  188.1 3.2 multiply_reduce_fusion.2
  191.4 0.9 copy-done.1
  192.3 0.9 constant_dynamic-update-slice_fusion.3
  193.1 1.3 fusion.62
  195.2 0.9 concatenate.63.refs_0_
  196.7 42.0 %collective-permute-done.3.refs_4_ = bf16[2,384,1536]{2,1,0:T(8,128)(2,1)} collective-permute-done((bf16[2,384,1536]{2,1,0:T(8,128)(2,1)}, bf16[2,384,1536]{2,1,0:T(8,128)(2,1)}, u32[]{:S(2)}, u32[]{:S(2)}) %collective-permute-start.3) | collective-permute-done | bytes 2359328 | tf_op jit(solution)/shard_map/ppermute | solution.py:1324
  238.7 118.3 %experts.1 = (f32[128,1664]{1,0:T(8,128)}, bf16[16,128,1536]{2,1,0:T(8,128)(2,1)}, bf16[2,384,1536]{2,1,0:T(8,128)(2,1)}, bf16[2,384,1536]{2,1,0:T(8,128)(2,1)},...) custom-call(bf16[128,1664]{1,0:T(8,128)(2,1)} %concatenate.63.refs_0_, ...), custom_call_target="tpu_custom_call" | custom-call | tf_op jit(solution)/shard_map/experts/pallas_call | solution.py:752
  357.0 1.0 slice_add_fusion.1
  361.0 1.9 multiply_reduce_fusion.1
  363.0 2.6 fusion.80
  365.6 4.1 fusion.19
  370.2 7.4 %fusion.1 = bf16[8,3,128,1024]{2,3,1,0:T(8,128)(2,1)S(1)} fusion(f32[8,1024,128,3]{2,1,3,0:T(8,128)} %copy-done, f32[8,3,128]{2,1,0:T(4,128)S(1)} %bitcast.207, f32[8,3,128]{2,1,0:T(4,128)S(1)} %copy-done.37, pred[128,1024]{0,1:T(8,128)(4,1)S(1)} %copy-done.17, bf16[1024,8,64,1]{0,2,3,1:T(8,128)(2,1)S(1)} %bitcast.185, bf16[128,8,3,64]{0,3,2,1:T(8,128)(2,1)S(1)} %bitcast.181), kind=kOutput, calls=%fused_computation.2 | convolution fusion | flops 424673280 | bytes 20471808 | tf_op jit(solution)/shard_map/tkgd,nkd->kgtn/dot_general | solution.py:1475
  377.6 2.0 convolution_multiply_fusion
  379.6 2.1 fusion.22
  381.8 4.1 bitcast_convert_fusion
  386.9 1.5 copy.122
  388.4 1.5 copy.107
  389.8 2.8 pad_maximum_fusion.1.refs_0_
  392.7 38.4 %shard_map.205 = f32[128,1024]{1,0:T(8,128)} custom-call(bf16[8,128,1024]{2,1,0:T(8,128)(2,1)} %pad_maximum_fusion.1.refs_0_), custom_call_target="tpu_custom_call" | custom-call | tf_op jit(solution)/shard_map/pallas_call | solution.py:340
  431.1 1.0 slice.112
  432.1 1.6 slice.183
  433.7 1.2 subtract_convert_fusion.2
  435.4 0.8 copy.110
  436.2 6.2 fusion.41
  442.4 1.9 pad_maximum_fusion.2.refs_1_
  444.4 1.7 collective-permute-start.6
  447.1 1.5 fusion.45
  448.7 195.7 %return_weights.1 = (f32[48,2560]{1,0:T(8,128)}, f32[48,1664]{1,0:T(8,128)}, bf16[128,1536]{1,0:T(8,128)(2,1)}) custom-call(bf16[128,1536]{1,0:T(8,128)(2,1)} %get-tuple-element.110.refs_0_, bf16[128,2560]{1,0:T(8,128)(2,1)} %pad_maximum_fusion.2.refs_1_, bf16[128,1536]{1,0:T(8,128)(2,1)} %copy.111.refs_2_, bf16[128,1536]{1,0:T(8,128)(2,1)} %copy-done.13, ...), custom_call_target="tpu_custom_call" | custom-call | tf_op jit(solution)/shard_map/return_weights/pallas_call | solution.py:869
  644.4 1.7 slice.121
  646.8 1.7 slice.118
  649.2 1.5 slice_reduce_fusion
  650.7 1.6 fusion.82
  652.4 7.7 %add_experts.1 = (f32[2,2,384,1024]{3,2,1,0:T(8,128)}, f32[2,2,384,512]{3,2,1,0:T(8,128)}) custom-call(s32[1]{0:T(128)} %bitcast.52.core_ref, bf16[2,384,1536]{2,1,0:T(8,128)(2,1)} %get-tuple-element.41.own, bf16[2,384,1536]{2,1,0:T(8,128)(2,1)} %collective-permute-done.5.core_part, bf16[2,384,1536]{2,1,0:T(8,128)(2,1)} %collective-permute-done.6.x_part, ...), custom_call_target="tpu_custom_call" | custom-call | tf_op jit(solution)/shard_map/add_experts/pallas_call | solution.py:902
  (165 shorter events, 15.3 us)
Async XLA Ops:
  3.2 17.6 %collective-permute-start = (bf16[48,2560]{1,0:T(8,128)(2,1)S(1)}, bf16[48,2560]{1,0:T(8,128)(2,1)S(1)}, u32[]{:S(2)}, u32[]{:S(2)}) collective-permute-start(bf16[48,2560]{1,0:T(8,128)(2,1)S(1)} %constant_dynamic-update-slice_fusion), channel_id=1, source_target_pairs={{0,2},{1,3},{2,0},{3,1},{4,6},{5,7},{6,4},{7,5},{8,10},{9,11},{10,... | collective-permute-start | bytes 737288 | tf_op jit(solution)/shard_map/ppermute | solution.py:1324
  9.5 11.3 %collective-permute-start.1 = (bf16[48,1664]{1,0:T(8,128)(2,1)S(1)}, bf16[48,1664]{1,0:T(8,128)(2,1)S(1)}, u32[]{:S(2)}, u32[]{:S(2)}) collective-permute-start(bf16[48,1664]{1,0:T(8,128)(2,1)S(1)} %concatenate.55), channel_id=1, source_target_pairs={{0,2},{1,3},{2,0},{3,1},{4,6},{5,7},{6,4},{7,5},{8,10},{9,11},{10,... | collective-permute-start | bytes 479240 | tf_op jit(solution)/shard_map/ppermute | solution.py:1324
  11.9 115.8 %copy-start.38 = (f32[128]{0:T(128)}, f32[128]{0:T(128)S(1)}, u32[]{:S(2)}) copy-start(f32[128]{0:T(128)S(1)} %add_rsqrt_fusion.1) | copy-start | bytes 1540
  15.5 3.3 copy-start.35
  16.2 119.3 %copy-start.32 = (f32[128,32]{0,1:T(8,128)}, f32[128,32]{0,1:T(8,128)S(1)}, u32[]{:S(2)}) copy-start(f32[128,32]{0,1:T(8,128)S(1)} %get-tuple-element.116) | copy-start | bytes 49156
  16.2 156.6 %copy-start.21 = (f32[128,32]{0,1:T(8,128)}, f32[128,32]{0,1:T(8,128)S(1)}, u32[]{:S(2)}) copy-start(f32[128,32]{0,1:T(8,128)S(1)} %get-tuple-element.117) | copy-start | bytes 49156
  16.2 112.0 %copy-start.3 = (bf16[1,128,1536]{2,1,0:T(8,128)(2,1)S(1)}, bf16[1,128,1536]{2,1,0:T(8,128)(2,1)}, u32[]{:S(2)}) copy-start(bf16[1,128,1536]{2,1,0:T(8,128)(2,1)} %param.12) | copy-start | bytes 1179652
  19.4 113.4 %copy-start.24 = (bf16[128,96]{1,0:T(8,128)(2,1)}, bf16[128,96]{1,0:T(8,128)(2,1)S(1)}, u32[]{:S(2)}) copy-start(bf16[128,96]{1,0:T(8,128)(2,1)S(1)} %broadcast.198) | copy-start | bytes 73732
  127.7 0.6 copy-start.29
  133.8 62.9 %collective-permute-start.2 = (bf16[2,384,1536]{2,1,0:T(8,128)(2,1)}, bf16[2,384,1536]{2,1,0:T(8,128)(2,1)}, u32[]{:S(2)}, u32[]{:S(2)}) collective-permute-start(bf16[2,384,1536]{2,1,0:T(8,128)(2,1)} %get-tuple-element.35), channel_id=1, source_target_pairs={{0,1},{1,0},{2,3},{3,2},{4,5},{5,4},{6,7},{7,6},{8,9},{9,8},{10,11... | collective-permute-start | bytes 7077896 | tf_op jit(solution)/shard_map/ppermute | solution.py:1324
  134.3 104.4 %collective-permute-start.4 = (bf16[2,384,1536]{2,1,0:T(8,128)(2,1)}, bf16[2,384,1536]{2,1,0:T(8,128)(2,1)}, u32[]{:S(2)}, u32[]{:S(2)}) collective-permute-start(bf16[2,384,1536]{2,1,0:T(8,128)(2,1)} %get-tuple-element.35), channel_id=1, source_target_pairs={{0,3},{1,2},{2,1},{3,0},{4,7},{5,6},{6,5},{7,4},{8,11},{9,10},{10,... | collective-permute-start | bytes 7077896 | tf_op jit(solution)/shard_map/ppermute | solution.py:1324
  171.0 8.1 %copy-start.5 = (bf16[1024,512]{0,1:T(8,128)(2,1)}, bf16[1024,512]{0,1:T(8,128)(2,1)S(1)}, u32[]{:S(2)}) copy-start(bf16[1024,512]{0,1:T(8,128)(2,1)S(1)} %copy.95) | copy-start | bytes 3145732
  174.3 4.8 copy-start.10
  175.6 63.1 %collective-permute-start.3 = (bf16[2,384,1536]{2,1,0:T(8,128)(2,1)}, bf16[2,384,1536]{2,1,0:T(8,128)(2,1)}, u32[]{:S(2)}, u32[]{:S(2)}) collective-permute-start(bf16[2,384,1536]{2,1,0:T(8,128)(2,1)} %get-tuple-element.34.refs_2_), channel_id=1, source_target_pairs={{0,2},{1,3},{2,0},{3,1},{4,6},{5,7},{6,4},{7,5},{8,10},{9,11},{10,... | collective-permute-start | bytes 7077896 | tf_op jit(solution)/shard_map/ppermute | solution.py:1324
  176.1 3.0 copy-start.16
  179.1 4.6 copy-start
  179.1 4.5 copy-start.18
  187.1 8.9 %copy-start.14 = (bf16[128,8,3,64]{0,3,2,1:T(8,128)(2,1)}, bf16[128,8,3,64]{0,3,2,1:T(8,128)(2,1)S(1)}, u32[]{:S(2)}) copy-start(bf16[128,8,3,64]{0,3,2,1:T(8,128)(2,1)S(1)} %fusion.37) | copy-start | bytes 1179652
  187.1 5.1 copy-start.34
  187.1 7.3 %copy-start.36 = (s32[1,128,8]{1,2,0:T(8,128)S(1)}, s32[1,128,8]{1,2,0:T(8,128)}, u32[]{:S(2)}) copy-start(s32[1,128,8]{1,2,0:T(8,128)} %param.13) | copy-start | bytes 12292
  187.2 8.0 %copy-start.25 = (bf16[128,96]{1,0:T(8,128)(2,1)S(1)}, bf16[128,96]{1,0:T(8,128)(2,1)}, u32[]{:S(2)}) copy-start(bf16[128,96]{1,0:T(8,128)(2,1)} %copy-done.24) | copy-start | bytes 73732
  191.3 0.9 copy-start.1
  191.4 1.8 copy-start.40
  194.4 2.2 copy-start.33
  194.5 0.6 copy-start.42
  194.5 0.5 copy-start.43
  361.0 1.9 copy-start.26
  362.9 7.0 %copy-start.15 = (bf16[128,8,3,64]{0,3,2,1:T(8,128)(2,1)S(1)}, bf16[128,8,3,64]{0,3,2,1:T(8,128)(2,1)}, u32[]{:S(2)}) copy-start(bf16[128,8,3,64]{0,3,2,1:T(8,128)(2,1)} %copy-done.14) | copy-start | bytes 1179652
  365.5 12.0 %copy-start.13 = (bf16[128,1536]{1,0:T(8,128)(2,1)}, bf16[128,1536]{1,0:T(8,128)(2,1)S(1)}, u32[]{:S(2)}) copy-start(bf16[128,1536]{1,0:T(8,128)(2,1)S(1)} %get-tuple-element.97.refs_3_) | copy-start | bytes 1179652
  365.5 4.6 copy-start.17
  365.5 4.6 copy-start.19
  365.5 4.6 copy-start.37
  370.1 7.4 %copy-start.6 = (bf16[1024,512]{0,1:T(8,128)(2,1)S(1)}, bf16[1024,512]{0,1:T(8,128)(2,1)}, u32[]{:S(2)}) copy-start(bf16[1024,512]{0,1:T(8,128)(2,1)} %copy-done.5) | copy-start | bytes 3145732
  370.1 11.6 %slice-start = ((s8[12582912]{0:T(1024)(128)(4,1)}), s8[4194304]{0:T(1024)(128)(4,1)S(1)}, s32[]{:S(2)}) async-start(s8[12582912]{0:T(1024)(128)(4,1)} %bitcast.161), calls=%async_computation | async-start | bytes 8388608
  370.1 11.6 %slice-start.1 = ((s8[12582912]{0:T(1024)(128)(4,1)}), s8[4194304]{0:T(1024)(128)(4,1)S(1)}, s32[]{:S(2)}) async-start(s8[12582912]{0:T(1024)(128)(4,1)} %bitcast.161), calls=%async_computation.1 | async-start | bytes 8388608
  377.6 2.1 copy-start.11
  377.6 2.1 copy-start.12
  377.6 4.2 slice-start.2
  388.4 45.3 %copy-start.22 = (f32[128,32]{0,1:T(8,128)S(1)}, f32[128,32]{0,1:T(8,128)}, u32[]{:S(2)}) copy-start(f32[128,32]{0,1:T(8,128)} %copy-done.21) | copy-start | bytes 49156
  388.4 45.3 %copy-start.31 = (f32[128,32]{0,1:T(8,128)S(1)}, f32[128,32]{0,1:T(8,128)}, u32[]{:S(2)}) copy-start(f32[128,32]{0,1:T(8,128)} %get-tuple-element.115) | copy-start | bytes 49156
  389.8 46.3 %copy-start.4 = (bf16[1,128,1536]{2,1,0:T(8,128)(2,1)S(1)}, bf16[1,128,1536]{2,1,0:T(8,128)(2,1)}, u32[]{:S(2)}) copy-start(bf16[1,128,1536]{2,1,0:T(8,128)(2,1)} %param.12) | copy-start | bytes 1179652
  389.8 46.3 %copy-start.30 = (f32[1536]{0:T(1024)S(1)}, f32[1536]{0:T(1024)}, u32[]{:S(2)}) copy-start(f32[1536]{0:T(1024)} %copy-done.29) | copy-start | bytes 18436
  389.8 46.3 %copy-start.39 = (f32[128]{0:T(128)S(1)}, f32[128]{0:T(128)}, u32[]{:S(2)}) copy-start(f32[128]{0:T(128)} %copy-done.38) | copy-start | bytes 1540
  436.1 6.3 copy-start.20
  436.1 8.2 %copy-start.27 = (bf16[128,32]{1,0:T(8,128)(2,1)S(1)}, bf16[128,32]{1,0:T(8,128)(2,1)}, u32[]{:S(2)}) copy-start(bf16[128,32]{1,0:T(8,128)(2,1)} %copy-done.26) | copy-start | bytes 24580
  436.1 10.1 %copy-start.44 = (bf16[128]{0:T(256)(128)(2,1)S(1)}, bf16[128]{0:T(256)(128)(2,1)}, u32[]{:S(2)}) copy-start(bf16[128]{0:T(256)(128)(2,1)} %compare_convert_fusion.1) | copy-start | bytes 772
  436.2 10.1 %copy-start.45 = (bf16[128]{0:T(256)(128)(2,1)S(1)}, bf16[128]{0:T(256)(128)(2,1)}, u32[]{:S(2)}) copy-start(bf16[128]{0:T(256)(128)(2,1)} %compare_convert_fusion) | copy-start | bytes 772
  436.2 10.2 %copy-start.8 = (bf16[640,1536]{1,0:T(8,128)(2,1)S(1)}, bf16[640,1536]{1,0:T(8,128)(2,1)}, u32[]{:S(2)}) copy-start(bf16[640,1536]{1,0:T(8,128)(2,1)} %get-tuple-element.95) | copy-start | bytes 5898244
  436.2 10.5 %copy-start.2 = (f32[128,1536]{1,0:T(8,128)S(1)}, f32[128,1536]{1,0:T(8,128)}, u32[]{:S(2)}) copy-start(f32[128,1536]{1,0:T(8,128)} %copy-done.1) | copy-start | bytes 2359300
  436.2 10.5 %copy-start.41 = (f32[128]{0:T(128)S(1)}, f32[128]{0:T(128)}, u32[]{:S(2)}) copy-start(f32[128]{0:T(128)} %copy-done.40) | copy-start | bytes 1540
  442.4 4.7 copy-start.7
  444.3 208.1 %collective-permute-start.5 = (bf16[2,384,1536]{2,1,0:T(8,128)(2,1)}, bf16[2,384,1536]{2,1,0:T(8,128)(2,1)}, u32[]{:S(2)}, u32[]{:S(2)}) collective-permute-start(bf16[2,384,1536]{2,1,0:T(8,128)(2,1)} %get-tuple-element.42), channel_id=1, source_target_pairs={{0,1},{1,0},{2,3},{3,2},{4,5},{5,4},{6,7},{7,6},{8,9},{9,8},{10,11... | collective-permute-start | bytes 7077896 | tf_op jit(solution)/shard_map/ppermute | solution.py:1324
  444.4 208.0 %collective-permute-start.6 = (bf16[2,384,1536]{2,1,0:T(8,128)(2,1)}, bf16[2,384,1536]{2,1,0:T(8,128)(2,1)}, u32[]{:S(2)}, u32[]{:S(2)}) collective-permute-start(bf16[2,384,1536]{2,1,0:T(8,128)(2,1)} %get-tuple-element.43), channel_id=1, source_target_pairs={{0,2},{1,3},{2,0},{3,1},{4,6},{5,7},{6,4},{7,5},{8,10},{9,11},{10,... | collective-permute-start | bytes 7077896 | tf_op jit(solution)/shard_map/ppermute | solution.py:1324
  446.1 206.3 %collective-permute-start.7 = (bf16[2,384,1536]{2,1,0:T(8,128)(2,1)}, bf16[2,384,1536]{2,1,0:T(8,128)(2,1)}, u32[]{:S(2)}, u32[]{:S(2)}) collective-permute-start(bf16[2,384,1536]{2,1,0:T(8,128)(2,1)} %get-tuple-element.44), channel_id=1, source_target_pairs={{0,3},{1,2},{2,1},{3,0},{4,7},{5,6},{6,5},{7,4},{8,11},{9,10},{10,... | collective-permute-start | bytes 7077896 | tf_op jit(solution)/shard_map/ppermute | solution.py:1324
  446.3 2.3 copy-start.28
  447.1 1.7 copy-start.9
  648.5 11.5 %copy-start.23 = (bf16[128,1536]{1,0:T(8,128)(2,1)S(1)}, bf16[128,1536]{1,0:T(8,128)(2,1)}, u32[]{:S(2)}) copy-start(bf16[128,1536]{1,0:T(8,128)(2,1)} %get-tuple-element.38) | copy-start | bytes 1179652

commit v6 on v5

--- a/solution.py
+++ b/solution.py
@@ -196,164 +196,6 @@
     acc[...] = (acc[...].astype(jnp.float32) + other[...].astype(jnp.float32)).astype(acc.dtype)
 
 
-def reduce_kernel(plans, n_in, *refs):
-    ins, outs = refs[:n_in], refs[n_in : 2 * n_in]
-    rest = list(refs[2 * n_in :])
-    send_sem, recv_sem, own_sem = rest[:3]
-    buffers = rest[3:]
-    place = Place()
-    z = place.at[Z]
-    greet(place, sorted({d for p in plans for d in p.order} | {Z}))
-    pending = []
-    slots = [0, 0]
-
-    def push(source, target, sem, dest):
-        copy = pltpu.make_async_remote_copy(
-            src_ref=source, dst_ref=target, send_sem=send_sem.at[slots[0]], recv_sem=sem,
-            device_id=dest, device_id_type=DEV,
-        )
-        slots[0] += 1
-        copy.start()
-        pending.append(copy)
-
-    def arrived(target, sem):
-        pltpu.make_async_remote_copy(
-            src_ref=target, dst_ref=target, send_sem=own_sem.at[0], recv_sem=sem,
-            device_id=place.across(C), device_id_type=DEV,
-        ).wait_recv()
-
-    work = []
-    far = list(reversed(range(NZ)))
-    own_slot = 1
-    state = []
-    base = 0
-    for n, plan in enumerate(plans):
-        dims = plan.order
-        acc = buffers[0]
-        levels = buffers[1 : 1 + len(dims)]
-        chain = buffers[1 + len(dims)]
-        buffers = buffers[2 + len(dims) :]
-        kept = [subsets(dims[p + 1 :]) for p in range(len(dims))]
-        counts = [NZ * len(f) for f in kept]
-        level_base = [base + sum(counts[:p]) for p in range(len(dims))]
-        chain_base = base + sum(counts)
-        base = chain_base + 2 * NZ
-        state.append((acc, levels, chain, kept, level_base, chain_base))
-        own_copies = {}
-        src = ins[plan.ref]
-        for k in far:
-            for f in kept[0]:
-                gone = flat_index(place.coords(place.order[k], (dims[0],) + f), plan.index)
-                spot = place.order[k] * len(kept[0]) + kept[0].index(f)
-                work.append((0, n, k, f, gone, spot))
-                mine = flat_index(place.coords(place.order[k], f), plan.index)
-                copy = pltpu.make_async_copy(src.at[mine], acc.at[spot], own_sem.at[own_slot])
-                own_slot += 1
-                own_copies[(k, f)] = copy
-        state[-1] += (own_copies,)
-    for _, n, k, f, gone, spot in sorted(work, key=lambda w: (-w[2],)):
-        plan = plans[n]
-        acc, levels, chain, kept, level_base, chain_base, own_copies = state[n]
-        push(ins[plan.ref].at[gone], levels[0].at[spot], recv_sem.at[level_base[0] + spot], place.across(plan.order[0]))
-        own_copies[(k, f)].start()
-
-    def level_step(n, p, k):
-        plan = plans[n]
-        dims = plan.order
-        acc, levels, _, kept, level_base, _, own_copies = state[n]
-        for f in sorted(kept[p], key=lambda f: -len(f)):
-            spot = place.order[k] * len(kept[p]) + kept[p].index(f)
-            at = place.order[k] * len(kept[0]) + kept[0].index(f)
-            if p == 0:
-                own_copies[(k, f)].wait()
-            arrived(levels[p].at[spot], recv_sem.at[level_base[p] + spot])
-            add_into(acc.at[at], levels[p].at[spot])
-            later = p + 1
-            if later < len(dims) and dims[later] in f:
-                left = tuple(d for d in f if d != dims[later])
-                there = place.order[k] * len(kept[later]) + kept[later].index(left)
-                push(
-                    acc.at[at], levels[later].at[there],
-                    recv_sem.at[level_base[later] + there], place.across(dims[later]),
-                )
-
-    def chain_step(n, k):
-        acc, _, chain, kept, _, chain_base, _ = state[n]
-        dest = place.order[k]
-        up = dest > z
-        lane = jnp.where(up, 0, 1)
-        at = dest * len(kept[0])
-        spot = lane * NZ + dest
-
-        @pl.when(jnp.where(up, z > 0, z < NZ - 1))
-        def _():
-            arrived(chain.at[spot], recv_sem.at[chain_base + spot])
-            add_into(acc.at[at], chain.at[spot])
-
-        push(acc.at[at], chain.at[spot], recv_sem.at[chain_base + spot], place.along(jnp.where(up, 1, -1)))
-
-    most = max(len(p.order) for p in plans)
-    for step in range(NZ + most):
-        for n, plan in enumerate(plans):
-            for p in range(len(plan.order)):
-                if 0 <= step - p < NZ:
-                    level_step(n, p, far[step - p])
-            p = len(plan.order)
-            if 0 <= step - p < NZ - 1:
-                chain_step(n, far[step - p])
-    for n, plan in enumerate(plans):
-        acc, levels, chain, kept, level_base, chain_base, own_copies = state[n]
-        at = z * len(kept[0])
-
-        @pl.when(z > 0)
-        def _():
-            spot = z
-            arrived(chain.at[spot], recv_sem.at[chain_base + spot])
-            add_into(acc.at[at], chain.at[spot])
-
-        @pl.when(z < NZ - 1)
-        def _():
-            spot = NZ + z
-            arrived(chain.at[spot], recv_sem.at[chain_base + spot])
-            add_into(acc.at[at], chain.at[spot])
-
-        outs[plan.ref][...] = acc[at].astype(outs[plan.ref].dtype)
-    for copy in pending:
-        copy.wait_send()
-
-
-def reduce_scatter(arrays, plans, out_dtypes, collective_id):
-    n = len(arrays)
-    scratch = []
-    sends = recvs = owns = 0
-    for p in plans:
-        a = arrays[p.ref]
-        block = a.shape[1:]
-        kept = [len(subsets(p.order[q + 1 :])) for q in range(len(p.order))]
-        scratch.append(pltpu.VMEM((NZ * kept[0],) + block, a.dtype))
-        for q in kept:
-            scratch.append(pltpu.VMEM((NZ * q,) + block, a.dtype))
-        scratch.append(pltpu.VMEM((2 * NZ,) + block, a.dtype))
-        sends += NZ * sum(kept) + NZ - 1
-        recvs += NZ * sum(kept) + 2 * NZ
-        owns += NZ * kept[0]
-    return pl.pallas_call(
-        functools.partial(reduce_kernel, plans, n),
-        out_shape=[jax.ShapeDtypeStruct(a.shape[1:], d) for a, d in zip(arrays, out_dtypes)],
-        in_specs=[pl.BlockSpec(memory_space=pl.ANY)] * n,
-        out_specs=[pl.BlockSpec(memory_space=pltpu.VMEM)] * n,
-        scratch_shapes=[
-            pltpu.SemaphoreType.DMA((sends,)),
-            pltpu.SemaphoreType.DMA((recvs,)),
-            pltpu.SemaphoreType.DMA((1 + owns,)),
-        ]
-        + scratch,
-        compiler_params=pltpu.CompilerParams(
-            collective_id=collective_id, has_side_effects=True, vmem_limit_bytes=60 * 1024 * 1024
-        ),
-    )(*arrays)
-
-
 class Gather:
     def __init__(self, place, plan, src, out, send_sem, recv_sem, spare_sem, slot, base):
         self.place, self.plan, self.src, self.out = place, plan, src, out
@@ -365,18 +207,24 @@
     def sends(plan):
         return sum(len(gather_sends(plan.order, k, f)) for k, f in gather_events(plan.order))
 
+    def goes(self, way, k):
+        z, z_from = self.place.at[Z], self.place.order[k]
+        if way == UP:
+            return z < NZ - 1 if k == 0 else jnp.logical_and(z < NZ - 1, z_from < z)
+        return z > 0 if k == 0 else jnp.logical_and(z > 0, z_from > z)
+
+    def part(self, ref):
+        rows = self.plan.rows
+        return ref if rows is None else ref.at[pl.ds(rows[0], rows[1])]
+
     def step(self, k, flips):
         place, plan = self.place, self.plan
-        z = place.at[Z]
-        z_from = place.order[k]
-        index = flat_index(place.coords(z_from, flips), plan.index)
-        rows = plan.rows
-        target = self.out.at[index] if rows is None else self.out.at[index, pl.ds(rows[0], rows[1])]
+        index = flat_index(place.coords(place.order[k], flips), plan.index)
+        target = self.part(self.out.at[index])
         sem = self.recv_sem.at[self.base + index]
-        own = k == 0 and not flips
         source = target
-        if own:
-            source = self.src if rows is None else self.src.at[pl.ds(rows[0], rows[1])]
+        if k == 0 and not flips:
+            source = self.part(self.src)
         else:
             pltpu.make_async_remote_copy(
                 src_ref=target, dst_ref=target, send_sem=self.spare_sem, recv_sem=sem,
@@ -384,30 +232,31 @@
             ).wait_recv()
         for way in gather_sends(plan.order, k, flips):
             if way in (UP, DOWN):
-                step = 1 if way == UP else -1
-                go = z < NZ - 1 if way == UP else z > 0
-                if k > 0:
-                    go = jnp.logical_and(go, z_from < z if way == UP else z_from > z)
-                dest = place.device(Z, jnp.clip(z + step, 0, NZ - 1))
+                dest = place.device(Z, jnp.clip(place.at[Z] + (1 if way == UP else -1), 0, NZ - 1))
             else:
-                go, dest = None, place.across(way)
+                dest = place.across(way)
             copy = pltpu.make_async_remote_copy(
                 src_ref=source, dst_ref=target, send_sem=self.send_sem.at[self.slot], recv_sem=sem,
                 device_id=dest, device_id_type=DEV,
             )
+            if way in (UP, DOWN):
+                pl.when(self.goes(way, k))(copy.start)
+            else:
+                copy.start()
+            self.pending.append((way, k, self.slot))
             self.slot += 1
-            if go is None:
-                copy.start()
+
+    def finish(self):
+        for way, k, slot in self.pending:
+            block = self.part(self.src)
+            copy = pltpu.make_async_remote_copy(
+                src_ref=block, dst_ref=block, send_sem=self.send_sem.at[slot], recv_sem=self.spare_sem,
+                device_id=self.place.across(C), device_id_type=DEV,
+            )
+            if way in (UP, DOWN):
+                pl.when(self.goes(way, k))(copy.wait_send)
             else:
-                pl.when(go)(copy.start)
-            self.pending.append((go, copy.wait_send))
-
-    def finish(self):
-        for go, wait in self.pending:
-            if go is None:
-                wait()
-            else:
-                pl.when(go)(wait)
+                copy.wait_send()
 
 
 class Reduce:
@@ -418,7 +267,6 @@
         self.kept = [subsets(dims[p + 1 :]) for p in range(len(dims))]
         self.base = [NZ * sum(len(f) for f in self.kept[:p]) for p in range(len(dims) + 1)]
         self.slot = 0
-        self.pending = []
 
     @staticmethod
     def counts(plan):
@@ -432,7 +280,6 @@
         )
         self.slot += 1
         copy.start()
-        self.pending.append(copy)
 
     def arrived(self, target, sem):
         pltpu.make_async_remote_copy(
@@ -511,8 +358,12 @@
         return [step for t in range(NZ + len(self.plan.order)) for step in self.at_time(t)]
 
     def finish(self):
-        for copy in self.pending:
-            copy.wait_send()
+        block = self.levels[0].at[0]
+        for slot in range(self.slot):
+            pltpu.make_async_remote_copy(
+                src_ref=block, dst_ref=block, send_sem=self.send_sem.at[slot], recv_sem=self.spare_sem,
+                device_id=self.place.across(C), device_id_type=DEV,
+            ).wait_send()
 
 
 def tile_up(n, m):
@@ -793,25 +644,17 @@
 
 
 def weights_kernel(plans, *refs):
-    left_one, right_one, left_two, right_two, left_small, right_small, part, mixed = refs[:8]
-    outs = refs[8:11]
-    held_one, held_two, held_out = refs[11:14]
-    buffers = refs[14:25]
-    send_one, recv_one, send_two, recv_two, send_out, recv_out, spare, load_sem = refs[25:]
+    left_one, right_one, left_two, right_two, left_small, right_small = refs[:6]
+    outs = refs[6:8]
+    held_one, held_two = refs[8:10]
+    buffers = refs[10:18]
+    send_one, recv_one, send_two, recv_two, spare = refs[18:]
     place = Place()
-    loads = []
     far = list(reversed(range(NZ)))
-    for k in far:
-        for h in (1 - place.at[C], place.at[C]):
-            at = pl.ds((h * NZ + place.order[k]) * NY, NY)
-            loads.append(pltpu.make_async_copy(part.at[at], held_out.at[at], load_sem.at[len(loads)]))
-    for copy in loads:
-        copy.start()
     greet(place, (Z, Y, X, C))
     ways = [
         Reduce(place, plans[0], held_one, buffers[0:3], buffers[3], send_one, recv_one, spare),
         Reduce(place, plans[1], held_two, buffers[4:7], buffers[7], send_two, recv_two, spare),
-        Reduce(place, plans[2], held_out, buffers[8:10], buffers[10], send_out, recv_out, spare),
     ]
     group = NY * NX * NC
     rows = group * held_one.shape[1]
@@ -834,9 +677,6 @@
         products(left_two, right_two, held_two, k, 0)
         products(left_small, right_small, held_two, k, right_two.shape[1])
         ways[1].first(k)
-        for copy in loads[2 * t : 2 * t + 2]:
-            copy.wait()
-        ways[2].first(k)
         if t > 0:
             for way in ways:
                 for step in way.at_time(t - 1):
@@ -846,70 +686,357 @@
             for step in way.at_time(t):
                 step()
     for way, out in zip(ways, outs):
-        way.last(out, mixed if way is ways[2] else None)
+        way.last(out)
     for way in ways:
         way.finish()
 
 
-def return_weights(lefts, rights, part, mixed, collective_id):
+def return_weights(lefts, rights, collective_id):
     width = lefts[0].shape[1]
     rows = width // (NZ * NY * NX * NC)
     widths = [rights[0].shape[1], rights[1].shape[1] + rights[2].shape[1]]
-    plans = [
-        Plan(0, (C, X, Y), (Z, Y, X, C)),
-        Plan(1, (C, X, Y), (Z, Y, X, C)),
-        Plan(2, (C, Y), (C, Z, Y)),
-    ]
+    plans = [Plan(0, (C, Y, X), (Z, Y, X, C)), Plan(1, (C, X, Y), (Z, Y, X, C))]
     bf = jnp.bfloat16
     levels, sends, recvs = Reduce.counts(plans[0])
-    out_levels, out_sends, out_recvs = Reduce.counts(plans[2])
     dma = pltpu.SemaphoreType.DMA
-    operands = [a for pair in zip(lefts, rights) for a in pair] + [part, mixed]
     vmem = pl.BlockSpec(memory_space=pltpu.VMEM)
     return pl.pallas_call(
         functools.partial(weights_kernel, plans),
-        out_shape=[jax.ShapeDtypeStruct((rows, w), jnp.float32) for w in widths]
-        + [jax.ShapeDtypeStruct(mixed.shape, bf)],
-        in_specs=[vmem] * 6 + [pl.BlockSpec(memory_space=pl.ANY), vmem],
+        out_shape=[jax.ShapeDtypeStruct((rows, w), jnp.float32) for w in widths],
+        in_specs=[vmem] * 6,
+        out_specs=[vmem] * 2,
+        scratch_shapes=[pltpu.VMEM((plans[0].blocks, rows, w), bf) for w in widths]
+        + [pltpu.VMEM((n, rows, w), bf) for w in widths for n in levels + [NZ + 1]]
+        + [dma((n,)) for n in (sends, recvs, sends, recvs)]
+        + [dma(())],
+        compiler_params=pltpu.CompilerParams(
+            collective_id=collective_id, has_side_effects=True, vmem_limit_bytes=60 * 1024 * 1024
+        ),
+        name="return_weights",
+    )(*[a for pair in zip(lefts, rights) for a in pair])
+
+
+def place_heads(source, target):
+    count = source.shape[0]
+    group = QUERY_HEADS // KEY_VALUE_HEADS
+    lane = lax.broadcasted_iota(jnp.int32, (1, 2 * HEAD_SIZE), 1)
+    for h in range(QUERY_HEADS):
+        m, g = h // group, h % group
+        block = source[:, h // 2 * 128 : h // 2 * 128 + 128].astype(jnp.float32)
+        if h % 2 != m % 2:
+            block = pltpu.roll(block, HEAD_SIZE, 1)
+        block = jnp.where(lane // HEAD_SIZE == m % 2, block, 0.0)
+        target[m, g * count : (g + 1) * count] = block.astype(target.dtype)
+
+
+def collect_heads(source, target):
+    count = target.shape[0]
+    group = QUERY_HEADS // KEY_VALUE_HEADS
+    lane = lax.broadcasted_iota(jnp.int32, (1, 2 * HEAD_SIZE), 1)
+    for pair in range(QUERY_HEADS // 2):
+        sides = []
+        for h in (2 * pair, 2 * pair + 1):
+            m, g = h // group, h % group
+            block = source[m, g * count : (g + 1) * count]
+            sides.append(block if h % 2 == m % 2 else pltpu.roll(block, HEAD_SIZE, 1))
+        target[:, pair * 128 : pair * 128 + 128] = jnp.where(lane < HEAD_SIZE, *sides).astype(target.dtype)
+
+
+class Scores:
+    def __init__(self, place, queries, keys):
+        self.queries, self.keys = queries, keys
+        group = QUERY_HEADS // KEY_VALUE_HEADS
+        count = keys.shape[1]
+        self.total = keys.shape[0] * count
+        row = lax.broadcasted_iota(jnp.int32, (group * count, 1), 0) % count
+        self.position = row + (place.at[Z] * NY + place.at[Y]) * count
+        self.column = lax.broadcasted_iota(jnp.int32, (1, self.total), 1)
+
+    def pair(self, m, shift):
+        at = pl.ds(pl.multiple_of(shift + m // 2 * 128, 128), 128)
+        return self.keys[:, :, at].reshape(self.total, 128)
+
+    def of(self, m, keys):
+        found = lax.dot_general(
+            self.queries[m], keys, (((1,), (1,)), ((), ())), preferred_element_type=jnp.float32
+        )
+        return jnp.where(self.column <= self.position, found * attn_scale, masked_logits)
+
+
+def attend_kernel(plans, own_kv, queries, own_cots, out, log_sums, kv_out, cots, seen, placed, raw, *sems):
+    send_kv, recv_kv, send_cot, recv_cot, spare, own_sem = sems
+    place = Place()
+    bf, f32 = jnp.bfloat16, jnp.float32
+    greet(place, (Z, Y, C))
+    kv_way = Gather(place, plans[0], own_kv, seen, send_kv, recv_kv, spare, 0, 0)
+    cot_ways, at = [], 0
+    for n, plan in enumerate(plans[1:]):
+        cot_ways.append(Gather(place, plan, own_cots, cots, send_cot, recv_cot, spare, at, n * plan.blocks))
+        at += Gather.sends(plan)
+    kv_way.step(0, ())
+    for way in cot_ways:
+        way.step(0, ())
+    mine = pltpu.make_async_copy(own_cots, cots.at[flat_index(place.at, plans[1].index)], own_sem.at[0])
+    mine.start()
+    seen[flat_index(place.at, plans[0].index)] = own_kv[...]
+    place_heads(queries, placed)
+    log_sums[...] = jnp.zeros(log_sums.shape, f32)
+    early = [e for e in gather_events(plans[1].order)[1:]]
+    kv_events = gather_events(plans[0].order)[1:]
+    for k, flips in kv_events:
+        kv_way.step(k, flips)
+        if len(early) > 8:
+            event = early.pop(0)
+            for way in cot_ways:
+                way.step(*event)
+    keep = pltpu.make_async_copy(seen, kv_out, own_sem.at[1])
+    keep.start()
+    scores = Scores(place, placed, seen)
+    lane = lax.broadcasted_iota(jnp.int32, (1, 128), 1)
+    width = KEY_VALUE_HEADS * HEAD_SIZE
+
+    def head(m, carry):
+        for i in range(KEY_VALUE_HEADS):
+            if early:
+                event = early.pop(0)
+
+                @pl.when(m == i)
+                def _():
+                    for way in cot_ways:
+                        way.step(*event)
+
+        s = scores.of(m, scores.pair(m, 0))
+        best = jnp.max(s, axis=1, keepdims=True)
+        weights = jnp.exp(s - best)
+        total = jnp.sum(weights, axis=1, keepdims=True)
+        mixed = jnp.dot(weights.astype(bf), scores.pair(m, width), preferred_element_type=f32)
+        raw[m] = mixed / total
+        log_sums[...] = jnp.where(lane == m, best + jnp.log(total), log_sums[...])
+        return carry
+
+    lax.fori_loop(0, KEY_VALUE_HEADS, head, 0)
+    collect_heads(raw, out)
+    keep.wait()
+    mine.wait()
+    kv_way.finish()
+    for way in cot_ways:
+        way.finish()
+
+
+def attend(own_kv, queries, own_cots, collective_id):
+    count, kv_width = own_kv.shape
+    cut = count * 3 // 4
+    plans = [
+        Plan(0, (Z, Y), (Z, Y)),
+        Plan(1, (Z, Y, C), (C, Z, Y), rows=(0, cut)),
+        Plan(1, (Y, Z, C), (C, Z, Y), rows=(cut, count - cut)),
+    ]
+    bf, f32 = jnp.bfloat16, jnp.float32
+    group = QUERY_HEADS // KEY_VALUE_HEADS
+    vmem = pl.BlockSpec(memory_space=pltpu.VMEM)
+    apart = pl.BlockSpec(memory_space=pl.ANY)
+    dma = pltpu.SemaphoreType.DMA
+    kv_shape = (plans[0].blocks, count, kv_width)
+    heads = (KEY_VALUE_HEADS, group * count, 2 * HEAD_SIZE)
+    return pl.pallas_call(
+        functools.partial(attend_kernel, plans),
+        out_shape=[
+            jax.ShapeDtypeStruct(queries.shape, bf),
+            jax.ShapeDtypeStruct((group * count, 128), f32),
+            jax.ShapeDtypeStruct(kv_shape, bf),
+            jax.ShapeDtypeStruct((plans[1].blocks,) + own_cots.shape, bf),
+        ],
+        in_specs=[vmem] * 3,
+        out_specs=[vmem, vmem, apart, apart],
+        scratch_shapes=[pltpu.VMEM(kv_shape, bf), pltpu.VMEM(heads, bf), pltpu.VMEM(heads, f32)]
+        + [
+            dma((Gather.sends(plans[0]),)),
+            dma((plans[0].blocks,)),
+            dma((Gather.sends(plans[1]) + Gather.sends(plans[2]),)),
+            dma((plans[1].blocks + plans[2].blocks,)),
+            dma(()),
+            dma((2,)),
+        ],
+        compiler_params=pltpu.CompilerParams(
+            collective_id=collective_id, has_side_effects=True, vmem_limit_bytes=56 * 1024 * 1024
+        ),
+        name="attend",
+    )(own_kv, queries, own_cots)
+
+
+def attend_back_kernel(plans, *refs):
+    queries, grads, outputs, log_sums, keys, part, mixed = refs[:7]
+    query_grad, kv_grad, layer_out = refs[7:10]
+    placed, grads_placed, raw, deltas, held, held_out = refs[10:16]
+    level, chain, out_level, out_level_two, out_chain = refs[16:21]
+    send_kv, recv_kv, send_out, recv_out, spare, load_sem = refs[21:]
+    place = Place()
+    bf, f32 = jnp.bfloat16, jnp.float32
+    far = list(reversed(range(NZ)))
+    loads = []
+    for k in far:
+        for h in (1 - place.at[C], place.at[C]):
+            at = pl.ds((h * NZ + place.order[k]) * NY, NY)
+            loads.append(pltpu.make_async_copy(part.at[at], held_out.at[at], load_sem.at[len(loads)]))
+    for copy in loads:
+        copy.start()
+    greet(place, (Z, Y, C))
+    kv_way = Reduce(place, plans[0], held, (level,), chain, send_kv, recv_kv, spare)
+    out_way = Reduce(place, plans[1], held_out, (out_level, out_level_two), out_chain, send_out, recv_out, spare)
+    for copy in loads:
+        copy.wait()
+    for k in far:
+        out_way.first(k)
+    place_heads(queries, placed)
+    place_heads(grads, grads_placed)
+    count = queries.shape[0]
+    group = QUERY_HEADS // KEY_VALUE_HEADS
+    lane = lax.broadcasted_iota(jnp.int32, (1, 128), 1)
+    for g in range(group):
+        found = jnp.zeros((count, 128), f32)
+        for m in range(KEY_VALUE_HEADS):
+            h = m * group + g
+            at = slice(h // 2 * 128, h // 2 * 128 + 128)
+            both = grads[:, at].astype(f32) * outputs[:, at].astype(f32)
+            delta = jnp.sum(jnp.where(lane // HEAD_SIZE == h % 2, both, 0.0), axis=1, keepdims=True)
+            found = jnp.where(lane == m, delta, found)
+        deltas[g * count : (g + 1) * count] = found
+    scores = Scores(place, placed, keys)
+    width = KEY_VALUE_HEADS * HEAD_SIZE
+    blocks = keys.shape[0]
+    steps = out_way.steps()
+    turns = KEY_VALUE_HEADS // 2
+
+    def pair(p, carry):
+        for i in range(turns):
+            now = [steps.pop(0) for _ in range(min(len(steps), 2))]
+
+            @pl.when(p == i)
+            def _():
+                for step in now:
+                    step()
+
+        key_sum = value_sum = None
+        for side in range(2):
+            m = 2 * p + side
+            k_pair, v_pair = scores.pair(m, 0), scores.pair(m, width)
+            of_head = lambda ref: jnp.sum(jnp.where(lane == m, ref[...], 0.0), axis=1, keepdims=True)
+            weights = jnp.exp(scores.of(m, k_pair) - of_head(log_sums))
+            grad = grads_placed[m]
+            grad_probs = lax.dot_general(grad, v_pair, (((1,), (1,)), ((), ())), preferred_element_type=f32)
+            grad_scores = (weights * (grad_probs - of_head(deltas))).astype(bf)
+            raw[m] = attn_scale * jnp.dot(grad_scores, k_pair, preferred_element_type=f32)
+            over_rows = (((0,), (0,)), ((), ()))
+            key_part = lax.dot_general(grad_scores, placed[m], over_rows, preferred_element_type=f32)
+            value_part = lax.dot_general(weights.astype(bf), grad, over_rows, preferred_element_type=f32)
+            key_sum = key_part if key_sum is None else key_sum + key_part
+            value_sum = value_part if value_sum is None else value_sum + value_part
+        at = pl.multiple_of(p * 128, 128)
+        held[:, :, pl.ds(at, 128)] = (attn_scale * key_sum).astype(bf).reshape(blocks, count, 128)
+        at = pl.multiple_of(width + p * 128, 128)
+        held[:, :, pl.ds(at, 128)] = value_sum.astype(bf).reshape(blocks, count, 128)
+        return carry
+
+    lax.fori_loop(0, turns, pair, 0)
+    for k in far:
+        kv_way.first(k)
+    collect_heads(raw, query_grad)
+    kv_steps = kv_way.steps()
+    while steps or kv_steps:
+        for way in (kv_steps, kv_steps, steps):
+            if way:
+                way.pop(0)()
+    kv_way.last(kv_grad)
+    out_way.last(layer_out, mixed)
+    kv_way.finish()
+    out_way.finish()
+
+
+def attend_back(queries, grads, outputs, log_sums, keys, part, mixed, collective_id):
+    count, kv_width = keys.shape[1:]
+    plans = [Plan(0, (Y,), (Z, Y)), Plan(1, (C, Y), (C, Z, Y))]
+    bf, f32 = jnp.bfloat16, jnp.float32
+    group = QUERY_HEADS // KEY_VALUE_HEADS
+    vmem = pl.BlockSpec(memory_space=pltpu.VMEM)
+    dma = pltpu.SemaphoreType.DMA
+    heads = (KEY_VALUE_HEADS, group * count, 2 * HEAD_SIZE)
+    levels, sends, recvs = Reduce.counts(plans[0])
+    out_levels, out_sends, out_recvs = Reduce.counts(plans[1])
+    return pl.pallas_call(
+        functools.partial(attend_back_kernel, plans),
+        out_shape=[
+            jax.ShapeDtypeStruct(queries.shape, f32),
+            jax.ShapeDtypeStruct((count, kv_width), f32),
+            jax.ShapeDtypeStruct(mixed.shape, bf),
+        ],
+        in_specs=[vmem] * 5 + [pl.BlockSpec(memory_space=pl.ANY), vmem],
         out_specs=[vmem] * 3,
-        scratch_shapes=[pltpu.VMEM((plans[0].blocks, rows, w), bf) for w in widths]
-        + [pltpu.VMEM(part.shape, bf)]
-        + [pltpu.VMEM((n, rows, w), bf) for w in widths for n in levels + [NZ + 1]]
+        scratch_shapes=[
+            pltpu.VMEM(heads, bf),
+            pltpu.VMEM(heads, bf),
+            pltpu.VMEM(heads, f32),
+            pltpu.VMEM((group * count, 128), f32),
+            pltpu.VMEM(keys.shape, bf),
+            pltpu.VMEM(part.shape, bf),
+        ]
+        + [pltpu.VMEM((n,) + keys.shape[1:], bf) for n in levels + [NZ + 1]]
         + [pltpu.VMEM((n,) + part.shape[1:], bf) for n in out_levels + [NZ + 1]]
-        + [dma((n,)) for n in (sends, recvs, sends, recvs, out_sends, out_recvs)]
+        + [dma((n,)) for n in (sends, recvs, out_sends, out_recvs)]
         + [dma(()), dma((NC * NZ,))],
         compiler_params=pltpu.CompilerParams(
             collective_id=collective_id, has_side_effects=True, vmem_limit_bytes=60 * 1024 * 1024
         ),
-        name="return_weights",
-    )(*operands)
-
-
-def add_kernel(core_ref, own, core_part, x_part, both_part, in_out, out_out):
+        name="attend_back",
+    )(queries, grads, outputs, log_sums, keys, part, mixed)
+
+
+def last_kernel(core_ref, own, core_part, x_part, both_part, one, two, *outs):
     core = core_ref[0]
+    in_out, out_out = outs[:2]
     split = in_out.shape[3]
     for at, left, right in ((core, own, x_part), (1 - core, core_part, both_part)):
         total = left[0].astype(jnp.float32) + right[0].astype(jnp.float32)
         in_out[at, 0] = total[:, :split]
         out_out[at, 0] = total[:, split:]
 
-
-def add_experts(pieces, core, split):
+    @pl.when(jnp.logical_and(pl.program_id(0) == 0, pl.program_id(1) == 0))
+    def _():
+        wq, wk, wv, wo, router, first_gain, second_gain = outs[2:]
+        q, k = wq.shape[1], wk.shape[1]
+        wq[...] = one[:, :q]
+        wk[...] = one[:, q : q + k]
+        wv[...] = one[:, q + k :]
+        width = wo.shape[1]
+        wo[...] = two[:, :width]
+        small = two[:, width:]
+        router[...] = small[:, : router.shape[1]]
+        turned = small.T
+        at = router.shape[1]
+        first_gain[...] = turned[at : at + 1]
+        second_gain[...] = turned[at + 1 : at + 2]
+
+
+def last_outputs(pieces, core, split, one, two, widths):
     held, quarter, columns = pieces[0].shape
     step = quarter // 2
+    rows = one.shape[0]
     spec = pl.BlockSpec((1, step, columns), lambda e, r, c: (e, r, 0))
+    fixed = lambda a, b: pl.BlockSpec((a, b), lambda e, r, c: (0, 0))
     outs = (split, columns - split)
+    shapes = [(rows, w) for w in widths] + [(1, rows)] * 2
     return pl.pallas_call(
-        add_kernel,
+        last_kernel,
         grid_spec=pltpu.PrefetchScalarGridSpec(
             num_scalar_prefetch=1,
             grid=(held, 2),
-            in_specs=[spec] * 4,
-            out_specs=[pl.BlockSpec((NC, 1, step, w), lambda e, r, c: (0, e, r, 0)) for w in outs],
+            in_specs=[spec] * 4 + [fixed(*one.shape), fixed(*two.shape)],
+            out_specs=[pl.BlockSpec((NC, 1, step, w), lambda e, r, c: (0, e, r, 0)) for w in outs]
+            + [fixed(*s) for s in shapes],
         ),
-        out_shape=[jax.ShapeDtypeStruct((NC, held, quarter, w), jnp.float32) for w in outs],
-        name="add_experts",
-    )(core[None], *pieces)
+        out_shape=[jax.ShapeDtypeStruct((NC, held, quarter, w), jnp.float32) for w in outs]
+        + [jax.ShapeDtypeStruct(s, jnp.float32) for s in shapes],
+        name="last_outputs",
+    )(core[None], *pieces, one, two)
 
 
 MODEL_WIDTH = 1536
@@ -1339,7 +1466,6 @@
     cotangent,
 ):
     tokens = hidden.shape[1]
-    group = QUERY_HEADS // KEY_VALUE_HEADS
     ctx_size = NZ * NY
     ctx = lax.axis_index(CTX)
     fsdp = lax.axis_index(FSDP)
@@ -1383,13 +1509,12 @@
     )
     part = rows // 3
     groups = ctx_size, NX, NC, rows
-    one, two, cots = gather(
-        [both(pack_one, far_one), both(pack_two, far_two), cot_pack],
+    one, two = gather(
+        [both(pack_one, far_one), both(pack_two, far_two)],
         [
             Plan(0, (Z, Y, C), (Z, Y, C), rows=(0, 2 * part), view=weight_view),
             Plan(0, (Y, Z, C), (Z, Y, C), rows=(2 * part, part), view=weight_view),
             Plan(1, (Z, Y, C), (Z, Y, C), rows=(0, rows), view=weight_view),
-            Plan(2, (Z, Y, C), (C, Z, Y)),
         ],
         0,
         {0: groups + pack_one.shape[1:], 1: groups + pack_two.shape[1:]},
@@ -1409,7 +1534,7 @@
     query_rows = (
         rotate_pairs(linear[:, :q_width].reshape(tokens, QUERY_HEADS, HEAD_SIZE), cosine_table, sine_table)
         .astype(bf)
-        .reshape(tokens, KEY_VALUE_HEADS, group, HEAD_SIZE)
+        .reshape(tokens, q_width)
     )
     key_rows = (
         rotate_pairs(
@@ -1421,22 +1546,8 @@
         .reshape(tokens, kv_width)
     )
     value_rows = linear[:, q_width + kv_width :].astype(bf)
-    (kv,) = gather(
-        [jnp.concatenate([key_rows, value_rows], axis=1)], [Plan(0, (Z, Y,), (Z, Y,))], 1
-    )
-    kv = kv.reshape(ctx_size * tokens, 2 * kv_width)
-    key_section, value_section = kv[:, :kv_width], kv[:, kv_width:]
-    value_tensor = value_section.reshape(ctx_size * tokens, KEY_VALUE_HEADS, HEAD_SIZE)
-    scores, visible, key_tensor = piece_scores(query_rows, key_section, positions)
-    best = jnp.max(scores, axis=-1)
-    weights = jnp.where(visible, jnp.exp(scores - best[..., None]), 0.0)
-    total = jnp.sum(weights, axis=-1)
-    weighted = jnp.einsum(
-        "kgtn,nkd->kgtd", weights.astype(bf), value_tensor, preferred_element_type=f32
-    )
-    log_sum_rows = best + jnp.log(total)
-    attention_output = (
-        jnp.transpose(weighted / total[..., None], (2, 0, 1, 3)).reshape(tokens, q_width).astype(bf)
+    attention_output, log_sums, kv, cots = attend(
+        jnp.concatenate([key_rows, value_rows], axis=1), query_rows, cot_pack, 1
     )
     mixed = wide + jnp.dot(attention_output, output_w, preferred_element_type=f32)
     ffn_unit, inverse_two, ffn_in = rms_forward(mixed, ffn_gain)
@@ -1464,35 +1575,9 @@
     attention_output_gradient = lax.dot_general(
         grad_attn, output_w, contract_cols, preferred_element_type=f32
     ).astype(bf)
-    head_gradient = attention_output_gradient.reshape(tokens, KEY_VALUE_HEADS, group, HEAD_SIZE)
-    delta_rows = jnp.sum(
-        head_gradient.astype(f32)
-        * attention_output.reshape(tokens, KEY_VALUE_HEADS, group, HEAD_SIZE).astype(f32),
-        axis=-1,
-    )
-    delta_rows = jnp.transpose(delta_rows, (1, 2, 0))
-    weights_full = jnp.where(visible, jnp.exp(scores - log_sum_rows[..., None]), 0.0)
-    grad_probs = jnp.einsum(
-        "tkgd,nkd->kgtn", head_gradient, value_tensor, preferred_element_type=f32
-    )
-    grad_scores = (weights_full * (grad_probs - delta_rows[..., None])).astype(bf)
-    grad_query = attn_scale * jnp.einsum(
-        "kgtn,nkd->tkgd", grad_scores, key_tensor, preferred_element_type=f32
-    )
-    key_portion = attn_scale * jnp.einsum(
-        "kgtn,tkgd->nkd", grad_scores, query_rows, preferred_element_type=f32
-    )
-    value_portion = jnp.einsum(
-        "kgtn,tkgd->nkd", weights_full.astype(bf), head_gradient, preferred_element_type=f32
-    )
-    update = jnp.concatenate(
-        [
-            key_portion.astype(bf).reshape(ctx_size, tokens, kv_width),
-            value_portion.astype(bf).reshape(ctx_size, tokens, kv_width),
-        ],
-        axis=2,
-    )
-    (local_gradients,) = reduce_scatter([update], [Plan(0, (Y,), (Z, Y,))], [f32], 4)
+    grad_query, local_gradients, layer_out = attend_back(
+        query_rows, attention_output_gradient, attention_output, log_sums, kv, moe_part, mixed, 4
+    )
     query_back = (
         rotate_pairs(
             grad_query.reshape(tokens, QUERY_HEADS, HEAD_SIZE), cosine_table, -sine_table
@@ -1518,7 +1603,7 @@
         high = factor.astype(bf)
         halves += [high, (factor - high.astype(f32)).astype(bf)]
     column = lambda n: jnp.broadcast_to((jnp.arange(128) == n).astype(bf), (tokens, 128))
-    sum_one, sum_two, layer_out = return_weights(
+    sum_one, sum_two = return_weights(
         [attention_input, attention_output, jnp.concatenate([ffn_in] + halves)],
         [
             back,
@@ -1533,27 +1618,24 @@
                 ]
             ),
         ],
-        moe_part,
-        mixed,
         5,
     )
-    grad_expert_in, grad_expert_out = (
-        g.reshape(NC * held, quarter, -1)
-        for g in add_experts([pieces[0]] + across, core, 2 * EXPERT_HIDDEN)
-    )
-    at = MODEL_WIDTH + EXPERT_COUNT
+    grad_expert_in, grad_expert_out, *rest, first_gain, second_gain = last_outputs(
+        [pieces[0]] + across,
+        core,
+        2 * EXPERT_HIDDEN,
+        sum_one,
+        sum_two,
+        (q_width, kv_width, kv_width, MODEL_WIDTH, EXPERT_COUNT),
+    )
     return (
         layer_out[None],
         grad_input[None],
-        sum_two[:, at],
-        sum_two[:, at + 1],
-        sum_one[:, :q_width],
-        sum_one[:, q_width : q_width + kv_width],
-        sum_one[:, q_width + kv_width :],
-        sum_two[:, :MODEL_WIDTH],
-        sum_two[:, MODEL_WIDTH:at],
-        grad_expert_in,
-        grad_expert_out,
+        first_gain.reshape(rows),
+        second_gain.reshape(rows),
+        *rest,
+        grad_expert_in.reshape(NC * held, quarter, -1),
+        grad_expert_out.reshape(NC * held, quarter, -1),
     )
 
 

time: 666 us -> 627 us (0.941)
  waiting for transfers between devices: 42 us -> 11.4 us
  Pallas kernels: 496 us -> 521 us
  matrix products: 44.6 us -> 23.3 us
  local copies, waits for them, and re-layouts: 38.8 us -> 28.6 us
  other arithmetic: 31 us -> 24.3 us
    pallas_call x2 -> x3, Pallas kernels: 46.1 us -> 173 us  [the longest x1 90.7 us: attend_back(): pl.pallas_call(functools.partial(attend_back_kernel, plans), out_shape=[j...]
    pallas_call x2 -> x1, Pallas kernels: 136 us -> 72.1 us  [gather(): pl.pallas_call(functools.partial(gather_kernel, plans, n), out_shape=[jax...]
    pallas_call x1, Pallas kernels: 196 us -> 158 us  [return_weights(): pl.pallas_call(functools.partial(weights_kernel, plans), out_shape=[jax.S...]
    ppermute x8, waiting for transfers between devices: 42 us -> 11.4 us  [swap(): return lax.ppermute(a, FSDP, [(i, i ^ flip) for i in range(NX * NC)])]
    dot_general x6 -> x0, matrix products: 22.1 us -> none  [the longest x1 7.38 us: fast_body(): jnp.einsum('tkgd,nkd->kgtn', head_gradient, value_tensor, preferred_eleme...]
    slice x8 -> x0, local copies, waits for them, and re-layouts: 10.8 us -> none  [the longest x3 3.51 us: fast_body(): key_section, value_section = (kv[:, :kv_width], kv[:, kv_width:])]
  transfers between devices with their start and end apart: 8 -> 8, of which waited for: 1 -> 1; matrix products, arithmetic and copies ran while one was open for 8% -> 6% of each run, Pallas kernels for 34% -> 38%
where the time goes in v6:
time: 627 us; the launch traced here: 619 us
  Pallas kernels  521 us (83%)
  local copies, waits for them, and re-layouts  28.6 us (5%)
  other arithmetic  24.3 us (4%)
  matrix products  23.3 us (4%)
  waiting for transfers between devices  11.4 us (2%)
  starting transfers between devices  8.12 us (1%)
    pallas_call x1, Pallas kernels, return_weights(): pl.pallas_call(functools.partial(weights_kernel, plans), out_shape=[jax.S...  158 us
    pallas_call x1, Pallas kernels, moe(): pl.pallas_call(functools.partial(moe_kernel, plans, back, width, hidden,...  118 us
    pallas_call x1, Pallas kernels, attend_back(): pl.pallas_call(functools.partial(attend_back_kernel, plans), out_shape=[j...  90.7 us
    pallas_call x1, Pallas kernels, attend(): pl.pallas_call(functools.partial(attend_kernel, plans), out_shape=[jax.Sh...  74.1 us
    pallas_call x1, Pallas kernels, gather(): pl.pallas_call(functools.partial(gather_kernel, plans, n), out_shape=[jax...  72.1 us
  transfers between devices with their start and end apart: 8, of which 1 were waited for; matrix products, arithmetic and copies ran while one was open for 6% of the time, Pallas kernels for 38%

profile of v6, /device:TPU:0, one launch (start us, length us, event | category | flops | bytes accessed | tf_op | source)
XLA Modules:
  0.0 618.6 jit_solution(7051047554517696232)
XLA Ops:
  0.7 1.0 constant_dynamic-update-slice_fusion.2
  1.7 0.8 constant_dynamic-update-slice_fusion.1
  2.5 0.8 constant_dynamic-update-slice_fusion
  3.3 3.0 collective-permute-start
  6.3 0.8 copy.61
  7.0 0.8 copy.62
  7.8 0.8 copy.63
  8.6 1.0 concatenate.47
  9.7 1.2 fusion.22
  10.9 1.2 bitcast_convert_fusion
  12.1 2.3 pad_maximum_fusion
  14.4 0.8 fusion.42
  15.1 1.7 dynamic-slice_bitcast_fusion
  17.5 0.7 compare_convert_fusion.1
  18.2 1.4 copy.67
  20.2 1.7 concatenate.52.own_cots
  22.4 1.8 maximum_select_fusion.1.refs_1_
  24.2 1.9 maximum_select_fusion.refs_0_
  26.1 72.1 %shard_map.203 = (bf16[8,2,2,48,2560]{4,3,2,1,0:T(8,128)(2,1)}, bf16[8,2,2,48,1664]{4,3,2,1,0:T(8,128)(2,1)}) custom-call(bf16[2,48,2560]{2,1,0:T(8,128)(2,1)} %maximum_select_fusion.refs_0_, bf16[2,48,1664]{2,1,0:T(8,128)(2,1)} %maximum_select_fusion.1.refs_1_), custom_call_target="tpu_custom_call" | custom-call | tf_op jit(solution)/shard_map/pallas_call | solution.py:178
  98.2 1.3 fusion.32
  99.5 0.6 slice_reduce_fusion
  100.1 4.5 fusion.30
  104.7 0.7 slice.92
  105.4 0.7 slice.144
  106.6 1.2 collective-permute-start.4
  107.8 1.8 copy.65
  109.6 1.0 subtract_convert_fusion.5
  110.6 0.7 pad_maximum_fusion.5
  111.3 1.7 copy.66
  112.9 1.1 copy.64
  114.6 1.2 subtract_convert_fusion.3
  115.9 0.9 copy.72.queries.refs_0_
  116.8 0.7 pad_maximum_fusion.4.own_kv
  117.6 74.1 %attend.1 = (bf16[128,1536]{1,0:T(8,128)(2,1)}, f32[384,128]{1,0:T(8,128)}, bf16[8,128,1024]{2,1,0:T(8,128)(2,1)}, bf16[16,128,1664]{2,1,0:T(8,128)(2,1)}) custom-call(bf16[128,1024]{1,0:T(8,128)(2,1)} %pad_maximum_fusion.4.own_kv, bf16[128,1536]{1,0:T(8,128)(2,1)} %copy.72.queries.refs_0_, bf16[128,1664]{1,0:T(8,128)(2,1)} %concatenate.52.own_cots), custom_call_target="tpu_custom_call" | custom-call | tf_op jit(solution)/shard_map/attend/pallas_call | solution.py:841
  191.7 3.3 multiply_reduce_fusion.1
  195.1 0.8 copy-done
  195.9 0.9 constant_dynamic-update-slice_fusion.3
  196.8 1.3 fusion.38
  198.8 0.9 concatenate.53.refs_0_
  199.7 11.3 %collective-permute-done.3.refs_4_ = bf16[2,384,1536]{2,1,0:T(8,128)(2,1)} collective-permute-done((bf16[2,384,1536]{2,1,0:T(8,128)(2,1)S(1)}, bf16[2,384,1536]{2,1,0:T(8,128)(2,1)}, u32[]{:S(2)}, u32[]{:S(2)}) %collective-permute-start.3) | collective-permute-done | bytes 2359328 | tf_op jit(solution)/shard_map/ppermute | solution.py:1451
  211.1 117.6 %experts.1 = (f32[128,1664]{1,0:T(8,128)}, bf16[16,128,1536]{2,1,0:T(8,128)(2,1)}, bf16[2,384,1536]{2,1,0:T(8,128)(2,1)}, bf16[2,384,1536]{2,1,0:T(8,128)(2,1)},...) custom-call(bf16[128,1664]{1,0:T(8,128)(2,1)} %concatenate.53.refs_0_, ...), custom_call_target="tpu_custom_call" | custom-call | tf_op jit(solution)/shard_map/experts/pallas_call | solution.py:603
  328.7 1.1 slice_add_fusion.1
  329.8 0.7 select_reduce_fusion.1
  330.6 0.7 multiply_reduce_fusion.2
  331.3 0.7 subtract_multiply_fusion
  332.0 0.7 select_reduce_fusion
  332.8 1.9 multiply_reduce_fusion
  335.0 4.9 fusion.7.refs_1_
  339.9 90.7 %attend_back.1 = (f32[128,1536]{1,0:T(8,128)}, f32[128,1024]{1,0:T(8,128)}, bf16[128,1536]{1,0:T(8,128)(2,1)}) custom-call(bf16[128,1536]{1,0:T(8,128)(2,1)} %copy.72.queries.refs_0_, bf16[128,1536]{1,0:T(8,128)(2,1)} %fusion.7.refs_1_, bf16[128,1536]{1,0:T(8,128)(2,1)} %get-tuple-element.45.refs_2_, f32[384,128]{1,0:T(8,128)} %get-tuple-element.50.refs_3_, ...), custom_call_target="tpu_custom_call" | custom-call | tf_op jit(solution)/shard_map/attend_back/pallas_call | solution.py:965
  430.6 1.0 slice.83
  431.6 1.0 slice.143
  432.5 0.6 pad_dynamic-update-slice_fusion
  433.2 1.4 copy.73
  434.6 0.9 subtract_convert_fusion.2
  435.8 0.8 subtract_convert_fusion.4
  436.8 6.1 fusion.16
  443.1 1.4 collective-permute-start.5
  444.4 1.5 collective-permute-start.6
  446.1 0.9 pad_maximum_fusion.1.refs_1_
  447.9 1.3 fusion.21
  449.2 158.3 %return_weights.1 = (f32[48,2560]{1,0:T(8,128)}, f32[48,1664]{1,0:T(8,128)}) custom-call(bf16[128,1536]{1,0:T(8,128)(2,1)} %get-tuple-element.127.refs_0_, bf16[128,2560]{1,0:T(8,128)(2,1)} %pad_maximum_fusion.1.refs_1_, bf16[128,1536]{1,0:T(8,128)(2,1)} %get-tuple-element.45.refs_2_, bf16[128,1536]{1,0:T(8,128)(2,1)} %copy-done.10, ...), custom_call_target="tpu_custom_call" | custom-call | tf_op jit(solution)/shard_map/return_weights/pallas_call | solution.py:703
  607.6 8.4 %last_outputs.1 = (f32[2,2,384,1024]{3,2,1,0:T(8,128)}, f32[2,2,384,512]{3,2,1,0:T(8,128)}, f32[48,1536]{1,0:T(8,128)}, f32[48,512]{1,0:T(8,128)}, f32[48,512]{1...) custom-call(s32[1]{0:T(128)} %bitcast.25.core_ref, ...), custom_call_target="tpu_custom_call" | custom-call | tf_op jit(solution)/shard_map/last_outputs/pallas_call | solution.py:1027
  616.0 1.4 copy.77
  617.4 0.7 copy.89
  (114 shorter events, 5.9 us)
Async XLA Ops:
  0.6 11.4 %copy-start.9 = (bf16[4,384,512]{2,1,0:T(8,128)(2,1)S(1)}, bf16[4,384,512]{2,1,0:T(8,128)(2,1)}, u32[]{:S(2)}) copy-start(bf16[4,384,512]{2,1,0:T(8,128)(2,1)} %param.22) | copy-start | bytes 4718596
  3.3 19.1 %collective-permute-start = (bf16[48,2560]{1,0:T(8,128)(2,1)S(1)}, bf16[48,2560]{1,0:T(8,128)(2,1)}, u32[]{:S(2)}, u32[]{:S(2)}) collective-permute-start(bf16[48,2560]{1,0:T(8,128)(2,1)S(1)} %constant_dynamic-update-slice_fusion), channel_id=1, source_target_pairs={{0,2},{1,3},{2,0},{3,1},{4,6},{5,7},{6,4},{7,5},{8,10},{9,11},{10,... | collective-permute-start | bytes 737288 | tf_op jit(solution)/shard_map/ppermute | solution.py:1451
  9.6 12.8 %collective-permute-start.1 = (bf16[48,1664]{1,0:T(8,128)(2,1)S(1)}, bf16[48,1664]{1,0:T(8,128)(2,1)}, u32[]{:S(2)}, u32[]{:S(2)}) collective-permute-start(bf16[48,1664]{1,0:T(8,128)(2,1)S(1)} %concatenate.47), channel_id=1, source_target_pairs={{0,2},{1,3},{2,0},{3,1},{4,6},{5,7},{6,4},{7,5},{8,10},{9,11},{10,... | collective-permute-start | bytes 479240 | tf_op jit(solution)/shard_map/ppermute | solution.py:1451
  10.9 89.3 %copy-start.26 = (f32[128]{0:T(128)}, f32[128]{0:T(128)S(1)}, u32[]{:S(2)}) copy-start(f32[128]{0:T(128)S(1)} %add_rsqrt_fusion.1) | copy-start | bytes 1540
  15.1 1.7 copy-start.24
  16.8 97.3 %copy-start.5 = (bf16[2,384,1536]{2,1,0:T(8,128)(2,1)}, bf16[2,384,1536]{2,1,0:T(8,128)(2,1)S(1)}, u32[]{:S(2)}) copy-start(bf16[2,384,1536]{2,1,0:T(8,128)(2,1)S(1)} %get-tuple-element.47.refs_2_) | copy-start | bytes 7077892
  16.8 83.3 %copy-start.3 = (bf16[1,128,1536]{2,1,0:T(8,128)(2,1)S(1)}, bf16[1,128,1536]{2,1,0:T(8,128)(2,1)}, u32[]{:S(2)}) copy-start(bf16[1,128,1536]{2,1,0:T(8,128)(2,1)} %param.12) | copy-start | bytes 1179652
  100.1 4.5 copy-start.19
  104.7 4.9 copy-start.13
  106.1 93.6 %collective-permute-start.2 = (bf16[2,384,1536]{2,1,0:T(8,128)(2,1)}, bf16[2,384,1536]{2,1,0:T(8,128)(2,1)}, u32[]{:S(2)}, u32[]{:S(2)}) collective-permute-start(bf16[2,384,1536]{2,1,0:T(8,128)(2,1)} %get-tuple-element.48), channel_id=1, source_target_pairs={{0,1},{1,0},{2,3},{3,2},{4,5},{5,4},{6,7},{7,6},{8,9},{9,8},{10,11... | collective-permute-start | bytes 7077896 | tf_op jit(solution)/shard_map/ppermute | solution.py:1451
  106.6 104.4 %collective-permute-start.4 = (bf16[2,384,1536]{2,1,0:T(8,128)(2,1)}, bf16[2,384,1536]{2,1,0:T(8,128)(2,1)}, u32[]{:S(2)}, u32[]{:S(2)}) collective-permute-start(bf16[2,384,1536]{2,1,0:T(8,128)(2,1)} %get-tuple-element.48), channel_id=1, source_target_pairs={{0,3},{1,2},{2,1},{3,0},{4,7},{5,6},{6,5},{7,4},{8,11},{9,10},{10,... | collective-permute-start | bytes 7077896 | tf_op jit(solution)/shard_map/ppermute | solution.py:1451
  114.1 2.7 copy-start.11
  114.1 2.7 copy-start.12
  114.1 97.0 %collective-permute-start.3 = (bf16[2,384,1536]{2,1,0:T(8,128)(2,1)S(1)}, bf16[2,384,1536]{2,1,0:T(8,128)(2,1)}, u32[]{:S(2)}, u32[]{:S(2)}) collective-permute-start(bf16[2,384,1536]{2,1,0:T(8,128)(2,1)S(1)} %get-tuple-element.47.refs_2_), channel_id=1, source_target_pairs={{0,2},{1,3},{2,0},{3,1},{4,6},{5,7},{6,4},{7,5},{8,10},{9,11},{10,... | collective-permute-start | bytes 7077896 | tf_op jit(solution)/shard_map/ppermute | solution.py:1451
  191.7 4.3 copy-start.22
  195.0 0.9 copy-start
  195.0 3.0 copy-start.25
  195.0 3.8 copy-start.16
  195.1 1.7 copy-start.28
  198.1 12.9 %copy-start.21 = (f32[128,8]{0,1:T(8,128)}, f32[128,8]{0,1:T(8,128)S(1)}, u32[]{:S(2)}) copy-start(f32[128,8]{0,1:T(8,128)S(1)} %select_reduce_fusion.3) | copy-start | bytes 12292
  198.1 0.5 copy-start.31
  198.2 0.5 copy-start.32
  328.7 6.1 copy-start.1
  328.7 6.1 copy-start.6
  328.7 6.1 copy-start.23
  328.7 6.1 copy-start.29
  335.0 4.9 copy-start.10
  430.6 4.0 copy-start.14
  434.6 2.2 copy-start.4
  436.7 6.2 %copy-start.17 = (bf16[640,128]{1,0:T(8,128)(2,1)S(1)}, bf16[640,128]{1,0:T(8,128)(2,1)}, u32[]{:S(2)}) copy-start(bf16[640,128]{1,0:T(8,128)(2,1)} %pad_dynamic-update-slice_fusion) | copy-start | bytes 491524
  436.8 6.2 %copy-start.33 = (bf16[128]{0:T(256)(128)(2,1)S(1)}, bf16[128]{0:T(256)(128)(2,1)}, u32[]{:S(2)}) copy-start(bf16[128]{0:T(256)(128)(2,1)} %compare_convert_fusion.1) | copy-start | bytes 772
  436.8 6.2 %copy-start.34 = (bf16[128]{0:T(256)(128)(2,1)S(1)}, bf16[128]{0:T(256)(128)(2,1)}, u32[]{:S(2)}) copy-start(bf16[128]{0:T(256)(128)(2,1)} %compare_convert_fusion) | copy-start | bytes 772
  436.8 9.2 %copy-start.7 = (bf16[640,1536]{1,0:T(8,128)(2,1)S(1)}, bf16[640,1536]{1,0:T(8,128)(2,1)}, u32[]{:S(2)}) copy-start(bf16[640,1536]{1,0:T(8,128)(2,1)} %get-tuple-element.117) | copy-start | bytes 5898244
  436.8 9.2 %copy-start.27 = (f32[128]{0:T(128)S(1)}, f32[128]{0:T(128)}, u32[]{:S(2)}) copy-start(f32[128]{0:T(128)} %copy-done.26) | copy-start | bytes 1540
  442.9 4.3 copy-start.2
  442.9 4.3 copy-start.30
  443.0 4.3 copy-start.18
  443.1 164.5 %collective-permute-start.5 = (bf16[2,384,1536]{2,1,0:T(8,128)(2,1)}, bf16[2,384,1536]{2,1,0:T(8,128)(2,1)}, u32[]{:S(2)}, u32[]{:S(2)}) collective-permute-start(bf16[2,384,1536]{2,1,0:T(8,128)(2,1)} %get-tuple-element.57), channel_id=1, source_target_pairs={{0,1},{1,0},{2,3},{3,2},{4,5},{5,4},{6,7},{7,6},{8,9},{9,8},{10,11... | collective-permute-start | bytes 7077896 | tf_op jit(solution)/shard_map/ppermute | solution.py:1451
  444.4 163.1 %collective-permute-start.6 = (bf16[2,384,1536]{2,1,0:T(8,128)(2,1)}, bf16[2,384,1536]{2,1,0:T(8,128)(2,1)}, u32[]{:S(2)}, u32[]{:S(2)}) collective-permute-start(bf16[2,384,1536]{2,1,0:T(8,128)(2,1)} %get-tuple-element.58), channel_id=1, source_target_pairs={{0,2},{1,3},{2,0},{3,1},{4,6},{5,7},{6,4},{7,5},{8,10},{9,11},{10,... | collective-permute-start | bytes 7077896 | tf_op jit(solution)/shard_map/ppermute | solution.py:1451
  445.9 161.6 %collective-permute-start.7 = (bf16[2,384,1536]{2,1,0:T(8,128)(2,1)}, bf16[2,384,1536]{2,1,0:T(8,128)(2,1)}, u32[]{:S(2)}, u32[]{:S(2)}) collective-permute-start(bf16[2,384,1536]{2,1,0:T(8,128)(2,1)} %get-tuple-element.59), channel_id=1, source_target_pairs={{0,3},{1,2},{2,1},{3,0},{4,7},{5,6},{6,5},{7,4},{8,11},{9,10},{10,... | collective-permute-start | bytes 7077896 | tf_op jit(solution)/shard_map/ppermute | solution.py:1451
  447.2 0.7 copy-start.20
  447.5 1.7 copy-start.8
  607.6 9.8 %copy-start.15 = (bf16[128,1536]{1,0:T(8,128)(2,1)S(1)}, bf16[128,1536]{1,0:T(8,128)(2,1)}, u32[]{:S(2)}) copy-start(bf16[128,1536]{1,0:T(8,128)(2,1)} %get-tuple-element.53) | copy-start | bytes 1179652

commit v7 on v6

--- a/solution.py
+++ b/solution.py
@@ -639,10 +639,6 @@
     )(payload, cots, *parts)
 
 
-def weight_view(out, spot, rows):
-    return out.at[spot[Z] * NY + spot[Y], :, spot[C], pl.ds(rows[0], rows[1])]
-
-
 def weights_kernel(plans, *refs):
     left_one, right_one, left_two, right_two, left_small, right_small = refs[:6]
     outs = refs[6:8]
@@ -716,21 +712,26 @@
     )(*[a for pair in zip(lefts, rights) for a in pair])
 
 
-def place_heads(source, target):
-    count = source.shape[0]
+def turn(block, cosine, sine):
+    lane = lax.broadcasted_iota(jnp.int32, (1, 128), 1)
+    half = HEAD_SIZE // 2
+    other = jnp.where(lane % HEAD_SIZE < half, pltpu.roll(block, 128 - half, 1), pltpu.roll(block, half, 1))
+    return block * cosine + other * sine
+
+
+def place_heads(read, target, count):
     group = QUERY_HEADS // KEY_VALUE_HEADS
     lane = lax.broadcasted_iota(jnp.int32, (1, 2 * HEAD_SIZE), 1)
-    for h in range(QUERY_HEADS):
-        m, g = h // group, h % group
-        block = source[:, h // 2 * 128 : h // 2 * 128 + 128].astype(jnp.float32)
-        if h % 2 != m % 2:
-            block = pltpu.roll(block, HEAD_SIZE, 1)
-        block = jnp.where(lane // HEAD_SIZE == m % 2, block, 0.0)
-        target[m, g * count : (g + 1) * count] = block.astype(target.dtype)
-
-
-def collect_heads(source, target):
-    count = target.shape[0]
+    for pair in range(QUERY_HEADS // 2):
+        both = read(pair)
+        for h in (2 * pair, 2 * pair + 1):
+            m, g = h // group, h % group
+            block = both if h % 2 == m % 2 else pltpu.roll(both, HEAD_SIZE, 1)
+            block = jnp.where(lane // HEAD_SIZE == m % 2, block, 0.0)
+            target[m, g * count : (g + 1) * count] = block.astype(target.dtype)
+
+
+def collect_heads(source, target, count, finish):
     group = QUERY_HEADS // KEY_VALUE_HEADS
     lane = lax.broadcasted_iota(jnp.int32, (1, 2 * HEAD_SIZE), 1)
     for pair in range(QUERY_HEADS // 2):
@@ -739,7 +740,8 @@
             m, g = h // group, h % group
             block = source[m, g * count : (g + 1) * count]
             sides.append(block if h % 2 == m % 2 else pltpu.roll(block, HEAD_SIZE, 1))
-        target[:, pair * 128 : pair * 128 + 128] = jnp.where(lane < HEAD_SIZE, *sides).astype(target.dtype)
+        both = finish(jnp.where(lane < HEAD_SIZE, *sides))
+        target[:, pair * 128 : pair * 128 + 128] = both.astype(target.dtype)
 
 
 class Scores:
@@ -763,10 +765,19 @@
         return jnp.where(self.column <= self.position, found * attn_scale, masked_logits)
 
 
-def attend_kernel(plans, own_kv, queries, own_cots, out, log_sums, kv_out, cots, seen, placed, raw, *sems):
+def attend_kernel(
+    plans, linear, own_cots, cosine, sine, out, log_sums, kv_out, cots, placed, seen, own_kv, raw, *sems
+):
     send_kv, recv_kv, send_cot, recv_cot, spare, own_sem = sems
     place = Place()
     bf, f32 = jnp.bfloat16, jnp.float32
+    count = linear.shape[0]
+    width = KEY_VALUE_HEADS * HEAD_SIZE
+    q_width = QUERY_HEADS * HEAD_SIZE
+    for c0 in range(0, width, 128):
+        block = linear[:, q_width + c0 : q_width + c0 + 128]
+        own_kv[:, c0 : c0 + 128] = turn(block, cosine[...], sine[...]).astype(bf)
+    own_kv[:, width:] = linear[:, q_width + width :].astype(bf)
     greet(place, (Z, Y, C))
     kv_way = Gather(place, plans[0], own_kv, seen, send_kv, recv_kv, spare, 0, 0)
     cot_ways, at = [], 0
@@ -779,7 +790,7 @@
     mine = pltpu.make_async_copy(own_cots, cots.at[flat_index(place.at, plans[1].index)], own_sem.at[0])
     mine.start()
     seen[flat_index(place.at, plans[0].index)] = own_kv[...]
-    place_heads(queries, placed)
+    place_heads(lambda pair: turn(linear[:, pair * 128 : pair * 128 + 128], cosine[...], sine[...]), placed, count)
     log_sums[...] = jnp.zeros(log_sums.shape, f32)
     early = [e for e in gather_events(plans[1].order)[1:]]
     kv_events = gather_events(plans[0].order)[1:]
@@ -793,7 +804,6 @@
     keep.start()
     scores = Scores(place, placed, seen)
     lane = lax.broadcasted_iota(jnp.int32, (1, 128), 1)
-    width = KEY_VALUE_HEADS * HEAD_SIZE
 
     def head(m, carry):
         for i in range(KEY_VALUE_HEADS):
@@ -815,7 +825,7 @@
         return carry
 
     lax.fori_loop(0, KEY_VALUE_HEADS, head, 0)
-    collect_heads(raw, out)
+    collect_heads(raw, out, count, lambda block: block)
     keep.wait()
     mine.wait()
     kv_way.finish()
@@ -823,8 +833,9 @@
         way.finish()
 
 
-def attend(own_kv, queries, own_cots, collective_id):
-    count, kv_width = own_kv.shape
+def attend(linear, own_cots, cosine, sine, collective_id):
+    count = linear.shape[0]
+    kv_width = 2 * KEY_VALUE_HEADS * HEAD_SIZE
     cut = count * 3 // 4
     plans = [
         Plan(0, (Z, Y), (Z, Y)),
@@ -841,14 +852,15 @@
     return pl.pallas_call(
         functools.partial(attend_kernel, plans),
         out_shape=[
-            jax.ShapeDtypeStruct(queries.shape, bf),
+            jax.ShapeDtypeStruct((count, QUERY_HEADS * HEAD_SIZE), bf),
             jax.ShapeDtypeStruct((group * count, 128), f32),
             jax.ShapeDtypeStruct(kv_shape, bf),
             jax.ShapeDtypeStruct((plans[1].blocks,) + own_cots.shape, bf),
+            jax.ShapeDtypeStruct(heads, bf),
         ],
-        in_specs=[vmem] * 3,
-        out_specs=[vmem, vmem, apart, apart],
-        scratch_shapes=[pltpu.VMEM(kv_shape, bf), pltpu.VMEM(heads, bf), pltpu.VMEM(heads, f32)]
+        in_specs=[vmem] * 4,
+        out_specs=[vmem, vmem, apart, apart, vmem],
+        scratch_shapes=[pltpu.VMEM(kv_shape, bf), pltpu.VMEM((count, kv_width), bf), pltpu.VMEM(heads, f32)]
         + [
             dma((Gather.sends(plans[0]),)),
             dma((plans[0].blocks,)),
@@ -861,15 +873,15 @@
             collective_id=collective_id, has_side_effects=True, vmem_limit_bytes=56 * 1024 * 1024
         ),
         name="attend",
-    )(own_kv, queries, own_cots)
+    )(linear, own_cots, cosine, sine)
 
 
 def attend_back_kernel(plans, *refs):
-    queries, grads, outputs, log_sums, keys, part, mixed = refs[:7]
-    query_grad, kv_grad, layer_out = refs[7:10]
-    placed, grads_placed, raw, deltas, held, held_out = refs[10:16]
-    level, chain, out_level, out_level_two, out_chain = refs[16:21]
-    send_kv, recv_kv, send_out, recv_out, spare, load_sem = refs[21:]
+    placed, grads, outputs, log_sums, keys, part, mixed, cosine, sine = refs[:9]
+    back, layer_out = refs[9:11]
+    kv_grad, grads_placed, raw, deltas, held, held_out = refs[11:17]
+    level, chain, out_level, out_level_two, out_chain = refs[17:22]
+    send_kv, recv_kv, send_out, recv_out, spare, load_sem = refs[22:]
     place = Place()
     bf, f32 = jnp.bfloat16, jnp.float32
     far = list(reversed(range(NZ)))
@@ -887,9 +899,8 @@
         copy.wait()
     for k in far:
         out_way.first(k)
-    place_heads(queries, placed)
-    place_heads(grads, grads_placed)
-    count = queries.shape[0]
+    count = grads.shape[0]
+    place_heads(lambda pair: grads[:, pair * 128 : pair * 128 + 128].astype(f32), grads_placed, count)
     group = QUERY_HEADS // KEY_VALUE_HEADS
     lane = lax.broadcasted_iota(jnp.int32, (1, 128), 1)
     for g in range(group):
@@ -904,17 +915,16 @@
     scores = Scores(place, placed, keys)
     width = KEY_VALUE_HEADS * HEAD_SIZE
     blocks = keys.shape[0]
-    steps = out_way.steps()
     turns = KEY_VALUE_HEADS // 2
+    early = [[(out_way.level, 0, 3)], [(out_way.level, 0, 2)], [(out_way.level, 1, 3)], [(out_way.level, 1, 2), (out_way.along, 3)]]
 
     def pair(p, carry):
         for i in range(turns):
-            now = [steps.pop(0) for _ in range(min(len(steps), 2))]
 
             @pl.when(p == i)
             def _():
-                for step in now:
-                    step()
+                for step, *at in early[i]:
+                    step(*at)
 
         key_sum = value_sum = None
         for side in range(2):
@@ -940,19 +950,32 @@
     lax.fori_loop(0, turns, pair, 0)
     for k in far:
         kv_way.first(k)
-    collect_heads(raw, query_grad)
-    kv_steps = kv_way.steps()
-    while steps or kv_steps:
-        for way in (kv_steps, kv_steps, steps):
-            if way:
-                way.pop(0)()
+    out_way.level(0, 1)
+    out_way.level(0, 0)
+    collect_heads(raw, back, count, lambda block: turn(block, cosine[...], -sine[...]))
+    kv_way.level(0, 3)
+    kv_way.level(0, 2)
+    kv_way.along(3)
+    kv_way.level(0, 1)
+    kv_way.along(2)
+    out_way.along(2)
+    kv_way.level(0, 0)
+    kv_way.along(1)
     kv_way.last(kv_grad)
+    q_width = QUERY_HEADS * HEAD_SIZE
+    for c0 in range(0, width, 128):
+        block = turn(kv_grad[:, c0 : c0 + 128], cosine[...], -sine[...])
+        back[:, q_width + c0 : q_width + c0 + 128] = block.astype(bf)
+    back[:, q_width + width :] = kv_grad[:, width:].astype(bf)
+    out_way.level(1, 1)
+    out_way.along(1)
+    out_way.level(1, 0)
     out_way.last(layer_out, mixed)
     kv_way.finish()
     out_way.finish()
 
 
-def attend_back(queries, grads, outputs, log_sums, keys, part, mixed, collective_id):
+def attend_back(placed, grads, outputs, log_sums, keys, part, mixed, cosine, sine, collective_id):
     count, kv_width = keys.shape[1:]
     plans = [Plan(0, (Y,), (Z, Y)), Plan(1, (C, Y), (C, Z, Y))]
     bf, f32 = jnp.bfloat16, jnp.float32
@@ -965,14 +988,13 @@
     return pl.pallas_call(
         functools.partial(attend_back_kernel, plans),
         out_shape=[
-            jax.ShapeDtypeStruct(queries.shape, f32),
-            jax.ShapeDtypeStruct((count, kv_width), f32),
+            jax.ShapeDtypeStruct((count, grads.shape[1] + kv_width), bf),
             jax.ShapeDtypeStruct(mixed.shape, bf),
         ],
-        in_specs=[vmem] * 5 + [pl.BlockSpec(memory_space=pl.ANY), vmem],
-        out_specs=[vmem] * 3,
+        in_specs=[vmem] * 5 + [pl.BlockSpec(memory_space=pl.ANY)] + [vmem] * 3,
+        out_specs=[vmem] * 2,
         scratch_shapes=[
-            pltpu.VMEM(heads, bf),
+            pltpu.VMEM((count, kv_width), f32),
             pltpu.VMEM(heads, bf),
             pltpu.VMEM(heads, f32),
             pltpu.VMEM((group * count, 128), f32),
@@ -987,7 +1009,7 @@
             collective_id=collective_id, has_side_effects=True, vmem_limit_bytes=60 * 1024 * 1024
         ),
         name="attend_back",
-    )(queries, grads, outputs, log_sums, keys, part, mixed)
+    )(placed, grads, outputs, log_sums, keys, part, mixed, cosine, sine)
 
 
 def last_kernel(core_ref, own, core_part, x_part, both_part, one, two, *outs):
@@ -1466,7 +1488,6 @@
     cotangent,
 ):
     tokens = hidden.shape[1]
-    ctx_size = NZ * NY
     ctx = lax.axis_index(CTX)
     fsdp = lax.axis_index(FSDP)
     core = fsdp % NC
@@ -1478,7 +1499,9 @@
     bf = jnp.bfloat16
     f32 = jnp.float32
     positions = ctx * tokens + jnp.arange(tokens, dtype=jnp.int32)
-    cosine_table, sine_table = rope_tables(positions)
+    cosine_table, sine_table = (table[:, 0] for table in rope_tables(positions))
+    cosine = jnp.concatenate([cosine_table] * 4, axis=1)
+    sine = jnp.concatenate([-sine_table, sine_table] * 2, axis=1)
     contract_cols = (((1,), (1,)), ((), ()))
     wide = hidden[0].astype(f32)
     cot = cotangent[0]
@@ -1501,24 +1524,19 @@
     experts = experts.reshape(NC, held, quarter, experts.shape[2])
     mine = lax.dynamic_index_in_dim(experts, core, 0, False)
     other = lax.dynamic_index_in_dim(experts, 1 - core, 0, False)
-    far_one, far_two = swap(pack_one, 2), swap(pack_two, 2)
-    far_one, far_two, mine, other = lax.optimization_barrier((far_one, far_two, mine, other))
-    parts = [mine, swap(other, 1), swap(mine, 2), swap(other, 3)]
-    both = lambda near, far: jnp.where(
-        fsdp < NC, jnp.stack([near, far]), jnp.stack([far, near])
-    )
     part = rows // 3
-    groups = ctx_size, NX, NC, rows
+    whole = (Z, Y, X, C)
     one, two = gather(
-        [both(pack_one, far_one), both(pack_two, far_two)],
+        [pack_one, pack_two],
         [
-            Plan(0, (Z, Y, C), (Z, Y, C), rows=(0, 2 * part), view=weight_view),
-            Plan(0, (Y, Z, C), (Z, Y, C), rows=(2 * part, part), view=weight_view),
-            Plan(1, (Z, Y, C), (Z, Y, C), rows=(0, rows), view=weight_view),
+            Plan(0, (X, Z, Y, C), whole, rows=(0, 2 * part)),
+            Plan(0, (X, Y, Z, C), whole, rows=(2 * part, part)),
+            Plan(1, (Z, Y, X, C), whole),
         ],
         0,
-        {0: groups + pack_one.shape[1:], 1: groups + pack_two.shape[1:]},
-    )
+    )
+    one, mine, other = lax.optimization_barrier((one, mine, other))
+    parts = [mine, swap(other, 1), swap(mine, 2), swap(other, 3)]
     one = one.reshape(MODEL_WIDTH, -1)
     two = two.reshape(MODEL_WIDTH, -1)
     output_w = two[:, :MODEL_WIDTH]
@@ -1531,24 +1549,7 @@
 
     attn_unit, inverse_one, attention_input = rms_forward(wide, attn_gain)
     linear = jnp.dot(attention_input, one, preferred_element_type=f32)
-    query_rows = (
-        rotate_pairs(linear[:, :q_width].reshape(tokens, QUERY_HEADS, HEAD_SIZE), cosine_table, sine_table)
-        .astype(bf)
-        .reshape(tokens, q_width)
-    )
-    key_rows = (
-        rotate_pairs(
-            linear[:, q_width : q_width + kv_width].reshape(tokens, KEY_VALUE_HEADS, HEAD_SIZE),
-            cosine_table,
-            sine_table,
-        )
-        .astype(bf)
-        .reshape(tokens, kv_width)
-    )
-    value_rows = linear[:, q_width + kv_width :].astype(bf)
-    attention_output, log_sums, kv, cots = attend(
-        jnp.concatenate([key_rows, value_rows], axis=1), query_rows, cot_pack, 1
-    )
+    attention_output, log_sums, kv, cots, queries = attend(linear, cot_pack, cosine, sine, 1)
     mixed = wide + jnp.dot(attention_output, output_w, preferred_element_type=f32)
     ffn_unit, inverse_two, ffn_in = rms_forward(mixed, ffn_gain)
     logits = jnp.dot(ffn_in, router_w, preferred_element_type=f32)
@@ -1575,26 +1576,9 @@
     attention_output_gradient = lax.dot_general(
         grad_attn, output_w, contract_cols, preferred_element_type=f32
     ).astype(bf)
-    grad_query, local_gradients, layer_out = attend_back(
-        query_rows, attention_output_gradient, attention_output, log_sums, kv, moe_part, mixed, 4
-    )
-    query_back = (
-        rotate_pairs(
-            grad_query.reshape(tokens, QUERY_HEADS, HEAD_SIZE), cosine_table, -sine_table
-        )
-        .astype(bf)
-        .reshape(tokens, q_width)
-    )
-    key_back = (
-        rotate_pairs(
-            local_gradients[:, :kv_width].reshape(tokens, KEY_VALUE_HEADS, HEAD_SIZE),
-            cosine_table,
-            -sine_table,
-        )
-        .astype(bf)
-        .reshape(tokens, kv_width)
-    )
-    back = jnp.concatenate([query_back, key_back, local_gradients[:, kv_width:].astype(bf)], axis=1)
+    back, layer_out = attend_back(
+        queries, attention_output_gradient, attention_output, log_sums, kv, moe_part, mixed, cosine, sine, 4
+    )
     grad_attn_in = lax.dot_general(back, one, contract_cols, preferred_element_type=f32)
     back_one, _ = rms_backward(grad_attn_in, attn_unit, inverse_one, attn_gain)
     grad_input = grad_mixed + back_one

time: 627 us -> 582 us (0.928)
  local copies, waits for them, and re-layouts: 28.6 us -> 13.9 us
  Pallas kernels: 521 us -> 508 us
  other arithmetic: 24.3 us -> 17.9 us
    pallas_call x1, Pallas kernels: 72.1 us -> 64.1 us  [gather(): pl.pallas_call(functools.partial(gather_kernel, plans, n), out_shape=[jax...]
    pallas_call x1, Pallas kernels: 90.7 us -> 82.6 us  [attend_back(): pl.pallas_call(functools.partial(attend_back_kernel, plans), out_shape=[j...]
    slice x8 -> x0, local copies, waits for them, and re-layouts: 6.44 us -> none  [the longest x2 2.51 us: fast_body(): linear[:, q_width:q_width + kv_width]]
  transfers between devices with their start and end apart: 8 -> 6, of which waited for: 1 -> 1; matrix products, arithmetic and copies ran while one was open for 6% -> 4% of each run, Pallas kernels for 38% -> 41%
where the time goes in v7:
time: 582 us; the launch traced here: 576 us
  Pallas kernels  508 us (87%)
  matrix products  24.6 us (4%)
  other arithmetic  17.9 us (3%)
  local copies, waits for them, and re-layouts  13.9 us (2%)
    pallas_call x1, Pallas kernels, return_weights(): pl.pallas_call(functools.partial(weights_kernel, plans), out_shape=[jax.S...  160 us
    pallas_call x1, Pallas kernels, moe(): pl.pallas_call(functools.partial(moe_kernel, plans, back, width, hidden,...  117 us
    pallas_call x1, Pallas kernels, attend_back(): pl.pallas_call(functools.partial(attend_back_kernel, plans), out_shape=[j...  82.6 us
    pallas_call x1, Pallas kernels, attend(): pl.pallas_call(functools.partial(attend_kernel, plans), out_shape=[jax.Sh...  76 us
    pallas_call x1, Pallas kernels, gather(): pl.pallas_call(functools.partial(gather_kernel, plans, n), out_shape=[jax...  64.1 us
  transfers between devices with their start and end apart: 6, of which 1 were waited for; matrix products, arithmetic and copies ran while one was open for 4% of the time, Pallas kernels for 41%

profile of v7, /device:TPU:0, one launch (start us, length us, event | category | flops | bytes accessed | tf_op | source)
XLA Modules:
  0.0 575.7 jit_solution(12233568655437284035)
XLA Ops:
  0.7 0.8 copy.37
  1.4 0.8 copy.38
  2.2 0.8 copy.39
  3.0 5.0 pad_maximum_fusion
  8.0 0.7 pad_maximum_fusion.1.refs_0_
  8.7 0.8 concatenate.31.refs_1_
  9.5 64.1 %shard_map.203 = (bf16[32,48,2560]{2,1,0:T(8,128)(2,1)}, bf16[32,48,1664]{2,1,0:T(8,128)(2,1)}) custom-call(bf16[48,2560]{1,0:T(8,128)(2,1)} %pad_maximum_fusion.1.refs_0_, bf16[48,1664]{1,0:T(8,128)(2,1)} %concatenate.31.refs_1_), custom_call_target="tpu_custom_call" | custom-call | tf_op jit(solution)/shard_map/pallas_call | solution.py:178
  73.6 4.3 dynamic-slice_bitcast_fusion
  77.9 0.5 collective-permute-start
  78.4 0.1 collective-permute-start.2
  78.6 1.5 collective-permute-start.1
  80.1 0.5 multiply_power_fusion
  80.6 1.3 fusion.32
  81.9 0.0 copy-start.13
  81.9 0.0 copy-start.19
  81.9 0.2 fusion.22
  82.1 0.5 add_rsqrt_fusion.1
  82.6 0.8 bitcast_convert_fusion
  83.4 1.0 fusion.42
  84.4 0.0 copy-start.21
  84.4 0.0 copy-start.10
  84.4 5.7 fusion.30.linear
  90.1 0.1 copy.40
  90.3 0.9 concatenate.33.own_cots
  91.1 0.8 pad_maximum_fusion.2
  92.0 76.0 %attend.1 = (bf16[128,1536]{1,0:T(8,128)(2,1)}, f32[384,128]{1,0:T(8,128)}, bf16[8,128,1024]{2,1,0:T(8,128)(2,1)}, bf16[16,128,1664]{2,1,0:T(8,128)(2,1)}, bf16[8,384,128]{2,1,0:T(8,128)(2,1)}) custom-call(f32[128,2560]{1,0:T(8,128)} %fusion.30.linear, bf16[128,1664]{1,0:T(8,128)(2,1)} %concatenate.33.own_cots, ...), custom_call_target="tpu_custom_call" | custom-call | tf_op jit(solution)/shard_map/attend/pallas_call | solution.py:852
  168.0 3.3 multiply_reduce_fusion.1
  171.3 0.0 copy-start
  171.3 0.8 copy-done
  172.2 0.9 constant_dynamic-update-slice_fusion
  173.1 1.3 fusion.38
  174.4 0.5 copy-done.27
  174.9 0.5 copy-done.28
  175.5 0.1 copy.42
  175.6 0.9 concatenate.36.refs_0_
  176.5 0.5 compare_convert_fusion.1
  177.0 0.6 compare_convert_fusion
  177.6 5.3 collective-permute-done.1.refs_4_
  182.9 117.5 %experts.1 = (f32[128,1664]{1,0:T(8,128)}, bf16[16,128,1536]{2,1,0:T(8,128)(2,1)}, bf16[2,384,1536]{2,1,0:T(8,128)(2,1)}, bf16[2,384,1536]{2,1,0:T(8,128)(2,1)},...) custom-call(bf16[128,1664]{1,0:T(8,128)(2,1)} %concatenate.36.refs_0_, ...), custom_call_target="tpu_custom_call" | custom-call | tf_op jit(solution)/shard_map/experts/pallas_call | solution.py:603
  300.4 1.1 slice_add_fusion.1
  301.4 0.1 copy.43
  301.5 0.7 select_reduce_fusion.1
  302.2 0.7 multiply_reduce_fusion.2
  303.0 0.7 subtract_multiply_fusion
  303.7 0.7 select_reduce_fusion
  304.4 0.1 copy.44
  304.5 1.9 multiply_reduce_fusion
  306.5 0.3 fusion.45
  306.7 4.9 fusion.7.refs_1_
  311.6 82.6 %attend_back.1 = (bf16[128,2560]{1,0:T(8,128)(2,1)}, bf16[128,1536]{1,0:T(8,128)(2,1)}) custom-call(bf16[8,384,128]{2,1,0:T(8,128)(2,1)} %get-tuple-element.43.refs_0_, bf16[128,1536]{1,0:T(8,128)(2,1)} %fusion.7.refs_1_, bf16[128,1536]{1,0:T(8,128)(2,1)} %get-tuple-element.44.refs_2_, f32[384,128]{1,0:T(8,128)} %get-tuple-element.49.refs_3_, ...), custom_call_target="tpu_custom_call" | custom-call | tf_op jit(solution)/shard_map/attend_back/pallas_call | solution.py:988
  394.3 6.3 %fusion.16 = (f32[128]{0:T(128)S(1)}, f32[128,1536]{1,0:T(8,128)S(1)}) fusion(bf16[1,128,1536]{2,1,0:T(8,128)(2,1)S(1)} %copy-done.4, f32[1536]{0:T(1024)S(1)} %copy-done.14, f32[128]{0:T(128)S(1)} %copy-done.24, bf16[128,2560]{1,0:T(8,128)(2,1)} %get-tuple-element.53.refs_1_, bf16[1536,2560]{1,0:T(8,128)(2,1)} %bitcast.73), kind=kOutput, calls=%fused_computation.17 | convolution fusion | flops 1007615872 | bytes 9706496 | tf_op jit(solution)/shard_map/dot_general | solution.py:1582
  400.7 0.1 collective-permute-start.3
  400.7 0.6 collective-permute-start.4
  401.4 1.2 collective-permute-start.5
  402.6 0.2 fusion.26
  402.8 0.2 fusion.27
  403.0 0.1 convert_dynamic-update-slice_fusion
  403.2 0.2 fusion.28.refs_4_
  403.3 1.5 fusion.21
  404.9 0.1 copy-done.9
  405.0 159.8 %return_weights.1 = (f32[48,2560]{1,0:T(8,128)}, f32[48,1664]{1,0:T(8,128)}) custom-call(bf16[128,1536]{1,0:T(8,128)(2,1)} %get-tuple-element.110.refs_0_, bf16[128,2560]{1,0:T(8,128)(2,1)} %get-tuple-element.53.refs_1_, bf16[128,1536]{1,0:T(8,128)(2,1)} %get-tuple-element.44.refs_2_, bf16[128,1536]{1,0:T(8,128)(2,1)} %copy-done.11, ...), custom_call_target="tpu_custom_call" | custom-call | tf_op jit(solution)/shard_map/return_weights/pallas_call | solution.py:699
  564.9 8.4 %last_outputs.1 = (f32[2,2,384,1024]{3,2,1,0:T(8,128)}, f32[2,2,384,512]{3,2,1,0:T(8,128)}, f32[48,1536]{1,0:T(8,128)}, f32[48,512]{1,0:T(8,128)}, f32[48,512]{1...) custom-call(s32[1]{0:T(128)} %bitcast.13.core_ref, ...), custom_call_target="tpu_custom_call" | custom-call | tf_op jit(solution)/shard_map/last_outputs/pallas_call | solution.py:1049
  573.3 1.4 copy.45
  574.7 0.7 copy.55
  (76 shorter events, 0.4 us)
Async XLA Ops:
  3.0 5.0 copy-start.17
  3.0 5.0 copy-start.22
  3.0 5.0 copy-start.23
  3.0 5.7 copy-start.18
  73.6 8.3 %copy-start.3 = (bf16[1,128,1536]{2,1,0:T(8,128)(2,1)S(1)}, bf16[1,128,1536]{2,1,0:T(8,128)(2,1)}, u32[]{:S(2)}) copy-start(bf16[1,128,1536]{2,1,0:T(8,128)(2,1)} %param.12) | copy-start | bytes 1179652
  73.6 9.0 %copy-start.6 = (f32[1,128,1536]{2,1,0:T(8,128)S(1)}, f32[1,128,1536]{2,1,0:T(8,128)}, u32[]{:S(2)}) copy-start(f32[1,128,1536]{2,1,0:T(8,128)} %param.23) | copy-start | bytes 2359300
  77.9 12.2 %copy-start.5 = (bf16[2,384,1536]{2,1,0:T(8,128)(2,1)}, bf16[2,384,1536]{2,1,0:T(8,128)(2,1)S(1)}, u32[]{:S(2)}) copy-start(bf16[2,384,1536]{2,1,0:T(8,128)(2,1)S(1)} %get-tuple-element.46.refs_2_) | copy-start | bytes 7077892
  77.9 99.6 %collective-permute-start = (bf16[2,384,1536]{2,1,0:T(8,128)(2,1)}, bf16[2,384,1536]{2,1,0:T(8,128)(2,1)}, u32[]{:S(2)}, u32[]{:S(2)}) collective-permute-start(bf16[2,384,1536]{2,1,0:T(8,128)(2,1)} %get-tuple-element.47), channel_id=1, source_target_pairs={{0,1},{1,0},{2,3},{3,2},{4,5},{5,4},{6,7},{7,6},{8,9},{9,8},{10,11... | collective-permute-start | bytes 7077896 | tf_op jit(solution)/shard_map/ppermute | solution.py:1473
  78.4 104.4 %collective-permute-start.2 = (bf16[2,384,1536]{2,1,0:T(8,128)(2,1)}, bf16[2,384,1536]{2,1,0:T(8,128)(2,1)}, u32[]{:S(2)}, u32[]{:S(2)}) collective-permute-start(bf16[2,384,1536]{2,1,0:T(8,128)(2,1)} %get-tuple-element.47), channel_id=1, source_target_pairs={{0,3},{1,2},{2,1},{3,0},{4,7},{5,6},{6,5},{7,4},{8,11},{9,10},{10,... | collective-permute-start | bytes 7077896 | tf_op jit(solution)/shard_map/ppermute | solution.py:1473
  78.6 104.3 %collective-permute-start.1 = (bf16[2,384,1536]{2,1,0:T(8,128)(2,1)S(1)}, bf16[2,384,1536]{2,1,0:T(8,128)(2,1)}, u32[]{:S(2)}, u32[]{:S(2)}) collective-permute-start(bf16[2,384,1536]{2,1,0:T(8,128)(2,1)S(1)} %get-tuple-element.46.refs_2_), channel_id=1, source_target_pairs={{0,2},{1,3},{2,0},{3,1},{4,6},{5,7},{6,4},{7,5},{8,10},{9,11},{10,... | collective-permute-start | bytes 7077896 | tf_op jit(solution)/shard_map/ppermute | solution.py:1473
  81.9 8.2 %copy-start.13 = (f32[1536]{0:T(1024)}, f32[1536]{0:T(1024)S(1)}, u32[]{:S(2)}) copy-start(f32[1536]{0:T(1024)S(1)} %get-tuple-element.103) | copy-start | bytes 18436
  81.9 89.4 %copy-start.19 = (f32[1536]{0:T(1024)}, f32[1536]{0:T(1024)S(1)}, u32[]{:S(2)}) copy-start(f32[1536]{0:T(1024)S(1)} %get-tuple-element.102) | copy-start | bytes 18436
  84.4 5.7 copy-start.21
  84.4 5.9 %copy-start.10 = (bf16[128,1536]{1,0:T(8,128)(2,1)S(1)}, bf16[128,1536]{1,0:T(8,128)(2,1)}, u32[]{:S(2)}) copy-start(bf16[128,1536]{1,0:T(8,128)(2,1)} %bitcast_convert_fusion) | copy-start | bytes 1179652
  171.3 0.9 copy-start
  171.3 11.6 %copy-start.25 = (f32[128]{0:T(128)}, f32[128]{0:T(128)S(1)}, u32[]{:S(2)}) copy-start(f32[128]{0:T(128)S(1)} %add_rsqrt_fusion) | copy-start | bytes 1540
  174.4 8.5 %copy-start.16 = (f32[128,8]{0,1:T(8,128)}, f32[128,8]{0,1:T(8,128)S(1)}, u32[]{:S(2)}) copy-start(f32[128,8]{0,1:T(8,128)S(1)} %select_reduce_fusion.3) | copy-start | bytes 12292
  174.4 0.5 copy-start.27
  174.9 0.5 copy-start.28
  300.3 6.1 %copy-start.1 = (f32[128,1536]{1,0:T(8,128)S(1)}, f32[128,1536]{1,0:T(8,128)}, u32[]{:S(2)}) copy-start(f32[128,1536]{1,0:T(8,128)} %copy-done) | copy-start | bytes 2359300
  300.3 6.1 %copy-start.7 = (f32[1,128,1536]{2,1,0:T(8,128)S(1)}, f32[1,128,1536]{2,1,0:T(8,128)}, u32[]{:S(2)}) copy-start(f32[1,128,1536]{2,1,0:T(8,128)} %param.23) | copy-start | bytes 2359300
  300.4 6.1 %copy-start.20 = (f32[1536]{0:T(1024)S(1)}, f32[1536]{0:T(1024)}, u32[]{:S(2)}) copy-start(f32[1536]{0:T(1024)} %copy-done.19) | copy-start | bytes 18436
  300.4 6.1 %copy-start.26 = (f32[128]{0:T(128)S(1)}, f32[128]{0:T(128)}, u32[]{:S(2)}) copy-start(f32[128]{0:T(128)} %copy-done.25) | copy-start | bytes 1540
  306.7 4.9 copy-start.11
  311.6 82.7 %copy-start.4 = (bf16[1,128,1536]{2,1,0:T(8,128)(2,1)S(1)}, bf16[1,128,1536]{2,1,0:T(8,128)(2,1)}, u32[]{:S(2)}) copy-start(bf16[1,128,1536]{2,1,0:T(8,128)(2,1)} %param.12) | copy-start | bytes 1179652
  311.6 82.7 %copy-start.14 = (f32[1536]{0:T(1024)S(1)}, f32[1536]{0:T(1024)}, u32[]{:S(2)}) copy-start(f32[1536]{0:T(1024)} %copy-done.13) | copy-start | bytes 18436
  311.6 82.7 %copy-start.24 = (f32[128]{0:T(128)S(1)}, f32[128]{0:T(128)}, u32[]{:S(2)}) copy-start(f32[128]{0:T(128)} %add_rsqrt_fusion.1) | copy-start | bytes 1540
  394.3 6.3 %copy-start.30 = (bf16[128]{0:T(256)(128)(2,1)S(1)}, bf16[128]{0:T(256)(128)(2,1)}, u32[]{:S(2)}) copy-start(bf16[128]{0:T(256)(128)(2,1)} %compare_convert_fusion.1) | copy-start | bytes 772
  394.3 8.3 %copy-start.8 = (bf16[640,1536]{1,0:T(8,128)(2,1)S(1)}, bf16[640,1536]{1,0:T(8,128)(2,1)}, u32[]{:S(2)}) copy-start(bf16[640,1536]{1,0:T(8,128)(2,1)} %get-tuple-element.104) | copy-start | bytes 5898244
  394.3 8.4 %copy-start.29 = (bf16[128]{0:T(256)(128)(2,1)S(1)}, bf16[128]{0:T(256)(128)(2,1)}, u32[]{:S(2)}) copy-start(bf16[128]{0:T(256)(128)(2,1)} %compare_convert_fusion) | copy-start | bytes 772
  400.6 2.4 copy-start.2
  400.7 164.2 %collective-permute-start.3 = (bf16[2,384,1536]{2,1,0:T(8,128)(2,1)}, bf16[2,384,1536]{2,1,0:T(8,128)(2,1)}, u32[]{:S(2)}, u32[]{:S(2)}) collective-permute-start(bf16[2,384,1536]{2,1,0:T(8,128)(2,1)} %get-tuple-element.55), channel_id=1, source_target_pairs={{0,1},{1,0},{2,3},{3,2},{4,5},{5,4},{6,7},{7,6},{8,9},{9,8},{10,11... | collective-permute-start | bytes 7077896 | tf_op jit(solution)/shard_map/ppermute | solution.py:1473
  400.7 164.1 %collective-permute-start.4 = (bf16[2,384,1536]{2,1,0:T(8,128)(2,1)}, bf16[2,384,1536]{2,1,0:T(8,128)(2,1)}, u32[]{:S(2)}, u32[]{:S(2)}) collective-permute-start(bf16[2,384,1536]{2,1,0:T(8,128)(2,1)} %get-tuple-element.56), channel_id=1, source_target_pairs={{0,2},{1,3},{2,0},{3,1},{4,6},{5,7},{6,4},{7,5},{8,10},{9,11},{10,... | collective-permute-start | bytes 7077896 | tf_op jit(solution)/shard_map/ppermute | solution.py:1473
  401.4 163.5 %collective-permute-start.5 = (bf16[2,384,1536]{2,1,0:T(8,128)(2,1)}, bf16[2,384,1536]{2,1,0:T(8,128)(2,1)}, u32[]{:S(2)}, u32[]{:S(2)}) collective-permute-start(bf16[2,384,1536]{2,1,0:T(8,128)(2,1)} %get-tuple-element.57), channel_id=1, source_target_pairs={{0,3},{1,2},{2,1},{3,0},{4,7},{5,6},{6,5},{7,4},{8,11},{9,10},{10,... | collective-permute-start | bytes 7077896 | tf_op jit(solution)/shard_map/ppermute | solution.py:1473
  402.8 2.0 copy-start.15
  403.3 1.7 copy-start.9
  564.9 9.8 %copy-start.12 = (bf16[128,1536]{1,0:T(8,128)(2,1)S(1)}, bf16[128,1536]{1,0:T(8,128)(2,1)}, u32[]{:S(2)}) copy-start(bf16[128,1536]{1,0:T(8,128)(2,1)} %get-tuple-element.52) | copy-start | bytes 1179652

commit v8 on v7

--- a/solution.py
+++ b/solution.py
@@ -107,9 +107,23 @@
 
 
 def gather_kernel(plans, n_in, *refs):
-    ins, outs = refs[:n_in], refs[n_in : 2 * n_in]
-    send_sem, recv_sem, own_sem = refs[2 * n_in :]
+    ins, (first_w, second_w), outs = refs[:n_in], refs[n_in : n_in + 2], refs[n_in + 2 : 2 * n_in + 2]
+    mine, other, send_sem, recv_sem, own_sem, stage, load_sem, store_sem = refs[2 * n_in + 2 :]
     place = Place()
+    held = mine.shape[0]
+    split = first_w.shape[2]
+    loads = []
+    for side in range(2):
+        base = (place.at[C] if side == 0 else 1 - place.at[C]) * held
+        for e in range(held):
+            to = stage.at[side * held + e]
+            for w, at in ((first_w, pl.ds(0, split)), (second_w, pl.ds(split, second_w.shape[2]))):
+                loads.append(pltpu.make_async_copy(w.at[base + e], to.at[:, at], load_sem.at[len(loads)]))
+    for copy in loads:
+        copy.start()
+    stores = [
+        pltpu.make_async_copy(stage.at[pl.ds(n * held, held)], out, store_sem.at[n]) for n, out in enumerate((mine, other))
+    ]
     z = place.at[Z]
     greet(place, sorted({d for p in plans for d in p.order}))
     pending = []
@@ -120,7 +134,12 @@
             queue.append((rank / len(gather_events(plan.order)), n, event))
     queue.sort(key=lambda q: (q[0], q[1]))
     bases = [sum(p.blocks for p in plans[:n]) for n in range(len(plans))]
-    for _, n, (k, flips) in queue:
+    for turn_at, (_, n, (k, flips)) in enumerate(queue):
+        if turn_at == len(queue) // 3:
+            for copy in loads:
+                copy.wait()
+            for copy in stores:
+                copy.start()
         plan = plans[n]
         src = ins[plan.ref]
         out = outs[plan.ref]
@@ -164,6 +183,8 @@
             copy = pltpu.make_async_copy(source, target, own_sem.at[1 + n])
             copy.start()
             pending.append((None, copy.wait))
+    for copy in stores:
+        copy.wait()
     for go, wait in pending:
         if go is None:
             wait()
@@ -171,25 +192,31 @@
             pl.when(go)(wait)
 
 
-def gather(arrays, plans, collective_id, shapes=None):
+def gather_weights(arrays, experts, plans, collective_id):
     n = len(arrays)
     sends = sum(len(gather_sends(p.order, k, f)) for p in plans for k, f in gather_events(p.order))
     blocks = {p.ref: p.blocks for p in plans}
+    held = experts[0].shape[0] // NC
+    pack = (held, experts[0].shape[1], experts[0].shape[2] + experts[1].shape[2])
+    apart = pl.BlockSpec(memory_space=pl.ANY)
+    dma = pltpu.SemaphoreType.DMA
     return pl.pallas_call(
         functools.partial(gather_kernel, plans, n),
-        out_shape=[
-            jax.ShapeDtypeStruct((shapes or {}).get(i, (blocks[i],) + a.shape), a.dtype)
-            for i, a in enumerate(arrays)
-        ],
-        in_specs=[pl.BlockSpec(memory_space=pltpu.VMEM)] * n,
-        out_specs=[pl.BlockSpec(memory_space=pl.ANY)] * n,
+        out_shape=[jax.ShapeDtypeStruct((blocks[i],) + a.shape, a.dtype) for i, a in enumerate(arrays)]
+        + [jax.ShapeDtypeStruct(pack, experts[0].dtype)] * 2,
+        in_specs=[pl.BlockSpec(memory_space=pltpu.VMEM)] * n + [apart] * 2,
+        out_specs=[apart] * (n + 2),
         scratch_shapes=[
-            pltpu.SemaphoreType.DMA((sends,)),
-            pltpu.SemaphoreType.DMA((sum(p.blocks for p in plans),)),
-            pltpu.SemaphoreType.DMA((1 + len(plans),)),
+            dma((sends,)),
+            dma((sum(p.blocks for p in plans),)),
+            dma((1 + len(plans),)),
+            pltpu.VMEM((NC * held,) + pack[1:], experts[0].dtype),
+            dma((2 * NC * held,)),
+            dma((2,)),
         ],
         compiler_params=pltpu.CompilerParams(collective_id=collective_id, has_side_effects=True),
-    )(*arrays)
+        name="gather_weights",
+    )(*arrays, *experts)
 
 
 def add_into(acc, other):
@@ -429,9 +456,11 @@
     pick_lane = lax.broadcasted_iota(jnp.int32, (NY * count, lanes), 1).astype(f32)
     y_shift = (lax.broadcasted_iota(jnp.int32, (NY * count, 1), 0) // count * cap).astype(f32)
 
+    row_of = lambda h, k: (k * NC + h) * pair
+
     def dispatch(source, target, h, k, cols):
         at = pl.ds(base_of(h, k), NY)
-        r = (h * NZ + k) * pair
+        r = row_of(h, k)
         for c0, cn in cols:
             block = source[at, :, c0 : c0 + cn].reshape(NY * count, cn)
             got = lax.dot_general(
@@ -474,13 +503,21 @@
         grad_act[e, rows, hidden + col : hidden + col + tile] = (grad_inner * gs).astype(bf)
         return jnp.sum(raw * inner, axis=1, keepdims=True)
 
-    def hidden_part(h, e):
-        tile = min(256, hidden)
-        gate_grad = sum(hidden_chunk(h, e, n, tile) for n in range(hidden // tile))
-        high = gate_grad.astype(bf).astype(f32)
-        there = pl.ds(h * half, half)
-        apart = (lane_id == EXPERT_COUNT + first + e).astype(f32)
-        rows_buf[e, there, width:wide] = (high * here[e] + (gate_grad - high) * apart).astype(bf)
+    tile = min(256, hidden)
+    found = {}
+
+    def hidden_step(h, e, n):
+        got = hidden_chunk(h, e, n, tile)
+        found[(h, e)] = got if n == 0 else found[(h, e)] + got
+        if n == hidden // tile - 1:
+            gate_grad = found.pop((h, e))
+            high = gate_grad.astype(bf).astype(f32)
+            there = pl.ds(h * half, half)
+            apart = (lane_id == EXPERT_COUNT + first + e).astype(f32)
+            rows_buf[e, there, width:wide] = (high * here[e] + (gate_grad - high) * apart).astype(bf)
+
+    def hidden_steps(h):
+        return [functools.partial(hidden_step, h, e, n) for e in range(held) for n in range(hidden // tile)]
 
     def project(h, e, left, weight_cols):
         rows = pl.ds(h * half, half)
@@ -492,7 +529,7 @@
 
     def combine(target, h, k, cols):
         at = pl.ds(base_of(h, k), NY)
-        r = (h * NZ + k) * pair
+        r = row_of(h, k)
         for c0, cn in cols:
             parts = [rows_buf[e, r : r + pair, c0 : c0 + cn] for e in range(held)]
             if lanes > held * pair:
@@ -522,6 +559,12 @@
     all_cols = columns_of(width) + [(width, 128)]
     ready = {(h, k): 0 for h in range(NC) for k in range(NZ)}
     ready[(0, 0)] = 1
+    near_begun = False
+
+    def wait_weights():
+        for copy in loads:
+            copy.wait()
+
     for k, flips in gather_events(plans[0].order)[1:]:
         for way in ways:
             way.step(k, flips)
@@ -529,29 +572,39 @@
         ready[key] += 1
         if ready[key] == NY:
             work.append(functools.partial(dispatch, seen, taken, *key, all_cols))
+            if all(ready[(g, n)] == NY for g in range(NC) for n in range(NZ // 2)) and not near_begun:
+                near_begun = True
+                work += [wait_weights] + hidden_steps(0)
         for _ in range(min(len(work), 1 if k < NZ - 1 else 2)):
             work.pop(0)()
     for chunk in work:
         chunk()
-    for copy in loads:
-        copy.wait()
-    for h in range(NC):
-        for e in range(held):
-            hidden_part(h, e)
-    for way in ways:
-        way.finish()
+    for chunk in hidden_steps(1):
+        chunk()
 
     far = list(reversed(range(NZ)))
     spare = spare_sem
     in_way = Reduce(place, back, cot_seen, (lvl_b0, lvl_b1), chain_b, send_b, recv_b, spare)
     in_steps = in_way.steps()
-    for h in reversed(range(NC)):
-        for e in range(held):
-            project(h, e, grad_act, (0, 2 * hidden))
-        for k in far:
-            combine(cot_seen, h, k, all_cols)
-            if h == 1:
-                in_way.first(k)
+    for e in range(held):
+        project(1, e, grad_act, (0, 2 * hidden))
+    for k in far[: NZ // 2]:
+        combine(cot_seen, 1, k, all_cols)
+        in_way.first(k)
+    for k in far[: NZ // 2]:
+        combine(cot_seen, 0, k, all_cols)
+    in_steps.pop(0)()
+    for e in range(held):
+        project(0, e, grad_act, (0, 2 * hidden))
+    in_steps.pop(0)()
+    for k in far[NZ // 2 :]:
+        combine(cot_seen, 1, k, all_cols)
+        in_way.first(k)
+    in_steps.pop(0)()
+    for k in far[NZ // 2 :]:
+        combine(cot_seen, 0, k, all_cols)
+    for way in ways:
+        way.finish()
     part_copies = []
     work = []
 
@@ -562,11 +615,12 @@
         copy.start()
         part_copies.append(copy)
 
-    for h in range(NC):
+    for n in range(2):
         for e in range(held):
-            work.append(functools.partial(project, h, e, scaled, (2 * hidden, hidden)))
-        for k in range(NZ):
-            work.append(functools.partial(out_part, h, k))
+            work.append(functools.partial(project, n, e, scaled, (2 * hidden, hidden)))
+        for k in range(n * NZ // 2, (n + 1) * NZ // 2):
+            for h in range(NC):
+                work.append(functools.partial(out_part, h, k))
     work += [functools.partial(weight_grad, e, j) for j in reversed(range(NX * NC)) for e in range(held)]
     while in_steps or work:
         if in_steps:
@@ -766,7 +820,7 @@
 
 
 def attend_kernel(
-    plans, linear, own_cots, cosine, sine, out, log_sums, kv_out, cots, placed, seen, own_kv, raw, *sems
+    plans, linear, cot, routes, cosine, sine, out, log_sums, kv_out, cots, placed, seen, own_kv, own_cots, raw, *sems
 ):
     send_kv, recv_kv, send_cot, recv_cot, spare, own_sem = sems
     place = Place()
@@ -778,6 +832,13 @@
         block = linear[:, q_width + c0 : q_width + c0 + 128]
         own_kv[:, c0 : c0 + 128] = turn(block, cosine[...], sine[...]).astype(bf)
     own_kv[:, width:] = linear[:, q_width + width :].astype(bf)
+    model = cot.shape[1]
+    own_cots[:, :model] = cot[...].astype(bf)
+    expert = lax.broadcasted_iota(jnp.int32, (1, 128), 1)
+    routed = routes[:, 0:1] == expert
+    for n in range(1, routes.shape[1]):
+        routed = jnp.logical_or(routed, routes[:, n : n + 1] == expert)
+    own_cots[:, model:] = routed.astype(f32).astype(bf)
     greet(place, (Z, Y, C))
     kv_way = Gather(place, plans[0], own_kv, seen, send_kv, recv_kv, spare, 0, 0)
     cot_ways, at = [], 0
@@ -833,7 +894,7 @@
         way.finish()
 
 
-def attend(linear, own_cots, cosine, sine, collective_id):
+def attend(linear, cot, routes, cosine, sine, collective_id):
     count = linear.shape[0]
     kv_width = 2 * KEY_VALUE_HEADS * HEAD_SIZE
     cut = count * 3 // 4
@@ -848,6 +909,7 @@
     apart = pl.BlockSpec(memory_space=pl.ANY)
     dma = pltpu.SemaphoreType.DMA
     kv_shape = (plans[0].blocks, count, kv_width)
+    cot_shape = (count, cot.shape[1] + 128)
     heads = (KEY_VALUE_HEADS, group * count, 2 * HEAD_SIZE)
     return pl.pallas_call(
         functools.partial(attend_kernel, plans),
@@ -855,12 +917,17 @@
             jax.ShapeDtypeStruct((count, QUERY_HEADS * HEAD_SIZE), bf),
             jax.ShapeDtypeStruct((group * count, 128), f32),
             jax.ShapeDtypeStruct(kv_shape, bf),
-            jax.ShapeDtypeStruct((plans[1].blocks,) + own_cots.shape, bf),
+            jax.ShapeDtypeStruct((plans[1].blocks,) + cot_shape, bf),
             jax.ShapeDtypeStruct(heads, bf),
         ],
-        in_specs=[vmem] * 4,
+        in_specs=[vmem] * 5,
         out_specs=[vmem, vmem, apart, apart, vmem],
-        scratch_shapes=[pltpu.VMEM(kv_shape, bf), pltpu.VMEM((count, kv_width), bf), pltpu.VMEM(heads, f32)]
+        scratch_shapes=[
+            pltpu.VMEM(kv_shape, bf),
+            pltpu.VMEM((count, kv_width), bf),
+            pltpu.VMEM(cot_shape, bf),
+            pltpu.VMEM(heads, f32),
+        ]
         + [
             dma((Gather.sends(plans[0]),)),
             dma((plans[0].blocks,)),
@@ -873,7 +940,7 @@
             collective_id=collective_id, has_side_effects=True, vmem_limit_bytes=56 * 1024 * 1024
         ),
         name="attend",
-    )(linear, own_cots, cosine, sine)
+    )(linear, cot, routes, cosine, sine)
 
 
 def attend_back_kernel(plans, *refs):
@@ -1512,22 +1579,11 @@
     )
     route = routes[0]
     indicator = (route[:, :, None] == jnp.arange(EXPERT_COUNT, dtype=jnp.int32)).astype(f32)
-    cot_pack = jnp.concatenate(
-        [
-            cot.astype(bf),
-            jnp.sum(indicator, axis=1).astype(bf),
-            jnp.zeros((tokens, 128 - EXPERT_COUNT), bf),
-        ],
-        axis=1,
-    )
-    experts = jnp.concatenate([expert_in, expert_out], axis=2)
-    experts = experts.reshape(NC, held, quarter, experts.shape[2])
-    mine = lax.dynamic_index_in_dim(experts, core, 0, False)
-    other = lax.dynamic_index_in_dim(experts, 1 - core, 0, False)
     part = rows // 3
     whole = (Z, Y, X, C)
-    one, two = gather(
+    one, two, mine, other = gather_weights(
         [pack_one, pack_two],
+        [expert_in, expert_out],
         [
             Plan(0, (X, Z, Y, C), whole, rows=(0, 2 * part)),
             Plan(0, (X, Y, Z, C), whole, rows=(2 * part, part)),
@@ -1535,7 +1591,6 @@
         ],
         0,
     )
-    one, mine, other = lax.optimization_barrier((one, mine, other))
     parts = [mine, swap(other, 1), swap(mine, 2), swap(other, 3)]
     one = one.reshape(MODEL_WIDTH, -1)
     two = two.reshape(MODEL_WIDTH, -1)
@@ -1549,7 +1604,7 @@
 
     attn_unit, inverse_one, attention_input = rms_forward(wide, attn_gain)
     linear = jnp.dot(attention_input, one, preferred_element_type=f32)
-    attention_output, log_sums, kv, cots, queries = attend(linear, cot_pack, cosine, sine, 1)
+    attention_output, log_sums, kv, cots, queries = attend(linear, cot, route, cosine, sine, 1)
     mixed = wide + jnp.dot(attention_output, output_w, preferred_element_type=f32)
     ffn_unit, inverse_two, ffn_in = rms_forward(mixed, ffn_gain)
     logits = jnp.dot(ffn_in, router_w, preferred_element_type=f32)

time: 582 us -> 573 us (0.985)
  other arithmetic: 17.9 us -> 11.4 us
  transfers between devices with their start and end apart: 6 -> 6, of which waited for: 1 -> 1; matrix products, arithmetic and copies ran while one was open for 4% -> 3% of each run, Pallas kernels for 41% -> 42%
where the time goes in v8:
time: 573 us; the launch traced here: 566 us
  Pallas kernels  506 us (88%)
  matrix products  24.5 us (4%)
  other arithmetic  11.4 us (2%)
  local copies, waits for them, and re-layouts  10.4 us (2%)
  waiting for transfers between devices  7.83 us (1%)
    pallas_call x1, Pallas kernels, return_weights(): pl.pallas_call(functools.partial(weights_kernel, plans), out_shape=[jax.S...  160 us
    pallas_call x1, Pallas kernels, moe(): pl.pallas_call(functools.partial(moe_kernel, plans, back, width, hidden,...  115 us
    pallas_call x1, Pallas kernels, attend_back(): pl.pallas_call(functools.partial(attend_back_kernel, plans), out_shape=[j...  82.9 us
    pallas_call x1, Pallas kernels, attend(): pl.pallas_call(functools.partial(attend_kernel, plans), out_shape=[jax.Sh...  76.2 us
    pallas_call x1, Pallas kernels, gather_weights(): pl.pallas_call(functools.partial(gather_kernel, plans, n), out_shape=[jax...  64.2 us
  transfers between devices with their start and end apart: 6, of which 1 were waited for; matrix products, arithmetic and copies ran while one was open for 3% of the time, Pallas kernels for 42%

profile of v8, /device:TPU:0, one launch (start us, length us, event | category | flops | bytes accessed | tf_op | source)
XLA Modules:
  0.0 566.5 jit_solution(3368399035206777519)
XLA Ops:
  0.6 0.8 copy.38
  1.4 0.8 copy.39
  2.2 0.8 copy.40
  2.9 1.7 pad_maximum_fusion.refs_0_
  4.6 1.7 concatenate.25.refs_1_
  6.3 64.2 %gather_weights.1 = (bf16[32,48,2560]{2,1,0:T(8,128)(2,1)}, bf16[32,48,1664]{2,1,0:T(8,128)(2,1)}, bf16[2,384,1536]{2,1,0:T(8,128)(2,1)}, bf16[2,384,1536]{2,1,0:T(8,128)(2,1)}) custom-call(bf16[48,2560]{1,0:T(8,128)(2,1)} %pad_maximum_fusion.refs_0_, bf16[48,1664]{1,0:T(8,128)(2,1)} %concatenate.25.refs_1_, bf16[4,384,1024]{2,1,0:T(8,128)(2,1)} %refs_2_.1, ...), custom_call_target="tpu_custom_call" | custom-call | tf_op jit(solution)/shard_map/gather_weights/pallas_call | solution.py:203
  70.5 0.6 collective-permute-start
  71.1 0.2 collective-permute-start.2
  71.3 1.5 collective-permute-start.1
  72.8 1.3 fusion.32
  74.2 0.0 copy-start.10
  74.2 0.0 copy-start.14
  74.2 0.2 fusion.22
  74.4 0.6 copy-done.17
  75.0 5.6 fusion.30.linear
  80.5 0.3 fusion.42
  80.9 0.7 copy.41
  81.6 0.8 pad_maximum_fusion.1
  82.4 76.2 %attend.1 = (bf16[128,1536]{1,0:T(8,128)(2,1)}, f32[384,128]{1,0:T(8,128)}, bf16[8,128,1024]{2,1,0:T(8,128)(2,1)}, bf16[16,128,1664]{2,1,0:T(8,128)(2,1)}, bf16[8,384,128]{2,1,0:T(8,128)(2,1)}) custom-call(f32[128,2560]{1,0:T(8,128)} %fusion.30.linear, f32[128,1536]{1,0:T(8,128)} %bitcast.69, s32[128,8]{1,0:T(8,128)} %bitcast.76, ...), custom_call_target="tpu_custom_call" | custom-call | tf_op jit(solution)/shard_map/attend/pallas_call | solution.py:914
  158.6 3.3 multiply_reduce_fusion.1
  161.9 0.0 copy-start
  162.0 0.0 copy-start.19
  162.0 0.8 copy-done
  162.8 0.9 constant_dynamic-update-slice_fusion
  163.7 1.3 fusion.38
  165.1 0.5 copy-done.21
  165.6 0.0 copy-done.22
  165.6 0.1 copy.44
  165.7 0.9 concatenate.28.refs_0_
  166.6 0.5 compare_convert_fusion.1
  167.1 0.6 compare_convert_fusion
  167.7 7.8 %collective-permute-done.1.refs_4_ = bf16[2,384,1536]{2,1,0:T(8,128)(2,1)} collective-permute-done((bf16[2,384,1536]{2,1,0:T(8,128)(2,1)}, bf16[2,384,1536]{2,1,0:T(8,128)(2,1)}, u32[]{:S(2)}, u32[]{:S(2)}) %collective-permute-start.1) | collective-permute-done | bytes 2359328 | tf_op jit(solution)/shard_map/ppermute | solution.py:1540
  175.5 114.6 %experts.1 = (f32[128,1664]{1,0:T(8,128)}, bf16[16,128,1536]{2,1,0:T(8,128)(2,1)}, bf16[2,384,1536]{2,1,0:T(8,128)(2,1)}, bf16[2,384,1536]{2,1,0:T(8,128)(2,1)},...) custom-call(bf16[128,1664]{1,0:T(8,128)(2,1)} %concatenate.28.refs_0_, ...), custom_call_target="tpu_custom_call" | custom-call | tf_op jit(solution)/shard_map/experts/pallas_call | solution.py:657
  290.2 0.0 copy-start.5
  290.2 0.0 copy-start.15
  290.2 1.1 slice_add_fusion.1
  291.3 0.1 copy.45
  291.3 0.7 select_reduce_fusion.1
  292.1 0.7 multiply_reduce_fusion.2
  292.8 0.7 subtract_multiply_fusion
  293.5 0.7 select_reduce_fusion
  294.2 0.1 copy.46
  294.3 1.9 multiply_reduce_fusion
  296.3 0.3 fusion.45
  296.6 4.9 fusion.7.refs_1_
  301.5 82.9 %attend_back.1 = (bf16[128,2560]{1,0:T(8,128)(2,1)}, bf16[128,1536]{1,0:T(8,128)(2,1)}) custom-call(bf16[8,384,128]{2,1,0:T(8,128)(2,1)} %get-tuple-element.41.refs_0_, bf16[128,1536]{1,0:T(8,128)(2,1)} %fusion.7.refs_1_, bf16[128,1536]{1,0:T(8,128)(2,1)} %get-tuple-element.42.refs_2_, f32[384,128]{1,0:T(8,128)} %get-tuple-element.47.refs_3_, ...), custom_call_target="tpu_custom_call" | custom-call | tf_op jit(solution)/shard_map/attend_back/pallas_call | solution.py:1055
  384.5 0.0 copy-start.6
  384.5 6.3 %fusion.16 = (f32[128]{0:T(128)S(1)}, f32[128,1536]{1,0:T(8,128)S(1)}) fusion(bf16[1,128,1536]{2,1,0:T(8,128)(2,1)S(1)} %copy-done.4, f32[1536]{0:T(1024)S(1)} %copy-done.11, f32[128]{0:T(128)S(1)} %copy-done.18, bf16[128,2560]{1,0:T(8,128)(2,1)} %get-tuple-element.51.refs_1_, bf16[1536,2560]{1,0:T(8,128)(2,1)} %bitcast.68), kind=kOutput, calls=%fused_computation.14 | convolution fusion | flops 1007615872 | bytes 9706496 | tf_op jit(solution)/shard_map/dot_general | solution.py:1637
  390.8 0.0 copy-start.2
  390.8 0.1 collective-permute-start.3
  390.9 0.5 collective-permute-start.4
  391.4 1.3 collective-permute-start.5
  392.7 0.2 fusion.26
  393.0 0.0 copy-start.12
  393.0 0.2 fusion.27
  393.2 0.1 convert_dynamic-update-slice_fusion
  393.3 0.2 fusion.28.refs_4_
  393.5 0.1 copy-done.12
  393.6 1.5 fusion.21
  395.2 0.1 copy-done.7
  395.3 160.1 %return_weights.1 = (f32[48,2560]{1,0:T(8,128)}, f32[48,1664]{1,0:T(8,128)}) custom-call(bf16[128,1536]{1,0:T(8,128)(2,1)} %get-tuple-element.106.refs_0_, bf16[128,2560]{1,0:T(8,128)(2,1)} %get-tuple-element.51.refs_1_, bf16[128,1536]{1,0:T(8,128)(2,1)} %get-tuple-element.42.refs_2_, bf16[128,1536]{1,0:T(8,128)(2,1)} %copy-done.8, ...), custom_call_target="tpu_custom_call" | custom-call | tf_op jit(solution)/shard_map/return_weights/pallas_call | solution.py:753
  555.5 8.4 %last_outputs.1 = (f32[2,2,384,1024]{3,2,1,0:T(8,128)}, f32[2,2,384,512]{3,2,1,0:T(8,128)}, f32[48,1536]{1,0:T(8,128)}, f32[48,512]{1,0:T(8,128)}, f32[48,512]{1...) custom-call(s32[1]{0:T(128)} %bitcast.11.core_ref, ...), custom_call_target="tpu_custom_call" | custom-call | tf_op jit(solution)/shard_map/last_outputs/pallas_call | solution.py:1116
  563.9 1.4 copy.47
  565.3 0.7 copy.58
  (59 shorter events, 0.3 us)
Async XLA Ops:
  6.3 67.9 %copy-start.3 = (bf16[1,128,1536]{2,1,0:T(8,128)(2,1)S(1)}, bf16[1,128,1536]{2,1,0:T(8,128)(2,1)}, u32[]{:S(2)}) copy-start(bf16[1,128,1536]{2,1,0:T(8,128)(2,1)} %param.12) | copy-start | bytes 1179652
  70.5 97.2 %collective-permute-start = (bf16[2,384,1536]{2,1,0:T(8,128)(2,1)}, bf16[2,384,1536]{2,1,0:T(8,128)(2,1)}, u32[]{:S(2)}, u32[]{:S(2)}) collective-permute-start(bf16[2,384,1536]{2,1,0:T(8,128)(2,1)} %get-tuple-element.45), channel_id=1, source_target_pairs={{0,1},{1,0},{2,3},{3,2},{4,5},{5,4},{6,7},{7,6},{8,9},{9,8},{10,11... | collective-permute-start | bytes 7077896 | tf_op jit(solution)/shard_map/ppermute | solution.py:1540
  71.1 104.4 %collective-permute-start.2 = (bf16[2,384,1536]{2,1,0:T(8,128)(2,1)}, bf16[2,384,1536]{2,1,0:T(8,128)(2,1)}, u32[]{:S(2)}, u32[]{:S(2)}) collective-permute-start(bf16[2,384,1536]{2,1,0:T(8,128)(2,1)} %get-tuple-element.45), channel_id=1, source_target_pairs={{0,3},{1,2},{2,1},{3,0},{4,7},{5,6},{6,5},{7,4},{8,11},{9,10},{10,... | collective-permute-start | bytes 7077896 | tf_op jit(solution)/shard_map/ppermute | solution.py:1540
  71.3 104.2 %collective-permute-start.1 = (bf16[2,384,1536]{2,1,0:T(8,128)(2,1)}, bf16[2,384,1536]{2,1,0:T(8,128)(2,1)}, u32[]{:S(2)}, u32[]{:S(2)}) collective-permute-start(bf16[2,384,1536]{2,1,0:T(8,128)(2,1)} %get-tuple-element.44.refs_2_), channel_id=1, source_target_pairs={{0,2},{1,3},{2,0},{3,1},{4,6},{5,7},{6,4},{7,5},{8,10},{9,11},{10,... | collective-permute-start | bytes 7077896 | tf_op jit(solution)/shard_map/ppermute | solution.py:1540
  74.2 6.4 %copy-start.10 = (f32[1536]{0:T(1024)}, f32[1536]{0:T(1024)S(1)}, u32[]{:S(2)}) copy-start(f32[1536]{0:T(1024)S(1)} %get-tuple-element.101) | copy-start | bytes 18436
  74.2 87.8 %copy-start.14 = (f32[1536]{0:T(1024)}, f32[1536]{0:T(1024)S(1)}, u32[]{:S(2)}) copy-start(f32[1536]{0:T(1024)S(1)} %get-tuple-element.100) | copy-start | bytes 18436
  74.4 0.6 copy-start.17
  75.0 5.9 %copy-start.16 = (s32[1,128,8]{1,2,0:T(8,128)S(1)}, s32[1,128,8]{1,2,0:T(8,128)}, u32[]{:S(2)}) copy-start(s32[1,128,8]{1,2,0:T(8,128)} %param.13) | copy-start | bytes 12292
  161.9 0.9 copy-start
  162.0 3.0 copy-start.19
  165.0 1.6 copy-start.13
  165.0 0.5 copy-start.21
  165.1 0.5 copy-start.22
  290.2 6.1 %copy-start.1 = (f32[128,1536]{1,0:T(8,128)S(1)}, f32[128,1536]{1,0:T(8,128)}, u32[]{:S(2)}) copy-start(f32[128,1536]{1,0:T(8,128)} %copy-done) | copy-start | bytes 2359300
  290.2 6.1 %copy-start.5 = (f32[1,128,1536]{2,1,0:T(8,128)S(1)}, f32[1,128,1536]{2,1,0:T(8,128)}, u32[]{:S(2)}) copy-start(f32[1,128,1536]{2,1,0:T(8,128)} %param.23) | copy-start | bytes 2359300
  290.2 6.1 %copy-start.15 = (f32[1536]{0:T(1024)S(1)}, f32[1536]{0:T(1024)}, u32[]{:S(2)}) copy-start(f32[1536]{0:T(1024)} %copy-done.14) | copy-start | bytes 18436
  290.2 6.1 %copy-start.20 = (f32[128]{0:T(128)S(1)}, f32[128]{0:T(128)}, u32[]{:S(2)}) copy-start(f32[128]{0:T(128)} %copy-done.19) | copy-start | bytes 1540
  296.6 4.9 copy-start.8
  301.4 83.0 %copy-start.4 = (bf16[1,128,1536]{2,1,0:T(8,128)(2,1)S(1)}, bf16[1,128,1536]{2,1,0:T(8,128)(2,1)}, u32[]{:S(2)}) copy-start(bf16[1,128,1536]{2,1,0:T(8,128)(2,1)} %param.12) | copy-start | bytes 1179652
  301.4 83.0 %copy-start.11 = (f32[1536]{0:T(1024)S(1)}, f32[1536]{0:T(1024)}, u32[]{:S(2)}) copy-start(f32[1536]{0:T(1024)} %copy-done.10) | copy-start | bytes 18436
  301.5 83.0 %copy-start.18 = (f32[128]{0:T(128)S(1)}, f32[128]{0:T(128)}, u32[]{:S(2)}) copy-start(f32[128]{0:T(128)} %copy-done.17) | copy-start | bytes 1540
  384.4 6.3 %copy-start.24 = (bf16[128]{0:T(256)(128)(2,1)S(1)}, bf16[128]{0:T(256)(128)(2,1)}, u32[]{:S(2)}) copy-start(bf16[128]{0:T(256)(128)(2,1)} %compare_convert_fusion.1) | copy-start | bytes 772
  384.5 8.3 %copy-start.6 = (bf16[640,1536]{1,0:T(8,128)(2,1)S(1)}, bf16[640,1536]{1,0:T(8,128)(2,1)}, u32[]{:S(2)}) copy-start(bf16[640,1536]{1,0:T(8,128)(2,1)} %get-tuple-element.102) | copy-start | bytes 5898244
  384.5 8.4 %copy-start.23 = (bf16[128]{0:T(256)(128)(2,1)S(1)}, bf16[128]{0:T(256)(128)(2,1)}, u32[]{:S(2)}) copy-start(bf16[128]{0:T(256)(128)(2,1)} %compare_convert_fusion) | copy-start | bytes 772
  390.8 2.4 copy-start.2
  390.8 164.6 %collective-permute-start.3 = (bf16[2,384,1536]{2,1,0:T(8,128)(2,1)}, bf16[2,384,1536]{2,1,0:T(8,128)(2,1)}, u32[]{:S(2)}, u32[]{:S(2)}) collective-permute-start(bf16[2,384,1536]{2,1,0:T(8,128)(2,1)} %get-tuple-element.53), channel_id=1, source_target_pairs={{0,1},{1,0},{2,3},{3,2},{4,5},{5,4},{6,7},{7,6},{8,9},{9,8},{10,11... | collective-permute-start | bytes 7077896 | tf_op jit(solution)/shard_map/ppermute | solution.py:1540
  390.9 164.5 %collective-permute-start.4 = (bf16[2,384,1536]{2,1,0:T(8,128)(2,1)}, bf16[2,384,1536]{2,1,0:T(8,128)(2,1)}, u32[]{:S(2)}, u32[]{:S(2)}) collective-permute-start(bf16[2,384,1536]{2,1,0:T(8,128)(2,1)} %get-tuple-element.54), channel_id=1, source_target_pairs={{0,2},{1,3},{2,0},{3,1},{4,6},{5,7},{6,4},{7,5},{8,10},{9,11},{10,... | collective-permute-start | bytes 7077896 | tf_op jit(solution)/shard_map/ppermute | solution.py:1540
  391.4 164.0 %collective-permute-start.5 = (bf16[2,384,1536]{2,1,0:T(8,128)(2,1)}, bf16[2,384,1536]{2,1,0:T(8,128)(2,1)}, u32[]{:S(2)}, u32[]{:S(2)}) collective-permute-start(bf16[2,384,1536]{2,1,0:T(8,128)(2,1)} %get-tuple-element.55), channel_id=1, source_target_pairs={{0,3},{1,2},{2,1},{3,0},{4,7},{5,6},{6,5},{7,4},{8,11},{9,10},{10,... | collective-permute-start | bytes 7077896 | tf_op jit(solution)/shard_map/ppermute | solution.py:1540
  393.0 0.7 copy-start.12
  393.6 1.7 copy-start.7
  555.4 9.8 %copy-start.9 = (bf16[128,1536]{1,0:T(8,128)(2,1)S(1)}, bf16[128,1536]{1,0:T(8,128)(2,1)}, u32[]{:S(2)}) copy-start(bf16[128,1536]{1,0:T(8,128)(2,1)} %get-tuple-element.50) | copy-start | bytes 1179652

commit v9 on v8

--- a/solution.py
+++ b/solution.py
@@ -67,7 +67,7 @@
     return [c for n in range(len(dims) + 1) for c in itertools.combinations(dims, n)]
 
 
-def greet(place, dims):
+def greet(place, dims, more=()):
     barrier = pltpu.get_barrier_semaphore()
     z = place.at[Z]
     count = jnp.int32(0)
@@ -85,6 +85,9 @@
         else:
             pl.semaphore_signal(barrier, inc=1, device_id=place.across(d), device_id_type=DEV)
             count = count + 1
+    for device in more:
+        pl.semaphore_signal(barrier, inc=1, device_id=device, device_id_type=DEV)
+        count = count + 1
     pl.semaphore_wait(barrier, count)
 
 
@@ -106,9 +109,11 @@
     return out
 
 
-def gather_kernel(plans, n_in, *refs):
-    ins, (first_w, second_w), outs = refs[:n_in], refs[n_in : n_in + 2], refs[n_in + 2 : 2 * n_in + 2]
-    mine, other, send_sem, recv_sem, own_sem, stage, load_sem, store_sem = refs[2 * n_in + 2 :]
+def gather_kernel(plans, *refs):
+    w_q, w_k, w_v, w_o, router, first_gain, second_gain, first_w, second_w = refs[:9]
+    outs, (mine, *others) = refs[9:11], refs[11:14]
+    send_sem, recv_sem, own_sem, stage, load_sem, store_sem, pack_one, pack_two = refs[14:]
+    ins = pack_one, pack_two
     place = Place()
     held = mine.shape[0]
     split = first_w.shape[2]
@@ -121,9 +126,23 @@
                 loads.append(pltpu.make_async_copy(w.at[base + e], to.at[:, at], load_sem.at[len(loads)]))
     for copy in loads:
         copy.start()
-    stores = [
-        pltpu.make_async_copy(stage.at[pl.ds(n * held, held)], out, store_sem.at[n]) for n, out in enumerate((mine, other))
+    stores = [pltpu.make_async_copy(stage.at[pl.ds(0, held)], mine, store_sem.at[0])] + [
+        pltpu.make_async_copy(stage.at[pl.ds(held + e, 1)], out, store_sem.at[1 + e]) for e, out in enumerate(others)
     ]
+    at = 0
+    for w in (w_q, w_k, w_v):
+        pack_one[:, at : at + w.shape[1]] = w[...]
+        at += w.shape[1]
+    model = w_o.shape[1]
+    rows = w_o.shape[0]
+    pack_two[:, :model] = w_o[...]
+    same = lax.broadcasted_iota(jnp.int32, (rows, rows), 0) == lax.broadcasted_iota(jnp.int32, (rows, rows), 1)
+    upright = lambda gain: jnp.sum(jnp.where(same, gain[...].astype(jnp.float32), 0.0), axis=1, keepdims=True)
+    lane = lax.broadcasted_iota(jnp.int32, (1, 128), 1)
+    count = router.shape[1]
+    small = jnp.where(lane == count, upright(first_gain), jnp.where(lane == count + 1, upright(second_gain), 0.0))
+    pack_two[:, model:] = small.astype(pack_two.dtype)
+    pack_two[:, model : model + count] = router[...]
     z = place.at[Z]
     greet(place, sorted({d for p in plans for d in p.order}))
     pending = []
@@ -192,31 +211,33 @@
             pl.when(go)(wait)
 
 
-def gather_weights(arrays, experts, plans, collective_id):
-    n = len(arrays)
+def gather_weights(weights, experts, plans, collective_id):
     sends = sum(len(gather_sends(p.order, k, f)) for p in plans for k, f in gather_events(p.order))
-    blocks = {p.ref: p.blocks for p in plans}
+    rows = weights[0].shape[0]
+    bf = weights[0].dtype
+    widths = [sum(w.shape[1] for w in weights[:3]), weights[3].shape[1] + 128]
     held = experts[0].shape[0] // NC
-    pack = (held, experts[0].shape[1], experts[0].shape[2] + experts[1].shape[2])
+    pack = (experts[0].shape[1], experts[0].shape[2] + experts[1].shape[2])
     apart = pl.BlockSpec(memory_space=pl.ANY)
     dma = pltpu.SemaphoreType.DMA
     return pl.pallas_call(
-        functools.partial(gather_kernel, plans, n),
-        out_shape=[jax.ShapeDtypeStruct((blocks[i],) + a.shape, a.dtype) for i, a in enumerate(arrays)]
-        + [jax.ShapeDtypeStruct(pack, experts[0].dtype)] * 2,
-        in_specs=[pl.BlockSpec(memory_space=pltpu.VMEM)] * n + [apart] * 2,
-        out_specs=[apart] * (n + 2),
+        functools.partial(gather_kernel, plans),
+        out_shape=[jax.ShapeDtypeStruct((plans[0].blocks, rows, w), bf) for w in widths]
+        + [jax.ShapeDtypeStruct((n,) + pack, bf) for n in [held] + [1] * held],
+        in_specs=[pl.BlockSpec(memory_space=pltpu.VMEM)] * len(weights) + [apart] * 2,
+        out_specs=[apart] * (3 + held),
         scratch_shapes=[
             dma((sends,)),
             dma((sum(p.blocks for p in plans),)),
             dma((1 + len(plans),)),
-            pltpu.VMEM((NC * held,) + pack[1:], experts[0].dtype),
+            pltpu.VMEM((NC * held,) + pack, bf),
             dma((2 * NC * held,)),
-            dma((2,)),
-        ],
+            dma((1 + held,)),
+        ]
+        + [pltpu.VMEM((rows, w), bf) for w in widths],
         compiler_params=pltpu.CompilerParams(collective_id=collective_id, has_side_effects=True),
         name="gather_weights",
-    )(*arrays, *experts)
+    )(*weights, *experts)
 
 
 def add_into(acc, other):
@@ -402,14 +423,14 @@
 
 
 def moe_kernel(plans, back, width, hidden, cap, *refs):
-    payload, cots, w_own, w_core, w_x, w_both = refs[:6]
-    gin_out, part_out = refs[6:8]
-    grads = refs[8:12]
+    payload, cots, w_own, w_x, w_core, w_core_last, w_both, w_send = refs[:8]
+    gin_out, part_out = refs[8:10]
+    grads = refs[10:14]
     (
         seen, cot_seen, weights, taken, cot_taken, rows_buf, scaled, grad_act, pick, stage,
         lvl_b0, lvl_b1, chain_b,
-        send_sem, recv_sem, spare_sem, send_b, recv_b, load_sem, store_sem, part_sem,
-    ) = refs[12:]
+        send_sem, recv_sem, spare_sem, send_b, recv_b, load_sem, store_sem, part_sem, piece_sem,
+    ) = refs[14:]
     bf, f32 = jnp.bfloat16, jnp.float32
     place = Place()
     count = payload.shape[0]
@@ -423,10 +444,16 @@
     first = (((place.at[Z] * NY + place.at[Y]) * NC) + place.at[C]) * held
 
     loads = []
-    for j, ref in enumerate((w_own, w_core, w_x, w_both)):
-        rows = pl.ds(pl.multiple_of((fsdp ^ j) * quarter, quarter), quarter)
-        for e in range(held):
-            loads.append(pltpu.make_async_copy(ref.at[e], weights.at[e, rows], load_sem.at[len(loads)]))
+    rows_of = lambda owner: pl.ds(pl.multiple_of(owner * quarter, quarter), quarter)
+    sources = [(w_own, e, e, 0) for e in range(held)] + [(w_x, e, e, 2) for e in range(held)]
+    sources += [(w_core, 0, 0, 1), (w_core_last, 0, held - 1, 1), (w_both, 0, 0, 3)]
+    for ref, at, e, j in sources:
+        loads.append(pltpu.make_async_copy(ref.at[at], weights.at[e, rows_of(fsdp ^ j)], load_sem.at[len(loads)]))
+    there = (place.at[Z] * NY + place.at[Y], (1 - place.at[X]) * NC + 1 - place.at[C])
+    piece = pltpu.make_async_remote_copy(
+        src_ref=w_send.at[0], dst_ref=weights.at[held - 1, rows_of(fsdp)],
+        send_sem=piece_sem.at[0], recv_sem=piece_sem.at[1], device_id=there, device_id_type=DEV,
+    )
     base_of = lambda h, k: (jnp.where(h == 0, place.at[C], 1 - place.at[C]) * NZ + place.order[k]) * NY
     cot_loads = {}
     for k in range(NZ):
@@ -434,7 +461,8 @@
             at = pl.ds(base_of(h, k), NY)
             cot_loads[(h, k)] = pltpu.make_async_copy(cots.at[at], cot_seen.at[at], load_sem.at[len(loads) + len(cot_loads)])
 
-    greet(place, (Z, Y, C))
+    greet(place, (Z, Y, C), (there,))
+    piece.start()
     ways = []
     send_at = 0
     for n, plan in enumerate(plans):
@@ -564,6 +592,11 @@
     def wait_weights():
         for copy in loads:
             copy.wait()
+        arrived = weights.at[held - 1, rows_of(fsdp ^ 3)]
+        pltpu.make_async_remote_copy(
+            src_ref=arrived, dst_ref=arrived, send_sem=piece_sem.at[0], recv_sem=piece_sem.at[1],
+            device_id=there, device_id_type=DEV,
+        ).wait_recv()
 
     for k, flips in gather_events(plans[0].order)[1:]:
         for way in ways:
@@ -629,6 +662,7 @@
             if work:
                 work.pop(0)()
     in_way.last(gin_out)
+    piece.wait_send()
     for copy in stores[-2:] + part_copies:
         copy.wait()
     in_way.finish()
@@ -661,7 +695,7 @@
             jax.ShapeDtypeStruct((blocks, count, width), bf),
         ]
         + [jax.ShapeDtypeStruct((held, quarter, columns), bf)] * (NX * NC),
-        in_specs=[whole] + [apart] * 5,
+        in_specs=[whole] + [apart] * 7,
         out_specs=[whole] + [apart] * (1 + NX * NC),
         scratch_shapes=[
             pltpu.VMEM((blocks, count, wide), bf),
@@ -685,6 +719,7 @@
             dma((held * NX * NC + blocks // NY,)),
             dma((held * NX * NC,)),
             dma((blocks // NY,)),
+            dma((2,)),
         ],
         compiler_params=pltpu.CompilerParams(
             collective_id=collective_id, has_side_effects=True, vmem_limit_bytes=67043328
@@ -693,77 +728,106 @@
     )(payload, cots, *parts)
 
 
-def weights_kernel(plans, *refs):
+def weights_kernel(plans, gain_at, *refs):
     left_one, right_one, left_two, right_two, left_small, right_small = refs[:6]
-    outs = refs[6:8]
-    held_one, held_two = refs[8:10]
-    buffers = refs[10:18]
-    send_one, recv_one, send_two, recv_two, spare = refs[18:]
+    matrix_in, unit, inverse, gain, grad_mixed = refs[6:11]
+    outs, grad_input = refs[11:14], refs[14]
+    held = refs[15:18]
+    buffers = refs[18:30]
+    matrix, grad_in, halves = refs[30:33]
+    sems, (spare, matrix_sem) = refs[33:39], refs[39:]
+    bf, f32 = jnp.bfloat16, jnp.float32
     place = Place()
     far = list(reversed(range(NZ)))
+    fetch = pltpu.make_async_copy(matrix_in, matrix, matrix_sem)
+    fetch.start()
     greet(place, (Z, Y, X, C))
-    ways = [
-        Reduce(place, plans[0], held_one, buffers[0:3], buffers[3], send_one, recv_one, spare),
-        Reduce(place, plans[1], held_two, buffers[4:7], buffers[7], send_two, recv_two, spare),
+    *ways, small_way = [
+        Reduce(place, plan, held[n], buffers[4 * n : 4 * n + 3], buffers[4 * n + 3], sems[2 * n], sems[2 * n + 1], spare)
+        for n, plan in enumerate(plans)
     ]
     group = NY * NX * NC
-    rows = group * held_one.shape[1]
-
-    def products(left, right, held, k, shift):
+    rows = group * held[0].shape[1]
+
+    def products(pairs, target, k):
         at = pl.ds(pl.multiple_of(place.order[k] * rows, 128), rows)
-        block = left[:, at]
-        for c0, cn in columns_of(right.shape[1]):
-            got = lax.dot_general(
-                block, right[:, c0 : c0 + cn], (((0,), (0,)), ((), ())), preferred_element_type=jnp.float32
+        for c0, cn in columns_of(target.shape[2]):
+            got = sum(
+                lax.dot_general(
+                    left[:, at], right[:, c0 : c0 + cn], (((0,), (0,)), ((), ())), preferred_element_type=f32
+                )
+                for left, right in pairs
             )
-            held[pl.ds(place.order[k] * group, group), :, shift + c0 : shift + c0 + cn] = got.astype(
-                held.dtype
-            ).reshape(group, rows // group, cn)
-
-    for t in range(NZ):
-        k = far[t]
-        products(left_one, right_one, held_one, k, 0)
-        ways[0].first(k)
-        products(left_two, right_two, held_two, k, 0)
-        products(left_small, right_small, held_two, k, right_two.shape[1])
-        ways[1].first(k)
-        if t > 0:
-            for way in ways:
-                for step in way.at_time(t - 1):
-                    step()
-    for t in range(NZ - 1, NZ + 3):
-        for way in ways:
+            target[pl.ds(place.order[k] * group, group), :, c0 : c0 + cn] = got.astype(target.dtype).reshape(
+                group, rows // group, cn
+            )
+
+    def round_of(some, t):
+        for way in some:
             for step in way.at_time(t):
                 step()
-    for way, out in zip(ways, outs):
+
+    for t in range(NZ):
+        products([(left_one, right_one)], held[0], far[t])
+        ways[0].first(far[t])
+        products([(left_two, right_two)], held[1], far[t])
+        ways[1].first(far[t])
+        if t > 0:
+            round_of(ways, t - 1)
+    fetch.wait()
+    for c0, cn in columns_of(grad_in.shape[1]):
+        grad_in[:, c0 : c0 + cn] = lax.dot_general(
+            right_one[...], matrix[c0 : c0 + cn], (((1,), (1,)), ((), ())), preferred_element_type=f32
+        )
+    count = grad_in.shape[0]
+    factor = grad_in[...] * unit[...]
+    high = factor.astype(bf)
+    halves[:count] = high
+    halves[count:] = (factor - high.astype(f32)).astype(bf)
+    scaled = grad_in[...] * gain[...]
+    mean = jnp.mean(scaled * unit[...], axis=1, keepdims=True)
+    grad_input[...] = grad_mixed[...] + inverse[...] * (scaled - unit[...] * mean)
+    column = (lax.broadcasted_iota(jnp.int32, (2 * count, 128), 1) == gain_at).astype(f32).astype(bf)
+    for k in far:
+        products([(left_small, right_small), (halves, column)], held[2], k)
+        small_way.first(k)
+    late = [(0, 1, 2), (3, 4), (5,), (6,)]
+    for n, t in enumerate(range(NZ - 1, NZ + 3)):
+        round_of(ways, t)
+        for t_small in late[n]:
+            round_of([small_way], t_small)
+    for way, out in zip(ways + [small_way], outs):
         way.last(out)
-    for way in ways:
+    for way in ways + [small_way]:
         way.finish()
 
 
-def return_weights(lefts, rights, collective_id):
+def return_weights(lefts, rights, matrix, unit, inverse, gain, grad_mixed, gain_at, collective_id):
     width = lefts[0].shape[1]
     rows = width // (NZ * NY * NX * NC)
-    widths = [rights[0].shape[1], rights[1].shape[1] + rights[2].shape[1]]
-    plans = [Plan(0, (C, Y, X), (Z, Y, X, C)), Plan(1, (C, X, Y), (Z, Y, X, C))]
-    bf = jnp.bfloat16
+    widths = [r.shape[1] for r in rights]
+    whole = (Z, Y, X, C)
+    plans = [Plan(0, (C, Y, X), whole), Plan(1, (C, X, Y), whole), Plan(2, (C, Y, X), whole)]
+    bf, f32 = jnp.bfloat16, jnp.float32
     levels, sends, recvs = Reduce.counts(plans[0])
     dma = pltpu.SemaphoreType.DMA
     vmem = pl.BlockSpec(memory_space=pltpu.VMEM)
+    count = unit.shape[0]
     return pl.pallas_call(
-        functools.partial(weights_kernel, plans),
-        out_shape=[jax.ShapeDtypeStruct((rows, w), jnp.float32) for w in widths],
-        in_specs=[vmem] * 6,
-        out_specs=[vmem] * 2,
+        functools.partial(weights_kernel, plans, gain_at),
+        out_shape=[jax.ShapeDtypeStruct((rows, w), f32) for w in widths] + [jax.ShapeDtypeStruct(unit.shape, f32)],
+        in_specs=[vmem] * 6 + [pl.BlockSpec(memory_space=pl.ANY)] + [vmem] * 4,
+        out_specs=[vmem] * 4,
         scratch_shapes=[pltpu.VMEM((plans[0].blocks, rows, w), bf) for w in widths]
         + [pltpu.VMEM((n, rows, w), bf) for w in widths for n in levels + [NZ + 1]]
-        + [dma((n,)) for n in (sends, recvs, sends, recvs)]
-        + [dma(())],
+        + [pltpu.VMEM(matrix.shape, bf), pltpu.VMEM(unit.shape, f32), pltpu.VMEM((2 * count, width), bf)]
+        + [dma((n,)) for _ in plans for n in (sends, recvs)]
+        + [dma(()), dma(())],
         compiler_params=pltpu.CompilerParams(
-            collective_id=collective_id, has_side_effects=True, vmem_limit_bytes=60 * 1024 * 1024
+            collective_id=collective_id, has_side_effects=True, vmem_limit_bytes=64 * 1024 * 1024
         ),
         name="return_weights",
-    )(*[a for pair in zip(lefts, rights) for a in pair])
+    )(*[a for pair in zip(lefts, rights) for a in pair], matrix, unit, inverse, gain, grad_mixed)
 
 
 def turn(block, cosine, sine):
@@ -944,11 +1008,11 @@
 
 
 def attend_back_kernel(plans, *refs):
-    placed, grads, outputs, log_sums, keys, part, mixed, cosine, sine = refs[:9]
-    back, layer_out = refs[9:11]
-    kv_grad, grads_placed, raw, deltas, held, held_out = refs[11:17]
-    level, chain, out_level, out_level_two, out_chain = refs[17:22]
-    send_kv, recv_kv, send_out, recv_out, spare, load_sem = refs[22:]
+    placed, grad_attn, outputs, log_sums, keys, part, w_o, mixed, cosine, sine = refs[:10]
+    back, layer_out = refs[10:12]
+    kv_grad, grads_placed, raw, deltas, held, held_out, grads, matrix = refs[12:20]
+    level, chain, out_level, out_level_two, out_chain = refs[20:25]
+    send_kv, recv_kv, send_out, recv_out, spare, load_sem, matrix_sem = refs[25:]
     place = Place()
     bf, f32 = jnp.bfloat16, jnp.float32
     far = list(reversed(range(NZ)))
@@ -959,6 +1023,8 @@
             loads.append(pltpu.make_async_copy(part.at[at], held_out.at[at], load_sem.at[len(loads)]))
     for copy in loads:
         copy.start()
+    fetch = pltpu.make_async_copy(w_o.at[:, pl.ds(0, matrix.shape[1])], matrix, matrix_sem)
+    fetch.start()
     greet(place, (Z, Y, C))
     kv_way = Reduce(place, plans[0], held, (level,), chain, send_kv, recv_kv, spare)
     out_way = Reduce(place, plans[1], held_out, (out_level, out_level_two), out_chain, send_out, recv_out, spare)
@@ -967,6 +1033,11 @@
     for k in far:
         out_way.first(k)
     count = grads.shape[0]
+    fetch.wait()
+    for c0, cn in columns_of(grads.shape[1]):
+        grads[:, c0 : c0 + cn] = lax.dot_general(
+            grad_attn[...], matrix[c0 : c0 + cn], (((1,), (1,)), ((), ())), preferred_element_type=f32
+        ).astype(bf)
     place_heads(lambda pair: grads[:, pair * 128 : pair * 128 + 128].astype(f32), grads_placed, count)
     group = QUERY_HEADS // KEY_VALUE_HEADS
     lane = lax.broadcasted_iota(jnp.int32, (1, 128), 1)
@@ -1042,7 +1113,7 @@
     out_way.finish()
 
 
-def attend_back(placed, grads, outputs, log_sums, keys, part, mixed, cosine, sine, collective_id):
+def attend_back(placed, grad_attn, outputs, log_sums, keys, part, w_o, mixed, cosine, sine, collective_id):
     count, kv_width = keys.shape[1:]
     plans = [Plan(0, (Y,), (Z, Y)), Plan(1, (C, Y), (C, Z, Y))]
     bf, f32 = jnp.bfloat16, jnp.float32
@@ -1055,10 +1126,10 @@
     return pl.pallas_call(
         functools.partial(attend_back_kernel, plans),
         out_shape=[
-            jax.ShapeDtypeStruct((count, grads.shape[1] + kv_width), bf),
+            jax.ShapeDtypeStruct((count, outputs.shape[1] + kv_width), bf),
             jax.ShapeDtypeStruct(mixed.shape, bf),
         ],
-        in_specs=[vmem] * 5 + [pl.BlockSpec(memory_space=pl.ANY)] + [vmem] * 3,
+        in_specs=[vmem] * 5 + [pl.BlockSpec(memory_space=pl.ANY)] * 2 + [vmem] * 3,
         out_specs=[vmem] * 2,
         scratch_shapes=[
             pltpu.VMEM((count, kv_width), f32),
@@ -1067,19 +1138,21 @@
             pltpu.VMEM((group * count, 128), f32),
             pltpu.VMEM(keys.shape, bf),
             pltpu.VMEM(part.shape, bf),
+            pltpu.VMEM(outputs.shape, bf),
+            pltpu.VMEM((w_o.shape[0], grad_attn.shape[1]), bf),
         ]
         + [pltpu.VMEM((n,) + keys.shape[1:], bf) for n in levels + [NZ + 1]]
         + [pltpu.VMEM((n,) + part.shape[1:], bf) for n in out_levels + [NZ + 1]]
         + [dma((n,)) for n in (sends, recvs, out_sends, out_recvs)]
-        + [dma(()), dma((NC * NZ,))],
+        + [dma(()), dma((NC * NZ,)), dma(())],
         compiler_params=pltpu.CompilerParams(
             collective_id=collective_id, has_side_effects=True, vmem_limit_bytes=60 * 1024 * 1024
         ),
         name="attend_back",
-    )(placed, grads, outputs, log_sums, keys, part, mixed, cosine, sine)
-
-
-def last_kernel(core_ref, own, core_part, x_part, both_part, one, two, *outs):
+    )(placed, grad_attn, outputs, log_sums, keys, part, w_o, mixed, cosine, sine)
+
+
+def last_kernel(core_ref, own, core_part, x_part, both_part, one, two, small, *outs):
     core = core_ref[0]
     in_out, out_out = outs[:2]
     split = in_out.shape[3]
@@ -1095,20 +1168,18 @@
         wq[...] = one[:, :q]
         wk[...] = one[:, q : q + k]
         wv[...] = one[:, q + k :]
-        width = wo.shape[1]
-        wo[...] = two[:, :width]
-        small = two[:, width:]
+        wo[...] = two[...]
         router[...] = small[:, : router.shape[1]]
-        turned = small.T
+        turned = small[...].T
         at = router.shape[1]
         first_gain[...] = turned[at : at + 1]
         second_gain[...] = turned[at + 1 : at + 2]
 
 
-def last_outputs(pieces, core, split, one, two, widths):
+def last_outputs(pieces, core, split, sums, widths):
     held, quarter, columns = pieces[0].shape
     step = quarter // 2
-    rows = one.shape[0]
+    rows = sums[0].shape[0]
     spec = pl.BlockSpec((1, step, columns), lambda e, r, c: (e, r, 0))
     fixed = lambda a, b: pl.BlockSpec((a, b), lambda e, r, c: (0, 0))
     outs = (split, columns - split)
@@ -1118,14 +1189,14 @@
         grid_spec=pltpu.PrefetchScalarGridSpec(
             num_scalar_prefetch=1,
             grid=(held, 2),
-            in_specs=[spec] * 4 + [fixed(*one.shape), fixed(*two.shape)],
+            in_specs=[spec] * 4 + [fixed(*a.shape) for a in sums],
             out_specs=[pl.BlockSpec((NC, 1, step, w), lambda e, r, c: (0, e, r, 0)) for w in outs]
             + [fixed(*s) for s in shapes],
         ),
         out_shape=[jax.ShapeDtypeStruct((NC, held, quarter, w), jnp.float32) for w in outs]
         + [jax.ShapeDtypeStruct(s, jnp.float32) for s in shapes],
         name="last_outputs",
-    )(core[None], *pieces, one, two)
+    )(core[None], *pieces, *sums)
 
 
 MODEL_WIDTH = 1536
@@ -1573,16 +1644,12 @@
     wide = hidden[0].astype(f32)
     cot = cotangent[0]
 
-    pack_one = jnp.concatenate([w_q, key_weight, value_weight], axis=1)
-    pack_two = jnp.concatenate(
-        [w_o, router, attn_norm[:, None], ffn_norm[:, None], jnp.zeros((rows, 94), bf)], axis=1
-    )
     route = routes[0]
     indicator = (route[:, :, None] == jnp.arange(EXPERT_COUNT, dtype=jnp.int32)).astype(f32)
     part = rows // 3
     whole = (Z, Y, X, C)
-    one, two, mine, other = gather_weights(
-        [pack_one, pack_two],
+    one, two, mine, *others = gather_weights(
+        [w_q, key_weight, value_weight, w_o, router, attn_norm[None], ffn_norm[None]],
         [expert_in, expert_out],
         [
             Plan(0, (X, Z, Y, C), whole, rows=(0, 2 * part)),
@@ -1591,7 +1658,7 @@
         ],
         0,
     )
-    parts = [mine, swap(other, 1), swap(mine, 2), swap(other, 3)]
+    parts = [mine, swap(mine, 2)] + [swap(other, 1) for other in others] + [swap(others[0], 3)]
     one = one.reshape(MODEL_WIDTH, -1)
     two = two.reshape(MODEL_WIDTH, -1)
     output_w = two[:, :MODEL_WIDTH]
@@ -1614,57 +1681,44 @@
     payload = jnp.concatenate(
         [ffn_in, gate_map.astype(bf), jnp.zeros((tokens, 128 - EXPERT_COUNT), bf)], axis=1
     )
-    gin, moe_part, *pieces = moe(payload, cots, parts, CAP, 2)
+    gin, moe_part, *pieces = moe(payload, cots, parts + others[-1:], CAP, 2)
     across = [swap(pieces[j], j) for j in range(1, NX * NC)]
     grad_gate_map = gin[:, MODEL_WIDTH : MODEL_WIDTH + EXPERT_COUNT] + gin[
         :, MODEL_WIDTH + EXPERT_COUNT : MODEL_WIDTH + 2 * EXPERT_COUNT
     ]
-    grad_gate = jnp.sum(indicator * grad_gate_map[:, None, :], axis=-1)
-    grad_chosen = gates * (grad_gate - jnp.sum(gates * grad_gate, axis=-1, keepdims=True))
-    grad_logits = jnp.sum(indicator * grad_chosen[..., None], axis=1).astype(bf)
+    grad_logits = (
+        gate_map * (grad_gate_map - jnp.sum(gate_map * grad_gate_map, axis=-1, keepdims=True))
+    ).astype(bf)
     grad_ffn_in = gin[:, :MODEL_WIDTH] + lax.dot_general(
         grad_logits, router_w, contract_cols, preferred_element_type=f32
     )
     back_two, _ = rms_backward(grad_ffn_in, ffn_unit, inverse_two, ffn_gain)
     grad_mixed = cot + back_two
     grad_attn = grad_mixed.astype(bf)
-    attention_output_gradient = lax.dot_general(
-        grad_attn, output_w, contract_cols, preferred_element_type=f32
-    ).astype(bf)
     back, layer_out = attend_back(
-        queries, attention_output_gradient, attention_output, log_sums, kv, moe_part, mixed, cosine, sine, 4
-    )
-    grad_attn_in = lax.dot_general(back, one, contract_cols, preferred_element_type=f32)
-    back_one, _ = rms_backward(grad_attn_in, attn_unit, inverse_one, attn_gain)
-    grad_input = grad_mixed + back_one
-    halves = []
-    for factor in (grad_attn_in * attn_unit, grad_ffn_in * ffn_unit):
-        high = factor.astype(bf)
-        halves += [high, (factor - high.astype(f32)).astype(bf)]
-    column = lambda n: jnp.broadcast_to((jnp.arange(128) == n).astype(bf), (tokens, 128))
-    sum_one, sum_two = return_weights(
-        [attention_input, attention_output, jnp.concatenate([ffn_in] + halves)],
-        [
-            back,
-            grad_attn,
-            jnp.concatenate(
-                [
-                    jnp.concatenate([grad_logits, jnp.zeros((tokens, 128 - EXPERT_COUNT), bf)], axis=1),
-                    column(EXPERT_COUNT),
-                    column(EXPERT_COUNT),
-                    column(EXPERT_COUNT + 1),
-                    column(EXPERT_COUNT + 1),
-                ]
-            ),
-        ],
+        queries, grad_attn, attention_output, log_sums, kv, moe_part, two, mixed, cosine, sine, 4
+    )
+    factor = grad_ffn_in * ffn_unit
+    high = factor.astype(bf)
+    low = (factor - high.astype(f32)).astype(bf)
+    column = jnp.broadcast_to((jnp.arange(128) == EXPERT_COUNT + 1).astype(bf), (tokens, 128))
+    logits_wide = jnp.concatenate([grad_logits, jnp.zeros((tokens, 128 - EXPERT_COUNT), bf)], axis=1)
+    *sums, grad_input = return_weights(
+        [attention_input, attention_output, jnp.concatenate([ffn_in, high, low])],
+        [back, grad_attn, jnp.concatenate([logits_wide, column, column])],
+        one,
+        attn_unit,
+        inverse_one,
+        attn_gain.astype(f32)[None],
+        grad_mixed,
+        EXPERT_COUNT,
         5,
     )
     grad_expert_in, grad_expert_out, *rest, first_gain, second_gain = last_outputs(
         [pieces[0]] + across,
         core,
         2 * EXPERT_HIDDEN,
-        sum_one,
-        sum_two,
+        sums,
         (q_width, kv_width, kv_width, MODEL_WIDTH, EXPERT_COUNT),
     )
     return (

time: 573 us -> 479 us (0.84)
  Pallas kernels: 506 us -> 437 us
  matrix products: 24.5 us -> 11.3 us
  waiting for transfers between devices: 7.83 us -> 0.02 us
    pallas_call x2, Pallas kernels: 224 us -> 155 us  [the longest x1 90.7 us: return_weights(): pl.pallas_call(functools.partial(weights_kernel, plans, gain_at), out_sha...]
    dot_general x2 -> x0, matrix products: 11.1 us -> none  [the longest x1 6.27 us: fast_body(): lax.dot_general(back, one, contract_cols, preferred_element_type=f32)]
    ppermute x6 -> x7, waiting for transfers between devices: 7.83 us -> 0.02 us  [swap(): return lax.ppermute(a, FSDP, [(i, i ^ flip) for i in range(NX * NC)])]
  transfers between devices with their start and end apart: 6 -> 7, of which waited for: 1 -> 0; matrix products, arithmetic and copies ran while one was open for 3% -> 5% of each run, Pallas kernels for 42% -> 53%
where the time goes in v9:
time: 479 us; the launch traced here: 473 us
  Pallas kernels  437 us (91%)
  matrix products  11.3 us (2%)
  local copies, waits for them, and re-layouts  10.5 us (2%)
  other arithmetic  8.38 us (2%)
    pallas_call x1, Pallas kernels, moe(): pl.pallas_call(functools.partial(moe_kernel, plans, back, width, hidden,...  114 us
    pallas_call x1, Pallas kernels, return_weights(): pl.pallas_call(functools.partial(weights_kernel, plans, gain_at), out_sha...  90.7 us
    pallas_call x1, Pallas kernels, attend_back(): pl.pallas_call(functools.partial(attend_back_kernel, plans), out_shape=[j...  83.7 us
    pallas_call x1, Pallas kernels, attend(): pl.pallas_call(functools.partial(attend_kernel, plans), out_shape=[jax.Sh...  76.5 us
    pallas_call x1, Pallas kernels, gather_weights(): pl.pallas_call(functools.partial(gather_kernel, plans), out_shape=[jax.Sh...  64.4 us
  transfers between devices with their start and end apart: 7, of which 0 were waited for; matrix products, arithmetic and copies ran while one was open for 5% of the time, Pallas kernels for 53%

profile of v9, /device:TPU:0, one launch (start us, length us, event | category | flops | bytes accessed | tf_op | source)
XLA Modules:
  0.0 473.2 jit_solution(15284825120691760684)
XLA Ops:
  0.6 1.4 copy.36.refs_4_
  2.0 64.4 %gather_weights.1 = (bf16[32,48,2560]{2,1,0:T(8,128)(2,1)}, bf16[32,48,1664]{2,1,0:T(8,128)(2,1)}, bf16[2,384,1536]{2,1,0:T(8,128)(2,1)}, bf16[1,384,1536]{2,1,0:T(8,128)(2,1)}, bf16[1,384,1536]{2,1,0:T(8,128)(2,1)}) custom-call(bf16[48,1536]{1,0:T(8,128)(2,1)} %refs_0_.1, bf16[48,512]{1,0:T(8,128)(2,1)} %refs_1_.1, bf16[48,512]{1,0:T(8,128)(2,1)} %refs_2_.1, ...), custom_call_target="tpu_custom_call" | custom-call | tf_op jit(solution)/shard_map/gather_weights/pallas_call | solution.py:223
  66.4 0.6 collective-permute-start.1
  67.0 0.2 collective-permute-start.3
  67.2 1.5 collective-permute-start
  68.7 0.2 collective-permute-start.2
  68.8 1.3 fusion.13
  70.1 0.6 slice_reduce_fusion
  70.7 0.0 copy-done.4
  70.7 0.2 fusion.7
  70.9 0.5 fusion.30
  71.4 0.3 fusion.27
  71.7 0.8 pad_maximum_fusion.1.cosine.refs_8_
  72.5 0.0 copy-done.14
  72.5 0.7 copy.37
  73.2 0.8 pad_maximum_fusion.2.sine.refs_9_
  74.0 6.0 %fusion.11.linear = f32[128,2560]{1,0:T(8,128)} fusion(bf16[1536,2560]{1,0:T(8,128)(2,1)} %bitcast.37, bf16[1,128,1536]{2,1,0:T(8,128)(2,1)S(1)} %copy-done.4, f32[1536]{0:T(1024)S(1)} %get-tuple-element.107, f32[128]{0:T(128)S(1)} %get-tuple-element.121), kind=kOutput, calls=%fused_computation.20 | convolution fusion | flops 1007419392 | bytes 9574912 | tf_op jit(solution)/shard_map/dot_general | solution.py:1673
  79.9 0.0 copy-done.9
  79.9 0.0 copy-done.15
  79.9 76.5 %attend.1 = (bf16[128,1536]{1,0:T(8,128)(2,1)}, f32[384,128]{1,0:T(8,128)}, bf16[8,128,1024]{2,1,0:T(8,128)(2,1)}, bf16[16,128,1664]{2,1,0:T(8,128)(2,1)}, bf16[8,384,128]{2,1,0:T(8,128)(2,1)}) custom-call(f32[128,2560]{1,0:T(8,128)} %fusion.11.linear, f32[128,1536]{1,0:T(8,128)} %bitcast.46, s32[128,8]{1,0:T(8,128)} %bitcast.49, ...), custom_call_target="tpu_custom_call" | custom-call | tf_op jit(solution)/shard_map/attend/pallas_call | solution.py:978
  156.4 0.0 slice-done
  156.5 1.9 multiply_reduce_fusion.1
  158.3 0.0 copy-start
  158.4 0.0 copy-start.17
  158.4 0.8 copy-done
  159.2 0.1 multiply_convert_fusion.1
  159.4 0.3 fusion.19
  159.7 0.0 copy-done.17
  159.8 0.0 copy-start.11
  159.8 0.6 copy-done.11
  160.4 0.1 copy.40
  160.5 0.9 concatenate.20.refs_0_
  161.4 0.0 collective-permute-done.1.refs_4_
  161.4 0.0 collective-permute-done.2.refs_5_
  161.4 0.0 collective-permute-done.3.refs_6_
  161.4 0.0 collective-permute-done.refs_3_
  161.4 113.6 %experts.1 = (f32[128,1664]{1,0:T(8,128)}, bf16[16,128,1536]{2,1,0:T(8,128)(2,1)}, bf16[2,384,1536]{2,1,0:T(8,128)(2,1)}, bf16[2,384,1536]{2,1,0:T(8,128)(2,1)},...) custom-call(bf16[128,1664]{1,0:T(8,128)(2,1)} %concatenate.20.refs_0_, ...), custom_call_target="tpu_custom_call" | custom-call | tf_op jit(solution)/shard_map/experts/pallas_call | solution.py:691
  275.0 0.0 copy-start.1
  275.0 0.0 copy-start.5
  275.0 0.0 copy-start.6
  275.0 0.0 copy-start.10
  275.0 0.0 copy-start.13
  275.0 0.0 copy-start.16
  275.1 0.0 copy-start.18
  275.1 0.1 collective-permute-start.4
  275.1 1.6 collective-permute-start.5
  276.8 0.2 collective-permute-start.6
  277.0 0.8 copy.42
  277.8 1.4 copy.43.refs_8_
  279.2 1.1 multiply_reduce_fusion.2
  280.3 1.0 multiply_convert_fusion.2
  281.3 1.9 multiply_reduce_fusion
  283.3 1.8 fusion.5
  285.1 83.7 %attend_back.1 = (bf16[128,2560]{1,0:T(8,128)(2,1)}, bf16[128,1536]{1,0:T(8,128)(2,1)}) custom-call(bf16[8,384,128]{2,1,0:T(8,128)(2,1)} %get-tuple-element.44.refs_0_, bf16[128,1536]{1,0:T(8,128)(2,1)} %get-tuple-element.126.refs_1_.refs_3_, bf16[128,1536]{1,0:T(8,128)(2,1)} %get-tuple-element.45.refs_2_, f32[384,128]{1,0:T(8,128)} %get-tuple-element.51.refs_3_, ...), custom_call_target="tpu_custom_call" | custom-call | tf_op jit(solution)/shard_map/attend_back/pallas_call | solution.py:1126
  368.8 0.7 fusion.26.refs_5_
  369.4 1.1 pad_maximum_fusion.refs_4_
  370.5 90.7 %return_weights.1 = (f32[48,2560]{1,0:T(8,128)}, f32[48,1536]{1,0:T(8,128)}, f32[48,128]{1,0:T(8,128)}, f32[128,1536]{1,0:T(8,128)}) custom-call(bf16[128,1536]{1,0:T(8,128)(2,1)} %get-tuple-element.116.refs_0_, bf16[128,2560]{1,0:T(8,128)(2,1)} %get-tuple-element.55.refs_1_, bf16[128,1536]{1,0:T(8,128)(2,1)} %get-tuple-element.45.refs_2_, ...), custom_call_target="tpu_custom_call" | custom-call | tf_op jit(solution)/shard_map/return_weights/pallas_call | solution.py:816
  461.2 0.0 collective-permute-done.4.core_part
  461.3 0.0 collective-permute-done.5.x_part
  461.3 0.0 collective-permute-done.6.both_part
  461.3 8.5 %last_outputs.1 = (f32[2,2,384,1024]{3,2,1,0:T(8,128)}, f32[2,2,384,512]{3,2,1,0:T(8,128)}, f32[48,1536]{1,0:T(8,128)}, f32[48,512]{1,0:T(8,128)}, f32[48,512]{1...) custom-call(s32[1]{0:T(128)} %bitcast.12.core_ref, ...), custom_call_target="tpu_custom_call" | custom-call | tf_op jit(solution)/shard_map/last_outputs/pallas_call | solution.py:1187
  469.8 1.4 copy.44
  471.2 0.7 copy.48
  471.9 0.9 copy.49
  (38 shorter events, 0.2 us)
Async XLA Ops:
  2.0 68.7 %copy-start.4 = (bf16[1,128,1536]{2,1,0:T(8,128)(2,1)S(1)}, bf16[1,128,1536]{2,1,0:T(8,128)(2,1)}, u32[]{:S(2)}) copy-start(bf16[1,128,1536]{2,1,0:T(8,128)(2,1)} %param.12) | copy-start | bytes 1179652
  2.0 70.5 %copy-start.14 = (s32[1,128,8]{1,2,0:T(8,128)S(1)}, s32[1,128,8]{1,2,0:T(8,128)}, u32[]{:S(2)}) copy-start(s32[1,128,8]{1,2,0:T(8,128)} %param.13) | copy-start | bytes 12292
  66.4 95.0 %collective-permute-start.1 = (bf16[1,384,1536]{2,1,0:T(8,128)(2,1)}, bf16[1,384,1536]{2,1,0:T(8,128)(2,1)}, u32[]{:S(2)}, u32[]{:S(2)}) collective-permute-start(bf16[1,384,1536]{2,1,0:T(8,128)(2,1)} %get-tuple-element.48), channel_id=1, source_target_pairs={{0,1},{1,0},{2,3},{3,2},{4,5},{5,4},{6,7},{7,6},{8,9},{9,8},{10,11... | collective-permute-start | bytes 3538952 | tf_op jit(solution)/shard_map/ppermute | solution.py:1611
  67.0 94.4 %collective-permute-start.3 = (bf16[1,384,1536]{2,1,0:T(8,128)(2,1)}, bf16[1,384,1536]{2,1,0:T(8,128)(2,1)}, u32[]{:S(2)}, u32[]{:S(2)}) collective-permute-start(bf16[1,384,1536]{2,1,0:T(8,128)(2,1)} %get-tuple-element.48), channel_id=1, source_target_pairs={{0,3},{1,2},{2,1},{3,0},{4,7},{5,6},{6,5},{7,4},{8,11},{9,10},{10,... | collective-permute-start | bytes 3538952 | tf_op jit(solution)/shard_map/ppermute | solution.py:1611
  67.2 94.2 %collective-permute-start = (bf16[2,384,1536]{2,1,0:T(8,128)(2,1)}, bf16[2,384,1536]{2,1,0:T(8,128)(2,1)}, u32[]{:S(2)}, u32[]{:S(2)}) collective-permute-start(bf16[2,384,1536]{2,1,0:T(8,128)(2,1)} %get-tuple-element.47.refs_2_), channel_id=1, source_target_pairs={{0,2},{1,3},{2,0},{3,1},{4,6},{5,7},{6,4},{7,5},{8,10},{9,11},{10,... | collective-permute-start | bytes 7077896 | tf_op jit(solution)/shard_map/ppermute | solution.py:1611
  68.7 92.7 %collective-permute-start.2 = (bf16[1,384,1536]{2,1,0:T(8,128)(2,1)}, bf16[1,384,1536]{2,1,0:T(8,128)(2,1)}, u32[]{:S(2)}, u32[]{:S(2)}) collective-permute-start(bf16[1,384,1536]{2,1,0:T(8,128)(2,1)} %get-tuple-element.49.refs_7_), channel_id=1, source_target_pairs={{0,1},{1,0},{2,3},{3,2},{4,5},{5,4},{6,7},{7,6},{8,9},{9,8},{10,11... | collective-permute-start | bytes 3538952 | tf_op jit(solution)/shard_map/ppermute | solution.py:1611
  70.7 9.2 %copy-start.9 = (f32[1536]{0:T(1024)}, f32[1536]{0:T(1024)S(1)}, u32[]{:S(2)}) copy-start(f32[1536]{0:T(1024)S(1)} %get-tuple-element.107) | copy-start | bytes 18436
  70.7 87.6 %copy-start.12 = (f32[1536]{0:T(1024)}, f32[1536]{0:T(1024)S(1)}, u32[]{:S(2)}) copy-start(f32[1536]{0:T(1024)S(1)} %get-tuple-element.106) | copy-start | bytes 18436
  71.4 8.5 %copy-start.15 = (f32[128]{0:T(128)}, f32[128]{0:T(128)S(1)}, u32[]{:S(2)}) copy-start(f32[128]{0:T(128)S(1)} %get-tuple-element.121) | copy-start | bytes 1540
  73.2 83.2 %slice-start = ((s8[5111808]{0:T(1024)(128)(4,1)}), s8[4194304]{0:T(1024)(128)(4,1)S(1)}, s32[]{:S(2)}) async-start(s8[5111808]{0:T(1024)(128)(4,1)} %bitcast.42), calls=%async_computation | async-start | bytes 8388608
  74.0 82.5 %slice-start.1 = ((s8[5111808]{0:T(1024)(128)(4,1)}), s8[917504]{0:T(1024)(128)(4,1)S(1)}, s32[]{:S(2)}) async-start(s8[5111808]{0:T(1024)(128)(4,1)} %bitcast.42), calls=%async_computation.1 | async-start | bytes 1835008
  158.3 0.9 copy-start
  158.4 1.3 copy-start.17
  159.4 1.2 copy-start.2
  159.8 0.6 copy-start.11
  275.0 8.3 %copy-start.1 = (f32[128,1536]{1,0:T(8,128)S(1)}, f32[128,1536]{1,0:T(8,128)}, u32[]{:S(2)}) copy-start(f32[128,1536]{1,0:T(8,128)} %copy-done) | copy-start | bytes 2359300
  275.0 8.3 %copy-start.5 = (bf16[1,128,1536]{2,1,0:T(8,128)(2,1)S(1)}, bf16[1,128,1536]{2,1,0:T(8,128)(2,1)}, u32[]{:S(2)}) copy-start(bf16[1,128,1536]{2,1,0:T(8,128)(2,1)} %param.12) | copy-start | bytes 1179652
  275.0 8.3 %copy-start.6 = (f32[1,128,1536]{2,1,0:T(8,128)S(1)}, f32[1,128,1536]{2,1,0:T(8,128)}, u32[]{:S(2)}) copy-start(f32[1,128,1536]{2,1,0:T(8,128)} %param.23) | copy-start | bytes 2359300
  275.0 8.3 %copy-start.10 = (f32[1536]{0:T(1024)S(1)}, f32[1536]{0:T(1024)}, u32[]{:S(2)}) copy-start(f32[1536]{0:T(1024)} %copy-done.9) | copy-start | bytes 18436
  275.0 8.3 %copy-start.13 = (f32[1536]{0:T(1024)S(1)}, f32[1536]{0:T(1024)}, u32[]{:S(2)}) copy-start(f32[1536]{0:T(1024)} %copy-done.12) | copy-start | bytes 18436
  275.0 8.3 %copy-start.16 = (f32[128]{0:T(128)S(1)}, f32[128]{0:T(128)}, u32[]{:S(2)}) copy-start(f32[128]{0:T(128)} %copy-done.15) | copy-start | bytes 1540
  275.1 8.3 %copy-start.18 = (f32[128]{0:T(128)S(1)}, f32[128]{0:T(128)}, u32[]{:S(2)}) copy-start(f32[128]{0:T(128)} %copy-done.17) | copy-start | bytes 1540
  275.1 186.2 %collective-permute-start.4 = (bf16[2,384,1536]{2,1,0:T(8,128)(2,1)}, bf16[2,384,1536]{2,1,0:T(8,128)(2,1)}, u32[]{:S(2)}, u32[]{:S(2)}) collective-permute-start(bf16[2,384,1536]{2,1,0:T(8,128)(2,1)} %get-tuple-element.58), channel_id=1, source_target_pairs={{0,1},{1,0},{2,3},{3,2},{4,5},{5,4},{6,7},{7,6},{8,9},{9,8},{10,11... | collective-permute-start | bytes 7077896 | tf_op jit(solution)/shard_map/ppermute | solution.py:1611
  275.1 186.1 %collective-permute-start.5 = (bf16[2,384,1536]{2,1,0:T(8,128)(2,1)}, bf16[2,384,1536]{2,1,0:T(8,128)(2,1)}, u32[]{:S(2)}, u32[]{:S(2)}) collective-permute-start(bf16[2,384,1536]{2,1,0:T(8,128)(2,1)} %get-tuple-element.59), channel_id=1, source_target_pairs={{0,2},{1,3},{2,0},{3,1},{4,6},{5,7},{6,4},{7,5},{8,10},{9,11},{10,... | collective-permute-start | bytes 7077896 | tf_op jit(solution)/shard_map/ppermute | solution.py:1611
  276.8 184.5 %collective-permute-start.6 = (bf16[2,384,1536]{2,1,0:T(8,128)(2,1)}, bf16[2,384,1536]{2,1,0:T(8,128)(2,1)}, u32[]{:S(2)}, u32[]{:S(2)}) collective-permute-start(bf16[2,384,1536]{2,1,0:T(8,128)(2,1)} %get-tuple-element.60), channel_id=1, source_target_pairs={{0,3},{1,2},{2,1},{3,0},{4,7},{5,6},{6,5},{7,4},{8,11},{9,10},{10,... | collective-permute-start | bytes 7077896 | tf_op jit(solution)/shard_map/ppermute | solution.py:1611
  285.1 84.3 %copy-start.3 = (bf16[128,1536]{1,0:T(8,128)(2,1)S(1)}, bf16[128,1536]{1,0:T(8,128)(2,1)}, u32[]{:S(2)}) copy-start(bf16[128,1536]{1,0:T(8,128)(2,1)} %copy-done.2) | copy-start | bytes 1179652
  461.3 9.9 %copy-start.8 = (bf16[128,1536]{1,0:T(8,128)(2,1)S(1)}, bf16[128,1536]{1,0:T(8,128)(2,1)}, u32[]{:S(2)}) copy-start(bf16[128,1536]{1,0:T(8,128)(2,1)} %get-tuple-element.54) | copy-start | bytes 1179652
  461.3 10.6 %copy-start.7 = (f32[128,1536]{1,0:T(8,128)S(1)}, f32[128,1536]{1,0:T(8,128)}, u32[]{:S(2)}) copy-start(f32[128,1536]{1,0:T(8,128)} %get-tuple-element.56) | copy-start | bytes 2359300

commit v10 on v9

--- a/solution.py
+++ b/solution.py
@@ -311,15 +311,26 @@
     def __init__(self, place, plan, held, levels, chain, send_sem, recv_sem, spare_sem):
         self.place, self.plan, self.held, self.levels, self.chain = place, plan, held, levels, chain
         self.send_sem, self.recv_sem, self.spare_sem = send_sem, recv_sem, spare_sem
-        dims = plan.order
-        self.kept = [subsets(dims[p + 1 :]) for p in range(len(dims))]
-        self.base = [NZ * sum(len(f) for f in self.kept[:p]) for p in range(len(dims) + 1)]
+        self.order, self.chain_at, self.kept, counts = Reduce.shape(plan)
+        self.base = [sum(counts[:p]) for p in range(len(counts))]
         self.slot = 0
+
+    @staticmethod
+    def shape(plan):
+        order = plan.order if Z in plan.order else plan.order + (Z,)
+        at = order.index(Z)
+        kept = [subsets(tuple(d for d in order[p + 1 :] if d != Z)) for p in range(len(order))]
+        times = [NZ if p < at else NZ + 1 if p == at else 1 for p in range(len(order))]
+        return order, at, kept, [n * len(f) for n, f in zip(times, kept)]
 
     @staticmethod
     def counts(plan):
-        kept = [NZ * len(subsets(plan.order[p + 1 :])) for p in range(len(plan.order))]
-        return kept, sum(kept) + NZ - 1, sum(kept) + NZ + 1
+        _, at, kept, counts = Reduce.shape(plan)
+        buffers = counts[:at] + counts[at + 1 :] + [counts[at]]
+        return buffers, sum(counts) - 2 * len(kept[at]), sum(counts)
+
+    def level_of(self, p):
+        return self.levels[p if p < self.chain_at else p - 1]
 
     def push(self, source, target, sem, dest):
         copy = pltpu.make_async_remote_copy(
@@ -336,77 +347,94 @@
         ).wait_recv()
 
     def block(self, k, flips):
-        return flat_index(self.place.coords(self.place.order[k], flips), self.plan.index)
+        return self.held.at[flat_index(self.place.coords(self.place.order[k], flips), self.plan.index)]
+
+    def spot(self, p, k, flips):
+        at = self.kept[p].index(flips)
+        return at if p > self.chain_at else self.place.order[k] * len(self.kept[p]) + at
+
+    def send(self, p, k, flips):
+        dim = self.order[p]
+        spot = self.spot(p, k, tuple(d for d in flips if d != dim))
+        self.push(
+            self.block(k, flips), self.level_of(p).at[spot],
+            self.recv_sem.at[self.base[p] + spot], self.place.across(dim),
+        )
 
     def first(self, k):
-        dim = self.plan.order[0]
-        for n, f in enumerate(self.kept[0]):
-            spot = self.place.order[k] * len(self.kept[0]) + n
-            self.push(
-                self.held.at[self.block(k, (dim,) + f)], self.levels[0].at[spot],
-                self.recv_sem.at[spot], self.place.across(dim),
-            )
+        for f in self.kept[0]:
+            self.send(0, k, (self.order[0],) + f)
+
+    def forward(self, p, k, flips):
+        later = p + 1
+        if later < len(self.order) and self.order[later] in flips:
+            self.send(later, k, flips)
 
     def level(self, p, k):
-        dims = self.plan.order
-        z_to = self.place.order[k]
         for f in sorted(self.kept[p], key=lambda f: -len(f)):
-            spot = z_to * len(self.kept[p]) + self.kept[p].index(f)
-            mine = self.held.at[self.block(k, f)]
-            self.arrived(self.levels[p].at[spot], self.recv_sem.at[self.base[p] + spot])
-            add_into(mine, self.levels[p].at[spot])
-            later = p + 1
-            if later < len(dims) and dims[later] in f:
-                left = tuple(d for d in f if d != dims[later])
-                there = z_to * len(self.kept[later]) + self.kept[later].index(left)
-                self.push(
-                    mine, self.levels[later].at[there],
-                    self.recv_sem.at[self.base[later] + there], self.place.across(dims[later]),
-                )
+            spot = self.spot(p, k, f)
+            self.arrived(self.level_of(p).at[spot], self.recv_sem.at[self.base[p] + spot])
+            add_into(self.block(k, f), self.level_of(p).at[spot])
+            self.forward(p, k, f)
+
+    def link(self, spot, n):
+        at = spot * len(self.kept[self.chain_at]) + n
+        return self.chain.at[at], self.recv_sem.at[self.base[self.chain_at] + at]
 
     def along(self, k):
         z = self.place.at[Z]
         dest = self.place.order[k]
         up = dest > z
-        spot = dest + jnp.where(up, 1, 0)
-        mine = self.held.at[self.block(k, ())]
-        sem = self.recv_sem.at[self.base[-1] + spot]
-
-        @pl.when(jnp.where(up, z > 0, z < NZ - 1))
-        def _():
-            self.arrived(self.chain.at[spot], sem)
-            add_into(mine, self.chain.at[spot])
-
-        self.push(mine, self.chain.at[spot], sem, self.place.along(jnp.where(up, 1, -1)))
+        for n, f in enumerate(self.kept[self.chain_at]):
+            mine = self.block(k, f)
+            target, sem = self.link(dest + jnp.where(up, 1, 0), n)
+
+            @pl.when(jnp.where(up, z > 0, z < NZ - 1))
+            def _():
+                self.arrived(target, sem)
+                add_into(mine, target)
+
+            self.push(mine, target, sem, self.place.along(jnp.where(up, 1, -1)))
+
+    def settle(self):
+        z = self.place.at[Z]
+        kept = self.kept[self.chain_at]
+        for f in sorted(kept, key=lambda f: -len(f)):
+            mine = self.block(0, f)
+            for go, spot in ((z > 0, z + 1), (z < NZ - 1, z)):
+                target, sem = self.link(spot, kept.index(f))
+
+                @pl.when(go)
+                def _():
+                    self.arrived(target, sem)
+                    add_into(mine, target)
+
+            self.forward(self.chain_at, 0, f)
 
     def last(self, out, base=None):
-        z = self.place.at[Z]
-        mine = self.held.at[self.block(0, ())]
-        for go, spot in ((z > 0, z + 1), (z < NZ - 1, z)):
-
-            @pl.when(go)
-            def _():
-                self.arrived(self.chain.at[spot], self.recv_sem.at[self.base[-1] + spot])
-                add_into(mine, self.chain.at[spot])
-
-        total = mine[...].astype(jnp.float32)
+        if self.chain_at == len(self.order) - 1:
+            self.settle()
+        total = self.block(0, ())[...].astype(jnp.float32)
         if base is not None:
             total = base[...] + total
         out[...] = total.astype(out.dtype)
 
     def at_time(self, t):
-        depth = len(self.plan.order)
         far = list(reversed(range(NZ)))
-        out = [functools.partial(self.level, p, far[t - p]) for p in range(depth) if 0 <= t - p < NZ]
-        if 0 <= t - depth < NZ - 1:
-            out.append(functools.partial(self.along, far[t - depth]))
+        at = self.chain_at
+        out = [functools.partial(self.level, p, far[t - p]) for p in range(at) if 0 <= t - p < NZ]
+        if 0 <= t - at < NZ - 1:
+            out.append(functools.partial(self.along, far[t - at]))
+        if t - at == NZ - 1 and at < len(self.order) - 1:
+            out.append(self.settle)
+        out += [functools.partial(self.level, p, 0) for p in range(at + 1, len(self.order)) if t == NZ - 1 + p]
         return out
 
     def steps(self):
-        return [step for t in range(NZ + len(self.plan.order)) for step in self.at_time(t)]
+        return [step for t in range(NZ + len(self.order)) for step in self.at_time(t)]
 
     def finish(self):
-        block = self.levels[0].at[0]
+        block = self.level_of(0).at[0]
         for slot in range(self.slot):
             pltpu.make_async_remote_copy(
                 src_ref=block, dst_ref=block, send_sem=self.send_sem.at[slot], recv_sem=self.spare_sem,
@@ -709,7 +737,7 @@
             pltpu.VMEM((blocks // NY, NY * count, lanes), bf),
             pltpu.VMEM((2, quarter, columns), bf),
         ]
-        + [pltpu.VMEM((n, count, wide), bf) for n in levels + [NZ + 1]]
+        + [pltpu.VMEM((n, count, wide), bf) for n in levels]
         + [
             dma((sum(Gather.sends(p) for p in plans),)),
             dma((sum(p.blocks for p in plans),)),
@@ -731,11 +759,12 @@
 def weights_kernel(plans, gain_at, *refs):
     left_one, right_one, left_two, right_two, left_small, right_small = refs[:6]
     matrix_in, unit, inverse, gain, grad_mixed = refs[6:11]
+    n_ways = len(plans)
     outs, grad_input = refs[11:14], refs[14]
-    held = refs[15:18]
-    buffers = refs[18:30]
-    matrix, grad_in, halves = refs[30:33]
-    sems, (spare, matrix_sem) = refs[33:39], refs[39:]
+    held = refs[15 : 15 + n_ways]
+    buffers, refs = refs[15 + n_ways : 15 + 5 * n_ways], refs[15 + 5 * n_ways :]
+    matrix, grad_in, halves = refs[:3]
+    sems, (spare, matrix_sem) = refs[3 : 3 + 2 * n_ways], refs[3 + 2 * n_ways :]
     bf, f32 = jnp.bfloat16, jnp.float32
     place = Place()
     far = list(reversed(range(NZ)))
@@ -749,12 +778,13 @@
     group = NY * NX * NC
     rows = group * held[0].shape[1]
 
-    def products(pairs, target, k):
+    def products(pairs, target, k, shift=0):
         at = pl.ds(pl.multiple_of(place.order[k] * rows, 128), rows)
         for c0, cn in columns_of(target.shape[2]):
             got = sum(
                 lax.dot_general(
-                    left[:, at], right[:, c0 : c0 + cn], (((0,), (0,)), ((), ())), preferred_element_type=f32
+                    left[:, at], right[:, shift + c0 : shift + c0 + cn], (((0,), (0,)), ((), ())),
+                    preferred_element_type=f32,
                 )
                 for left, right in pairs
             )
@@ -768,10 +798,10 @@
                 step()
 
     for t in range(NZ):
-        products([(left_one, right_one)], held[0], far[t])
-        ways[0].first(far[t])
-        products([(left_two, right_two)], held[1], far[t])
-        ways[1].first(far[t])
+        for n, way in enumerate(ways):
+            width = held[n].shape[2]
+            products([(left_one, right_one) if n < 2 else (left_two, right_two)], held[n], far[t], n % 2 * width)
+            way.first(far[t])
         if t > 0:
             round_of(ways, t - 1)
     fetch.wait()
@@ -789,15 +819,17 @@
     grad_input[...] = grad_mixed[...] + inverse[...] * (scaled - unit[...] * mean)
     column = (lax.broadcasted_iota(jnp.int32, (2 * count, 128), 1) == gain_at).astype(f32).astype(bf)
     for k in far:
-        products([(left_small, right_small), (halves, column)], held[2], k)
+        products([(left_small, right_small), (halves, column)], held[-1], k)
         small_way.first(k)
     late = [(0, 1, 2), (3, 4), (5,), (6,)]
     for n, t in enumerate(range(NZ - 1, NZ + 3)):
         round_of(ways, t)
         for t_small in late[n]:
             round_of([small_way], t_small)
-    for way, out in zip(ways + [small_way], outs):
-        way.last(out)
+    for n, way in enumerate(ways):
+        width = held[n].shape[2]
+        way.last(outs[n // 2].at[:, pl.ds(n % 2 * width, width)])
+    small_way.last(outs[2])
     for way in ways + [small_way]:
         way.finish()
 
@@ -807,9 +839,10 @@
     rows = width // (NZ * NY * NX * NC)
     widths = [r.shape[1] for r in rights]
     whole = (Z, Y, X, C)
-    plans = [Plan(0, (C, Y, X), whole), Plan(1, (C, X, Y), whole), Plan(2, (C, Y, X), whole)]
+    orders = ((C, Y, Z, X), (C, X, Z, Y), (C, Y, X, Z), (C, X, Y, Z), (C, Y, X, Z))
+    plans = [Plan(0, order, whole) for order in orders]
+    parts = [widths[0] // 2] * 2 + [widths[1] // 2] * 2 + [widths[2]]
     bf, f32 = jnp.bfloat16, jnp.float32
-    levels, sends, recvs = Reduce.counts(plans[0])
     dma = pltpu.SemaphoreType.DMA
     vmem = pl.BlockSpec(memory_space=pltpu.VMEM)
     count = unit.shape[0]
@@ -818,10 +851,10 @@
         out_shape=[jax.ShapeDtypeStruct((rows, w), f32) for w in widths] + [jax.ShapeDtypeStruct(unit.shape, f32)],
         in_specs=[vmem] * 6 + [pl.BlockSpec(memory_space=pl.ANY)] + [vmem] * 4,
         out_specs=[vmem] * 4,
-        scratch_shapes=[pltpu.VMEM((plans[0].blocks, rows, w), bf) for w in widths]
-        + [pltpu.VMEM((n, rows, w), bf) for w in widths for n in levels + [NZ + 1]]
+        scratch_shapes=[pltpu.VMEM((plans[0].blocks, rows, w), bf) for w in parts]
+        + [pltpu.VMEM((n, rows, w), bf) for p, w in zip(plans, parts) for n in Reduce.counts(p)[0]]
         + [pltpu.VMEM(matrix.shape, bf), pltpu.VMEM(unit.shape, f32), pltpu.VMEM((2 * count, width), bf)]
-        + [dma((n,)) for _ in plans for n in (sends, recvs)]
+        + [dma((n,)) for p in plans for n in Reduce.counts(p)[1:]]
         + [dma(()), dma(())],
         compiler_params=pltpu.CompilerParams(
             collective_id=collective_id, has_side_effects=True, vmem_limit_bytes=64 * 1024 * 1024
@@ -1141,8 +1174,8 @@
             pltpu.VMEM(outputs.shape, bf),
             pltpu.VMEM((w_o.shape[0], grad_attn.shape[1]), bf),
         ]
-        + [pltpu.VMEM((n,) + keys.shape[1:], bf) for n in levels + [NZ + 1]]
-        + [pltpu.VMEM((n,) + part.shape[1:], bf) for n in out_levels + [NZ + 1]]
+        + [pltpu.VMEM((n,) + keys.shape[1:], bf) for n in levels]
+        + [pltpu.VMEM((n,) + part.shape[1:], bf) for n in out_levels]
         + [dma((n,)) for n in (sends, recvs, out_sends, out_recvs)]
         + [dma(()), dma((NC * NZ,)), dma(())],
         compiler_params=pltpu.CompilerParams(
@@ -1652,9 +1685,11 @@
         [w_q, key_weight, value_weight, w_o, router, attn_norm[None], ffn_norm[None]],
         [expert_in, expert_out],
         [
-            Plan(0, (X, Z, Y, C), whole, rows=(0, 2 * part)),
-            Plan(0, (X, Y, Z, C), whole, rows=(2 * part, part)),
-            Plan(1, (Z, Y, X, C), whole),
+            Plan(0, (X, Z, Y, C), whole, rows=(2 * part, part)),
+            Plan(1, (X, Z, Y, C), whole, rows=(part, part)),
+            Plan(1, (X, Y, Z, C), whole, rows=(2 * part, part)),
+            Plan(0, (Z, Y, X, C), whole, rows=(0, 2 * part)),
+            Plan(1, (Z, Y, X, C), whole, rows=(0, part)),
         ],
         0,
     )

time: 479 us -> 465 us (0.971)
  Pallas kernels: 437 us -> 423 us
    pallas_call x1, Pallas kernels: 90.7 us -> 80.5 us  [return_weights(): pl.pallas_call(functools.partial(weights_kernel, plans, gain_at), out_sha...]
  transfers between devices with their start and end apart: 7 -> 7, of which waited for: 0 -> 0; matrix products, arithmetic and copies ran while one was open for 5% -> 5% of each run, Pallas kernels for 53% -> 52%
where the time goes in v10:
time: 465 us; the launch traced here: 459 us
  Pallas kernels  423 us (91%)
  matrix products  11.3 us (2%)
  local copies, waits for them, and re-layouts  10.5 us (2%)
  other arithmetic  8.38 us (2%)
    pallas_call x1, Pallas kernels, moe(): pl.pallas_call(functools.partial(moe_kernel, plans, back, width, hidden,...  114 us
    pallas_call x1, Pallas kernels, attend_back(): pl.pallas_call(functools.partial(attend_back_kernel, plans), out_shape=[j...  83.6 us
    pallas_call x1, Pallas kernels, return_weights(): pl.pallas_call(functools.partial(weights_kernel, plans, gain_at), out_sha...  80.5 us
    pallas_call x1, Pallas kernels, attend(): pl.pallas_call(functools.partial(attend_kernel, plans), out_shape=[jax.Sh...  76.6 us
    pallas_call x1, Pallas kernels, gather_weights(): pl.pallas_call(functools.partial(gather_kernel, plans), out_shape=[jax.Sh...  60 us
  transfers between devices with their start and end apart: 7, of which 0 were waited for; matrix products, arithmetic and copies ran while one was open for 5% of the time, Pallas kernels for 52%

profile of v10, /device:TPU:0, one launch (start us, length us, event | category | flops | bytes accessed | tf_op | source)
XLA Modules:
  0.0 458.8 jit_solution(4733577399375629763)
XLA Ops:
  0.6 1.4 copy.36.refs_4_
  2.0 60.0 %gather_weights.1 = (bf16[32,48,2560]{2,1,0:T(8,128)(2,1)}, bf16[32,48,1664]{2,1,0:T(8,128)(2,1)}, bf16[2,384,1536]{2,1,0:T(8,128)(2,1)}, bf16[1,384,1536]{2,1,0:T(8,128)(2,1)}, bf16[1,384,1536]{2,1,0:T(8,128)(2,1)}) custom-call(bf16[48,1536]{1,0:T(8,128)(2,1)} %refs_0_.1, bf16[48,512]{1,0:T(8,128)(2,1)} %refs_1_.1, bf16[48,512]{1,0:T(8,128)(2,1)} %refs_2_.1, ...), custom_call_target="tpu_custom_call" | custom-call | tf_op jit(solution)/shard_map/gather_weights/pallas_call | solution.py:223
  62.0 0.6 collective-permute-start.1
  62.7 0.5 collective-permute-start.3
  63.2 1.2 collective-permute-start
  64.4 0.2 collective-permute-start.2
  64.5 1.3 fusion.13
  65.8 0.6 slice_reduce_fusion
  66.4 0.2 fusion.7
  66.6 0.5 fusion.30
  67.1 0.3 fusion.27
  67.4 0.8 pad_maximum_fusion.1.cosine.refs_8_
  68.2 0.0 copy-done.14
  68.2 0.7 copy.37
  68.9 0.8 pad_maximum_fusion.2.sine.refs_9_
  69.7 6.0 %fusion.11.linear = f32[128,2560]{1,0:T(8,128)} fusion(bf16[1536,2560]{1,0:T(8,128)(2,1)} %bitcast.37, bf16[1,128,1536]{2,1,0:T(8,128)(2,1)S(1)} %copy-done.4, f32[1536]{0:T(1024)S(1)} %get-tuple-element.107, f32[128]{0:T(128)S(1)} %get-tuple-element.121), kind=kOutput, calls=%fused_computation.20 | convolution fusion | flops 1007419392 | bytes 9574912 | tf_op jit(solution)/shard_map/dot_general | solution.py:1708
  75.6 0.0 copy-done.9
  75.6 76.6 %attend.1 = (bf16[128,1536]{1,0:T(8,128)(2,1)}, f32[384,128]{1,0:T(8,128)}, bf16[8,128,1024]{2,1,0:T(8,128)(2,1)}, bf16[16,128,1664]{2,1,0:T(8,128)(2,1)}, bf16[8,384,128]{2,1,0:T(8,128)(2,1)}) custom-call(f32[128,2560]{1,0:T(8,128)} %fusion.11.linear, f32[128,1536]{1,0:T(8,128)} %bitcast.46, s32[128,8]{1,0:T(8,128)} %bitcast.49, ...), custom_call_target="tpu_custom_call" | custom-call | tf_op jit(solution)/shard_map/attend/pallas_call | solution.py:1011
  152.2 1.9 multiply_reduce_fusion.1
  154.1 0.0 copy-start
  154.1 0.0 copy-start.17
  154.1 0.0 copy-done.12
  154.1 0.8 copy-done
  155.0 0.1 multiply_convert_fusion.1
  155.1 0.0 copy-start.2
  155.1 0.3 fusion.19
  155.5 0.0 copy-start.11
  155.5 0.6 copy-done.11
  156.1 0.1 copy.40
  156.3 0.0 copy-done.2
  156.3 0.9 concatenate.20.refs_0_
  157.1 0.0 collective-permute-done.1.refs_4_
  157.1 0.0 collective-permute-done.2.refs_5_
  157.2 0.0 collective-permute-done.3.refs_6_
  157.2 0.0 collective-permute-done.refs_3_
  157.2 113.6 %experts.1 = (f32[128,1664]{1,0:T(8,128)}, bf16[16,128,1536]{2,1,0:T(8,128)(2,1)}, bf16[2,384,1536]{2,1,0:T(8,128)(2,1)}, bf16[2,384,1536]{2,1,0:T(8,128)(2,1)},...) custom-call(bf16[128,1664]{1,0:T(8,128)(2,1)} %concatenate.20.refs_0_, ...), custom_call_target="tpu_custom_call" | custom-call | tf_op jit(solution)/shard_map/experts/pallas_call | solution.py:719
  270.7 0.0 copy-start.1
  270.8 0.0 copy-start.5
  270.8 0.0 copy-start.6
  270.8 0.0 copy-start.10
  270.8 0.0 copy-start.13
  270.8 0.0 copy-start.16
  270.8 0.0 copy-start.18
  270.8 0.1 collective-permute-start.4
  270.9 1.9 collective-permute-start.5
  272.8 0.0 collective-permute-start.6
  272.8 0.8 copy.42
  273.6 1.4 copy.43.refs_8_
  275.0 1.1 multiply_reduce_fusion.2
  276.1 1.0 multiply_convert_fusion.2
  277.1 1.9 multiply_reduce_fusion
  279.1 1.8 fusion.5
  280.9 83.6 %attend_back.1 = (bf16[128,2560]{1,0:T(8,128)(2,1)}, bf16[128,1536]{1,0:T(8,128)(2,1)}) custom-call(bf16[8,384,128]{2,1,0:T(8,128)(2,1)} %get-tuple-element.44.refs_0_, bf16[128,1536]{1,0:T(8,128)(2,1)} %get-tuple-element.126.refs_1_.refs_3_, bf16[128,1536]{1,0:T(8,128)(2,1)} %get-tuple-element.45.refs_2_, f32[384,128]{1,0:T(8,128)} %get-tuple-element.51.refs_3_, ...), custom_call_target="tpu_custom_call" | custom-call | tf_op jit(solution)/shard_map/attend_back/pallas_call | solution.py:1159
  364.6 0.7 fusion.26.refs_5_
  365.2 0.0 copy-done.3
  365.2 1.1 pad_maximum_fusion.refs_4_
  366.3 80.5 %return_weights.1 = (f32[48,2560]{1,0:T(8,128)}, f32[48,1536]{1,0:T(8,128)}, f32[48,128]{1,0:T(8,128)}, f32[128,1536]{1,0:T(8,128)}) custom-call(bf16[128,1536]{1,0:T(8,128)(2,1)} %get-tuple-element.116.refs_0_, bf16[128,2560]{1,0:T(8,128)(2,1)} %get-tuple-element.55.refs_1_, bf16[128,1536]{1,0:T(8,128)(2,1)} %get-tuple-element.45.refs_2_, ...), custom_call_target="tpu_custom_call" | custom-call | tf_op jit(solution)/shard_map/return_weights/pallas_call | solution.py:849
  446.8 0.0 collective-permute-done.4.core_part
  446.8 0.0 collective-permute-done.5.x_part
  446.8 0.0 collective-permute-done.6.both_part
  446.8 8.5 %last_outputs.1 = (f32[2,2,384,1024]{3,2,1,0:T(8,128)}, f32[2,2,384,512]{3,2,1,0:T(8,128)}, f32[48,1536]{1,0:T(8,128)}, f32[48,512]{1,0:T(8,128)}, f32[48,512]{1...) custom-call(s32[1]{0:T(128)} %bitcast.12.core_ref, ...), custom_call_target="tpu_custom_call" | custom-call | tf_op jit(solution)/shard_map/last_outputs/pallas_call | solution.py:1220
  455.3 1.4 copy.44
  456.7 0.7 copy.48
  457.5 0.9 copy.49
  (38 shorter events, 0.2 us)
Async XLA Ops:
  2.0 64.4 %copy-start.4 = (bf16[1,128,1536]{2,1,0:T(8,128)(2,1)S(1)}, bf16[1,128,1536]{2,1,0:T(8,128)(2,1)}, u32[]{:S(2)}) copy-start(bf16[1,128,1536]{2,1,0:T(8,128)(2,1)} %param.12) | copy-start | bytes 1179652
  2.0 66.2 %copy-start.14 = (s32[1,128,8]{1,2,0:T(8,128)S(1)}, s32[1,128,8]{1,2,0:T(8,128)}, u32[]{:S(2)}) copy-start(s32[1,128,8]{1,2,0:T(8,128)} %param.13) | copy-start | bytes 12292
  62.0 95.1 %collective-permute-start.1 = (bf16[1,384,1536]{2,1,0:T(8,128)(2,1)}, bf16[1,384,1536]{2,1,0:T(8,128)(2,1)}, u32[]{:S(2)}, u32[]{:S(2)}) collective-permute-start(bf16[1,384,1536]{2,1,0:T(8,128)(2,1)} %get-tuple-element.48), channel_id=1, source_target_pairs={{0,1},{1,0},{2,3},{3,2},{4,5},{5,4},{6,7},{7,6},{8,9},{9,8},{10,11... | collective-permute-start | bytes 3538952 | tf_op jit(solution)/shard_map/ppermute | solution.py:1644
  62.7 94.5 %collective-permute-start.3 = (bf16[1,384,1536]{2,1,0:T(8,128)(2,1)}, bf16[1,384,1536]{2,1,0:T(8,128)(2,1)}, u32[]{:S(2)}, u32[]{:S(2)}) collective-permute-start(bf16[1,384,1536]{2,1,0:T(8,128)(2,1)} %get-tuple-element.48), channel_id=1, source_target_pairs={{0,3},{1,2},{2,1},{3,0},{4,7},{5,6},{6,5},{7,4},{8,11},{9,10},{10,... | collective-permute-start | bytes 3538952 | tf_op jit(solution)/shard_map/ppermute | solution.py:1644
  63.2 94.0 %collective-permute-start = (bf16[2,384,1536]{2,1,0:T(8,128)(2,1)}, bf16[2,384,1536]{2,1,0:T(8,128)(2,1)}, u32[]{:S(2)}, u32[]{:S(2)}) collective-permute-start(bf16[2,384,1536]{2,1,0:T(8,128)(2,1)} %get-tuple-element.47.refs_2_), channel_id=1, source_target_pairs={{0,2},{1,3},{2,0},{3,1},{4,6},{5,7},{6,4},{7,5},{8,10},{9,11},{10,... | collective-permute-start | bytes 7077896 | tf_op jit(solution)/shard_map/ppermute | solution.py:1644
  64.4 92.8 %collective-permute-start.2 = (bf16[1,384,1536]{2,1,0:T(8,128)(2,1)}, bf16[1,384,1536]{2,1,0:T(8,128)(2,1)}, u32[]{:S(2)}, u32[]{:S(2)}) collective-permute-start(bf16[1,384,1536]{2,1,0:T(8,128)(2,1)} %get-tuple-element.49.refs_7_), channel_id=1, source_target_pairs={{0,1},{1,0},{2,3},{3,2},{4,5},{5,4},{6,7},{7,6},{8,9},{9,8},{10,11... | collective-permute-start | bytes 3538952 | tf_op jit(solution)/shard_map/ppermute | solution.py:1644
  66.4 9.2 %copy-start.9 = (f32[1536]{0:T(1024)}, f32[1536]{0:T(1024)S(1)}, u32[]{:S(2)}) copy-start(f32[1536]{0:T(1024)S(1)} %get-tuple-element.107) | copy-start | bytes 18436
  66.4 87.7 %copy-start.12 = (f32[1536]{0:T(1024)}, f32[1536]{0:T(1024)S(1)}, u32[]{:S(2)}) copy-start(f32[1536]{0:T(1024)S(1)} %get-tuple-element.106) | copy-start | bytes 18436
  67.1 8.5 %copy-start.15 = (f32[128]{0:T(128)}, f32[128]{0:T(128)S(1)}, u32[]{:S(2)}) copy-start(f32[128]{0:T(128)S(1)} %get-tuple-element.121) | copy-start | bytes 1540
  68.9 83.3 %slice-start = ((s8[5111808]{0:T(1024)(128)(4,1)}), s8[4194304]{0:T(1024)(128)(4,1)S(1)}, s32[]{:S(2)}) async-start(s8[5111808]{0:T(1024)(128)(4,1)} %bitcast.42), calls=%async_computation | async-start | bytes 8388608
  69.7 82.5 %slice-start.1 = ((s8[5111808]{0:T(1024)(128)(4,1)}), s8[917504]{0:T(1024)(128)(4,1)S(1)}, s32[]{:S(2)}) async-start(s8[5111808]{0:T(1024)(128)(4,1)} %bitcast.42), calls=%async_computation.1 | async-start | bytes 1835008
  154.1 0.9 copy-start
  154.1 1.3 copy-start.17
  155.1 1.2 copy-start.2
  155.5 0.6 copy-start.11
  270.7 8.3 %copy-start.1 = (f32[128,1536]{1,0:T(8,128)S(1)}, f32[128,1536]{1,0:T(8,128)}, u32[]{:S(2)}) copy-start(f32[128,1536]{1,0:T(8,128)} %copy-done) | copy-start | bytes 2359300
  270.8 8.3 %copy-start.5 = (bf16[1,128,1536]{2,1,0:T(8,128)(2,1)S(1)}, bf16[1,128,1536]{2,1,0:T(8,128)(2,1)}, u32[]{:S(2)}) copy-start(bf16[1,128,1536]{2,1,0:T(8,128)(2,1)} %param.12) | copy-start | bytes 1179652
  270.8 8.3 %copy-start.6 = (f32[1,128,1536]{2,1,0:T(8,128)S(1)}, f32[1,128,1536]{2,1,0:T(8,128)}, u32[]{:S(2)}) copy-start(f32[1,128,1536]{2,1,0:T(8,128)} %param.23) | copy-start | bytes 2359300
  270.8 8.3 %copy-start.10 = (f32[1536]{0:T(1024)S(1)}, f32[1536]{0:T(1024)}, u32[]{:S(2)}) copy-start(f32[1536]{0:T(1024)} %copy-done.9) | copy-start | bytes 18436
  270.8 8.3 %copy-start.13 = (f32[1536]{0:T(1024)S(1)}, f32[1536]{0:T(1024)}, u32[]{:S(2)}) copy-start(f32[1536]{0:T(1024)} %copy-done.12) | copy-start | bytes 18436
  270.8 8.3 %copy-start.16 = (f32[128]{0:T(128)S(1)}, f32[128]{0:T(128)}, u32[]{:S(2)}) copy-start(f32[128]{0:T(128)} %copy-done.15) | copy-start | bytes 1540
  270.8 8.3 %copy-start.18 = (f32[128]{0:T(128)S(1)}, f32[128]{0:T(128)}, u32[]{:S(2)}) copy-start(f32[128]{0:T(128)} %copy-done.17) | copy-start | bytes 1540
  270.8 176.0 %collective-permute-start.4 = (bf16[2,384,1536]{2,1,0:T(8,128)(2,1)}, bf16[2,384,1536]{2,1,0:T(8,128)(2,1)}, u32[]{:S(2)}, u32[]{:S(2)}) collective-permute-start(bf16[2,384,1536]{2,1,0:T(8,128)(2,1)} %get-tuple-element.58), channel_id=1, source_target_pairs={{0,1},{1,0},{2,3},{3,2},{4,5},{5,4},{6,7},{7,6},{8,9},{9,8},{10,11... | collective-permute-start | bytes 7077896 | tf_op jit(solution)/shard_map/ppermute | solution.py:1644
  270.9 175.9 %collective-permute-start.5 = (bf16[2,384,1536]{2,1,0:T(8,128)(2,1)}, bf16[2,384,1536]{2,1,0:T(8,128)(2,1)}, u32[]{:S(2)}, u32[]{:S(2)}) collective-permute-start(bf16[2,384,1536]{2,1,0:T(8,128)(2,1)} %get-tuple-element.59), channel_id=1, source_target_pairs={{0,2},{1,3},{2,0},{3,1},{4,6},{5,7},{6,4},{7,5},{8,10},{9,11},{10,... | collective-permute-start | bytes 7077896 | tf_op jit(solution)/shard_map/ppermute | solution.py:1644
  272.8 174.0 %collective-permute-start.6 = (bf16[2,384,1536]{2,1,0:T(8,128)(2,1)}, bf16[2,384,1536]{2,1,0:T(8,128)(2,1)}, u32[]{:S(2)}, u32[]{:S(2)}) collective-permute-start(bf16[2,384,1536]{2,1,0:T(8,128)(2,1)} %get-tuple-element.60), channel_id=1, source_target_pairs={{0,3},{1,2},{2,1},{3,0},{4,7},{5,6},{6,5},{7,4},{8,11},{9,10},{10,... | collective-permute-start | bytes 7077896 | tf_op jit(solution)/shard_map/ppermute | solution.py:1644
  280.9 84.3 %copy-start.3 = (bf16[128,1536]{1,0:T(8,128)(2,1)S(1)}, bf16[128,1536]{1,0:T(8,128)(2,1)}, u32[]{:S(2)}) copy-start(bf16[128,1536]{1,0:T(8,128)(2,1)} %copy-done.2) | copy-start | bytes 1179652
  446.8 9.9 %copy-start.8 = (bf16[128,1536]{1,0:T(8,128)(2,1)S(1)}, bf16[128,1536]{1,0:T(8,128)(2,1)}, u32[]{:S(2)}) copy-start(bf16[128,1536]{1,0:T(8,128)(2,1)} %get-tuple-element.54) | copy-start | bytes 1179652
  446.8 10.6 %copy-start.7 = (f32[128,1536]{1,0:T(8,128)S(1)}, f32[128,1536]{1,0:T(8,128)}, u32[]{:S(2)}) copy-start(f32[128,1536]{1,0:T(8,128)} %get-tuple-element.56) | copy-start | bytes 2359300

commit v11 on v10

--- a/solution.py
+++ b/solution.py
@@ -456,8 +456,8 @@
     grads = refs[10:14]
     (
         seen, cot_seen, weights, taken, cot_taken, rows_buf, scaled, grad_act, pick, stage,
-        lvl_b0, lvl_b1, chain_b,
-        send_sem, recv_sem, spare_sem, send_b, recv_b, load_sem, store_sem, part_sem, piece_sem,
+        lvl_b0, lvl_b1, chain_b, lvl_c0, lvl_c1, chain_c,
+        send_sem, recv_sem, spare_sem, send_b, recv_b, send_c, recv_c, load_sem, store_sem, part_sem, piece_sem,
     ) = refs[14:]
     bf, f32 = jnp.bfloat16, jnp.float32
     place = Place()
@@ -645,23 +645,31 @@
 
     far = list(reversed(range(NZ)))
     spare = spare_sem
-    in_way = Reduce(place, back, cot_seen, (lvl_b0, lvl_b1), chain_b, send_b, recv_b, spare)
-    in_steps = in_way.steps()
+    cut = lvl_b0.shape[2]
+    in_ways = [
+        Reduce(place, back[0], cot_seen.at[:, :, pl.ds(0, cut)], (lvl_b0, lvl_b1), chain_b, send_b, recv_b, spare),
+        Reduce(place, back[1], cot_seen.at[:, :, pl.ds(cut, wide - cut)], (lvl_c0, lvl_c1), chain_c, send_c, recv_c, spare),
+    ]
+    in_steps = [step for t in range(NZ + 3) for way in in_ways for step in way.at_time(t)]
     for e in range(held):
         project(1, e, grad_act, (0, 2 * hidden))
     for k in far[: NZ // 2]:
         combine(cot_seen, 1, k, all_cols)
-        in_way.first(k)
+        for way in in_ways:
+            way.first(k)
     for k in far[: NZ // 2]:
         combine(cot_seen, 0, k, all_cols)
+    in_steps.pop(0)()
     in_steps.pop(0)()
     for e in range(held):
         project(0, e, grad_act, (0, 2 * hidden))
     in_steps.pop(0)()
     for k in far[NZ // 2 :]:
         combine(cot_seen, 1, k, all_cols)
-        in_way.first(k)
-    in_steps.pop(0)()
+        for way in in_ways:
+            way.first(k)
+    for _ in range(3):
+        in_steps.pop(0)()
     for k in far[NZ // 2 :]:
         combine(cot_seen, 0, k, all_cols)
     for way in ways:
@@ -684,16 +692,19 @@
                 work.append(functools.partial(out_part, h, k))
     work += [functools.partial(weight_grad, e, j) for j in reversed(range(NX * NC)) for e in range(held)]
     while in_steps or work:
-        if in_steps:
-            in_steps.pop(0)()
+        for _ in range(2):
+            if in_steps:
+                in_steps.pop(0)()
         for _ in range(2):
             if work:
                 work.pop(0)()
-    in_way.last(gin_out)
+    in_ways[0].last(gin_out.at[:, pl.ds(0, cut)])
+    in_ways[1].last(gin_out.at[:, pl.ds(cut, wide - cut)])
     piece.wait_send()
     for copy in stores[-2:] + part_copies:
         copy.wait()
-    in_way.finish()
+    for way in in_ways:
+        way.finish()
 
 
 def moe(payload, cots, parts, cap, collective_id):
@@ -706,8 +717,8 @@
         Plan(0, (Z, Y, C), (C, Z, Y), rows=(0, cut)),
         Plan(0, (Y, Z, C), (C, Z, Y), rows=(cut, count - cut)),
     ]
-    back = Plan(0, (C, Y), (C, Z, Y))
-    levels, sends, recvs = Reduce.counts(back)
+    back = [Plan(0, (C, Y, Z), (C, Z, Y)), Plan(0, (C, Z, Y), (C, Z, Y))]
+    widths = (wide - wide // 4 // 128 * 128, wide // 4 // 128 * 128)
     blocks = NC * NZ * NY
     pair = NY * cap
     rows = blocks // NY * pair
@@ -737,13 +748,12 @@
             pltpu.VMEM((blocks // NY, NY * count, lanes), bf),
             pltpu.VMEM((2, quarter, columns), bf),
         ]
-        + [pltpu.VMEM((n, count, wide), bf) for n in levels]
+        + [pltpu.VMEM((n, count, w), bf) for p, w in zip(back, widths) for n in Reduce.counts(p)[0]]
         + [
             dma((sum(Gather.sends(p) for p in plans),)),
             dma((sum(p.blocks for p in plans),)),
             dma(()),
-            dma((sends,)),
-            dma((recvs,)),
+            *[dma((n,)) for p in back for n in Reduce.counts(p)[1:]],
             dma((held * NX * NC + blocks // NY,)),
             dma((held * NX * NC,)),
             dma((blocks // NY,)),
@@ -758,11 +768,11 @@
 
 def weights_kernel(plans, gain_at, *refs):
     left_one, right_one, left_two, right_two, left_small, right_small = refs[:6]
-    matrix_in, unit, inverse, gain, grad_mixed = refs[6:11]
+    matrix_in, hidden, gain, grad_mixed = refs[6:10]
     n_ways = len(plans)
-    outs, grad_input = refs[11:14], refs[14]
-    held = refs[15 : 15 + n_ways]
-    buffers, refs = refs[15 + n_ways : 15 + 5 * n_ways], refs[15 + 5 * n_ways :]
+    outs, grad_input = refs[10:13], refs[13]
+    held = refs[14 : 14 + n_ways]
+    buffers, refs = refs[14 + n_ways : 14 + 5 * n_ways], refs[14 + 5 * n_ways :]
     matrix, grad_in, halves = refs[:3]
     sems, (spare, matrix_sem) = refs[3 : 3 + 2 * n_ways], refs[3 + 2 * n_ways :]
     bf, f32 = jnp.bfloat16, jnp.float32
@@ -810,13 +820,16 @@
             right_one[...], matrix[c0 : c0 + cn], (((1,), (1,)), ((), ())), preferred_element_type=f32
         )
     count = grad_in.shape[0]
-    factor = grad_in[...] * unit[...]
+    wide = hidden[...].astype(f32)
+    inverse = lax.rsqrt(jnp.mean(wide * wide, axis=1, keepdims=True) + norm_eps)
+    unit = wide * inverse
+    factor = grad_in[...] * unit
     high = factor.astype(bf)
     halves[:count] = high
     halves[count:] = (factor - high.astype(f32)).astype(bf)
     scaled = grad_in[...] * gain[...]
-    mean = jnp.mean(scaled * unit[...], axis=1, keepdims=True)
-    grad_input[...] = grad_mixed[...] + inverse[...] * (scaled - unit[...] * mean)
+    mean = jnp.mean(scaled * unit, axis=1, keepdims=True)
+    grad_input[...] = grad_mixed[...] + inverse * (scaled - unit * mean)
     column = (lax.broadcasted_iota(jnp.int32, (2 * count, 128), 1) == gain_at).astype(f32).astype(bf)
     for k in far:
         products([(left_small, right_small), (halves, column)], held[-1], k)
@@ -834,7 +847,7 @@
         way.finish()
 
 
-def return_weights(lefts, rights, matrix, unit, inverse, gain, grad_mixed, gain_at, collective_id):
+def return_weights(lefts, rights, matrix, hidden, gain, grad_mixed, gain_at, collective_id):
     width = lefts[0].shape[1]
     rows = width // (NZ * NY * NX * NC)
     widths = [r.shape[1] for r in rights]
@@ -845,22 +858,22 @@
     bf, f32 = jnp.bfloat16, jnp.float32
     dma = pltpu.SemaphoreType.DMA
     vmem = pl.BlockSpec(memory_space=pltpu.VMEM)
-    count = unit.shape[0]
+    count = hidden.shape[0]
     return pl.pallas_call(
         functools.partial(weights_kernel, plans, gain_at),
-        out_shape=[jax.ShapeDtypeStruct((rows, w), f32) for w in widths] + [jax.ShapeDtypeStruct(unit.shape, f32)],
-        in_specs=[vmem] * 6 + [pl.BlockSpec(memory_space=pl.ANY)] + [vmem] * 4,
+        out_shape=[jax.ShapeDtypeStruct((rows, w), f32) for w in widths] + [jax.ShapeDtypeStruct(hidden.shape, f32)],
+        in_specs=[vmem] * 6 + [pl.BlockSpec(memory_space=pl.ANY)] + [vmem] * 3,
         out_specs=[vmem] * 4,
         scratch_shapes=[pltpu.VMEM((plans[0].blocks, rows, w), bf) for w in parts]
         + [pltpu.VMEM((n, rows, w), bf) for p, w in zip(plans, parts) for n in Reduce.counts(p)[0]]
-        + [pltpu.VMEM(matrix.shape, bf), pltpu.VMEM(unit.shape, f32), pltpu.VMEM((2 * count, width), bf)]
+        + [pltpu.VMEM(matrix.shape, bf), pltpu.VMEM(hidden.shape, f32), pltpu.VMEM((2 * count, width), bf)]
         + [dma((n,)) for p in plans for n in Reduce.counts(p)[1:]]
         + [dma(()), dma(())],
         compiler_params=pltpu.CompilerParams(
             collective_id=collective_id, has_side_effects=True, vmem_limit_bytes=64 * 1024 * 1024
         ),
         name="return_weights",
-    )(*[a for pair in zip(lefts, rights) for a in pair], matrix, unit, inverse, gain, grad_mixed)
+    )(*[a for pair in zip(lefts, rights) for a in pair], matrix, hidden, gain, grad_mixed)
 
 
 def turn(block, cosine, sine):
@@ -1041,11 +1054,11 @@
 
 
 def attend_back_kernel(plans, *refs):
-    placed, grad_attn, outputs, log_sums, keys, part, w_o, mixed, cosine, sine = refs[:10]
-    back, layer_out = refs[10:12]
-    kv_grad, grads_placed, raw, deltas, held, held_out, grads, matrix = refs[12:20]
-    level, chain, out_level, out_level_two, out_chain = refs[20:25]
-    send_kv, recv_kv, send_out, recv_out, spare, load_sem, matrix_sem = refs[25:]
+    placed, gin, gate_map, cot, ffn_gain, outputs, log_sums, keys, part, w_o, mixed, cosine, sine = refs[:13]
+    back, layer_out, grad_mixed, grad_attn, left_small, right_small = refs[13:19]
+    kv_grad, grads_placed, raw, deltas, held, held_out, grads, matrix = refs[19:27]
+    level, chain, v_level, v_chain, out_level, out_level_two, out_chain = refs[27:34]
+    send_kv, recv_kv, send_v, recv_v, send_out, recv_out, spare, load_sem, matrix_sem = refs[34:]
     place = Place()
     bf, f32 = jnp.bfloat16, jnp.float32
     far = list(reversed(range(NZ)))
@@ -1056,20 +1069,44 @@
             loads.append(pltpu.make_async_copy(part.at[at], held_out.at[at], load_sem.at[len(loads)]))
     for copy in loads:
         copy.start()
-    fetch = pltpu.make_async_copy(w_o.at[:, pl.ds(0, matrix.shape[1])], matrix, matrix_sem)
+    fetch = pltpu.make_async_copy(w_o, matrix, matrix_sem)
     fetch.start()
     greet(place, (Z, Y, C))
-    kv_way = Reduce(place, plans[0], held, (level,), chain, send_kv, recv_kv, spare)
-    out_way = Reduce(place, plans[1], held_out, (out_level, out_level_two), out_chain, send_out, recv_out, spare)
+    width = KEY_VALUE_HEADS * HEAD_SIZE
+    k_way = Reduce(place, plans[0], held.at[:, :, pl.ds(0, width)], (level,), chain, send_kv, recv_kv, spare)
+    v_way = Reduce(place, plans[1], held.at[:, :, pl.ds(width, width)], (v_level,), v_chain, send_v, recv_v, spare)
+    out_way = Reduce(place, plans[2], held_out, (out_level, out_level_two), out_chain, send_out, recv_out, spare)
     for copy in loads:
         copy.wait()
     for k in far:
         out_way.first(k)
     count = grads.shape[0]
     fetch.wait()
+    model = cot.shape[1]
+    lane = lax.broadcasted_iota(jnp.int32, (1, 128), 1)
+    halves = gin[:, model:]
+    gate_grad = jnp.where(lane < EXPERT_COUNT, halves + pltpu.roll(halves, 128 - EXPERT_COUNT, 1), 0.0)
+    weighted = jnp.sum(gate_map[...] * gate_grad, axis=1, keepdims=True)
+    grad_logits = (gate_map[...] * (gate_grad - weighted)).astype(bf)
+    over_cols = (((1,), (1,)), ((), ()))
+    inverse = lax.rsqrt(jnp.mean(mixed[...] * mixed[...], axis=1, keepdims=True) + norm_eps)
+    unit = mixed[...] * inverse
+    grad_in = gin[:, :model] + lax.dot_general(
+        grad_logits, matrix[:, model:], over_cols, preferred_element_type=f32
+    )
+    scaled = grad_in * ffn_gain[...]
+    grad_mixed[...] = cot[...] + inverse * (scaled - unit * jnp.mean(scaled * unit, axis=1, keepdims=True))
+    grad_attn[...] = grad_mixed[...].astype(bf)
+    factor = grad_in * unit
+    high = factor.astype(bf)
+    left_small[:count] = (unit * ffn_gain[...]).astype(bf)
+    left_small[count : 2 * count] = high
+    left_small[2 * count :] = (factor - high.astype(f32)).astype(bf)
+    right_small[:count] = grad_logits
+    right_small[count:] = jnp.broadcast_to(jnp.where(lane == EXPERT_COUNT + 1, 1.0, 0.0), (2 * count, 128)).astype(bf)
     for c0, cn in columns_of(grads.shape[1]):
         grads[:, c0 : c0 + cn] = lax.dot_general(
-            grad_attn[...], matrix[c0 : c0 + cn], (((1,), (1,)), ((), ())), preferred_element_type=f32
+            grad_attn[...], matrix[c0 : c0 + cn, :model], over_cols, preferred_element_type=f32
         ).astype(bf)
     place_heads(lambda pair: grads[:, pair * 128 : pair * 128 + 128].astype(f32), grads_placed, count)
     group = QUERY_HEADS // KEY_VALUE_HEADS
@@ -1084,7 +1121,6 @@
             found = jnp.where(lane == m, delta, found)
         deltas[g * count : (g + 1) * count] = found
     scores = Scores(place, placed, keys)
-    width = KEY_VALUE_HEADS * HEAD_SIZE
     blocks = keys.shape[0]
     turns = KEY_VALUE_HEADS // 2
     early = [[(out_way.level, 0, 3)], [(out_way.level, 0, 2)], [(out_way.level, 1, 3)], [(out_way.level, 1, 2), (out_way.along, 3)]]
@@ -1120,19 +1156,25 @@
 
     lax.fori_loop(0, turns, pair, 0)
     for k in far:
-        kv_way.first(k)
+        k_way.first(k)
+    v_way.along(3)
     out_way.level(0, 1)
     out_way.level(0, 0)
     collect_heads(raw, back, count, lambda block: turn(block, cosine[...], -sine[...]))
-    kv_way.level(0, 3)
-    kv_way.level(0, 2)
-    kv_way.along(3)
-    kv_way.level(0, 1)
-    kv_way.along(2)
+    k_way.level(0, 3)
+    v_way.along(2)
+    k_way.level(0, 2)
+    k_way.along(3)
+    v_way.along(1)
+    k_way.level(0, 1)
+    k_way.along(2)
     out_way.along(2)
-    kv_way.level(0, 0)
-    kv_way.along(1)
-    kv_way.last(kv_grad)
+    v_way.settle()
+    k_way.level(0, 0)
+    k_way.along(1)
+    k_way.last(kv_grad.at[:, pl.ds(0, width)])
+    v_way.level(1, 0)
+    v_way.last(kv_grad.at[:, pl.ds(width, width)])
     q_width = QUERY_HEADS * HEAD_SIZE
     for c0 in range(0, width, 128):
         block = turn(kv_grad[:, c0 : c0 + 128], cosine[...], -sine[...])
@@ -1142,28 +1184,34 @@
     out_way.along(1)
     out_way.level(1, 0)
     out_way.last(layer_out, mixed)
-    kv_way.finish()
-    out_way.finish()
-
-
-def attend_back(placed, grad_attn, outputs, log_sums, keys, part, w_o, mixed, cosine, sine, collective_id):
+    for way in (k_way, v_way, out_way):
+        way.finish()
+
+
+def attend_back(
+    placed, gin, gate_map, cot, ffn_gain, outputs, log_sums, keys, part, w_o, mixed, cosine, sine, collective_id
+):
     count, kv_width = keys.shape[1:]
-    plans = [Plan(0, (Y,), (Z, Y)), Plan(1, (C, Y), (C, Z, Y))]
+    plans = [Plan(0, (Y, Z), (Z, Y)), Plan(0, (Z, Y), (Z, Y)), Plan(1, (C, Y, Z), (C, Z, Y))]
     bf, f32 = jnp.bfloat16, jnp.float32
     group = QUERY_HEADS // KEY_VALUE_HEADS
     vmem = pl.BlockSpec(memory_space=pltpu.VMEM)
+    apart = pl.BlockSpec(memory_space=pl.ANY)
     dma = pltpu.SemaphoreType.DMA
     heads = (KEY_VALUE_HEADS, group * count, 2 * HEAD_SIZE)
-    levels, sends, recvs = Reduce.counts(plans[0])
-    out_levels, out_sends, out_recvs = Reduce.counts(plans[1])
+    blocks = [(count, kv_width // 2)] * 2 + [part.shape[1:]]
     return pl.pallas_call(
         functools.partial(attend_back_kernel, plans),
         out_shape=[
             jax.ShapeDtypeStruct((count, outputs.shape[1] + kv_width), bf),
             jax.ShapeDtypeStruct(mixed.shape, bf),
+            jax.ShapeDtypeStruct(mixed.shape, f32),
+            jax.ShapeDtypeStruct(mixed.shape, bf),
+            jax.ShapeDtypeStruct((3 * count, mixed.shape[1]), bf),
+            jax.ShapeDtypeStruct((3 * count, 128), bf),
         ],
-        in_specs=[vmem] * 5 + [pl.BlockSpec(memory_space=pl.ANY)] * 2 + [vmem] * 3,
-        out_specs=[vmem] * 2,
+        in_specs=[vmem] * 8 + [apart] * 2 + [vmem] * 3,
+        out_specs=[vmem] * 6,
         scratch_shapes=[
             pltpu.VMEM((count, kv_width), f32),
             pltpu.VMEM(heads, bf),
@@ -1172,20 +1220,19 @@
             pltpu.VMEM(keys.shape, bf),
             pltpu.VMEM(part.shape, bf),
             pltpu.VMEM(outputs.shape, bf),
-            pltpu.VMEM((w_o.shape[0], grad_attn.shape[1]), bf),
+            pltpu.VMEM(w_o.shape, bf),
         ]
-        + [pltpu.VMEM((n,) + keys.shape[1:], bf) for n in levels]
-        + [pltpu.VMEM((n,) + part.shape[1:], bf) for n in out_levels]
-        + [dma((n,)) for n in (sends, recvs, out_sends, out_recvs)]
+        + [pltpu.VMEM((n,) + b, bf) for p, b in zip(plans, blocks) for n in Reduce.counts(p)[0]]
+        + [dma((n,)) for p in plans for n in Reduce.counts(p)[1:]]
         + [dma(()), dma((NC * NZ,)), dma(())],
         compiler_params=pltpu.CompilerParams(
-            collective_id=collective_id, has_side_effects=True, vmem_limit_bytes=60 * 1024 * 1024
+            collective_id=collective_id, has_side_effects=True, vmem_limit_bytes=64 * 1024 * 1024
         ),
         name="attend_back",
-    )(placed, grad_attn, outputs, log_sums, keys, part, w_o, mixed, cosine, sine)
-
-
-def last_kernel(core_ref, own, core_part, x_part, both_part, one, two, small, *outs):
+    )(placed, gin, gate_map, cot, ffn_gain, outputs, log_sums, keys, part, w_o, mixed, cosine, sine)
+
+
+def last_kernel(core_ref, own, core_part, x_part, both_part, one, two, small, layer, grad, *outs):
     core = core_ref[0]
     in_out, out_out = outs[:2]
     split = in_out.shape[3]
@@ -1196,7 +1243,9 @@
 
     @pl.when(jnp.logical_and(pl.program_id(0) == 0, pl.program_id(1) == 0))
     def _():
-        wq, wk, wv, wo, router, first_gain, second_gain = outs[2:]
+        wq, wk, wv, wo, router, first_gain, second_gain, layer_out, grad_out = outs[2:]
+        layer_out[...] = layer[...]
+        grad_out[...] = grad[...]
         q, k = wq.shape[1], wk.shape[1]
         wq[...] = one[:, :q]
         wk[...] = one[:, q : q + k]
@@ -1211,23 +1260,24 @@
 
 def last_outputs(pieces, core, split, sums, widths):
     held, quarter, columns = pieces[0].shape
-    step = quarter // 2
+    step = quarter // 4
     rows = sums[0].shape[0]
     spec = pl.BlockSpec((1, step, columns), lambda e, r, c: (e, r, 0))
     fixed = lambda a, b: pl.BlockSpec((a, b), lambda e, r, c: (0, 0))
     outs = (split, columns - split)
-    shapes = [(rows, w) for w in widths] + [(1, rows)] * 2
+    shapes = [(rows, w) for w in widths] + [(1, rows)] * 2 + [a.shape for a in sums[3:]]
+    types = [jnp.float32] * 7 + [a.dtype for a in sums[3:]]
     return pl.pallas_call(
         last_kernel,
         grid_spec=pltpu.PrefetchScalarGridSpec(
             num_scalar_prefetch=1,
-            grid=(held, 2),
+            grid=(held, 4),
             in_specs=[spec] * 4 + [fixed(*a.shape) for a in sums],
             out_specs=[pl.BlockSpec((NC, 1, step, w), lambda e, r, c: (0, e, r, 0)) for w in outs]
             + [fixed(*s) for s in shapes],
         ),
         out_shape=[jax.ShapeDtypeStruct((NC, held, quarter, w), jnp.float32) for w in outs]
-        + [jax.ShapeDtypeStruct(s, jnp.float32) for s in shapes],
+        + [jax.ShapeDtypeStruct(s, d) for s, d in zip(shapes, types)],
         name="last_outputs",
     )(core[None], *pieces, *sums)
 
@@ -1704,11 +1754,11 @@
     )
     attn_gain, ffn_gain = gains[EXPERT_COUNT], gains[EXPERT_COUNT + 1]
 
-    attn_unit, inverse_one, attention_input = rms_forward(wide, attn_gain)
+    _, _, attention_input = rms_forward(wide, attn_gain)
     linear = jnp.dot(attention_input, one, preferred_element_type=f32)
     attention_output, log_sums, kv, cots, queries = attend(linear, cot, route, cosine, sine, 1)
     mixed = wide + jnp.dot(attention_output, output_w, preferred_element_type=f32)
-    ffn_unit, inverse_two, ffn_in = rms_forward(mixed, ffn_gain)
+    _, _, ffn_in = rms_forward(mixed, ffn_gain)
     logits = jnp.dot(ffn_in, router_w, preferred_element_type=f32)
     chosen = jnp.sum(indicator * logits[:, None, :], axis=-1)
     gates = jax.nn.softmax(chosen, axis=-1)
@@ -1718,42 +1768,38 @@
     )
     gin, moe_part, *pieces = moe(payload, cots, parts + others[-1:], CAP, 2)
     across = [swap(pieces[j], j) for j in range(1, NX * NC)]
-    grad_gate_map = gin[:, MODEL_WIDTH : MODEL_WIDTH + EXPERT_COUNT] + gin[
-        :, MODEL_WIDTH + EXPERT_COUNT : MODEL_WIDTH + 2 * EXPERT_COUNT
-    ]
-    grad_logits = (
-        gate_map * (grad_gate_map - jnp.sum(gate_map * grad_gate_map, axis=-1, keepdims=True))
-    ).astype(bf)
-    grad_ffn_in = gin[:, :MODEL_WIDTH] + lax.dot_general(
-        grad_logits, router_w, contract_cols, preferred_element_type=f32
-    )
-    back_two, _ = rms_backward(grad_ffn_in, ffn_unit, inverse_two, ffn_gain)
-    grad_mixed = cot + back_two
-    grad_attn = grad_mixed.astype(bf)
-    back, layer_out = attend_back(
-        queries, grad_attn, attention_output, log_sums, kv, moe_part, two, mixed, cosine, sine, 4
-    )
-    factor = grad_ffn_in * ffn_unit
-    high = factor.astype(bf)
-    low = (factor - high.astype(f32)).astype(bf)
-    column = jnp.broadcast_to((jnp.arange(128) == EXPERT_COUNT + 1).astype(bf), (tokens, 128))
-    logits_wide = jnp.concatenate([grad_logits, jnp.zeros((tokens, 128 - EXPERT_COUNT), bf)], axis=1)
+    gate_wide = jnp.concatenate([gate_map, jnp.zeros((tokens, 128 - EXPERT_COUNT), f32)], axis=1)
+    back, layer_out, grad_mixed, grad_attn, left_small, right_small = attend_back(
+        queries,
+        gin,
+        gate_wide,
+        cot,
+        ffn_gain.astype(f32)[None],
+        attention_output,
+        log_sums,
+        kv,
+        moe_part,
+        two,
+        mixed,
+        cosine,
+        sine,
+        4,
+    )
     *sums, grad_input = return_weights(
-        [attention_input, attention_output, jnp.concatenate([ffn_in, high, low])],
-        [back, grad_attn, jnp.concatenate([logits_wide, column, column])],
+        [attention_input, attention_output, left_small],
+        [back, grad_attn, right_small],
         one,
-        attn_unit,
-        inverse_one,
+        hidden[0],
         attn_gain.astype(f32)[None],
         grad_mixed,
         EXPERT_COUNT,
         5,
     )
-    grad_expert_in, grad_expert_out, *rest, first_gain, second_gain = last_outputs(
+    grad_expert_in, grad_expert_out, *rest, first_gain, second_gain, layer_out, grad_input = last_outputs(
         [pieces[0]] + across,
         core,
         2 * EXPERT_HIDDEN,
-        sums,
+        sums + [layer_out, grad_input],
         (q_width, kv_width, kv_width, MODEL_WIDTH, EXPERT_COUNT),
     )
     return (

time: 465 us -> 468 us (level)
  Pallas kernels: 423 us -> 432 us
  other arithmetic: 8.38 us -> 3.49 us
  transfers between devices with their start and end apart: 7 -> 7, of which waited for: 0 -> 0; matrix products, arithmetic and copies ran while one was open for 5% -> 4% of each run, Pallas kernels for 52% -> 53%
where the time goes in v11:
time: 468 us; the launch traced here: 461 us
  Pallas kernels  432 us (92%)
  matrix products  11.4 us (2%)
  local copies, waits for them, and re-layouts  8.06 us (2%)
  starting transfers between devices  5.04 us (1%)
    pallas_call x1, Pallas kernels, moe(): pl.pallas_call(functools.partial(moe_kernel, plans, back, width, hidden,...  116 us
    pallas_call x1, Pallas kernels, attend_back(): pl.pallas_call(functools.partial(attend_back_kernel, plans), out_shape=[j...  86.8 us
    pallas_call x1, Pallas kernels, return_weights(): pl.pallas_call(functools.partial(weights_kernel, plans, gain_at), out_sha...  81.7 us
    pallas_call x1, Pallas kernels, attend(): pl.pallas_call(functools.partial(attend_kernel, plans), out_shape=[jax.Sh...  76.6 us
    pallas_call x1, Pallas kernels, gather_weights(): pl.pallas_call(functools.partial(gather_kernel, plans), out_shape=[jax.Sh...  60 us
    pallas_call x1, Pallas kernels, last_outputs(): pl.pallas_call(last_kernel, grid_spec=pltpu.PrefetchScalarGridSpec(num_sc...  11 us
  transfers between devices with their start and end apart: 7, of which 0 were waited for; matrix products, arithmetic and copies ran while one was open for 4% of the time, Pallas kernels for 53%

profile of v11, /device:TPU:0, one launch (start us, length us, event | category | flops | bytes accessed | tf_op | source)
XLA Modules:
  0.0 461.0 jit_solution(3497250813675797755)
XLA Ops:
  0.6 1.4 copy.33.refs_4_
  2.0 0.0 copy-start
  2.0 0.0 copy-start.4
  2.0 60.0 %gather_weights.1 = (bf16[32,48,2560]{2,1,0:T(8,128)(2,1)}, bf16[32,48,1664]{2,1,0:T(8,128)(2,1)}, bf16[2,384,1536]{2,1,0:T(8,128)(2,1)}, bf16[1,384,1536]{2,1,0:T(8,128)(2,1)}, bf16[1,384,1536]{2,1,0:T(8,128)(2,1)}) custom-call(bf16[48,1536]{1,0:T(8,128)(2,1)} %refs_0_.1, bf16[48,512]{1,0:T(8,128)(2,1)} %refs_1_.1, bf16[48,512]{1,0:T(8,128)(2,1)} %refs_2_.1, ...), custom_call_target="tpu_custom_call" | custom-call | tf_op jit(solution)/shard_map/gather_weights/pallas_call | solution.py:223
  62.0 0.6 collective-permute-start.1
  62.7 0.5 collective-permute-start.3
  63.2 1.2 collective-permute-start
  64.4 0.2 collective-permute-start.2
  64.5 1.3 fusion.13
  65.8 0.6 slice_reduce_fusion
  66.4 0.0 copy-done
  66.4 0.0 copy-start.2
  66.4 0.2 fusion.5
  66.6 0.0 copy-start.5
  66.6 0.0 copy-done.4
  66.6 0.7 copy.34
  67.4 0.3 fusion.17
  67.7 0.8 pad_maximum_fusion
  68.5 5.6 %fusion.9.linear = f32[128,2560]{1,0:T(8,128)} fusion(bf16[1536,2560]{1,0:T(8,128)(2,1)} %bitcast.24, bf16[1,128,1536]{2,1,0:T(8,128)(2,1)S(1)} %copy-done, f32[1536]{0:T(1024)S(1)} %get-tuple-element.119, f32[128]{0:T(128)S(1)} %add_rsqrt_fusion.1), kind=kOutput, calls=%fused_computation.12 | convolution fusion | flops 1007419392 | bytes 9574912 | tf_op jit(solution)/shard_map/dot_general | solution.py:1758
  74.1 0.0 copy-done.2
  74.1 0.0 copy-done.5
  74.1 76.6 %attend.1 = (bf16[128,1536]{1,0:T(8,128)(2,1)}, f32[384,128]{1,0:T(8,128)}, bf16[8,128,1024]{2,1,0:T(8,128)(2,1)}, bf16[16,128,1664]{2,1,0:T(8,128)(2,1)}, bf16[8,384,128]{2,1,0:T(8,128)(2,1)}) custom-call(f32[128,2560]{1,0:T(8,128)} %fusion.9.linear, f32[128,1536]{1,0:T(8,128)} %bitcast.31, s32[128,8]{1,0:T(8,128)} %bitcast.33, ...), custom_call_target="tpu_custom_call" | custom-call | tf_op jit(solution)/shard_map/attend/pallas_call | solution.py:1024
  150.6 3.3 multiply_reduce_fusion
  154.0 0.0 copy-start.1
  154.0 0.9 copy-done.1
  154.9 0.1 multiply_convert_fusion
  155.0 1.3 fusion.11
  156.4 0.0 copy-start.3
  156.4 0.6 copy-done.3
  157.0 0.1 copy.37
  157.1 0.9 concatenate.14.refs_0_
  158.0 0.0 collective-permute-done.1.refs_4_
  158.0 0.0 collective-permute-done.2.refs_5_
  158.0 0.0 collective-permute-done.3.refs_6_
  158.0 0.0 collective-permute-done.refs_3_
  158.0 115.6 %experts.1 = (f32[128,1664]{1,0:T(8,128)}, bf16[16,128,1536]{2,1,0:T(8,128)(2,1)}, bf16[2,384,1536]{2,1,0:T(8,128)(2,1)}, bf16[2,384,1536]{2,1,0:T(8,128)(2,1)},...) custom-call(bf16[128,1664]{1,0:T(8,128)(2,1)} %concatenate.14.refs_0_, ...), custom_call_target="tpu_custom_call" | custom-call | tf_op jit(solution)/shard_map/experts/pallas_call | solution.py:730
  273.6 0.1 collective-permute-start.4
  273.7 2.4 collective-permute-start.5
  276.1 0.0 collective-permute-start.6
  276.1 0.8 copy.38
  277.0 0.6 concatenate.15.refs_2_
  277.6 1.9 fusion.7.refs_0_
  279.5 86.8 %attend_back.1 = (bf16[128,2560]{1,0:T(8,128)(2,1)}, bf16[128,1536]{1,0:T(8,128)(2,1)}, f32[128,1536]{1,0:T(8,128)}, bf16[128,1536]{1,0:T(8,128)(2,1)}, bf16[384...) custom-call(bf16[8,384,128]{2,1,0:T(8,128)(2,1)} %get-tuple-element.59.refs_0_, f32[128,1664]{1,0:T(8,128)} %get-tuple-element.60.refs_1_, ...), custom_call_target="tpu_custom_call" | custom-call | tf_op jit(solution)/shard_map/attend_back/pallas_call | solution.py:1203
  366.4 81.7 %return_weights.1 = (f32[48,2560]{1,0:T(8,128)}, f32[48,1536]{1,0:T(8,128)}, f32[48,128]{1,0:T(8,128)}, f32[128,1536]{1,0:T(8,128)}) custom-call(bf16[128,1536]{1,0:T(8,128)(2,1)} %fusion.7.refs_0_, bf16[128,2560]{1,0:T(8,128)(2,1)} %get-tuple-element.64.refs_1_, bf16[128,1536]{1,0:T(8,128)(2,1)} %get-tuple-element.50.refs_5_.refs_2_, ...), custom_call_target="tpu_custom_call" | custom-call | tf_op jit(solution)/shard_map/return_weights/pallas_call | solution.py:862
  448.1 0.0 collective-permute-done.4.core_part
  448.1 0.0 collective-permute-done.5.x_part
  448.1 0.0 collective-permute-done.6.both_part
  448.1 11.0 %last_outputs.1 = (f32[2,2,384,1024]{3,2,1,0:T(8,128)}, f32[2,2,384,512]{3,2,1,0:T(8,128)}, f32[48,1536]{1,0:T(8,128)}, f32[48,512]{1,0:T(8,128)}, f32[48,512]{1...) custom-call(s32[1]{0:T(128)} %bitcast.core_ref, ...), custom_call_target="tpu_custom_call" | custom-call | tf_op jit(solution)/shard_map/last_outputs/pallas_call | solution.py:1270
  459.2 1.4 copy.39
  (11 shorter events, 0.1 us)
Async XLA Ops:
  2.0 64.4 %copy-start = (bf16[1,128,1536]{2,1,0:T(8,128)(2,1)S(1)}, bf16[1,128,1536]{2,1,0:T(8,128)(2,1)}, u32[]{:S(2)}) copy-start(bf16[1,128,1536]{2,1,0:T(8,128)(2,1)} %param.12) | copy-start | bytes 1179652
  2.0 64.6 %copy-start.4 = (s32[1,128,8]{1,2,0:T(8,128)S(1)}, s32[1,128,8]{1,2,0:T(8,128)}, u32[]{:S(2)}) copy-start(s32[1,128,8]{1,2,0:T(8,128)} %param.13) | copy-start | bytes 12292
  62.0 96.0 %collective-permute-start.1 = (bf16[1,384,1536]{2,1,0:T(8,128)(2,1)}, bf16[1,384,1536]{2,1,0:T(8,128)(2,1)}, u32[]{:S(2)}, u32[]{:S(2)}) collective-permute-start(bf16[1,384,1536]{2,1,0:T(8,128)(2,1)} %get-tuple-element.53), channel_id=1, source_target_pairs={{0,1},{1,0},{2,3},{3,2},{4,5},{5,4},{6,7},{7,6},{8,9},{9,8},{10,11... | collective-permute-start | bytes 3538952 | tf_op jit(solution)/shard_map/ppermute | solution.py:1694
  62.7 95.4 %collective-permute-start.3 = (bf16[1,384,1536]{2,1,0:T(8,128)(2,1)}, bf16[1,384,1536]{2,1,0:T(8,128)(2,1)}, u32[]{:S(2)}, u32[]{:S(2)}) collective-permute-start(bf16[1,384,1536]{2,1,0:T(8,128)(2,1)} %get-tuple-element.53), channel_id=1, source_target_pairs={{0,3},{1,2},{2,1},{3,0},{4,7},{5,6},{6,5},{7,4},{8,11},{9,10},{10,... | collective-permute-start | bytes 3538952 | tf_op jit(solution)/shard_map/ppermute | solution.py:1694
  63.2 94.9 %collective-permute-start = (bf16[2,384,1536]{2,1,0:T(8,128)(2,1)}, bf16[2,384,1536]{2,1,0:T(8,128)(2,1)}, u32[]{:S(2)}, u32[]{:S(2)}) collective-permute-start(bf16[2,384,1536]{2,1,0:T(8,128)(2,1)} %get-tuple-element.52.refs_2_), channel_id=1, source_target_pairs={{0,2},{1,3},{2,0},{3,1},{4,6},{5,7},{6,4},{7,5},{8,10},{9,11},{10,... | collective-permute-start | bytes 7077896 | tf_op jit(solution)/shard_map/ppermute | solution.py:1694
  64.4 93.6 %collective-permute-start.2 = (bf16[1,384,1536]{2,1,0:T(8,128)(2,1)}, bf16[1,384,1536]{2,1,0:T(8,128)(2,1)}, u32[]{:S(2)}, u32[]{:S(2)}) collective-permute-start(bf16[1,384,1536]{2,1,0:T(8,128)(2,1)} %get-tuple-element.54.refs_7_), channel_id=1, source_target_pairs={{0,1},{1,0},{2,3},{3,2},{4,5},{5,4},{6,7},{7,6},{8,9},{9,8},{10,11... | collective-permute-start | bytes 3538952 | tf_op jit(solution)/shard_map/ppermute | solution.py:1694
  66.4 7.7 %copy-start.2 = (f32[1536]{0:T(1024)}, f32[1536]{0:T(1024)S(1)}, u32[]{:S(2)}) copy-start(f32[1536]{0:T(1024)S(1)} %get-tuple-element.119) | copy-start | bytes 18436
  66.6 7.5 %copy-start.5 = (f32[128]{0:T(128)}, f32[128]{0:T(128)S(1)}, u32[]{:S(2)}) copy-start(f32[128]{0:T(128)S(1)} %add_rsqrt_fusion.1) | copy-start | bytes 1540
  154.0 0.9 copy-start.1
  156.4 0.6 copy-start.3
  273.6 174.5 %collective-permute-start.4 = (bf16[2,384,1536]{2,1,0:T(8,128)(2,1)}, bf16[2,384,1536]{2,1,0:T(8,128)(2,1)}, u32[]{:S(2)}, u32[]{:S(2)}) collective-permute-start(bf16[2,384,1536]{2,1,0:T(8,128)(2,1)} %get-tuple-element.56), channel_id=1, source_target_pairs={{0,1},{1,0},{2,3},{3,2},{4,5},{5,4},{6,7},{7,6},{8,9},{9,8},{10,11... | collective-permute-start | bytes 7077896 | tf_op jit(solution)/shard_map/ppermute | solution.py:1694
  273.7 174.4 %collective-permute-start.5 = (bf16[2,384,1536]{2,1,0:T(8,128)(2,1)}, bf16[2,384,1536]{2,1,0:T(8,128)(2,1)}, u32[]{:S(2)}, u32[]{:S(2)}) collective-permute-start(bf16[2,384,1536]{2,1,0:T(8,128)(2,1)} %get-tuple-element.57), channel_id=1, source_target_pairs={{0,2},{1,3},{2,0},{3,1},{4,6},{5,7},{6,4},{7,5},{8,10},{9,11},{10,... | collective-permute-start | bytes 7077896 | tf_op jit(solution)/shard_map/ppermute | solution.py:1694
  276.1 172.0 %collective-permute-start.6 = (bf16[2,384,1536]{2,1,0:T(8,128)(2,1)}, bf16[2,384,1536]{2,1,0:T(8,128)(2,1)}, u32[]{:S(2)}, u32[]{:S(2)}) collective-permute-start(bf16[2,384,1536]{2,1,0:T(8,128)(2,1)} %get-tuple-element.58), channel_id=1, source_target_pairs={{0,3},{1,2},{2,1},{3,0},{4,7},{5,6},{6,5},{7,4},{8,11},{9,10},{10,... | collective-permute-start | bytes 7077896 | tf_op jit(solution)/shard_map/ppermute | solution.py:1694
